TPU v7x, 32 devices: a whole 2x2x4 slice. The times are simulated.
32 devices in a mesh: patch: 4 (over y, x), hid: 8 (over z, core).
Axes of the slice: x: 2, y: 2, z: 4, core: 2. Of those that a mesh axis runs over, the one named last changes fastest.
Arguments:
- frames: bfloat16 [4, 2, 16, 64, 512], P(None, None, 'patch', None, 'hid'), may hold values from -6 to 6
- hidden_start: bfloat16 [2, 16, 64, 512], P(None, 'patch', None, 'hid'), may hold values from -4 to 4
- cell_start: float32 [2, 16, 64, 512], P(None, 'patch', None, 'hid'), may hold values from -6 to 6
- input_weight: bfloat16 [3, 3, 512, 4, 512], P(None, None, None, None, 'hid'), may hold values from -0.09375 to 0.09375
- hidden_weight: bfloat16 [3, 3, 512, 4, 512], P(None, None, None, None, 'hid'), may hold values from -0.09375 to 0.09375
- gate_bias: float32 [4, 512], P(None, 'hid'), may hold values from -3 to 3
- first_weight: bfloat16 [3, 3, 512, 512], replicated, may hold values from -0.09375 to 0.09375
- first_bias: float32 [512], replicated, may hold values from -3 to 3
- second_weight: bfloat16 [3, 3, 512, 512], replicated, may hold values from -0.09375 to 0.09375
- second_bias: float32 [512], replicated, may hold values from -3 to 3
Outputs:
- decoded: bfloat16 [2, 16, 64, 512], P(None, 'patch', 'hid')
- cell_final: float32 [2, 16, 64, 512], P(None, 'patch', None, 'hid')
All inputs are finite; a program needn't handle non-finite values.
Results may differ from a plain program's by a relative error of at most 0.0045.
Values may be sent and summed in bfloat16 or wider, within the bound.
No kernel may reach another device: no remote copies, remote signals or barrier semaphores. Data moves between devices by JAX's collectives and lax.ppermute only.
A program may use at most 128 MiB of HBM per device.

v0:
```python
import jax
import jax.numpy as jnp
from jax import lax
from jax.sharding import PartitionSpec as P

STEPS = 4


FORGET_BIAS = 1.0


def extended_2(block, sides, width):
    for axis, dim in sides:
        count = lax.axis_size(axis)
        forward = [(i, i + 1) for i in range(count - 1)]
        backward = [(target, source) for source, target in forward]
        low = lax.ppermute(
            lax.slice_in_dim(block, block.shape[dim] - width, None, axis=dim), axis, forward
        )
        high = lax.ppermute(lax.slice_in_dim(block, 0, width, axis=dim), axis, backward)
        block = jnp.concatenate([low, block, high], axis=dim)
    return block


def conv_taps(padded, weight):
    batch_count, padded_rows, padded_cols, channel_count = padded.shape
    row_count = padded_rows - 2
    col_count = padded_cols - 2
    summed = jnp.zeros((batch_count * row_count * col_count, weight.shape[-1]), jnp.float32)
    for tap_row in range(3):
        for tap_col in range(3):
            window = padded[:, tap_row : tap_row + row_count, tap_col : tap_col + col_count, :]
            summed = summed + jnp.dot(
                window.reshape(-1, channel_count),
                weight[tap_row, tap_col],
                preferred_element_type=jnp.float32,
            )
    return summed.reshape(batch_count, row_count, col_count, weight.shape[-1])


def lstm_update(gates, cell):
    shaped = gates.reshape(gates.shape[:-1] + (4, gates.shape[-1] // 4))
    input_gate = jax.nn.sigmoid(shaped[..., 0, :])
    forget_gate = jax.nn.sigmoid(shaped[..., 1, :] + FORGET_BIAS)
    candidate = jnp.tanh(shaped[..., 2, :])
    output_gate = jax.nn.sigmoid(shaped[..., 3, :])
    cell = forget_gate * cell + input_gate * candidate
    hidden = (output_gate * jnp.tanh(cell)).astype(jnp.bfloat16)
    return (hidden, cell)


def pad_columns(image):
    return jnp.pad(image, ((0, 0), (0, 0), (1, 1), (0, 0)))


def per_device(
    frames,
    hidden_start,
    cell_start,
    input_weight,
    hidden_weight,
    gate_bias,
    first_weight,
    first_bias,
    second_weight,
    second_bias,
):
    local_gates = 4 * input_weight.shape[-1]
    wide_input = input_weight.reshape(3, 3, input_weight.shape[2], local_gates)
    wide_hidden = hidden_weight.reshape(3, 3, hidden_weight.shape[2], local_gates)
    bias_row = gate_bias.reshape(-1)
    all_frames = lax.all_gather(frames, "hid", axis=4, tiled=True)
    framed = extended_2(all_frames, (("patch", 2),), 1)
    hidden = hidden_start
    cell = cell_start
    for time_index in range(STEPS):
        gathered = lax.all_gather(hidden, "hid", axis=3, tiled=True)
        rimmed = extended_2(gathered, (("patch", 1),), 1)
        gates = (
            conv_taps(pad_columns(framed[time_index]), wide_input)
            + conv_taps(pad_columns(rimmed), wide_hidden)
            + bias_row
        )
        hidden, cell = lstm_update(gates, cell)
    tiled = lax.all_to_all(hidden, "hid", split_axis=2, concat_axis=3, tiled=True)
    outer = extended_2(tiled, (("patch", 1), ("hid", 2)), 2)
    extended = jax.nn.silu(conv_taps(outer, first_weight) + first_bias)
    tile_rows = tiled.shape[1]
    tile_cols = tiled.shape[2]
    row_place = lax.axis_index("patch") * tile_rows + jnp.arange(tile_rows + 2, dtype=jnp.int32) - 1
    col_place = lax.axis_index("hid") * tile_cols + jnp.arange(tile_cols + 2, dtype=jnp.int32) - 1
    row_inside = (row_place >= 0) & (row_place < tile_rows * lax.axis_size("patch"))
    col_inside = (col_place >= 0) & (col_place < tile_cols * lax.axis_size("hid"))
    inside = row_inside[:, None] & col_inside[None, :]
    middle_rimmed = jnp.where(inside[None, :, :, None], extended, 0.0).astype(jnp.bfloat16)
    decoded = (conv_taps(middle_rimmed, second_weight) + second_bias).astype(jnp.bfloat16)
    return (decoded, cell)


def solution(mesh):
    return jax.shard_map(
        per_device,
        mesh=mesh,
        in_specs=(
            P(None, None, "patch", None, "hid"),
            P(None, "patch", None, "hid"),
            P(None, "patch", None, "hid"),
            P(None, None, None, None, "hid"),
            P(None, None, None, None, "hid"),
            P(None, "hid"),
            P(),
            P(),
            P(),
            P(),
        ),
        out_specs=(P(None, "patch", "hid", None), P(None, "patch", None, "hid")),
        check_vma=False,
    )
```

profile of v0, /device:TPU:10, one launch (start us, length us, event | category | flops | bytes accessed | tf_op | source)
XLA Modules:
  0.0 303.0 jit_solution(3378548768735336446)
XLA Ops:
  7.2 2.6 copy.31
  10.9 20.4 %all_gather.16 = bf16[2,4,64,512]{2,1,0,3:T(4,128)(2,1)S(1)} all-gather(bf16[2,4,64,64]{2,1,0,3:T(4,128)(2,1)S(1)} %copy.35), channel_id=1, replica_groups=mesh['patch'=4,'hid'=8] {'hid'}, dimensions={3}, use_global_device_ids=true | all-gather | bytes 589824 | tf_op jit(solution)/shard_map/all_gather | solution.py:77
  32.2 2.4 collective-permute-start.3
  34.7 4.3 %collective-permute-start.2 = (bf16[2,1,64,512]{3,2,1,0:T(8,128)(2,1)S(1)}, bf16[2,1,64,512]{3,2,1,0:T(8,128)(2,1)S(1)}, u32[]{:S(2)}, u32[]{:S(2)}) collective-permute-start(bf16[2,1,64,512]{3,2,1,0:T(8,128)(2,1)S(1)} %get-tuple-element.94), channel_id=1, source_target_pairs={{0,8},{8,16},{16,24},{1,9},{9,17},{17,25},{2,10},{10,18},{18,26},{... | collective-permute-start | bytes 393224 | tf_op jit(solution)/shard_map/ppermute | solution.py:17
  47.0 13.5 %all-gather.2.cloned.1.call-done = bf16[4,2,4,64,512]{3,2,1,0,4:T(4,128)(2,1)} async-done(((bf16[4,2,4,64,64]{3,2,1,0,4:T(4,128)(2,1)}), bf16[4,2,4,64,512]{3,2,1,0,4:T(4,128)(2,1)}) %all-gather.2.cloned.1.call-update) | async-done | bytes 2097168 | tf_op jit(solution)/shard_map/all_gather | solution.py:72
  60.5 6.9 %copy.32 = bf16[4,2,4,64,512]{4,3,2,1,0:T(8,128)(2,1)} copy(bf16[4,2,4,64,512]{3,2,1,0,4:T(4,128)(2,1)} %all-gather.2.cloned.1.call-done) | data formatting | bytes 4194304 | tf_op jit(solution)/shard_map/all_gather | solution.py:72
  68.9 2.4 collective-permute-start.1
  71.3 4.8 %collective-permute-start = (bf16[4,2,1,64,512]{4,3,2,1,0:T(8,128)(2,1)S(1)}, bf16[4,2,1,64,512]{4,3,2,1,0:T(8,128)(2,1)S(1)}, u32[]{:S(2)}, u32[]{:S(2)}) collective-permute-start(bf16[4,2,1,64,512]{4,3,2,1,0:T(8,128)(2,1)S(1)} %get-tuple-element.18), channel_id=1, source_target_pairs={{0,8},{8,16},{16,24},{1,9},{9,17},{17,25},{2,10},{10,18},{18,26},{... | collective-permute-start | bytes 1572872 | tf_op jit(solution)/shard_map/ppermute | solution.py:17
  77.9 8.6 %collective-permute-done.1 = bf16[4,2,1,64,512]{4,3,2,1,0:T(8,128)(2,1)S(1)} collective-permute-done((bf16[4,2,1,64,512]{4,3,2,1,0:T(8,128)(2,1)S(1)}, bf16[4,2,1,64,512]{4,3,2,1,0:T(8,128)(2,1)S(1)}, u32[]{:S(2)}, u32[]{:S(2)}) %collective-permute-start.1) | collective-permute-done | bytes 524320 | tf_op jit(solution)/shard_map/ppermute | solution.py:20
  86.4 7.7 %collective-permute-done = bf16[4,2,1,64,512]{4,3,2,1,0:T(8,128)(2,1)S(1)} collective-permute-done((bf16[4,2,1,64,512]{4,3,2,1,0:T(8,128)(2,1)S(1)}, bf16[4,2,1,64,512]{4,3,2,1,0:T(8,128)(2,1)S(1)}, u32[]{:S(2)}, u32[]{:S(2)}) %collective-permute-start) | collective-permute-done | bytes 524320 | tf_op jit(solution)/shard_map/ppermute | solution.py:17
  94.8 4.3 %pad_slice_fusion.12 = (bf16[2,4,64,512]{3,2,1,0:T(8,128)(2,1)}, bf16[2,4,64,512]{3,2,1,0:T(8,128)(2,1)}, bf16[2,4,64,512]{3,2,1,0:T(8,128)(2,1)}, bf16[2,4,64,5...) fusion(bf16[2,6,64,512]{3,2,1,0:T(8,128)(2,1)S(1)} %get-tuple-e, ...), kind=kLoop, calls=%fused_computation.121 | loop fusion | bytes 14155776 | tf_op jit(solution)/shard_map/slice | solution.py:32
  101.4 4.5 %pad_slice_fusion = (bf16[2,4,64,512]{3,2,1,0:T(8,128)(2,1)S(1)}, bf16[2,4,64,512]{3,2,1,0:T(8,128)(2,1)S(1)}, bf16[2,4,64,512]{3,2,1,0:T(8,128)(2,1)S(1)}, bf16...) fusion(bf16[2,6,64,512]{3,2,1,0:T(8,128)(2,1)S(1)} %get-tuple-e, ...), kind=kLoop, calls=%fused_computation.109 | loop fusion | bytes 14155776 | tf_op jit(solution)/shard_map/slice | solution.py:32
  114.8 2.2 fusion.120
  117.0 16.5 %all_gather.17 = bf16[2,4,64,512]{2,1,0,3:T(4,128)(2,1)} all-gather(bf16[2,4,64,64]{2,1,0,3:T(4,128)(2,1)S(1)} %get-tuple-element.12), channel_id=1, replica_groups=mesh['patch'=4,'hid'=8] {'hid'}, dimensions={3}, use_global_device_ids=true | all-gather | bytes 589824 | tf_op jit(solution)/shard_map/all_gather | solution.py:77
  135.1 2.1 collective-permute-start.5
  137.2 5.5 %collective-permute-start.4 = (bf16[2,1,64,512]{3,2,1,0:T(8,128)(2,1)S(1)}, bf16[2,1,64,512]{3,2,1,0:T(8,128)(2,1)S(1)}, u32[]{:S(2)}, u32[]{:S(2)}) collective-permute-start(bf16[2,1,64,512]{3,2,1,0:T(8,128)(2,1)S(1)} %get-tuple-element.90), channel_id=1, source_target_pairs={{0,8},{8,16},{16,24},{1,9},{9,17},{17,25},{2,10},{10,18},{18,26},{... | collective-permute-start | bytes 393224 | tf_op jit(solution)/shard_map/ppermute | solution.py:17
  161.9 2.3 fusion.121
  164.2 17.7 %all_gather.18 = bf16[2,4,64,512]{2,1,0,3:T(4,128)(2,1)} all-gather(bf16[2,4,64,64]{2,1,0,3:T(4,128)(2,1)S(1)} %get-tuple-element.10), channel_id=1, replica_groups=mesh['patch'=4,'hid'=8] {'hid'}, dimensions={3}, use_global_device_ids=true | all-gather | bytes 589824 | tf_op jit(solution)/shard_map/all_gather | solution.py:77
  183.5 1.9 collective-permute-start.7
  185.4 5.0 %collective-permute-start.6 = (bf16[2,1,64,512]{3,2,1,0:T(8,128)(2,1)S(1)}, bf16[2,1,64,512]{3,2,1,0:T(8,128)(2,1)S(1)}, u32[]{:S(2)}, u32[]{:S(2)}) collective-permute-start(bf16[2,1,64,512]{3,2,1,0:T(8,128)(2,1)S(1)} %get-tuple-element.86), channel_id=1, source_target_pairs={{0,8},{8,16},{16,24},{1,9},{9,17},{17,25},{2,10},{10,18},{18,26},{... | collective-permute-start | bytes 393224 | tf_op jit(solution)/shard_map/ppermute | solution.py:17
  201.6 2.3 fusion.122
  203.9 17.1 %all_gather.19 = bf16[2,4,64,512]{2,1,0,3:T(4,128)(2,1)} all-gather(bf16[2,4,64,64]{2,1,0,3:T(4,128)(2,1)S(1)} %get-tuple-element.8), channel_id=1, replica_groups=mesh['patch'=4,'hid'=8] {'hid'}, dimensions={3}, use_global_device_ids=true | all-gather | bytes 589824 | tf_op jit(solution)/shard_map/all_gather | solution.py:77
  222.6 1.9 collective-permute-start.9
  224.6 5.3 %collective-permute-start.8 = (bf16[2,1,64,512]{3,2,1,0:T(8,128)(2,1)S(1)}, bf16[2,1,64,512]{3,2,1,0:T(8,128)(2,1)S(1)}, u32[]{:S(2)}, u32[]{:S(2)}) collective-permute-start(bf16[2,1,64,512]{3,2,1,0:T(8,128)(2,1)S(1)} %get-tuple-element.82), channel_id=1, source_target_pairs={{0,8},{8,16},{16,24},{1,9},{9,17},{17,25},{2,10},{10,18},{18,26},{... | collective-permute-start | bytes 393224 | tf_op jit(solution)/shard_map/ppermute | solution.py:17
  241.1 5.7 %all-to-all-start = ((bf16[8,2,2048]{2,1,0:T(2,128)(2,1)}), bf16[8,2,2048]{2,1,0:T(2,128)(2,1)S(1)}, u32[]{:S(2)}, u32[]{:S(2)}) async-start(bf16[8,2,2048]{2,1,0:T(2,128)(2,1)} %reshape.550), calls=%async_computation | async-start | bytes 131072 | tf_op jit(solution)/shard_map/all_to_all | solution.py:85
  246.9 4.7 %all-to-all-done = bf16[8,2,2048]{2,1,0:T(2,128)(2,1)S(1)} async-done(((bf16[8,2,2048]{2,1,0:T(2,128)(2,1)}), bf16[8,2,2048]{2,1,0:T(2,128)(2,1)S(1)}, u32[]{:S(2)}, u32[]{:S(2)}) %all-to-all-start) | async-done | bytes 65568 | tf_op jit(solution)/shard_map/all_to_all | solution.py:85
  251.9 5.3 %collective-permute-start.10 = (bf16[2,2,8,512]{3,2,1,0:T(8,128)(2,1)S(1)}, bf16[2,2,8,512]{3,2,1,0:T(8,128)(2,1)S(1)}, u32[]{:S(2)}, u32[]{:S(2)}) collective-permute-start(bf16[2,2,8,512]{3,2,1,0:T(8,128)(2,1)S(1)} %get-tuple-element.120), channel_id=1, source_target_pairs={{0,8},{8,16},{16,24},{1,9},{9,17},{17,25},{2,10},{10,18},{18,26},{... | collective-permute-start | bytes 98312 | tf_op jit(solution)/shard_map/ppermute | solution.py:17
  257.2 1.9 collective-permute-start.11
  259.2 4.7 %collective-permute-done.11 = bf16[2,2,8,512]{3,2,1,0:T(8,128)(2,1)S(1)} collective-permute-done((bf16[2,2,8,512]{3,2,1,0:T(8,128)(2,1)S(1)}, bf16[2,2,8,512]{3,2,1,0:T(8,128)(2,1)S(1)}, u32[]{:S(2)}, u32[]{:S(2)}) %collective-permute-start.11) | collective-permute-done | bytes 32800 | tf_op jit(solution)/shard_map/ppermute | solution.py:20
  264.0 1.9 collective-permute-start.13
  265.9 2.7 collective-permute-start.12
  269.5 1.6 collective-permute-done.12
  (244 shorter events, 96.5 us)
Async XLA Ops:
  7.2 31.8 %copy-start.33 = (f32[2,4,64,64]{3,2,1,0:T(8,128)S(1)}, f32[2,4,64,64]{3,2,1,0:T(8,128)}, u32[]{:S(2)}) copy-start(f32[2,4,64,64]{3,2,1,0:T(8,128)} %param.12) | copy-start | bytes 393220
  7.2 53.3 %all-gather.2.cloned.1.call-start = ((), (), s32[]{:S(2)}) async-start(), calls=%async_computation.1 | async-start | bytes 4718592 | tf_op jit(solution)/shard_map/all_gather | solution.py:72
  32.2 9.1 %collective-permute-start.3 = (bf16[2,1,64,512]{3,2,1,0:T(8,128)(2,1)S(1)}, bf16[2,1,64,512]{3,2,1,0:T(8,128)(2,1)S(1)}, u32[]{:S(2)}, u32[]{:S(2)}) collective-permute-start(bf16[2,1,64,512]{3,2,1,0:T(8,128)(2,1)S(1)} %get-tuple-element.95), channel_id=1, source_target_pairs={{8,0},{16,8},{24,16},{9,1},{17,9},{25,17},{10,2},{18,10},{26,18},{... | collective-permute-start | bytes 393224 | tf_op jit(solution)/shard_map/ppermute | solution.py:20
  34.7 7.4 %collective-permute-start.2 = (bf16[2,1,64,512]{3,2,1,0:T(8,128)(2,1)S(1)}, bf16[2,1,64,512]{3,2,1,0:T(8,128)(2,1)S(1)}, u32[]{:S(2)}, u32[]{:S(2)}) collective-permute-start(bf16[2,1,64,512]{3,2,1,0:T(8,128)(2,1)S(1)} %get-tuple-element.94), channel_id=1, source_target_pairs={{0,8},{8,16},{16,24},{1,9},{9,17},{17,25},{2,10},{10,18},{18,26},{... | collective-permute-start | bytes 393224 | tf_op jit(solution)/shard_map/ppermute | solution.py:17
  67.4 26.7 %copy-start.5 = (bf16[4,2,4,64,512]{4,3,2,1,0:T(8,128)(2,1)S(1)}, bf16[4,2,4,64,512]{4,3,2,1,0:T(8,128)(2,1)}, u32[]{:S(2)}) copy-start(bf16[4,2,4,64,512]{4,3,2,1,0:T(8,128)(2,1)} %copy.32) | copy-start | bytes 6291460
  68.9 17.6 %collective-permute-start.1 = (bf16[4,2,1,64,512]{4,3,2,1,0:T(8,128)(2,1)S(1)}, bf16[4,2,1,64,512]{4,3,2,1,0:T(8,128)(2,1)S(1)}, u32[]{:S(2)}, u32[]{:S(2)}) collective-permute-start(bf16[4,2,1,64,512]{4,3,2,1,0:T(8,128)(2,1)S(1)} %get-tuple-element.19), channel_id=1, source_target_pairs={{8,0},{16,8},{24,16},{9,1},{17,9},{25,17},{10,2},{18,10},{26,18},{... | collective-permute-start | bytes 1572872 | tf_op jit(solution)/shard_map/ppermute | solution.py:20
  71.3 22.8 %collective-permute-start = (bf16[4,2,1,64,512]{4,3,2,1,0:T(8,128)(2,1)S(1)}, bf16[4,2,1,64,512]{4,3,2,1,0:T(8,128)(2,1)S(1)}, u32[]{:S(2)}, u32[]{:S(2)}) collective-permute-start(bf16[4,2,1,64,512]{4,3,2,1,0:T(8,128)(2,1)S(1)} %get-tuple-element.18), channel_id=1, source_target_pairs={{0,8},{8,16},{16,24},{1,9},{9,17},{17,25},{2,10},{10,18},{18,26},{... | collective-permute-start | bytes 1572872 | tf_op jit(solution)/shard_map/ppermute | solution.py:17
  94.8 4.3 %copy-start = (bf16[3,3,512,4,64]{2,4,3,1,0:T(8,128)(2,1)S(1)}, bf16[3,3,512,4,64]{2,4,3,1,0:T(8,128)(2,1)}, u32[]{:S(2)}) copy-start(bf16[3,3,512,4,64]{2,4,3,1,0:T(8,128)(2,1)} %param.13) | copy-start | bytes 7077892
  111.4 3.0 copy-start.34
  117.0 27.3 %copy-start.28 = (bf16[2,4,64,512]{3,2,1,0:T(8,128)(2,1)S(1)}, bf16[2,4,64,512]{3,2,1,0:T(8,128)(2,1)}, u32[]{:S(2)}) copy-start(bf16[2,4,64,512]{3,2,1,0:T(8,128)(2,1)} %get-tuple-element.137) | copy-start | bytes 1572868
  135.1 9.5 %copy-start.27 = (bf16[2,4,64,512]{3,2,1,0:T(8,128)(2,1)S(1)}, bf16[2,4,64,512]{3,2,1,0:T(8,128)(2,1)}, u32[]{:S(2)}) copy-start(bf16[2,4,64,512]{3,2,1,0:T(8,128)(2,1)} %get-tuple-element.136) | copy-start | bytes 1572868
  135.1 18.4 %collective-permute-start.5 = (bf16[2,1,64,512]{3,2,1,0:T(8,128)(2,1)S(1)}, bf16[2,1,64,512]{3,2,1,0:T(8,128)(2,1)S(1)}, u32[]{:S(2)}, u32[]{:S(2)}) collective-permute-start(bf16[2,1,64,512]{3,2,1,0:T(8,128)(2,1)S(1)} %get-tuple-element.91), channel_id=1, source_target_pairs={{8,0},{16,8},{24,16},{9,1},{17,9},{25,17},{10,2},{18,10},{26,18},{... | collective-permute-start | bytes 393224 | tf_op jit(solution)/shard_map/ppermute | solution.py:20
  137.2 16.3 %collective-permute-start.4 = (bf16[2,1,64,512]{3,2,1,0:T(8,128)(2,1)S(1)}, bf16[2,1,64,512]{3,2,1,0:T(8,128)(2,1)S(1)}, u32[]{:S(2)}, u32[]{:S(2)}) collective-permute-start(bf16[2,1,64,512]{3,2,1,0:T(8,128)(2,1)S(1)} %get-tuple-element.90), channel_id=1, source_target_pairs={{0,8},{8,16},{16,24},{1,9},{9,17},{17,25},{2,10},{10,18},{18,26},{... | collective-permute-start | bytes 393224 | tf_op jit(solution)/shard_map/ppermute | solution.py:17
  142.7 2.3 copy-start.26
  145.4 1.9 copy-start.18
  145.4 1.9 copy-start.29
  148.7 1.9 copy-start.25
  148.7 1.9 copy-start.30
  149.1 1.9 copy-start.23
  161.9 28.5 %copy-start.7 = (bf16[2,4,64,512]{3,2,1,0:T(8,128)(2,1)S(1)}, bf16[2,4,64,512]{3,2,1,0:T(8,128)(2,1)}, u32[]{:S(2)}) copy-start(bf16[2,4,64,512]{3,2,1,0:T(8,128)(2,1)} %get-tuple-element.62) | copy-start | bytes 1572868
  183.5 8.9 %collective-permute-start.7 = (bf16[2,1,64,512]{3,2,1,0:T(8,128)(2,1)S(1)}, bf16[2,1,64,512]{3,2,1,0:T(8,128)(2,1)S(1)}, u32[]{:S(2)}, u32[]{:S(2)}) collective-permute-start(bf16[2,1,64,512]{3,2,1,0:T(8,128)(2,1)S(1)} %get-tuple-element.87), channel_id=1, source_target_pairs={{8,0},{16,8},{24,16},{9,1},{17,9},{25,17},{10,2},{18,10},{26,18},{... | collective-permute-start | bytes 393224 | tf_op jit(solution)/shard_map/ppermute | solution.py:20
  185.4 7.8 %collective-permute-start.6 = (bf16[2,1,64,512]{3,2,1,0:T(8,128)(2,1)S(1)}, bf16[2,1,64,512]{3,2,1,0:T(8,128)(2,1)S(1)}, u32[]{:S(2)}, u32[]{:S(2)}) collective-permute-start(bf16[2,1,64,512]{3,2,1,0:T(8,128)(2,1)S(1)} %get-tuple-element.86), channel_id=1, source_target_pairs={{0,8},{8,16},{16,24},{1,9},{9,17},{17,25},{2,10},{10,18},{18,26},{... | collective-permute-start | bytes 393224 | tf_op jit(solution)/shard_map/ppermute | solution.py:17
  201.6 28.3 %copy-start.6 = (bf16[2,4,64,512]{3,2,1,0:T(8,128)(2,1)S(1)}, bf16[2,4,64,512]{3,2,1,0:T(8,128)(2,1)}, u32[]{:S(2)}) copy-start(bf16[2,4,64,512]{3,2,1,0:T(8,128)(2,1)} %get-tuple-element.138) | copy-start | bytes 1572868
  222.6 9.3 %collective-permute-start.9 = (bf16[2,1,64,512]{3,2,1,0:T(8,128)(2,1)S(1)}, bf16[2,1,64,512]{3,2,1,0:T(8,128)(2,1)S(1)}, u32[]{:S(2)}, u32[]{:S(2)}) collective-permute-start(bf16[2,1,64,512]{3,2,1,0:T(8,128)(2,1)S(1)} %get-tuple-element.83), channel_id=1, source_target_pairs={{8,0},{16,8},{24,16},{9,1},{17,9},{25,17},{10,2},{18,10},{26,18},{... | collective-permute-start | bytes 393224 | tf_op jit(solution)/shard_map/ppermute | solution.py:20
  224.6 8.6 %collective-permute-start.8 = (bf16[2,1,64,512]{3,2,1,0:T(8,128)(2,1)S(1)}, bf16[2,1,64,512]{3,2,1,0:T(8,128)(2,1)S(1)}, u32[]{:S(2)}, u32[]{:S(2)}) collective-permute-start(bf16[2,1,64,512]{3,2,1,0:T(8,128)(2,1)S(1)} %get-tuple-element.82), channel_id=1, source_target_pairs={{0,8},{8,16},{16,24},{1,9},{9,17},{17,25},{2,10},{10,18},{18,26},{... | collective-permute-start | bytes 393224 | tf_op jit(solution)/shard_map/ppermute | solution.py:17
  241.1 10.4 %all-to-all-start = ((bf16[8,2,2048]{2,1,0:T(2,128)(2,1)}), bf16[8,2,2048]{2,1,0:T(2,128)(2,1)S(1)}, u32[]{:S(2)}, u32[]{:S(2)}) async-start(bf16[8,2,2048]{2,1,0:T(2,128)(2,1)} %reshape.550), calls=%async_computation | async-start | bytes 131072 | tf_op jit(solution)/shard_map/all_to_all | solution.py:85
  251.9 7.2 %collective-permute-start.10 = (bf16[2,2,8,512]{3,2,1,0:T(8,128)(2,1)S(1)}, bf16[2,2,8,512]{3,2,1,0:T(8,128)(2,1)S(1)}, u32[]{:S(2)}, u32[]{:S(2)}) collective-permute-start(bf16[2,2,8,512]{3,2,1,0:T(8,128)(2,1)S(1)} %get-tuple-element.120), channel_id=1, source_target_pairs={{0,8},{8,16},{16,24},{1,9},{9,17},{17,25},{2,10},{10,18},{18,26},{... | collective-permute-start | bytes 98312 | tf_op jit(solution)/shard_map/ppermute | solution.py:17
  257.2 6.7 %collective-permute-start.11 = (bf16[2,2,8,512]{3,2,1,0:T(8,128)(2,1)S(1)}, bf16[2,2,8,512]{3,2,1,0:T(8,128)(2,1)S(1)}, u32[]{:S(2)}, u32[]{:S(2)}) collective-permute-start(bf16[2,2,8,512]{3,2,1,0:T(8,128)(2,1)S(1)} %get-tuple-element.119), channel_id=1, source_target_pairs={{8,0},{16,8},{24,16},{9,1},{17,9},{25,17},{10,2},{18,10},{26,18},{... | collective-permute-start | bytes 98312 | tf_op jit(solution)/shard_map/ppermute | solution.py:20
  264.0 5.5 %collective-permute-start.13 = (bf16[2,8,2,512]{3,2,1,0:T(2,128)(2,1)S(1)}, bf16[2,8,2,512]{3,2,1,0:T(2,128)(2,1)S(1)}, u32[]{:S(2)}, u32[]{:S(2)}) collective-permute-start(bf16[2,8,2,512]{3,2,1,0:T(2,128)(2,1)S(1)} %get-tuple-element.118), channel_id=1, source_target_pairs={{1,0},{2,1},{3,2},{4,3},{5,4},{6,5},{7,6},{9,8},{10,9},{11,10},{12... | collective-permute-start | bytes 98312 | tf_op jit(solution)/shard_map/ppermute | solution.py:20
  265.9 5.2 %collective-permute-start.12 = (bf16[2,8,2,512]{3,2,1,0:T(2,128)(2,1)S(1)}, bf16[2,8,2,512]{3,2,1,0:T(2,128)(2,1)S(1)}, u32[]{:S(2)}, u32[]{:S(2)}) collective-permute-start(bf16[2,8,2,512]{3,2,1,0:T(2,128)(2,1)S(1)} %get-tuple-element.117), channel_id=1, source_target_pairs={{0,1},{1,2},{2,3},{3,4},{4,5},{5,6},{6,7},{8,9},{9,10},{10,11},{11... | collective-permute-start | bytes 98312 | tf_op jit(solution)/shard_map/ppermute | solution.py:17
  279.8 3.9 %copy-start.35 = (f32[512]{0:T(512)S(1)}, f32[512]{0:T(512)}, u32[]{:S(2)}) copy-start(f32[512]{0:T(512)} %param.17) | copy-start | bytes 6148
  287.7 7.6 %copy-start.36 = (f32[512]{0:T(512)S(1)}, f32[512]{0:T(512)}, u32[]{:S(2)}) copy-start(f32[512]{0:T(512)} %param.19) | copy-start | bytes 6148
  (21 other events, 27.6 us)
Sparse Core Ops, SparseCore 0:
  10.0 50.4 all-gather.1
where the time goes:
time: 309 us; the launch traced here: 303 us
  blocking collectives  71.7 us (23%)
  matrix products  56 us (18%)
  starting transfers between devices  53.2 us (17%)
  local copies, waits for them, and re-layouts  47.7 us (15%)
  waiting for transfers between devices  46.2 us (15%)
  between operations  15.9 us (5%)
  other arithmetic  12.3 us (4%)
    all_gather x4, blocking collectives, per_device(): gathered = lax.all_gather(hidden, 'hid', axis=3, tiled=True)  71.7 us
    dot_general x90, matrix products, conv_taps(): jnp.dot(window.reshape(-1, channel_count), weight[tap_row, tap_col], pref...  56 us
    ppermute x7, starting transfers between devices, extended_2(): lax.ppermute(lax.slice_in_dim(block, block.shape[dim] - width, None, axis...  32.9 us
    ppermute x7, waiting for transfers between devices, extended_2(): lax.ppermute(lax.slice_in_dim(block, 0, width, axis=dim), axis, backward)  16 us
    ppermute x7, starting transfers between devices, extended_2(): lax.ppermute(lax.slice_in_dim(block, 0, width, axis=dim), axis, backward)  14.6 us
    all_gather x1, waiting for transfers between devices, per_device(): all_frames = lax.all_gather(frames, 'hid', axis=4, tiled=True)  13.5 us
    ppermute x7, waiting for transfers between devices, extended_2(): lax.ppermute(lax.slice_in_dim(block, block.shape[dim] - width, None, axis...  12 us
    slice x8, local copies, waits for them, and re-layouts, conv_taps(): padded[:, tap_row:tap_row + row_count, tap_col:tap_col + col_count, :]  11.4 us
  transfers between devices with their start and end apart: 16, of which 12 were waited for; matrix products, arithmetic and copies ran while one was open for 7% of the time, Pallas kernels for 0%

commit v1 on v0

v1 whole, which is shorter than its diff:
```python
import functools

import jax
import jax.numpy as jnp
from jax import lax
from jax.experimental import pallas as pl
from jax.experimental.pallas import tpu as pltpu
from jax.sharding import PartitionSpec as P

FORGET_BIAS = 1.0
VMEM_LIMIT = 14 * 1024 * 1024

NT = (((1,), (1,)), ((), ()))
NN = (((1,), (0,)), ((), ()))


def place_columns(dst, row0, pieces, group, cols, masked):
    count, width = pieces[0].shape
    groups = len(pieces)
    place = lax.rem(lax.broadcasted_iota(jnp.int32, (count, width), 0), cols)

    def shifts(piece):
        wide = piece.astype(jnp.float32)
        low = pltpu.roll(wide, 1, 0)
        high = pltpu.roll(wide, count - 1, 0)
        if masked:
            low = jnp.where(place == 0, 0.0, low)
            high = jnp.where(place == cols - 1, 0.0, high)
        return (low.astype(dst.dtype), wide.astype(dst.dtype), high.astype(dst.dtype))

    shifted = [shifts(piece) for piece in pieces]
    rows = pl.ds(row0, count)
    if width % 128 == 0:
        for k in range(groups):
            lanes = pl.ds(pl.multiple_of(lax.bitwise_xor(group, k) * width, width), width)
            for q in range(3):
                dst[q, rows, lanes] = shifted[k][q]
    else:
        for j in range(groups):

            @pl.when(group == j)
            def _():
                for q in range(3):
                    dst[q, rows, :] = jnp.concatenate(
                        [shifted[j ^ i][q] for i in range(groups)], axis=1
                    )


def halo_pieces(a_ref, b_ref):
    patch = lax.axis_index("patch")
    even = lax.rem(patch, 2) == 0
    above = patch > 0
    below = patch < lax.axis_size("patch") - 1
    top, bottom = [], []
    for k in range(a_ref.shape[1]):
        a = a_ref[0, k].astype(jnp.float32)
        b = b_ref[0, k].astype(jnp.float32)
        top.append(jnp.where(above, jnp.where(even, b, a), 0.0))
        bottom.append(jnp.where(below, jnp.where(even, a, b), 0.0))
    return top, bottom


def conv_kernel(groups, cols, halo, *refs):
    refs = list(refs)
    parts = [refs.pop(0) for _ in range(groups)]
    if halo:
        edge_a, edge_b = refs.pop(0), refs.pop(0)
    own_ref, pair_ref, init_ref, out_ref, held = refs
    count = out_ref.shape[1]
    step = pl.program_id(0)
    group = lax.axis_index("hid") // 2

    @pl.when(step == 0)
    def _():
        place_columns(held, cols, [part[0] for part in parts], group, cols, True)
        if halo:
            top, bottom = halo_pieces(edge_a, edge_b)
            place_columns(held, 0, top, group, cols, True)
            place_columns(held, cols + count, bottom, group, cols, True)
        else:
            zero = jnp.zeros((cols, held.shape[2]), held.dtype)
            for q in range(3):
                held[q, pl.ds(0, cols), :] = zero
                held[q, pl.ds(cols + count, cols), :] = zero
        out_ref[...] = jnp.broadcast_to(init_ref[...], out_ref.shape)

    total = out_ref[...]
    for q in range(3):
        window = held[q, pl.ds(pl.multiple_of(step * cols, cols), count), :]
        weight = jnp.concatenate([own_ref[0, q], pair_ref[0, q]], axis=0)
        total = total + lax.dot_general(weight, window, NT, preferred_element_type=jnp.float32)
    out_ref[...] = total


def gate_kernel(cols, edge_a, edge_b, own_ref, pair_ref, total_ref, cell_ref, hidden_ref, cell_out, held, turned, summed):
    step = pl.program_id(0)
    group = lax.axis_index("hid") // 2
    core = lax.rem(lax.axis_index("hid"), 2)
    count = total_ref.shape[1]
    channels = cell_ref.shape[1]
    side = 2 * cols

    @pl.when(step == 0)
    def _():
        top, bottom = halo_pieces(edge_a, edge_b)
        zero = jnp.zeros((cols, held.shape[2]), held.dtype)
        for q in range(3):
            held[q, pl.ds(cols, cols), :] = zero
            held[q, pl.ds(2 * cols, cols), :] = zero
        place_columns(held, 0, top, group, cols, True)
        place_columns(held, 3 * cols, bottom, group, cols, True)
        summed[...] = total_ref[...]

    def add(row0, lane0):
        total = summed[:, lane0 : lane0 + side]
        for q in range(3):
            window = held[q, row0 : row0 + side, :]
            weight = jnp.concatenate([own_ref[0, q], pair_ref[0, q]], axis=0)
            total = total + lax.dot_general(weight, window, NT, preferred_element_type=jnp.float32)
        summed[:, lane0 : lane0 + side] = total

    @pl.when(step == 0)
    def _():
        add(0, 0)

    @pl.when(step == 1)
    def _():
        add(side, count - side)
        for half in range(2):
            base = half * 4 * channels
            z0, z1, z2, z3 = (summed[base + i * channels : base + (i + 1) * channels, :] for i in range(4))
            cell = jax.nn.sigmoid(z1 + FORGET_BIAS) * cell_ref[half] + jax.nn.sigmoid(z0) * jnp.tanh(z2)
            cell_out[half] = cell
            rows = pl.ds(pl.multiple_of(lax.bitwise_xor(core, half) * channels, channels), channels)
            turned[rows, :] = jax.nn.sigmoid(z3) * jnp.tanh(cell)
        hidden_ref[...] = turned[...].T.astype(hidden_ref.dtype)


def decoder_kernel(groups, rows, width, margin, inner, *refs):
    parts = refs[:groups]
    edge_a, edge_b, first_ref, bias1_ref, second_ref, bias2_ref, out_ref, held, middle, total1, total2 = refs[groups:]
    step = pl.program_id(0)
    hid = lax.axis_index("hid")
    group = hid // 2
    patch = lax.axis_index("patch")
    image_rows = rows * lax.axis_size("patch")
    image_cols = inner * groups

    @pl.when(step == 0)
    def _():
        top, bottom = halo_pieces(edge_a, edge_b)
        place_columns(held, 0, top, group, width, False)
        place_columns(held, 2 * width, [part[...] for part in parts], group, width, False)
        place_columns(held, (2 + rows) * width, bottom, group, width, False)
        total1[...] = jnp.broadcast_to(bias1_ref[...], total1.shape)

    @pl.when(step < 3)
    def _():
        total = total1[...]
        for q in range(3):
            window = held[q, pl.ds(pl.multiple_of(step * width, width), (rows + 2) * width), :]
            total = total + lax.dot_general(window, first_ref[0, q], NN, preferred_element_type=jnp.float32)
        total1[...] = total

    @pl.when(step == 3)
    def _():
        value = total1[...]
        place = lax.broadcasted_iota(jnp.int32, value.shape, 0)
        row = patch * rows + place // width - 1
        col = group * inner - margin + lax.rem(place, width)
        inside = (row >= 0) & (row < image_rows) & (col >= 0) & (col < image_cols)
        value = jnp.where(inside, value * jax.nn.sigmoid(value), 0.0)
        value = value.astype(middle.dtype).astype(jnp.float32)
        count = value.shape[0]
        middle[0] = pltpu.roll(value, 1, 0).astype(middle.dtype)
        middle[1] = value.astype(middle.dtype)
        middle[2] = pltpu.roll(value, count - 1, 0).astype(middle.dtype)
        total2[...] = jnp.broadcast_to(bias2_ref[...], total2.shape)

    @pl.when(step >= 3)
    def _():
        total = total2[...]
        for q in range(3):
            window = middle[q, pl.ds(pl.multiple_of((step - 3) * width, width), rows * width), :]
            total = total + lax.dot_general(window, second_ref[0, q], NN, preferred_element_type=jnp.float32)
        total2[...] = total

        @pl.when(step == 5)
        def _():
            out_ref[...] = total.astype(out_ref.dtype)


def constant(shape, index=None):
    index = (0,) * len(shape) if index is None else index
    return pl.BlockSpec(shape, lambda i: index)


def params():
    return pltpu.CompilerParams(vmem_limit_bytes=VMEM_LIMIT, dimension_semantics=("arbitrary",))


def conv_call(parts, index, edges, own, pair, init, cols):
    groups = len(parts)
    _, count, width = parts[0].shape
    channels = own.shape[3]
    outs = 2 * own.shape[2]
    tap = pl.BlockSpec((1, 3) + own.shape[2:], lambda i: (i, 0, 0, 0))
    specs = [constant((1, count, width), (index, 0, 0))] * groups
    operands = list(parts)
    if edges is not None:
        specs += [constant((1,) + edges[0].shape[1:], (index, 0, 0, 0))] * 2
        operands += list(edges)
    specs += [tap, tap, constant(init.shape)]
    operands += [own, pair, init]
    return pl.pallas_call(
        functools.partial(conv_kernel, groups, cols, edges is not None),
        grid=(3,),
        in_specs=specs,
        out_specs=constant((outs, count)),
        out_shape=jax.ShapeDtypeStruct((outs, count), jnp.float32),
        scratch_shapes=[pltpu.VMEM((3, count + 2 * cols, channels), jnp.bfloat16)],
        compiler_params=params(),
        cost_estimate=pl.CostEstimate(
            flops=2 * outs * count * 9 * channels, bytes_accessed=18 * outs * channels, transcendentals=0
        ),
    )(*operands)


def gate_call(edges, own, pair, total, cell, cols):
    outs, count = total.shape
    channels = own.shape[3]
    width = 2 * cell.shape[1]
    tap = pl.BlockSpec((1, 3) + own.shape[2:], lambda i: (2 * i, 0, 0, 0))
    edge = constant((1,) + edges[0].shape[1:])
    return pl.pallas_call(
        functools.partial(gate_kernel, cols),
        grid=(2,),
        in_specs=[edge, edge, tap, tap, constant(total.shape), constant(cell.shape)],
        out_specs=[constant((count, width)), constant(cell.shape)],
        out_shape=[
            jax.ShapeDtypeStruct((count, width), jnp.bfloat16),
            jax.ShapeDtypeStruct(cell.shape, jnp.float32),
        ],
        scratch_shapes=[
            pltpu.VMEM((3, 4 * cols, channels), jnp.bfloat16),
            pltpu.VMEM((width, count), jnp.float32),
            pltpu.VMEM((outs, count), jnp.float32),
        ],
        compiler_params=params(),
        cost_estimate=pl.CostEstimate(
            flops=2 * outs * cols * 2 * 6 * channels, bytes_accessed=12 * outs * channels, transcendentals=0
        ),
    )(edges[0], edges[1], own, pair, total, cell)


def decoder_call(parts, edges, first, first_bias, second, second_bias, rows, width, margin, inner):
    groups = len(parts)
    channels = first.shape[2]
    outs = second.shape[3]
    return pl.pallas_call(
        functools.partial(decoder_kernel, groups, rows, width, margin, inner),
        grid=(6,),
        in_specs=[constant(part.shape) for part in parts]
        + [constant(edges[0].shape)] * 2
        + [
            pl.BlockSpec((1, 3) + first.shape[2:], lambda i: (jnp.minimum(i, 2), 0, 0, 0)),
            constant((1, first.shape[3])),
            pl.BlockSpec((1, 3) + second.shape[2:], lambda i: (jnp.maximum(i - 3, 0), 0, 0, 0)),
            constant((1, outs)),
        ],
        out_specs=constant((rows * width, outs)),
        out_shape=jax.ShapeDtypeStruct((rows * width, outs), jnp.bfloat16),
        scratch_shapes=[
            pltpu.VMEM((3, (rows + 4) * width, channels), jnp.bfloat16),
            pltpu.VMEM((3, (rows + 2) * width, first.shape[3]), jnp.bfloat16),
            pltpu.VMEM(((rows + 2) * width, first.shape[3]), jnp.float32),
            pltpu.VMEM((rows * width, outs), jnp.float32),
        ],
        compiler_params=params(),
        cost_estimate=pl.CostEstimate(
            flops=2 * 9 * channels * outs * (2 * rows + 2) * width,
            bytes_accessed=36 * channels * outs,
            transcendentals=0,
        ),
    )(*parts, *edges, first, first_bias.reshape(1, -1), second, second_bias.reshape(1, -1))


def per_device(
    frames,
    hidden_start,
    cell_start,
    input_weight,
    hidden_weight,
    gate_bias,
    first_weight,
    first_bias,
    second_weight,
    second_bias,
):
    steps, batch, rows, cols, share = frames.shape
    groups = lax.axis_size("hid") // 2
    patches = lax.axis_size("patch")
    assert batch == 2 and groups & (groups - 1) == 0 and patches % 2 == 0
    hid = lax.axis_index("hid")
    core = lax.rem(hid, 2)
    group = hid // 2
    even = lax.rem(lax.axis_index("patch"), 2) == 0
    count = rows * cols
    width = 2 * share

    pairs = [(i, i ^ 1) for i in range(2 * groups)]
    inner_pairs = [(i, i ^ 1) for i in range(patches)]
    outer_pairs = [(i, (i - 1) % patches if i % 2 == 0 else (i + 1) % patches) for i in range(patches)]

    def swap(value):
        return lax.ppermute(value, "hid", pairs)

    def own_batch(value, axis):
        mine = lax.dynamic_index_in_dim(value, core, axis, keepdims=False)
        other = lax.dynamic_index_in_dim(value, 1 - core, axis, keepdims=False)
        return mine, swap(other)

    def joined(value, axis):
        mine, other = own_batch(value, axis)
        return jnp.where(core == 0, jnp.concatenate([mine, other], -1), jnp.concatenate([other, mine], -1))

    def gathered(value):
        return [value] + [
            lax.ppermute(value, "hid", [(i, i ^ (2 * k)) for i in range(2 * groups)]) for k in range(1, groups)
        ]

    def swapped_edges(top, bottom):
        first = lax.ppermute(jnp.where(even, bottom, top), "patch", inner_pairs)
        second = lax.ppermute(jnp.where(even, top, bottom), "patch", outer_pairs)
        return first, second

    def edges_of(parts):
        top = jnp.stack([part[:, :cols] for part in parts], 1)
        bottom = jnp.stack([part[:, count - cols :] for part in parts], 1)
        return swapped_edges(top, bottom)

    def gate_major(weight):
        turned = jnp.transpose(weight, (0, 1, 3, 4, 2))
        return turned.reshape(turned.shape[:2] + (-1,) + turned.shape[-1:])

    hidden = joined(hidden_start, 0).reshape(1, count, width)
    images = joined(frames, 1).reshape(steps, count, width)
    input_own, hidden_own = gate_major(input_weight), gate_major(hidden_weight)
    lead = jnp.concatenate([images[:1], hidden], 0)
    lead_parts = gathered(lead)
    input_pair, hidden_pair = swap(input_own), swap(hidden_own)
    bias_own = gate_bias.reshape(-1)
    bias = jnp.concatenate([bias_own, swap(bias_own)]).reshape(-1, 1)
    cell_mine, cell_other = own_batch(cell_start, 0)
    cell = jnp.stack([cell_mine.reshape(count, share).T, cell_other.reshape(count, share).T])
    lead_edges = edges_of(lead_parts)

    rest, lead_edges = lax.optimization_barrier((images[1:], lead_edges))
    rest_parts = gathered(rest)
    rest_edges = edges_of(rest_parts)

    for time_index in range(steps):
        if time_index == 0:
            total = conv_call(lead_parts, 0, lead_edges, input_own, input_pair, bias, cols)
            parts, part_index = lead_parts, 1
            edges = tuple(edge[1:2] for edge in lead_edges)
        else:
            total = conv_call(rest_parts, time_index - 1, rest_edges, input_own, input_pair, bias, cols)
            parts, part_index = gathered(hidden[None]), 0
            edges = edges_of(parts)
        total = conv_call(parts, part_index, None, hidden_own, hidden_pair, total, cols)
        hidden, cell = gate_call(edges, hidden_own, hidden_pair, total, cell, cols)

    inner = cols // groups
    tile = -(-(inner + 4) // 16) * 16
    margin = (tile - inner) // 2
    image = jnp.pad(hidden.reshape(rows, cols, width), ((0, 0), (margin, margin), (0, 0)))

    def columns_for(k):
        start = lax.bitwise_xor(group, k) * inner
        return lax.dynamic_slice_in_dim(image, start, tile, axis=1).reshape(rows * tile, width)

    tiles = [columns_for(0)] + [
        lax.ppermute(columns_for(k), "hid", [(i, i ^ (2 * k)) for i in range(2 * groups)]) for k in range(1, groups)
    ]
    rim = 2 * tile
    tile_edges = swapped_edges(
        jnp.stack([part[:rim] for part in tiles])[None],
        jnp.stack([part[rows * tile - rim :] for part in tiles])[None],
    )
    decoded = decoder_call(
        tiles, tile_edges, first_weight, first_bias, second_weight, second_bias, rows, tile, margin, inner
    )
    decoded = decoded.reshape(rows, tile, -1)
    half = inner // 2
    mine = lax.dynamic_slice_in_dim(decoded, margin + core * half, half, axis=1)
    other = swap(lax.dynamic_slice_in_dim(decoded, margin + (1 - core) * half, half, axis=1))
    decoded = jnp.where(core == 0, jnp.stack([mine, other]), jnp.stack([other, mine]))

    cell_mine = cell[0].T.reshape(rows, cols, share)
    cell_other = swap(cell[1]).T.reshape(rows, cols, share)
    cell_final = jnp.where(core == 0, jnp.stack([cell_mine, cell_other]), jnp.stack([cell_other, cell_mine]))
    return decoded, cell_final


def solution(mesh):
    return jax.shard_map(
        per_device,
        mesh=mesh,
        in_specs=(
            P(None, None, "patch", None, "hid"),
            P(None, "patch", None, "hid"),
            P(None, "patch", None, "hid"),
            P(None, None, None, None, "hid"),
            P(None, None, None, None, "hid"),
            P(None, "hid"),
            P(),
            P(),
            P(),
            P(),
        ),
        out_specs=(P(None, "patch", "hid", None), P(None, "patch", None, "hid")),
        check_vma=False,
    )
```

time: 309 us -> 152 us (0.49)
  the two profiles are of different devices: /device:TPU:10 before, /device:TPU:0 now
where the time goes in v1:
time: 152 us; the launch traced here: 151 us
  waiting for transfers between devices  51.4 us (34%)
  starting transfers between devices  49.2 us (32%)
  Pallas kernels  33.2 us (22%)
  local copies, waits for them, and re-layouts  12.8 us (8%)
  other arithmetic  3.6 us (2%)
    ppermute x15, waiting for transfers between devices, gathered(): lax.ppermute(value, 'hid', [(i, i ^ 2 * k) for i in range(2 * groups)])  34.6 us
    ppermute x15, starting transfers between devices, gathered(): lax.ppermute(value, 'hid', [(i, i ^ 2 * k) for i in range(2 * groups)])  27.3 us
    pallas_call x8, Pallas kernels, conv_call(): pl.pallas_call(functools.partial(conv_kernel, groups, cols, edges is not...  24.3 us
    ppermute x6, waiting for transfers between devices, swapped_edges(): second = lax.ppermute(jnp.where(even, top, bottom), 'patch', outer_pairs)  9.01 us
    ppermute x6, starting transfers between devices, swapped_edges(): second = lax.ppermute(jnp.where(even, top, bottom), 'patch', outer_pairs)  8.21 us
    ppermute x6, starting transfers between devices, swapped_edges(): first = lax.ppermute(jnp.where(even, bottom, top), 'patch', inner_pairs)  7.38 us
    unnamed x18, local copies, waits for them, and re-layouts  6.01 us
    pallas_call x4, Pallas kernels, gate_call(): pl.pallas_call(functools.partial(gate_kernel, cols), grid=(2,), in_specs=...  5.68 us
  transfers between devices with their start and end apart: 38, of which 21 were waited for; matrix products, arithmetic and copies ran while one was open for 5% of the time, Pallas kernels for 17%

profile of v1, /device:TPU:0, one launch (start us, length us, event | category | flops | bytes accessed | tf_op | source)
XLA Modules:
  0.0 151.3 jit_solution(3158072802617107852)
XLA Ops:
  8.3 2.7 %collective-permute-start.2 = (bf16[2,256,128]{2,1,0:T(8,128)(2,1)S(1)}, bf16[2,256,128]{2,1,0:T(8,128)(2,1)S(1)}, u32[]{:S(2)}, u32[]{:S(2)}) collective-permute-start(bf16[2,256,128]{2,1,0:T(8,128)(2,1)S(1)} %pad_maximum_fusion.2.refs_0_), channel_id=1, source_target_pairs={{0,2},{1,3},{2,0},{3,1},{4,6},{5,7},{6,4},{7,5},{8,10},{9,11},{10,... | collective-permute-start | bytes 393224 | tf_op jit(solution)/shard_map/ppermute | solution.py:329
  12.0 3.1 %collective-permute-done.2.refs_1_ = bf16[2,256,128]{2,1,0:T(8,128)(2,1)S(1)} collective-permute-done((bf16[2,256,128]{2,1,0:T(8,128)(2,1)S(1)}, bf16[2,256,128]{2,1,0:T(8,128)(2,1)S(1)}, u32[]{:S(2)}, u32[]{:S(2)}) %collective-permute-start.2) | collective-permute-done | bytes 131104 | tf_op jit(solution)/shard_map/ppermute | solution.py:329
  15.1 2.8 %collective-permute-start.3 = (bf16[2,256,128]{2,1,0:T(8,128)(2,1)S(1)}, bf16[2,256,128]{2,1,0:T(8,128)(2,1)S(1)}, u32[]{:S(2)}, u32[]{:S(2)}) collective-permute-start(bf16[2,256,128]{2,1,0:T(8,128)(2,1)S(1)} %pad_maximum_fusion.2.refs_0_), channel_id=1, source_target_pairs={{0,4},{1,5},{2,6},{3,7},{4,0},{5,1},{6,2},{7,3},{8,12},{9,13},{10,... | collective-permute-start | bytes 393224 | tf_op jit(solution)/shard_map/ppermute | solution.py:329
  17.9 6.2 %collective-permute-done.3.refs_2_ = bf16[2,256,128]{2,1,0:T(8,128)(2,1)S(1)} collective-permute-done((bf16[2,256,128]{2,1,0:T(8,128)(2,1)S(1)}, bf16[2,256,128]{2,1,0:T(8,128)(2,1)S(1)}, u32[]{:S(2)}, u32[]{:S(2)}) %collective-permute-start.3) | collective-permute-done | bytes 131104 | tf_op jit(solution)/shard_map/ppermute | solution.py:329
  24.1 3.4 %collective-permute-start.4 = (bf16[2,256,128]{2,1,0:T(8,128)(2,1)S(1)}, bf16[2,256,128]{2,1,0:T(8,128)(2,1)S(1)}, u32[]{:S(2)}, u32[]{:S(2)}) collective-permute-start(bf16[2,256,128]{2,1,0:T(8,128)(2,1)S(1)} %pad_maximum_fusion.2.refs_0_), channel_id=1, source_target_pairs={{0,6},{1,7},{2,4},{3,5},{4,2},{5,3},{6,0},{7,1},{8,14},{9,15},{10,... | collective-permute-start | bytes 393224 | tf_op jit(solution)/shard_map/ppermute | solution.py:329
  27.5 3.8 %collective-permute-done.4.refs_3_ = bf16[2,256,128]{2,1,0:T(8,128)(2,1)S(1)} collective-permute-done((bf16[2,256,128]{2,1,0:T(8,128)(2,1)S(1)}, bf16[2,256,128]{2,1,0:T(8,128)(2,1)S(1)}, u32[]{:S(2)}, u32[]{:S(2)}) %collective-permute-start.4) | collective-permute-done | bytes 131104 | tf_op jit(solution)/shard_map/ppermute | solution.py:329
  38.3 2.2 %collective-permute-done.6.refs_5_ = bf16[2,4,64,128]{3,2,1,0:T(8,128)(2,1)S(1)} collective-permute-done((bf16[2,4,64,128]{3,2,1,0:T(8,128)(2,1)}, bf16[2,4,64,128]{3,2,1,0:T(8,128)(2,1)S(1)}, u32[]{:S(2)}, u32[]{:S(2)}) %collective-permute-start.6) | collective-permute-done | bytes 131104 | tf_op jit(solution)/shard_map/ppermute | solution.py:334
  42.2 2.4 %collective-permute-start.17 = (bf16[3,256,128]{2,1,0:T(8,128)(2,1)S(1)}, bf16[3,256,128]{2,1,0:T(8,128)(2,1)S(1)}, u32[]{:S(2)}, u32[]{:S(2)}) collective-permute-start(bf16[3,256,128]{2,1,0:T(8,128)(2,1)S(1)} %bitcast.187), channel_id=1, source_target_pairs={{0,4},{1,5},{2,6},{3,7},{4,0},{5,1},{6,2},{7,3},{8,12},{9,13},{10,... | collective-permute-start | bytes 589832 | tf_op jit(solution)/shard_map/ppermute | solution.py:329
  44.9 3.0 %collective-permute-done.16.refs_1_ = bf16[3,256,128]{2,1,0:T(8,128)(2,1)S(1)} collective-permute-done((bf16[3,256,128]{2,1,0:T(8,128)(2,1)S(1)}, bf16[3,256,128]{2,1,0:T(8,128)(2,1)S(1)}, u32[]{:S(2)}, u32[]{:S(2)}) %collective-permute-start.16) | collective-permute-done | bytes 196640 | tf_op jit(solution)/shard_map/ppermute | solution.py:329
  47.9 10.2 %collective-permute-done.17.refs_2_ = bf16[3,256,128]{2,1,0:T(8,128)(2,1)S(1)} collective-permute-done((bf16[3,256,128]{2,1,0:T(8,128)(2,1)S(1)}, bf16[3,256,128]{2,1,0:T(8,128)(2,1)S(1)}, u32[]{:S(2)}, u32[]{:S(2)}) %collective-permute-start.17) | collective-permute-done | bytes 196640 | tf_op jit(solution)/shard_map/ppermute | solution.py:329
  61.7 3.9 %shard_map.113.refs_6_ = f32[512,256]{1,0:T(8,128)S(1)} custom-call(bf16[2,256,128]{2,1,0:T(8,128)(2,1)S(1)} %pad_maximum_fusion.2.refs_0_, bf16[2,256,128]{2,1,0:T(8,128)(2,1)S(1)} %collective-permute-done.2.refs_1_, bf16[2,256,128]{2,1,0:T(8,128)(2,1)S(1)} %collective-permute-done.3.refs_2_, bf16[2,256,128]{2,1,0:T(8,128)(2,1)S(1)} %collective-permute-done.4.refs_3_, ...), custom_call_target="tpu_custom_call" | custom-call | flops 1207959552 | bytes 4718592 | tf_op jit(solution)/shard_map/pallas_call | solution.py:215
  65.7 2.2 %shard_map.114.total_ref = f32[512,256]{1,0:T(8,128)S(1)} custom-call(bf16[2,256,128]{2,1,0:T(8,128)(2,1)S(1)} %pad_maximum_fusion.2.refs_0_, bf16[2,256,128]{2,1,0:T(8,128)(2,1)S(1)} %collective-permute-done.2.refs_1_, bf16[2,256,128]{2,1,0:T(8,128)(2,1)S(1)} %collective-permute-done.3.refs_2_, bf16[2,256,128]{2,1,0:T(8,128)(2,1)S(1)} %collective-permute-done.4.refs_3_, ...), custom_call_target="tpu_custom_call" | custom-call | flops 1207959552 | bytes 4718592 | tf_op jit(solution)/shard_map/pallas_call | solution.py:215
  69.3 2.7 %collective-permute-start.11 = (bf16[1,256,128]{2,1,0:T(8,128)(2,1)S(1)}, bf16[1,256,128]{2,1,0:T(8,128)(2,1)S(1)}, u32[]{:S(2)}, u32[]{:S(2)}) collective-permute-start(bf16[1,256,128]{2,1,0:T(8,128)(2,1)S(1)} %bitcast.196), channel_id=1, source_target_pairs={{0,2},{1,3},{2,0},{3,1},{4,6},{5,7},{6,4},{7,5},{8,10},{9,11},{10,... | collective-permute-start | bytes 196616 | tf_op jit(solution)/shard_map/ppermute | solution.py:329
  74.5 3.9 %shard_map.122.refs_6_ = f32[512,256]{1,0:T(8,128)S(1)} custom-call(bf16[3,256,128]{2,1,0:T(8,128)(2,1)S(1)} %bitcast.190, bf16[3,256,128]{2,1,0:T(8,128)(2,1)S(1)} %collective-permute-done.16.refs_1_, bf16[3,256,128]{2,1,0:T(8,128)(2,1)S(1)} %collective-permute-done.17.refs_2_, bf16[3,256,128]{2,1,0:T(8,128)(2,1)S(1)} %collective-permute-done.18.refs_3_, ...), custom_call_target="tpu_custom_call" | custom-call | flops 1207959552 | bytes 4718592 | tf_op jit(solution)/shard_map/pallas_call | solution.py:215
  78.4 3.9 %shard_map.119.refs_6_ = f32[512,256]{1,0:T(8,128)S(1)} custom-call(bf16[3,256,128]{2,1,0:T(8,128)(2,1)S(1)} %bitcast.191, bf16[3,256,128]{2,1,0:T(8,128)(2,1)S(1)} %collective-permute-done.16.refs_1_, bf16[3,256,128]{2,1,0:T(8,128)(2,1)S(1)} %collective-permute-done.17.refs_2_, bf16[3,256,128]{2,1,0:T(8,128)(2,1)S(1)} %collective-permute-done.18.refs_3_, ...), custom_call_target="tpu_custom_call" | custom-call | flops 1207959552 | bytes 4718592 | tf_op jit(solution)/shard_map/pallas_call | solution.py:215
  82.4 3.9 %shard_map.116.refs_6_ = f32[512,256]{1,0:T(8,128)S(1)} custom-call(bf16[3,256,128]{2,1,0:T(8,128)(2,1)S(1)} %bitcast.192, bf16[3,256,128]{2,1,0:T(8,128)(2,1)S(1)} %collective-permute-done.16.refs_1_, bf16[3,256,128]{2,1,0:T(8,128)(2,1)S(1)} %collective-permute-done.17.refs_2_, bf16[3,256,128]{2,1,0:T(8,128)(2,1)S(1)} %collective-permute-done.18.refs_3_, ...), custom_call_target="tpu_custom_call" | custom-call | flops 1207959552 | bytes 4718592 | tf_op jit(solution)/shard_map/pallas_call | solution.py:215
  87.9 2.2 %shard_map.117.total_ref = f32[512,256]{1,0:T(8,128)S(1)} custom-call(bf16[1,256,128]{2,1,0:T(8,128)(2,1)S(1)} %bitcast.200, bf16[1,256,128]{2,1,0:T(8,128)(2,1)S(1)} %collective-permute-done.11.refs_1_, bf16[1,256,128]{2,1,0:T(8,128)(2,1)S(1)} %collective-permute-done.12.refs_2_, bf16[1,256,128]{2,1,0:T(8,128)(2,1)S(1)} %collective-permute-done.13.refs_3_, ...), custom_call_target="tpu_custom_call" | custom-call | flops 1207959552 | bytes 4718592 | tf_op jit(solution)/shard_map/pallas_call | solution.py:215
  97.6 2.5 %collective-permute-done.22.refs_2_ = bf16[1,256,128]{2,1,0:T(8,128)(2,1)S(1)} collective-permute-done((bf16[1,256,128]{2,1,0:T(8,128)(2,1)S(1)}, bf16[1,256,128]{2,1,0:T(8,128)(2,1)S(1)}, u32[]{:S(2)}, u32[]{:S(2)}) %collective-permute-start.22) | collective-permute-done | bytes 65568 | tf_op jit(solution)/shard_map/ppermute | solution.py:329
  101.9 2.0 %collective-permute-start.24 = (bf16[1,4,64,128]{3,2,1,0:T(8,128)(2,1)S(1)}, bf16[1,4,64,128]{3,2,1,0:T(8,128)(2,1)S(1)}, u32[]{:S(2)}, u32[]{:S(2)}) collective-permute-start(bf16[1,4,64,128]{3,2,1,0:T(8,128)(2,1)S(1)} %get-tuple-element.49), channel_id=1, source_target_pairs={{0,8},{8,0},{16,24},{24,16},{1,9},{9,1},{17,25},{25,17},{2,10},{10... | collective-permute-start | bytes 196616 | tf_op jit(solution)/shard_map/ppermute | solution.py:333
  105.0 2.2 %shard_map.120.total_ref = f32[512,256]{1,0:T(8,128)S(1)} custom-call(bf16[1,256,128]{2,1,0:T(8,128)(2,1)S(1)} %bitcast.205, bf16[1,256,128]{2,1,0:T(8,128)(2,1)S(1)} %collective-permute-done.21.refs_1_, bf16[1,256,128]{2,1,0:T(8,128)(2,1)S(1)} %collective-permute-done.22.refs_2_, bf16[1,256,128]{2,1,0:T(8,128)(2,1)S(1)} %collective-permute-done.23.refs_3_, ...), custom_call_target="tpu_custom_call" | custom-call | flops 1207959552 | bytes 4718592 | tf_op jit(solution)/shard_map/pallas_call | solution.py:215
  107.1 2.0 %collective-permute-done.25.edge_b = bf16[1,4,64,128]{3,2,1,0:T(8,128)(2,1)S(1)} collective-permute-done((bf16[1,4,64,128]{3,2,1,0:T(8,128)(2,1)S(1)}, bf16[1,4,64,128]{3,2,1,0:T(8,128)(2,1)S(1)}, u32[]{:S(2)}, u32[]{:S(2)}) %collective-permute-start.25) | collective-permute-done | bytes 65568 | tf_op jit(solution)/shard_map/ppermute | solution.py:334
  110.6 2.3 %collective-permute-start.27 = (bf16[1,256,128]{2,1,0:T(8,128)(2,1)S(1)}, bf16[1,256,128]{2,1,0:T(8,128)(2,1)S(1)}, u32[]{:S(2)}, u32[]{:S(2)}) collective-permute-start(bf16[1,256,128]{2,1,0:T(8,128)(2,1)S(1)} %bitcast.207), channel_id=1, source_target_pairs={{0,4},{1,5},{2,6},{3,7},{4,0},{5,1},{6,2},{7,3},{8,12},{9,13},{10,... | collective-permute-start | bytes 196616 | tf_op jit(solution)/shard_map/ppermute | solution.py:329
  112.9 2.1 %collective-permute-start.28 = (bf16[1,256,128]{2,1,0:T(8,128)(2,1)S(1)}, bf16[1,256,128]{2,1,0:T(8,128)(2,1)S(1)}, u32[]{:S(2)}, u32[]{:S(2)}) collective-permute-start(bf16[1,256,128]{2,1,0:T(8,128)(2,1)S(1)} %bitcast.208), channel_id=1, source_target_pairs={{0,6},{1,7},{2,4},{3,5},{4,2},{5,3},{6,0},{7,1},{8,14},{9,15},{10,... | collective-permute-start | bytes 196616 | tf_op jit(solution)/shard_map/ppermute | solution.py:329
  115.8 3.1 %collective-permute-done.28.refs_3_ = bf16[1,256,128]{2,1,0:T(8,128)(2,1)S(1)} collective-permute-done((bf16[1,256,128]{2,1,0:T(8,128)(2,1)S(1)}, bf16[1,256,128]{2,1,0:T(8,128)(2,1)S(1)}, u32[]{:S(2)}, u32[]{:S(2)}) %collective-permute-start.28) | collective-permute-done | bytes 65568 | tf_op jit(solution)/shard_map/ppermute | solution.py:329
  120.5 2.2 %shard_map.123.total_ref = f32[512,256]{1,0:T(8,128)S(1)} custom-call(bf16[1,256,128]{2,1,0:T(8,128)(2,1)S(1)} %bitcast.210, bf16[1,256,128]{2,1,0:T(8,128)(2,1)S(1)} %collective-permute-done.26.refs_1_, bf16[1,256,128]{2,1,0:T(8,128)(2,1)S(1)} %collective-permute-done.27.refs_2_, bf16[1,256,128]{2,1,0:T(8,128)(2,1)S(1)} %collective-permute-done.28.refs_3_, ...), custom_call_target="tpu_custom_call" | custom-call | flops 1207959552 | bytes 4718592 | tf_op jit(solution)/shard_map/pallas_call | solution.py:215
  126.0 2.6 %collective-permute-start.32 = (bf16[128,128]{1,0:T(8,128)(2,1)S(1)}, bf16[128,128]{1,0:T(8,128)(2,1)S(1)}, u32[]{:S(2)}, u32[]{:S(2)}) collective-permute-start(bf16[128,128]{1,0:T(8,128)(2,1)S(1)} %bitcast.227), channel_id=1, source_target_pairs={{0,4},{1,5},{2,6},{3,7},{4,0},{5,1},{6,2},{7,3},{8,12},{9,13},{10,... | collective-permute-start | bytes 98312 | tf_op jit(solution)/shard_map/ppermute | solution.py:384
  130.9 3.5 %collective-permute-done.33.refs_3_ = bf16[128,128]{1,0:T(8,128)(2,1)S(1)} collective-permute-done((bf16[128,128]{1,0:T(8,128)(2,1)S(1)}, bf16[128,128]{1,0:T(8,128)(2,1)S(1)}, u32[]{:S(2)}, u32[]{:S(2)}) %collective-permute-start.33) | collective-permute-done | bytes 32800 | tf_op jit(solution)/shard_map/ppermute | solution.py:384
  134.4 2.0 %collective-permute-start.34 = (bf16[1,4,64,128]{3,2,1,0:T(8,128)(2,1)S(1)}, bf16[1,4,64,128]{3,2,1,0:T(8,128)(2,1)S(1)}, u32[]{:S(2)}, u32[]{:S(2)}) collective-permute-start(bf16[1,4,64,128]{3,2,1,0:T(8,128)(2,1)S(1)} %get-tuple-element.45), channel_id=1, source_target_pairs={{0,8},{8,0},{16,24},{24,16},{1,9},{9,1},{17,25},{25,17},{2,10},{10... | collective-permute-start | bytes 196616 | tf_op jit(solution)/shard_map/ppermute | solution.py:333
  138.7 2.8 %collective-permute-done.35.refs_5_ = bf16[1,4,64,128]{3,2,1,0:T(8,128)(2,1)S(1)} collective-permute-done((bf16[1,4,64,128]{3,2,1,0:T(8,128)(2,1)S(1)}, bf16[1,4,64,128]{3,2,1,0:T(8,128)(2,1)S(1)}, u32[]{:S(2)}, u32[]{:S(2)}) %collective-permute-start.35) | collective-permute-done | bytes 65568 | tf_op jit(solution)/shard_map/ppermute | solution.py:334
  141.5 2.3 %copy-done.2 = bf16[3,3,512,512]{3,2,1,0:T(8,128)(2,1)S(1)} copy-done((bf16[3,3,512,512]{3,2,1,0:T(8,128)(2,1)S(1)}, bf16[3,3,512,512]{3,2,1,0:T(8,128)(2,1)}, u32[]{:S(2)}) %copy-start.2) | copy-done | bytes 4718616
  143.9 2.3 %copy-done.3 = bf16[3,3,512,512]{3,2,1,0:T(8,128)(2,1)S(1)} copy-done((bf16[3,3,512,512]{3,2,1,0:T(8,128)(2,1)S(1)}, bf16[3,3,512,512]{3,2,1,0:T(8,128)(2,1)}, u32[]{:S(2)}) %copy-start.3) | copy-done | bytes 4718616
  146.2 3.2 %shard_map.125 = bf16[128,512]{1,0:T(8,128)(2,1)S(1)} custom-call(bf16[128,128]{1,0:T(8,128)(2,1)S(1)} %bitcast.211, bf16[128,128]{1,0:T(8,128)(2,1)S(1)} %collective-permute-done.31.refs_1_, bf16[128,128]{1,0:T(8,128)(2,1)S(1)} %collective-permute-done.32.refs_2_, bf16[128,128]{1,0:T(8,128)(2,1)S(1)} %collective-permute-done.33.refs_3_, ...), custom_call_target="tpu_custom_call" | custom-call | flops 1509949440 | bytes 9437184 | tf_op jit(solution)/shard_map/pallas_call | solution.py:260
  (128 shorter events, 50.6 us)
Async XLA Ops:
  3.9 57.9 %collective-permute-start.8 = (bf16[3,3,256,512]{3,2,1,0:T(8,128)(2,1)}, bf16[3,3,256,512]{3,2,1,0:T(8,128)(2,1)}, u32[]{:S(2)}, u32[]{:S(2)}) collective-permute-start(bf16[3,3,256,512]{3,2,1,0:T(8,128)(2,1)} %bitcast.181), channel_id=1, source_target_pairs={{0,1},{1,0},{2,3},{3,2},{4,5},{5,4},{6,7},{7,6},{8,9},{9,8},{10,11... | collective-permute-start | bytes 7077896 | tf_op jit(solution)/shard_map/ppermute | solution.py:316
  5.1 28.4 %collective-permute-start.9 = (f32[256]{0:T(256)S(1)}, f32[256]{0:T(256)S(1)}, u32[]{:S(2)}, u32[]{:S(2)}) collective-permute-start(f32[256]{0:T(256)S(1)} %reshape.1138), channel_id=1, source_target_pairs={{0,1},{1,0},{2,3},{3,2},{4,5},{5,4},{6,7},{7,6},{8,9},{9,8},{10,11... | collective-permute-start | bytes 3080 | tf_op jit(solution)/shard_map/ppermute | solution.py:316
  5.2 60.5 %collective-permute-start.7 = (bf16[3,3,256,512]{3,2,1,0:T(8,128)(2,1)}, bf16[3,3,256,512]{3,2,1,0:T(8,128)(2,1)S(1)}, u32[]{:S(2)}, u32[]{:S(2)}) collective-permute-start(bf16[3,3,256,512]{3,2,1,0:T(8,128)(2,1)} %bitcast.172), channel_id=1, source_target_pairs={{0,1},{1,0},{2,3},{3,2},{4,5},{5,4},{6,7},{7,6},{8,9},{9,8},{10,11... | collective-permute-start | bytes 7077896 | tf_op jit(solution)/shard_map/ppermute | solution.py:316
  8.3 6.8 %collective-permute-start.2 = (bf16[2,256,128]{2,1,0:T(8,128)(2,1)S(1)}, bf16[2,256,128]{2,1,0:T(8,128)(2,1)S(1)}, u32[]{:S(2)}, u32[]{:S(2)}) collective-permute-start(bf16[2,256,128]{2,1,0:T(8,128)(2,1)S(1)} %pad_maximum_fusion.2.refs_0_), channel_id=1, source_target_pairs={{0,2},{1,3},{2,0},{3,1},{4,6},{5,7},{6,4},{7,5},{8,10},{9,11},{10,... | collective-permute-start | bytes 393224 | tf_op jit(solution)/shard_map/ppermute | solution.py:329
  11.7 23.4 %collective-permute-start.10 = (f32[4,64,64]{2,1,0:T(8,128)}, f32[4,64,64]{2,1,0:T(8,128)}, u32[]{:S(2)}, u32[]{:S(2)}) collective-permute-start(f32[4,64,64]{2,1,0:T(8,128)} %get-tuple-element.29), channel_id=1, source_target_pairs={{0,1},{1,0},{2,3},{3,2},{4,5},{5,4},{6,7},{7,6},{8,9},{9,8},{10,11... | collective-permute-start | bytes 196616 | tf_op jit(solution)/shard_map/ppermute | solution.py:316
  15.1 9.0 %collective-permute-start.3 = (bf16[2,256,128]{2,1,0:T(8,128)(2,1)S(1)}, bf16[2,256,128]{2,1,0:T(8,128)(2,1)S(1)}, u32[]{:S(2)}, u32[]{:S(2)}) collective-permute-start(bf16[2,256,128]{2,1,0:T(8,128)(2,1)S(1)} %pad_maximum_fusion.2.refs_0_), channel_id=1, source_target_pairs={{0,4},{1,5},{2,6},{3,7},{4,0},{5,1},{6,2},{7,3},{8,12},{9,13},{10,... | collective-permute-start | bytes 393224 | tf_op jit(solution)/shard_map/ppermute | solution.py:329
  24.1 7.2 %collective-permute-start.4 = (bf16[2,256,128]{2,1,0:T(8,128)(2,1)S(1)}, bf16[2,256,128]{2,1,0:T(8,128)(2,1)S(1)}, u32[]{:S(2)}, u32[]{:S(2)}) collective-permute-start(bf16[2,256,128]{2,1,0:T(8,128)(2,1)S(1)} %pad_maximum_fusion.2.refs_0_), channel_id=1, source_target_pairs={{0,6},{1,7},{2,4},{3,5},{4,2},{5,3},{6,0},{7,1},{8,14},{9,15},{10,... | collective-permute-start | bytes 393224 | tf_op jit(solution)/shard_map/ppermute | solution.py:329
  32.0 6.3 %collective-permute-start.5 = (bf16[2,4,64,128]{3,2,1,0:T(8,128)(2,1)}, bf16[2,4,64,128]{3,2,1,0:T(8,128)(2,1)S(1)}, u32[]{:S(2)}, u32[]{:S(2)}) collective-permute-start(bf16[2,4,64,128]{3,2,1,0:T(8,128)(2,1)} %get-tuple-element.31), channel_id=1, source_target_pairs={{0,8},{8,0},{16,24},{24,16},{1,9},{9,1},{17,25},{25,17},{2,10},{10... | collective-permute-start | bytes 393224 | tf_op jit(solution)/shard_map/ppermute | solution.py:333
  33.5 7.0 %collective-permute-start.6 = (bf16[2,4,64,128]{3,2,1,0:T(8,128)(2,1)}, bf16[2,4,64,128]{3,2,1,0:T(8,128)(2,1)S(1)}, u32[]{:S(2)}, u32[]{:S(2)}) collective-permute-start(bf16[2,4,64,128]{3,2,1,0:T(8,128)(2,1)} %get-tuple-element.30), channel_id=1, source_target_pairs={{0,24},{8,16},{16,8},{24,0},{1,25},{9,17},{17,9},{25,1},{2,26},{10... | collective-permute-start | bytes 393224 | tf_op jit(solution)/shard_map/ppermute | solution.py:334
  40.5 7.5 %collective-permute-start.16 = (bf16[3,256,128]{2,1,0:T(8,128)(2,1)S(1)}, bf16[3,256,128]{2,1,0:T(8,128)(2,1)S(1)}, u32[]{:S(2)}, u32[]{:S(2)}) collective-permute-start(bf16[3,256,128]{2,1,0:T(8,128)(2,1)S(1)} %bitcast.186), channel_id=1, source_target_pairs={{0,2},{1,3},{2,0},{3,1},{4,6},{5,7},{6,4},{7,5},{8,10},{9,11},{10,... | collective-permute-start | bytes 589832 | tf_op jit(solution)/shard_map/ppermute | solution.py:329
  42.2 16.0 %collective-permute-start.17 = (bf16[3,256,128]{2,1,0:T(8,128)(2,1)S(1)}, bf16[3,256,128]{2,1,0:T(8,128)(2,1)S(1)}, u32[]{:S(2)}, u32[]{:S(2)}) collective-permute-start(bf16[3,256,128]{2,1,0:T(8,128)(2,1)S(1)} %bitcast.187), channel_id=1, source_target_pairs={{0,4},{1,5},{2,6},{3,7},{4,0},{5,1},{6,2},{7,3},{8,12},{9,13},{10,... | collective-permute-start | bytes 589832 | tf_op jit(solution)/shard_map/ppermute | solution.py:329
  44.5 13.6 %collective-permute-start.18 = (bf16[3,256,128]{2,1,0:T(8,128)(2,1)S(1)}, bf16[3,256,128]{2,1,0:T(8,128)(2,1)S(1)}, u32[]{:S(2)}, u32[]{:S(2)}) collective-permute-start(bf16[3,256,128]{2,1,0:T(8,128)(2,1)S(1)} %bitcast.188), channel_id=1, source_target_pairs={{0,6},{1,7},{2,4},{3,5},{4,2},{5,3},{6,0},{7,1},{8,14},{9,15},{10,... | collective-permute-start | bytes 589832 | tf_op jit(solution)/shard_map/ppermute | solution.py:329
  58.2 16.3 %collective-permute-start.19 = (bf16[3,4,64,128]{3,2,1,0:T(8,128)(2,1)S(1)}, bf16[3,4,64,128]{3,2,1,0:T(8,128)(2,1)S(1)}, u32[]{:S(2)}, u32[]{:S(2)}) collective-permute-start(bf16[3,4,64,128]{3,2,1,0:T(8,128)(2,1)S(1)} %get-tuple-element.27), channel_id=1, source_target_pairs={{0,8},{8,0},{16,24},{24,16},{1,9},{9,1},{17,25},{25,17},{2,10},{10... | collective-permute-start | bytes 589832 | tf_op jit(solution)/shard_map/ppermute | solution.py:333
  59.8 14.7 %collective-permute-start.20 = (bf16[3,4,64,128]{3,2,1,0:T(8,128)(2,1)S(1)}, bf16[3,4,64,128]{3,2,1,0:T(8,128)(2,1)S(1)}, u32[]{:S(2)}, u32[]{:S(2)}) collective-permute-start(bf16[3,4,64,128]{3,2,1,0:T(8,128)(2,1)S(1)} %get-tuple-element.26), channel_id=1, source_target_pairs={{0,24},{8,16},{16,8},{24,0},{1,25},{9,17},{17,9},{25,1},{2,26},{10... | collective-permute-start | bytes 589832 | tf_op jit(solution)/shard_map/ppermute | solution.py:334
  69.3 17.0 %collective-permute-start.11 = (bf16[1,256,128]{2,1,0:T(8,128)(2,1)S(1)}, bf16[1,256,128]{2,1,0:T(8,128)(2,1)S(1)}, u32[]{:S(2)}, u32[]{:S(2)}) collective-permute-start(bf16[1,256,128]{2,1,0:T(8,128)(2,1)S(1)} %bitcast.196), channel_id=1, source_target_pairs={{0,2},{1,3},{2,0},{3,1},{4,6},{5,7},{6,4},{7,5},{8,10},{9,11},{10,... | collective-permute-start | bytes 196616 | tf_op jit(solution)/shard_map/ppermute | solution.py:329
  72.1 14.2 %collective-permute-start.12 = (bf16[1,256,128]{2,1,0:T(8,128)(2,1)S(1)}, bf16[1,256,128]{2,1,0:T(8,128)(2,1)S(1)}, u32[]{:S(2)}, u32[]{:S(2)}) collective-permute-start(bf16[1,256,128]{2,1,0:T(8,128)(2,1)S(1)} %bitcast.197), channel_id=1, source_target_pairs={{0,4},{1,5},{2,6},{3,7},{4,0},{5,1},{6,2},{7,3},{8,12},{9,13},{10,... | collective-permute-start | bytes 196616 | tf_op jit(solution)/shard_map/ppermute | solution.py:329
  72.8 13.6 %collective-permute-start.13 = (bf16[1,256,128]{2,1,0:T(8,128)(2,1)S(1)}, bf16[1,256,128]{2,1,0:T(8,128)(2,1)S(1)}, u32[]{:S(2)}, u32[]{:S(2)}) collective-permute-start(bf16[1,256,128]{2,1,0:T(8,128)(2,1)S(1)} %bitcast.198), channel_id=1, source_target_pairs={{0,6},{1,7},{2,4},{3,5},{4,2},{5,3},{6,0},{7,1},{8,14},{9,15},{10,... | collective-permute-start | bytes 196616 | tf_op jit(solution)/shard_map/ppermute | solution.py:329
  86.6 5.2 %collective-permute-start.15 = (bf16[1,4,64,128]{3,2,1,0:T(8,128)(2,1)S(1)}, bf16[1,4,64,128]{3,2,1,0:T(8,128)(2,1)S(1)}, u32[]{:S(2)}, u32[]{:S(2)}) collective-permute-start(bf16[1,4,64,128]{3,2,1,0:T(8,128)(2,1)S(1)} %get-tuple-element.50), channel_id=1, source_target_pairs={{0,24},{8,16},{16,8},{24,0},{1,25},{9,17},{17,9},{25,1},{2,26},{10... | collective-permute-start | bytes 196616 | tf_op jit(solution)/shard_map/ppermute | solution.py:334
  93.1 4.5 %collective-permute-start.21 = (bf16[1,256,128]{2,1,0:T(8,128)(2,1)S(1)}, bf16[1,256,128]{2,1,0:T(8,128)(2,1)S(1)}, u32[]{:S(2)}, u32[]{:S(2)}) collective-permute-start(bf16[1,256,128]{2,1,0:T(8,128)(2,1)S(1)} %bitcast.201), channel_id=1, source_target_pairs={{0,2},{1,3},{2,0},{3,1},{4,6},{5,7},{6,4},{7,5},{8,10},{9,11},{10,... | collective-permute-start | bytes 196616 | tf_op jit(solution)/shard_map/ppermute | solution.py:329
  94.3 5.9 %collective-permute-start.22 = (bf16[1,256,128]{2,1,0:T(8,128)(2,1)S(1)}, bf16[1,256,128]{2,1,0:T(8,128)(2,1)S(1)}, u32[]{:S(2)}, u32[]{:S(2)}) collective-permute-start(bf16[1,256,128]{2,1,0:T(8,128)(2,1)S(1)} %bitcast.202), channel_id=1, source_target_pairs={{0,4},{1,5},{2,6},{3,7},{4,0},{5,1},{6,2},{7,3},{8,12},{9,13},{10,... | collective-permute-start | bytes 196616 | tf_op jit(solution)/shard_map/ppermute | solution.py:329
  95.9 6.1 %collective-permute-start.23 = (bf16[1,256,128]{2,1,0:T(8,128)(2,1)S(1)}, bf16[1,256,128]{2,1,0:T(8,128)(2,1)S(1)}, u32[]{:S(2)}, u32[]{:S(2)}) collective-permute-start(bf16[1,256,128]{2,1,0:T(8,128)(2,1)S(1)} %bitcast.203), channel_id=1, source_target_pairs={{0,6},{1,7},{2,4},{3,5},{4,2},{5,3},{6,0},{7,1},{8,14},{9,15},{10,... | collective-permute-start | bytes 196616 | tf_op jit(solution)/shard_map/ppermute | solution.py:329
  101.9 5.2 %collective-permute-start.24 = (bf16[1,4,64,128]{3,2,1,0:T(8,128)(2,1)S(1)}, bf16[1,4,64,128]{3,2,1,0:T(8,128)(2,1)S(1)}, u32[]{:S(2)}, u32[]{:S(2)}) collective-permute-start(bf16[1,4,64,128]{3,2,1,0:T(8,128)(2,1)S(1)} %get-tuple-element.49), channel_id=1, source_target_pairs={{0,8},{8,0},{16,24},{24,16},{1,9},{9,1},{17,25},{25,17},{2,10},{10... | collective-permute-start | bytes 196616 | tf_op jit(solution)/shard_map/ppermute | solution.py:333
  103.9 5.2 %collective-permute-start.25 = (bf16[1,4,64,128]{3,2,1,0:T(8,128)(2,1)S(1)}, bf16[1,4,64,128]{3,2,1,0:T(8,128)(2,1)S(1)}, u32[]{:S(2)}, u32[]{:S(2)}) collective-permute-start(bf16[1,4,64,128]{3,2,1,0:T(8,128)(2,1)S(1)} %get-tuple-element.48), channel_id=1, source_target_pairs={{0,24},{8,16},{16,8},{24,0},{1,25},{9,17},{17,9},{25,1},{2,26},{10... | collective-permute-start | bytes 196616 | tf_op jit(solution)/shard_map/ppermute | solution.py:334
  110.5 4.5 %collective-permute-start.26 = (bf16[1,256,128]{2,1,0:T(8,128)(2,1)S(1)}, bf16[1,256,128]{2,1,0:T(8,128)(2,1)S(1)}, u32[]{:S(2)}, u32[]{:S(2)}) collective-permute-start(bf16[1,256,128]{2,1,0:T(8,128)(2,1)S(1)} %bitcast.206), channel_id=1, source_target_pairs={{0,2},{1,3},{2,0},{3,1},{4,6},{5,7},{6,4},{7,5},{8,10},{9,11},{10,... | collective-permute-start | bytes 196616 | tf_op jit(solution)/shard_map/ppermute | solution.py:329
  110.6 5.2 %collective-permute-start.27 = (bf16[1,256,128]{2,1,0:T(8,128)(2,1)S(1)}, bf16[1,256,128]{2,1,0:T(8,128)(2,1)S(1)}, u32[]{:S(2)}, u32[]{:S(2)}) collective-permute-start(bf16[1,256,128]{2,1,0:T(8,128)(2,1)S(1)} %bitcast.207), channel_id=1, source_target_pairs={{0,4},{1,5},{2,6},{3,7},{4,0},{5,1},{6,2},{7,3},{8,12},{9,13},{10,... | collective-permute-start | bytes 196616 | tf_op jit(solution)/shard_map/ppermute | solution.py:329
  112.9 6.1 %collective-permute-start.28 = (bf16[1,256,128]{2,1,0:T(8,128)(2,1)S(1)}, bf16[1,256,128]{2,1,0:T(8,128)(2,1)S(1)}, u32[]{:S(2)}, u32[]{:S(2)}) collective-permute-start(bf16[1,256,128]{2,1,0:T(8,128)(2,1)S(1)} %bitcast.208), channel_id=1, source_target_pairs={{0,6},{1,7},{2,4},{3,5},{4,2},{5,3},{6,0},{7,1},{8,14},{9,15},{10,... | collective-permute-start | bytes 196616 | tf_op jit(solution)/shard_map/ppermute | solution.py:329
  119.2 5.2 %collective-permute-start.30 = (bf16[1,4,64,128]{3,2,1,0:T(8,128)(2,1)S(1)}, bf16[1,4,64,128]{3,2,1,0:T(8,128)(2,1)S(1)}, u32[]{:S(2)}, u32[]{:S(2)}) collective-permute-start(bf16[1,4,64,128]{3,2,1,0:T(8,128)(2,1)S(1)} %get-tuple-element.46), channel_id=1, source_target_pairs={{0,24},{8,16},{16,8},{24,0},{1,25},{9,17},{17,9},{25,1},{2,26},{10... | collective-permute-start | bytes 196616 | tf_op jit(solution)/shard_map/ppermute | solution.py:334
  125.8 11.7 %collective-permute-start.37 = (f32[64,256]{1,0:T(8,128)S(1)}, f32[64,256]{1,0:T(8,128)S(1)}, u32[]{:S(2)}, u32[]{:S(2)}) collective-permute-start(f32[64,256]{1,0:T(8,128)S(1)} %get-tuple-element.41), channel_id=1, source_target_pairs={{0,1},{1,0},{2,3},{3,2},{4,5},{5,4},{6,7},{7,6},{8,9},{9,8},{10,11... | collective-permute-start | bytes 196616 | tf_op jit(solution)/shard_map/ppermute | solution.py:316
  125.9 4.5 %collective-permute-start.31 = (bf16[128,128]{1,0:T(8,128)(2,1)S(1)}, bf16[128,128]{1,0:T(8,128)(2,1)S(1)}, u32[]{:S(2)}, u32[]{:S(2)}) collective-permute-start(bf16[128,128]{1,0:T(8,128)(2,1)S(1)} %bitcast.228), channel_id=1, source_target_pairs={{0,2},{1,3},{2,0},{3,1},{4,6},{5,7},{6,4},{7,5},{8,10},{9,11},{10,... | collective-permute-start | bytes 98312 | tf_op jit(solution)/shard_map/ppermute | solution.py:384
  126.0 4.9 %collective-permute-start.32 = (bf16[128,128]{1,0:T(8,128)(2,1)S(1)}, bf16[128,128]{1,0:T(8,128)(2,1)S(1)}, u32[]{:S(2)}, u32[]{:S(2)}) collective-permute-start(bf16[128,128]{1,0:T(8,128)(2,1)S(1)} %bitcast.227), channel_id=1, source_target_pairs={{0,4},{1,5},{2,6},{3,7},{4,0},{5,1},{6,2},{7,3},{8,12},{9,13},{10,... | collective-permute-start | bytes 98312 | tf_op jit(solution)/shard_map/ppermute | solution.py:384
  128.6 5.7 %collective-permute-start.33 = (bf16[128,128]{1,0:T(8,128)(2,1)S(1)}, bf16[128,128]{1,0:T(8,128)(2,1)S(1)}, u32[]{:S(2)}, u32[]{:S(2)}) collective-permute-start(bf16[128,128]{1,0:T(8,128)(2,1)S(1)} %bitcast.226), channel_id=1, source_target_pairs={{0,6},{1,7},{2,4},{3,5},{4,2},{5,3},{6,0},{7,1},{8,14},{9,15},{10,... | collective-permute-start | bytes 98312 | tf_op jit(solution)/shard_map/ppermute | solution.py:384
  136.4 5.2 %collective-permute-start.35 = (bf16[1,4,64,128]{3,2,1,0:T(8,128)(2,1)S(1)}, bf16[1,4,64,128]{3,2,1,0:T(8,128)(2,1)S(1)}, u32[]{:S(2)}, u32[]{:S(2)}) collective-permute-start(bf16[1,4,64,128]{3,2,1,0:T(8,128)(2,1)S(1)} %get-tuple-element.44), channel_id=1, source_target_pairs={{0,24},{8,16},{16,8},{24,0},{1,25},{9,17},{17,9},{25,1},{2,26},{10... | collective-permute-start | bytes 196616 | tf_op jit(solution)/shard_map/ppermute | solution.py:334
  (15 other events, 103.5 us)

commit v2 on v1

--- a/solution.py
+++ b/solution.py
@@ -6,6 +6,7 @@
 from jax.experimental import pallas as pl
 from jax.experimental.pallas import tpu as pltpu
 from jax.sharding import PartitionSpec as P
+
 
 FORGET_BIAS = 1.0
 VMEM_LIMIT = 14 * 1024 * 1024
@@ -211,6 +212,8 @@
         specs += [constant((1,) + edges[0].shape[1:], (index, 0, 0, 0))] * 2
         operands += list(edges)
     specs += [tap, tap, constant(init.shape)]
+    if edges is not None:
+        own, pair = (pltpu.with_memory_space_constraint(weight, pltpu.HBM) for weight in (own, pair))
     operands += [own, pair, init]
     return pl.pallas_call(
         functools.partial(conv_kernel, groups, cols, edges is not None),
@@ -282,10 +285,17 @@
             bytes_accessed=36 * channels * outs,
             transcendentals=0,
         ),
-    )(*parts, *edges, first, first_bias.reshape(1, -1), second, second_bias.reshape(1, -1))
-
-
-def per_device(
+    )(
+        *parts,
+        *edges,
+        pltpu.with_memory_space_constraint(first, pltpu.HBM),
+        first_bias.reshape(1, -1),
+        pltpu.with_memory_space_constraint(second, pltpu.HBM),
+        second_bias.reshape(1, -1),
+    )
+
+
+def program(
     frames,
     hidden_start,
     cell_start,
@@ -343,19 +353,31 @@
         turned = jnp.transpose(weight, (0, 1, 3, 4, 2))
         return turned.reshape(turned.shape[:2] + (-1,) + turned.shape[-1:])
 
-    hidden = joined(hidden_start, 0).reshape(1, count, width)
-    images = joined(frames, 1).reshape(steps, count, width)
-    input_own, hidden_own = gate_major(input_weight), gate_major(hidden_weight)
-    lead = jnp.concatenate([images[:1], hidden], 0)
+    def ordered(mine, other, axis):
+        return jnp.where(core == 0, jnp.concatenate([mine, other], axis), jnp.concatenate([other, mine], axis))
+
+    def of_batch(index):
+        return jnp.stack(
+            [
+                lax.dynamic_index_in_dim(frames[0], index, 0, keepdims=False),
+                lax.dynamic_index_in_dim(hidden_start, index, 0, keepdims=False),
+            ]
+        )
+
+    lead = ordered(of_batch(core), swap(of_batch(1 - core)), -1).reshape(2, count, width)
+    lead, frames, cell_start, gate_bias = lax.optimization_barrier((lead, frames, cell_start, gate_bias))
     lead_parts = gathered(lead)
-    input_pair, hidden_pair = swap(input_own), swap(hidden_own)
+    rest = joined(frames[1:], 1).reshape(steps - 1, count, width)
+    cell_mine, cell_other = own_batch(cell_start, 0)
+    cell = jnp.stack([cell_mine.reshape(count, share).T, cell_other.reshape(count, share).T])
     bias_own = gate_bias.reshape(-1)
     bias = jnp.concatenate([bias_own, swap(bias_own)]).reshape(-1, 1)
-    cell_mine, cell_other = own_batch(cell_start, 0)
-    cell = jnp.stack([cell_mine.reshape(count, share).T, cell_other.reshape(count, share).T])
+
+    lead_parts, rest, cell, bias, input_own, hidden_own = lax.optimization_barrier(
+        (lead_parts, rest, cell, bias, gate_major(input_weight), gate_major(hidden_weight))
+    )
+    input_pair, hidden_pair = swap(input_own), swap(hidden_own)
     lead_edges = edges_of(lead_parts)
-
-    rest, lead_edges = lax.optimization_barrier((images[1:], lead_edges))
     rest_parts = gathered(rest)
     rest_edges = edges_of(rest_parts)
 
@@ -405,7 +427,7 @@
 
 def solution(mesh):
     return jax.shard_map(
-        per_device,
+        program,
         mesh=mesh,
         in_specs=(
             P(None, None, "patch", None, "hid"),

time: 152 us -> 147 us (0.967)
  Pallas kernels: 33.2 us -> 50.1 us
  waiting for transfers between devices: 51.4 us -> 36.4 us
  local copies, waits for them, and re-layouts: 12.8 us -> 7.01 us
    ppermute x15, waiting for transfers between devices: 34.6 us -> 21.8 us  [gathered(): lax.ppermute(value, 'hid', [(i, i ^ 2 * k) for i in range(2 * groups)])]
    pallas_call x8, Pallas kernels: 24.3 us -> 32.8 us  [conv_call(): pl.pallas_call(functools.partial(conv_kernel, groups, cols, edges is not...]
    unnamed x18 -> x10, local copies, waits for them, and re-layouts: 6.01 us -> 0.03 us
    ppermute x6, waiting for transfers between devices: 9.01 us -> 4.17 us  [swapped_edges(): second = lax.ppermute(jnp.where(even, top, bottom), 'patch', outer_pairs)]
    pallas_call x4, Pallas kernels: 5.68 us -> 10.3 us  [gate_call(): pl.pallas_call(functools.partial(gate_kernel, cols), grid=(2,), in_specs=...]
    pallas_call x1, Pallas kernels: 3.16 us -> 7.07 us  [decoder_call(): pl.pallas_call(functools.partial(decoder_kernel, groups, rows, width, mar...]
  transfers between devices with their start and end apart: 38 -> 38, of which waited for: 21 -> 16; matrix products, arithmetic and copies ran while one was open for 5% -> 5% of each run, Pallas kernels for 17% -> 24%
where the time goes in v2:
time: 147 us; the launch traced here: 146 us
  Pallas kernels  50.1 us (34%)
  starting transfers between devices  49.1 us (33%)
  waiting for transfers between devices  36.4 us (25%)
  local copies, waits for them, and re-layouts  7.01 us (5%)
  other arithmetic  2.61 us (2%)
    pallas_call x8, Pallas kernels, conv_call(): pl.pallas_call(functools.partial(conv_kernel, groups, cols, edges is not...  32.8 us
    ppermute x15, starting transfers between devices, gathered(): lax.ppermute(value, 'hid', [(i, i ^ 2 * k) for i in range(2 * groups)])  26.9 us
    ppermute x15, waiting for transfers between devices, gathered(): lax.ppermute(value, 'hid', [(i, i ^ 2 * k) for i in range(2 * groups)])  21.8 us
    pallas_call x4, Pallas kernels, gate_call(): pl.pallas_call(functools.partial(gate_kernel, cols), grid=(2,), in_specs=...  10.3 us
    ppermute x6, starting transfers between devices, swapped_edges(): first = lax.ppermute(jnp.where(even, bottom, top), 'patch', inner_pairs)  8.04 us
    ppermute x6, starting transfers between devices, swapped_edges(): second = lax.ppermute(jnp.where(even, top, bottom), 'patch', outer_pairs)  7.82 us
    pallas_call x1, Pallas kernels, decoder_call(): pl.pallas_call(functools.partial(decoder_kernel, groups, rows, width, mar...  7.07 us
    ppermute x6, waiting for transfers between devices, swapped_edges(): first = lax.ppermute(jnp.where(even, bottom, top), 'patch', inner_pairs)  4.78 us
  transfers between devices with their start and end apart: 38, of which 16 were waited for; matrix products, arithmetic and copies ran while one was open for 5% of the time, Pallas kernels for 24%

profile of v2, /device:TPU:0, one launch (start us, length us, event | category | flops | bytes accessed | tf_op | source)
XLA Modules:
  0.0 146.4 jit_solution(14483293036619854143)
XLA Ops:
  4.4 3.0 %collective-permute-start.1 = (bf16[2,256,128]{2,1,0:T(8,128)(2,1)S(1)}, bf16[2,256,128]{2,1,0:T(8,128)(2,1)S(1)}, u32[]{:S(2)}, u32[]{:S(2)}) collective-permute-start(bf16[2,256,128]{2,1,0:T(8,128)(2,1)S(1)} %maximum_select_fusion.2.refs_0_), channel_id=1, source_target_pairs={{0,2},{1,3},{2,0},{3,1},{4,6},{5,7},{6,4},{7,5},{8,10},{9,11},{10,... | collective-permute-start | bytes 393224 | tf_op jit(solution)/shard_map/ppermute | solution.py:339
  7.4 2.6 %collective-permute-start.2 = (bf16[2,256,128]{2,1,0:T(8,128)(2,1)S(1)}, bf16[2,256,128]{2,1,0:T(8,128)(2,1)S(1)}, u32[]{:S(2)}, u32[]{:S(2)}) collective-permute-start(bf16[2,256,128]{2,1,0:T(8,128)(2,1)S(1)} %maximum_select_fusion.2.refs_0_), channel_id=1, source_target_pairs={{0,4},{1,5},{2,6},{3,7},{4,0},{5,1},{6,2},{7,3},{8,12},{9,13},{10,... | collective-permute-start | bytes 393224 | tf_op jit(solution)/shard_map/ppermute | solution.py:339
  16.0 4.3 %collective-permute-done.2.refs_2_ = bf16[2,256,128]{2,1,0:T(8,128)(2,1)S(1)} collective-permute-done((bf16[2,256,128]{2,1,0:T(8,128)(2,1)S(1)}, bf16[2,256,128]{2,1,0:T(8,128)(2,1)S(1)}, u32[]{:S(2)}, u32[]{:S(2)}) %collective-permute-start.2) | collective-permute-done | bytes 131104 | tf_op jit(solution)/shard_map/ppermute | solution.py:339
  20.8 2.3 %collective-permute-start.16 = (bf16[3,256,128]{2,1,0:T(8,128)(2,1)S(1)}, bf16[3,256,128]{2,1,0:T(8,128)(2,1)S(1)}, u32[]{:S(2)}, u32[]{:S(2)}) collective-permute-start(bf16[3,256,128]{2,1,0:T(8,128)(2,1)S(1)} %maximum_select_fusion.1.refs_0_), channel_id=1, source_target_pairs={{0,2},{1,3},{2,0},{3,1},{4,6},{5,7},{6,4},{7,5},{8,10},{9,11},{10,... | collective-permute-start | bytes 589832 | tf_op jit(solution)/shard_map/ppermute | solution.py:339
  26.4 2.8 %collective-permute-done.7.refs_4_ = bf16[2,4,64,128]{3,2,1,0:T(8,128)(2,1)S(1)} collective-permute-done((bf16[2,4,64,128]{3,2,1,0:T(8,128)(2,1)S(1)}, bf16[2,4,64,128]{3,2,1,0:T(8,128)(2,1)S(1)}, u32[]{:S(2)}, u32[]{:S(2)}) %collective-permute-start.7) | collective-permute-done | bytes 131104 | tf_op jit(solution)/shard_map/ppermute | solution.py:343
  30.5 1.8 %collective-permute-done.8.refs_5_ = bf16[2,4,64,128]{3,2,1,0:T(8,128)(2,1)S(1)} collective-permute-done((bf16[2,4,64,128]{3,2,1,0:T(8,128)(2,1)S(1)}, bf16[2,4,64,128]{3,2,1,0:T(8,128)(2,1)S(1)}, u32[]{:S(2)}, u32[]{:S(2)}) %collective-permute-start.8) | collective-permute-done | bytes 131104 | tf_op jit(solution)/shard_map/ppermute | solution.py:344
  32.3 2.5 %collective-permute-start.18 = (bf16[3,256,128]{2,1,0:T(8,128)(2,1)S(1)}, bf16[3,256,128]{2,1,0:T(8,128)(2,1)S(1)}, u32[]{:S(2)}, u32[]{:S(2)}) collective-permute-start(bf16[3,256,128]{2,1,0:T(8,128)(2,1)S(1)} %maximum_select_fusion.1.refs_0_), channel_id=1, source_target_pairs={{0,6},{1,7},{2,4},{3,5},{4,2},{5,3},{6,0},{7,1},{8,14},{9,15},{10,... | collective-permute-start | bytes 589832 | tf_op jit(solution)/shard_map/ppermute | solution.py:339
  34.8 9.1 %collective-permute-done.17.refs_2_ = bf16[3,256,128]{2,1,0:T(8,128)(2,1)S(1)} collective-permute-done((bf16[3,256,128]{2,1,0:T(8,128)(2,1)S(1)}, bf16[3,256,128]{2,1,0:T(8,128)(2,1)S(1)}, u32[]{:S(2)}, u32[]{:S(2)}) %collective-permute-start.17) | collective-permute-done | bytes 196640 | tf_op jit(solution)/shard_map/ppermute | solution.py:339
  44.0 2.1 %collective-permute-start.19 = (bf16[3,4,64,128]{3,2,1,0:T(8,128)(2,1)S(1)}, bf16[3,4,64,128]{3,2,1,0:T(8,128)(2,1)S(1)}, u32[]{:S(2)}, u32[]{:S(2)}) collective-permute-start(bf16[3,4,64,128]{3,2,1,0:T(8,128)(2,1)S(1)} %get-tuple-element.45), channel_id=1, source_target_pairs={{0,8},{8,0},{16,24},{24,16},{1,9},{9,1},{17,25},{25,17},{2,10},{10... | collective-permute-start | bytes 589832 | tf_op jit(solution)/shard_map/ppermute | solution.py:343
  47.6 4.4 %shard_map.113.refs_6_ = f32[512,256]{1,0:T(8,128)S(1)} custom-call(bf16[2,256,128]{2,1,0:T(8,128)(2,1)S(1)} %maximum_select_fusion.2.refs_0_, bf16[2,256,128]{2,1,0:T(8,128)(2,1)S(1)} %collective-permute-done.1.refs_1_, bf16[2,256,128]{2,1,0:T(8,128)(2,1)S(1)} %collective-permute-done.2.refs_2_, bf16[2,256,128]{2,1,0:T(8,128)(2,1)S(1)} %collective-permute-done.3.refs_3_, ...), custom_call_target="tpu_custom_call" | custom-call | flops 1207959552 | bytes 4718592 | tf_op jit(solution)/shard_map/pallas_call | solution.py:218
  52.0 3.8 %shard_map.114.total_ref = f32[512,256]{1,0:T(8,128)S(1)} custom-call(bf16[2,256,128]{2,1,0:T(8,128)(2,1)S(1)} %maximum_select_fusion.2.refs_0_, bf16[2,256,128]{2,1,0:T(8,128)(2,1)S(1)} %collective-permute-done.1.refs_1_, bf16[2,256,128]{2,1,0:T(8,128)(2,1)S(1)} %collective-permute-done.2.refs_2_, bf16[2,256,128]{2,1,0:T(8,128)(2,1)S(1)} %collective-permute-done.3.refs_3_, ...), custom_call_target="tpu_custom_call" | custom-call | flops 1207959552 | bytes 4718592 | tf_op jit(solution)/shard_map/pallas_call | solution.py:218
  55.8 2.6 %shard_map.115 = (bf16[256,128]{1,0:T(8,128)(2,1)S(1)}, f32[2,64,256]{2,1,0:T(8,128)S(1)}) custom-call(bf16[1,4,64,128]{3,2,1,0:T(8,128)(2,1)S(1)} %slice.219.edge_a, bf16[1,4,64,128]{3,2,1,0:T(8,128)(2,1)S(1)} %slice.220.edge_b, bf16[3,3,256,512]{3,2,1,0:T(8,128)(2,1)S(1)} %bitcast.173, bf16[3,3,256,512]{3,2,1,0:T(8,128)(2,1)} %collective-permute-done.9.refs_5_.pair_ref, ...), custom_call_target="tpu_custom_call" | custom-call | flops 402653184 | bytes 3145728 | tf_op jit(solution)/shard_map/pallas_call | solution.py:238
  58.4 3.9 %collective-permute-start.11 = (bf16[1,256,128]{2,1,0:T(8,128)(2,1)S(1)}, bf16[1,256,128]{2,1,0:T(8,128)(2,1)S(1)}, u32[]{:S(2)}, u32[]{:S(2)}) collective-permute-start(bf16[1,256,128]{2,1,0:T(8,128)(2,1)S(1)} %bitcast.183), channel_id=1, source_target_pairs={{0,2},{1,3},{2,0},{3,1},{4,6},{5,7},{6,4},{7,5},{8,10},{9,11},{10,... | collective-permute-start | bytes 196616 | tf_op jit(solution)/shard_map/ppermute | solution.py:339
  64.8 4.4 %shard_map.122.refs_6_ = f32[512,256]{1,0:T(8,128)S(1)} custom-call(bf16[3,256,128]{2,1,0:T(8,128)(2,1)S(1)} %maximum_select_fusion.1.refs_0_, bf16[3,256,128]{2,1,0:T(8,128)(2,1)S(1)} %collective-permute-done.16.refs_1_, bf16[3,256,128]{2,1,0:T(8,128)(2,1)S(1)} %collective-permute-done.17.refs_2_, bf16[3,256,128]{2,1,0:T(8,128)(2,1)S(1)} %collective-permute-done.18.refs_3_, ...), custom_call_target="tpu_custom_call" | custom-call | flops 1207959552 | bytes 4718592 | tf_op jit(solution)/shard_map/pallas_call | solution.py:218
  69.2 4.4 %shard_map.119.refs_6_ = f32[512,256]{1,0:T(8,128)S(1)} custom-call(bf16[3,256,128]{2,1,0:T(8,128)(2,1)S(1)} %maximum_select_fusion.1.refs_0_, bf16[3,256,128]{2,1,0:T(8,128)(2,1)S(1)} %collective-permute-done.16.refs_1_, bf16[3,256,128]{2,1,0:T(8,128)(2,1)S(1)} %collective-permute-done.17.refs_2_, bf16[3,256,128]{2,1,0:T(8,128)(2,1)S(1)} %collective-permute-done.18.refs_3_, ...), custom_call_target="tpu_custom_call" | custom-call | flops 1207959552 | bytes 4718592 | tf_op jit(solution)/shard_map/pallas_call | solution.py:218
  73.7 4.4 %shard_map.116.refs_6_ = f32[512,256]{1,0:T(8,128)S(1)} custom-call(bf16[3,256,128]{2,1,0:T(8,128)(2,1)S(1)} %maximum_select_fusion.1.refs_0_, bf16[3,256,128]{2,1,0:T(8,128)(2,1)S(1)} %collective-permute-done.16.refs_1_, bf16[3,256,128]{2,1,0:T(8,128)(2,1)S(1)} %collective-permute-done.17.refs_2_, bf16[3,256,128]{2,1,0:T(8,128)(2,1)S(1)} %collective-permute-done.18.refs_3_, ...), custom_call_target="tpu_custom_call" | custom-call | flops 1207959552 | bytes 4718592 | tf_op jit(solution)/shard_map/pallas_call | solution.py:218
  80.2 3.8 %shard_map.117.total_ref = f32[512,256]{1,0:T(8,128)S(1)} custom-call(bf16[1,256,128]{2,1,0:T(8,128)(2,1)S(1)} %bitcast.187, bf16[1,256,128]{2,1,0:T(8,128)(2,1)S(1)} %collective-permute-done.11.refs_1_, bf16[1,256,128]{2,1,0:T(8,128)(2,1)S(1)} %collective-permute-done.12.refs_2_, bf16[1,256,128]{2,1,0:T(8,128)(2,1)S(1)} %collective-permute-done.13.refs_3_, ...), custom_call_target="tpu_custom_call" | custom-call | flops 1207959552 | bytes 4718592 | tf_op jit(solution)/shard_map/pallas_call | solution.py:218
  84.9 2.6 %shard_map.118 = (bf16[256,128]{1,0:T(8,128)(2,1)S(1)}, f32[2,64,256]{2,1,0:T(8,128)S(1)}) custom-call(bf16[1,4,64,128]{3,2,1,0:T(8,128)(2,1)S(1)} %collective-permute-done.14.edge_a, bf16[1,4,64,128]{3,2,1,0:T(8,128)(2,1)S(1)} %collective-permute-done.15.edge_b, bf16[3,3,256,512]{3,2,1,0:T(8,128)(2,1)S(1)} %bitcast.175, ...), custom_call_target="tpu_custom_call" | custom-call | flops 402653184 | bytes 3145728 | tf_op jit(solution)/shard_map/pallas_call | solution.py:238
  88.6 2.0 %collective-permute-start.22 = (bf16[1,256,128]{2,1,0:T(8,128)(2,1)S(1)}, bf16[1,256,128]{2,1,0:T(8,128)(2,1)S(1)}, u32[]{:S(2)}, u32[]{:S(2)}) collective-permute-start(bf16[1,256,128]{2,1,0:T(8,128)(2,1)S(1)} %bitcast.189), channel_id=1, source_target_pairs={{0,4},{1,5},{2,6},{3,7},{4,0},{5,1},{6,2},{7,3},{8,12},{9,13},{10,... | collective-permute-start | bytes 196616 | tf_op jit(solution)/shard_map/ppermute | solution.py:339
  92.5 1.9 %collective-permute-done.22.refs_2_ = bf16[1,256,128]{2,1,0:T(8,128)(2,1)S(1)} collective-permute-done((bf16[1,256,128]{2,1,0:T(8,128)(2,1)S(1)}, bf16[1,256,128]{2,1,0:T(8,128)(2,1)S(1)}, u32[]{:S(2)}, u32[]{:S(2)}) %collective-permute-start.22) | collective-permute-done | bytes 65568 | tf_op jit(solution)/shard_map/ppermute | solution.py:339
  94.4 2.2 %collective-permute-done.23.refs_3_ = bf16[1,256,128]{2,1,0:T(8,128)(2,1)S(1)} collective-permute-done((bf16[1,256,128]{2,1,0:T(8,128)(2,1)S(1)}, bf16[1,256,128]{2,1,0:T(8,128)(2,1)S(1)}, u32[]{:S(2)}, u32[]{:S(2)}) %collective-permute-start.23) | collective-permute-done | bytes 65568 | tf_op jit(solution)/shard_map/ppermute | solution.py:339
  98.8 3.8 %shard_map.120.total_ref = f32[512,256]{1,0:T(8,128)S(1)} custom-call(bf16[1,256,128]{2,1,0:T(8,128)(2,1)S(1)} %bitcast.192, bf16[1,256,128]{2,1,0:T(8,128)(2,1)S(1)} %collective-permute-done.21.refs_1_, bf16[1,256,128]{2,1,0:T(8,128)(2,1)S(1)} %collective-permute-done.22.refs_2_, bf16[1,256,128]{2,1,0:T(8,128)(2,1)S(1)} %collective-permute-done.23.refs_3_, ...), custom_call_target="tpu_custom_call" | custom-call | flops 1207959552 | bytes 4718592 | tf_op jit(solution)/shard_map/pallas_call | solution.py:218
  102.6 2.6 %shard_map.121 = (bf16[256,128]{1,0:T(8,128)(2,1)S(1)}, f32[2,64,256]{2,1,0:T(8,128)S(1)}) custom-call(bf16[1,4,64,128]{3,2,1,0:T(8,128)(2,1)S(1)} %collective-permute-done.24.edge_a, bf16[1,4,64,128]{3,2,1,0:T(8,128)(2,1)S(1)} %collective-permute-done.25.edge_b, bf16[3,3,256,512]{3,2,1,0:T(8,128)(2,1)S(1)} %bitcast.177, ...), custom_call_target="tpu_custom_call" | custom-call | flops 402653184 | bytes 3145728 | tf_op jit(solution)/shard_map/pallas_call | solution.py:238
  105.2 2.1 %collective-permute-start.27 = (bf16[1,256,128]{2,1,0:T(8,128)(2,1)S(1)}, bf16[1,256,128]{2,1,0:T(8,128)(2,1)S(1)}, u32[]{:S(2)}, u32[]{:S(2)}) collective-permute-start(bf16[1,256,128]{2,1,0:T(8,128)(2,1)S(1)} %bitcast.194), channel_id=1, source_target_pairs={{0,4},{1,5},{2,6},{3,7},{4,0},{5,1},{6,2},{7,3},{8,12},{9,13},{10,... | collective-permute-start | bytes 196616 | tf_op jit(solution)/shard_map/ppermute | solution.py:339
  107.3 2.3 %collective-permute-start.28 = (bf16[1,256,128]{2,1,0:T(8,128)(2,1)S(1)}, bf16[1,256,128]{2,1,0:T(8,128)(2,1)S(1)}, u32[]{:S(2)}, u32[]{:S(2)}) collective-permute-start(bf16[1,256,128]{2,1,0:T(8,128)(2,1)S(1)} %bitcast.195), channel_id=1, source_target_pairs={{0,6},{1,7},{2,4},{3,5},{4,2},{5,3},{6,0},{7,1},{8,14},{9,15},{10,... | collective-permute-start | bytes 196616 | tf_op jit(solution)/shard_map/ppermute | solution.py:339
  110.5 2.9 %collective-permute-done.28.refs_3_ = bf16[1,256,128]{2,1,0:T(8,128)(2,1)S(1)} collective-permute-done((bf16[1,256,128]{2,1,0:T(8,128)(2,1)S(1)}, bf16[1,256,128]{2,1,0:T(8,128)(2,1)S(1)}, u32[]{:S(2)}, u32[]{:S(2)}) %collective-permute-start.28) | collective-permute-done | bytes 65568 | tf_op jit(solution)/shard_map/ppermute | solution.py:339
  116.3 3.8 %shard_map.123.total_ref = f32[512,256]{1,0:T(8,128)S(1)} custom-call(bf16[1,256,128]{2,1,0:T(8,128)(2,1)S(1)} %bitcast.197, bf16[1,256,128]{2,1,0:T(8,128)(2,1)S(1)} %collective-permute-done.26.refs_1_, bf16[1,256,128]{2,1,0:T(8,128)(2,1)S(1)} %collective-permute-done.27.refs_2_, bf16[1,256,128]{2,1,0:T(8,128)(2,1)S(1)} %collective-permute-done.28.refs_3_, ...), custom_call_target="tpu_custom_call" | custom-call | flops 1207959552 | bytes 4718592 | tf_op jit(solution)/shard_map/pallas_call | solution.py:218
  120.1 2.6 %shard_map.124 = (bf16[256,128]{1,0:T(8,128)(2,1)S(1)}, f32[2,64,256]{2,1,0:T(8,128)S(1)}) custom-call(bf16[1,4,64,128]{3,2,1,0:T(8,128)(2,1)S(1)} %collective-permute-done.29.edge_a, bf16[1,4,64,128]{3,2,1,0:T(8,128)(2,1)S(1)} %collective-permute-done.30.edge_b, bf16[3,3,256,512]{3,2,1,0:T(8,128)(2,1)S(1)} %bitcast.179, ...), custom_call_target="tpu_custom_call" | custom-call | flops 402653184 | bytes 3145728 | tf_op jit(solution)/shard_map/pallas_call | solution.py:238
  123.0 2.9 %collective-permute-start.32 = (bf16[128,128]{1,0:T(8,128)(2,1)S(1)}, bf16[128,128]{1,0:T(8,128)(2,1)S(1)}, u32[]{:S(2)}, u32[]{:S(2)}) collective-permute-start(bf16[128,128]{1,0:T(8,128)(2,1)S(1)} %bitcast.220), channel_id=1, source_target_pairs={{0,4},{1,5},{2,6},{3,7},{4,0},{5,1},{6,2},{7,3},{8,12},{9,13},{10,... | collective-permute-start | bytes 98312 | tf_op jit(solution)/shard_map/ppermute | solution.py:406
  127.8 3.7 %collective-permute-done.33.refs_3_ = bf16[128,128]{1,0:T(8,128)(2,1)S(1)} collective-permute-done((bf16[128,128]{1,0:T(8,128)(2,1)S(1)}, bf16[128,128]{1,0:T(8,128)(2,1)S(1)}, u32[]{:S(2)}, u32[]{:S(2)}) %collective-permute-start.33) | collective-permute-done | bytes 32800 | tf_op jit(solution)/shard_map/ppermute | solution.py:406
  133.9 2.0 %collective-permute-done.34.refs_4_ = bf16[1,4,64,128]{3,2,1,0:T(8,128)(2,1)S(1)} collective-permute-done((bf16[1,4,64,128]{3,2,1,0:T(8,128)(2,1)S(1)}, bf16[1,4,64,128]{3,2,1,0:T(8,128)(2,1)S(1)}, u32[]{:S(2)}, u32[]{:S(2)}) %collective-permute-start.34) | collective-permute-done | bytes 65568 | tf_op jit(solution)/shard_map/ppermute | solution.py:343
  137.4 7.1 %shard_map.125 = bf16[128,512]{1,0:T(8,128)(2,1)S(1)} custom-call(bf16[128,128]{1,0:T(8,128)(2,1)S(1)} %bitcast.198, bf16[128,128]{1,0:T(8,128)(2,1)S(1)} %collective-permute-done.31.refs_1_, bf16[128,128]{1,0:T(8,128)(2,1)S(1)} %collective-permute-done.32.refs_2_, bf16[128,128]{1,0:T(8,128)(2,1)S(1)} %collective-permute-done.33.refs_3_, ...), custom_call_target="tpu_custom_call" | custom-call | flops 1509949440 | bytes 9437184 | tf_op jit(solution)/shard_map/pallas_call | solution.py:263
  (120 shorter events, 38.8 us)
Async XLA Ops:
  4.4 11.6 %collective-permute-start.1 = (bf16[2,256,128]{2,1,0:T(8,128)(2,1)S(1)}, bf16[2,256,128]{2,1,0:T(8,128)(2,1)S(1)}, u32[]{:S(2)}, u32[]{:S(2)}) collective-permute-start(bf16[2,256,128]{2,1,0:T(8,128)(2,1)S(1)} %maximum_select_fusion.2.refs_0_), channel_id=1, source_target_pairs={{0,2},{1,3},{2,0},{3,1},{4,6},{5,7},{6,4},{7,5},{8,10},{9,11},{10,... | collective-permute-start | bytes 393224 | tf_op jit(solution)/shard_map/ppermute | solution.py:339
  7.4 12.9 %collective-permute-start.2 = (bf16[2,256,128]{2,1,0:T(8,128)(2,1)S(1)}, bf16[2,256,128]{2,1,0:T(8,128)(2,1)S(1)}, u32[]{:S(2)}, u32[]{:S(2)}) collective-permute-start(bf16[2,256,128]{2,1,0:T(8,128)(2,1)S(1)} %maximum_select_fusion.2.refs_0_), channel_id=1, source_target_pairs={{0,4},{1,5},{2,6},{3,7},{4,0},{5,1},{6,2},{7,3},{8,12},{9,13},{10,... | collective-permute-start | bytes 393224 | tf_op jit(solution)/shard_map/ppermute | solution.py:339
  10.0 10.3 %collective-permute-start.3 = (bf16[2,256,128]{2,1,0:T(8,128)(2,1)S(1)}, bf16[2,256,128]{2,1,0:T(8,128)(2,1)S(1)}, u32[]{:S(2)}, u32[]{:S(2)}) collective-permute-start(bf16[2,256,128]{2,1,0:T(8,128)(2,1)S(1)} %maximum_select_fusion.2.refs_0_), channel_id=1, source_target_pairs={{0,6},{1,7},{2,4},{3,5},{4,2},{5,3},{6,0},{7,1},{8,14},{9,15},{10,... | collective-permute-start | bytes 393224 | tf_op jit(solution)/shard_map/ppermute | solution.py:339
  20.3 27.3 %collective-permute-start.10 = (bf16[3,3,256,512]{3,2,1,0:T(8,128)(2,1)}, bf16[3,3,256,512]{3,2,1,0:T(8,128)(2,1)}, u32[]{:S(2)}, u32[]{:S(2)}) collective-permute-start(bf16[3,3,256,512]{3,2,1,0:T(8,128)(2,1)} %bitcast.201), channel_id=1, source_target_pairs={{0,1},{1,0},{2,3},{3,2},{4,5},{5,4},{6,7},{7,6},{8,9},{9,8},{10,11... | collective-permute-start | bytes 7077896 | tf_op jit(solution)/shard_map/ppermute | solution.py:326
  20.3 31.7 %collective-permute-start.9 = (bf16[3,3,256,512]{3,2,1,0:T(8,128)(2,1)S(1)}, bf16[3,3,256,512]{3,2,1,0:T(8,128)(2,1)}, u32[]{:S(2)}, u32[]{:S(2)}) collective-permute-start(bf16[3,3,256,512]{3,2,1,0:T(8,128)(2,1)S(1)} %bitcast.171), channel_id=1, source_target_pairs={{0,1},{1,0},{2,3},{3,2},{4,5},{5,4},{6,7},{7,6},{8,9},{9,8},{10,11... | collective-permute-start | bytes 7077896 | tf_op jit(solution)/shard_map/ppermute | solution.py:326
  20.8 14.0 %collective-permute-start.16 = (bf16[3,256,128]{2,1,0:T(8,128)(2,1)S(1)}, bf16[3,256,128]{2,1,0:T(8,128)(2,1)S(1)}, u32[]{:S(2)}, u32[]{:S(2)}) collective-permute-start(bf16[3,256,128]{2,1,0:T(8,128)(2,1)S(1)} %maximum_select_fusion.1.refs_0_), channel_id=1, source_target_pairs={{0,2},{1,3},{2,0},{3,1},{4,6},{5,7},{6,4},{7,5},{8,10},{9,11},{10,... | collective-permute-start | bytes 589832 | tf_op jit(solution)/shard_map/ppermute | solution.py:339
  23.3 5.8 %collective-permute-start.7 = (bf16[2,4,64,128]{3,2,1,0:T(8,128)(2,1)S(1)}, bf16[2,4,64,128]{3,2,1,0:T(8,128)(2,1)S(1)}, u32[]{:S(2)}, u32[]{:S(2)}) collective-permute-start(bf16[2,4,64,128]{3,2,1,0:T(8,128)(2,1)S(1)} %get-tuple-element.49), channel_id=1, source_target_pairs={{0,8},{8,0},{16,24},{24,16},{1,9},{9,1},{17,25},{25,17},{2,10},{10... | collective-permute-start | bytes 393224 | tf_op jit(solution)/shard_map/ppermute | solution.py:343
  24.9 7.4 %collective-permute-start.8 = (bf16[2,4,64,128]{3,2,1,0:T(8,128)(2,1)S(1)}, bf16[2,4,64,128]{3,2,1,0:T(8,128)(2,1)S(1)}, u32[]{:S(2)}, u32[]{:S(2)}) collective-permute-start(bf16[2,4,64,128]{3,2,1,0:T(8,128)(2,1)S(1)} %get-tuple-element.48), channel_id=1, source_target_pairs={{0,24},{8,16},{16,8},{24,0},{1,25},{9,17},{17,9},{25,1},{2,26},{10... | collective-permute-start | bytes 393224 | tf_op jit(solution)/shard_map/ppermute | solution.py:344
  29.2 14.7 %collective-permute-start.17 = (bf16[3,256,128]{2,1,0:T(8,128)(2,1)S(1)}, bf16[3,256,128]{2,1,0:T(8,128)(2,1)S(1)}, u32[]{:S(2)}, u32[]{:S(2)}) collective-permute-start(bf16[3,256,128]{2,1,0:T(8,128)(2,1)S(1)} %maximum_select_fusion.1.refs_0_), channel_id=1, source_target_pairs={{0,4},{1,5},{2,6},{3,7},{4,0},{5,1},{6,2},{7,3},{8,12},{9,13},{10,... | collective-permute-start | bytes 589832 | tf_op jit(solution)/shard_map/ppermute | solution.py:339
  32.3 11.6 %collective-permute-start.18 = (bf16[3,256,128]{2,1,0:T(8,128)(2,1)S(1)}, bf16[3,256,128]{2,1,0:T(8,128)(2,1)S(1)}, u32[]{:S(2)}, u32[]{:S(2)}) collective-permute-start(bf16[3,256,128]{2,1,0:T(8,128)(2,1)S(1)} %maximum_select_fusion.1.refs_0_), channel_id=1, source_target_pairs={{0,6},{1,7},{2,4},{3,5},{4,2},{5,3},{6,0},{7,1},{8,14},{9,15},{10,... | collective-permute-start | bytes 589832 | tf_op jit(solution)/shard_map/ppermute | solution.py:339
  44.0 20.8 %collective-permute-start.19 = (bf16[3,4,64,128]{3,2,1,0:T(8,128)(2,1)S(1)}, bf16[3,4,64,128]{3,2,1,0:T(8,128)(2,1)S(1)}, u32[]{:S(2)}, u32[]{:S(2)}) collective-permute-start(bf16[3,4,64,128]{3,2,1,0:T(8,128)(2,1)S(1)} %get-tuple-element.45), channel_id=1, source_target_pairs={{0,8},{8,0},{16,24},{24,16},{1,9},{9,1},{17,25},{25,17},{2,10},{10... | collective-permute-start | bytes 589832 | tf_op jit(solution)/shard_map/ppermute | solution.py:343
  46.1 18.7 %collective-permute-start.20 = (bf16[3,4,64,128]{3,2,1,0:T(8,128)(2,1)S(1)}, bf16[3,4,64,128]{3,2,1,0:T(8,128)(2,1)S(1)}, u32[]{:S(2)}, u32[]{:S(2)}) collective-permute-start(bf16[3,4,64,128]{3,2,1,0:T(8,128)(2,1)S(1)} %get-tuple-element.44), channel_id=1, source_target_pairs={{0,24},{8,16},{16,8},{24,0},{1,25},{9,17},{17,9},{25,1},{2,26},{10... | collective-permute-start | bytes 589832 | tf_op jit(solution)/shard_map/ppermute | solution.py:344
  58.4 19.7 %collective-permute-start.11 = (bf16[1,256,128]{2,1,0:T(8,128)(2,1)S(1)}, bf16[1,256,128]{2,1,0:T(8,128)(2,1)S(1)}, u32[]{:S(2)}, u32[]{:S(2)}) collective-permute-start(bf16[1,256,128]{2,1,0:T(8,128)(2,1)S(1)} %bitcast.183), channel_id=1, source_target_pairs={{0,2},{1,3},{2,0},{3,1},{4,6},{5,7},{6,4},{7,5},{8,10},{9,11},{10,... | collective-permute-start | bytes 196616 | tf_op jit(solution)/shard_map/ppermute | solution.py:339
  62.3 15.8 %collective-permute-start.12 = (bf16[1,256,128]{2,1,0:T(8,128)(2,1)S(1)}, bf16[1,256,128]{2,1,0:T(8,128)(2,1)S(1)}, u32[]{:S(2)}, u32[]{:S(2)}) collective-permute-start(bf16[1,256,128]{2,1,0:T(8,128)(2,1)S(1)} %bitcast.184), channel_id=1, source_target_pairs={{0,4},{1,5},{2,6},{3,7},{4,0},{5,1},{6,2},{7,3},{8,12},{9,13},{10,... | collective-permute-start | bytes 196616 | tf_op jit(solution)/shard_map/ppermute | solution.py:339
  63.4 14.7 %collective-permute-start.13 = (bf16[1,256,128]{2,1,0:T(8,128)(2,1)S(1)}, bf16[1,256,128]{2,1,0:T(8,128)(2,1)S(1)}, u32[]{:S(2)}, u32[]{:S(2)}) collective-permute-start(bf16[1,256,128]{2,1,0:T(8,128)(2,1)S(1)} %bitcast.185), channel_id=1, source_target_pairs={{0,6},{1,7},{2,4},{3,5},{4,2},{5,3},{6,0},{7,1},{8,14},{9,15},{10,... | collective-permute-start | bytes 196616 | tf_op jit(solution)/shard_map/ppermute | solution.py:339
  78.2 5.8 %collective-permute-start.14 = (bf16[1,4,64,128]{3,2,1,0:T(8,128)(2,1)S(1)}, bf16[1,4,64,128]{3,2,1,0:T(8,128)(2,1)S(1)}, u32[]{:S(2)}, u32[]{:S(2)}) collective-permute-start(bf16[1,4,64,128]{3,2,1,0:T(8,128)(2,1)S(1)} %get-tuple-element.71), channel_id=1, source_target_pairs={{0,8},{8,0},{16,24},{24,16},{1,9},{9,1},{17,25},{25,17},{2,10},{10... | collective-permute-start | bytes 196616 | tf_op jit(solution)/shard_map/ppermute | solution.py:343
  79.7 5.2 %collective-permute-start.15 = (bf16[1,4,64,128]{3,2,1,0:T(8,128)(2,1)S(1)}, bf16[1,4,64,128]{3,2,1,0:T(8,128)(2,1)S(1)}, u32[]{:S(2)}, u32[]{:S(2)}) collective-permute-start(bf16[1,4,64,128]{3,2,1,0:T(8,128)(2,1)S(1)} %get-tuple-element.70), channel_id=1, source_target_pairs={{0,24},{8,16},{16,8},{24,0},{1,25},{9,17},{17,9},{25,1},{2,26},{10... | collective-permute-start | bytes 196616 | tf_op jit(solution)/shard_map/ppermute | solution.py:344
  87.5 5.0 %collective-permute-start.21 = (bf16[1,256,128]{2,1,0:T(8,128)(2,1)S(1)}, bf16[1,256,128]{2,1,0:T(8,128)(2,1)S(1)}, u32[]{:S(2)}, u32[]{:S(2)}) collective-permute-start(bf16[1,256,128]{2,1,0:T(8,128)(2,1)S(1)} %bitcast.188), channel_id=1, source_target_pairs={{0,2},{1,3},{2,0},{3,1},{4,6},{5,7},{6,4},{7,5},{8,10},{9,11},{10,... | collective-permute-start | bytes 196616 | tf_op jit(solution)/shard_map/ppermute | solution.py:339
  88.6 5.9 %collective-permute-start.22 = (bf16[1,256,128]{2,1,0:T(8,128)(2,1)S(1)}, bf16[1,256,128]{2,1,0:T(8,128)(2,1)S(1)}, u32[]{:S(2)}, u32[]{:S(2)}) collective-permute-start(bf16[1,256,128]{2,1,0:T(8,128)(2,1)S(1)} %bitcast.189), channel_id=1, source_target_pairs={{0,4},{1,5},{2,6},{3,7},{4,0},{5,1},{6,2},{7,3},{8,12},{9,13},{10,... | collective-permute-start | bytes 196616 | tf_op jit(solution)/shard_map/ppermute | solution.py:339
  90.5 6.1 %collective-permute-start.23 = (bf16[1,256,128]{2,1,0:T(8,128)(2,1)S(1)}, bf16[1,256,128]{2,1,0:T(8,128)(2,1)S(1)}, u32[]{:S(2)}, u32[]{:S(2)}) collective-permute-start(bf16[1,256,128]{2,1,0:T(8,128)(2,1)S(1)} %bitcast.190), channel_id=1, source_target_pairs={{0,6},{1,7},{2,4},{3,5},{4,2},{5,3},{6,0},{7,1},{8,14},{9,15},{10,... | collective-permute-start | bytes 196616 | tf_op jit(solution)/shard_map/ppermute | solution.py:339
  96.6 5.9 %collective-permute-start.24 = (bf16[1,4,64,128]{3,2,1,0:T(8,128)(2,1)S(1)}, bf16[1,4,64,128]{3,2,1,0:T(8,128)(2,1)S(1)}, u32[]{:S(2)}, u32[]{:S(2)}) collective-permute-start(bf16[1,4,64,128]{3,2,1,0:T(8,128)(2,1)S(1)} %get-tuple-element.69), channel_id=1, source_target_pairs={{0,8},{8,0},{16,24},{24,16},{1,9},{9,1},{17,25},{25,17},{2,10},{10... | collective-permute-start | bytes 196616 | tf_op jit(solution)/shard_map/ppermute | solution.py:343
  97.3 5.3 %collective-permute-start.25 = (bf16[1,4,64,128]{3,2,1,0:T(8,128)(2,1)S(1)}, bf16[1,4,64,128]{3,2,1,0:T(8,128)(2,1)S(1)}, u32[]{:S(2)}, u32[]{:S(2)}) collective-permute-start(bf16[1,4,64,128]{3,2,1,0:T(8,128)(2,1)S(1)} %get-tuple-element.68), channel_id=1, source_target_pairs={{0,24},{8,16},{16,8},{24,0},{1,25},{9,17},{17,9},{25,1},{2,26},{10... | collective-permute-start | bytes 196616 | tf_op jit(solution)/shard_map/ppermute | solution.py:344
  105.2 4.5 %collective-permute-start.26 = (bf16[1,256,128]{2,1,0:T(8,128)(2,1)S(1)}, bf16[1,256,128]{2,1,0:T(8,128)(2,1)S(1)}, u32[]{:S(2)}, u32[]{:S(2)}) collective-permute-start(bf16[1,256,128]{2,1,0:T(8,128)(2,1)S(1)} %bitcast.193), channel_id=1, source_target_pairs={{0,2},{1,3},{2,0},{3,1},{4,6},{5,7},{6,4},{7,5},{8,10},{9,11},{10,... | collective-permute-start | bytes 196616 | tf_op jit(solution)/shard_map/ppermute | solution.py:339
  105.2 5.2 %collective-permute-start.27 = (bf16[1,256,128]{2,1,0:T(8,128)(2,1)S(1)}, bf16[1,256,128]{2,1,0:T(8,128)(2,1)S(1)}, u32[]{:S(2)}, u32[]{:S(2)}) collective-permute-start(bf16[1,256,128]{2,1,0:T(8,128)(2,1)S(1)} %bitcast.194), channel_id=1, source_target_pairs={{0,4},{1,5},{2,6},{3,7},{4,0},{5,1},{6,2},{7,3},{8,12},{9,13},{10,... | collective-permute-start | bytes 196616 | tf_op jit(solution)/shard_map/ppermute | solution.py:339
  107.3 6.1 %collective-permute-start.28 = (bf16[1,256,128]{2,1,0:T(8,128)(2,1)S(1)}, bf16[1,256,128]{2,1,0:T(8,128)(2,1)S(1)}, u32[]{:S(2)}, u32[]{:S(2)}) collective-permute-start(bf16[1,256,128]{2,1,0:T(8,128)(2,1)S(1)} %bitcast.195), channel_id=1, source_target_pairs={{0,6},{1,7},{2,4},{3,5},{4,2},{5,3},{6,0},{7,1},{8,14},{9,15},{10,... | collective-permute-start | bytes 196616 | tf_op jit(solution)/shard_map/ppermute | solution.py:339
  113.4 6.7 %collective-permute-start.29 = (bf16[1,4,64,128]{3,2,1,0:T(8,128)(2,1)S(1)}, bf16[1,4,64,128]{3,2,1,0:T(8,128)(2,1)S(1)}, u32[]{:S(2)}, u32[]{:S(2)}) collective-permute-start(bf16[1,4,64,128]{3,2,1,0:T(8,128)(2,1)S(1)} %get-tuple-element.67), channel_id=1, source_target_pairs={{0,8},{8,0},{16,24},{24,16},{1,9},{9,1},{17,25},{25,17},{2,10},{10... | collective-permute-start | bytes 196616 | tf_op jit(solution)/shard_map/ppermute | solution.py:343
  115.0 5.2 %collective-permute-start.30 = (bf16[1,4,64,128]{3,2,1,0:T(8,128)(2,1)S(1)}, bf16[1,4,64,128]{3,2,1,0:T(8,128)(2,1)S(1)}, u32[]{:S(2)}, u32[]{:S(2)}) collective-permute-start(bf16[1,4,64,128]{3,2,1,0:T(8,128)(2,1)S(1)} %get-tuple-element.66), channel_id=1, source_target_pairs={{0,24},{8,16},{16,8},{24,0},{1,25},{9,17},{17,9},{25,1},{2,26},{10... | collective-permute-start | bytes 196616 | tf_op jit(solution)/shard_map/ppermute | solution.py:344
  122.7 11.1 %collective-permute-start.37 = (f32[64,256]{1,0:T(8,128)S(1)}, f32[64,256]{1,0:T(8,128)S(1)}, u32[]{:S(2)}, u32[]{:S(2)}) collective-permute-start(f32[64,256]{1,0:T(8,128)S(1)} %get-tuple-element.61), channel_id=1, source_target_pairs={{0,1},{1,0},{2,3},{3,2},{4,5},{5,4},{6,7},{7,6},{8,9},{9,8},{10,11... | collective-permute-start | bytes 196616 | tf_op jit(solution)/shard_map/ppermute | solution.py:326
  122.9 4.5 %collective-permute-start.31 = (bf16[128,128]{1,0:T(8,128)(2,1)S(1)}, bf16[128,128]{1,0:T(8,128)(2,1)S(1)}, u32[]{:S(2)}, u32[]{:S(2)}) collective-permute-start(bf16[128,128]{1,0:T(8,128)(2,1)S(1)} %bitcast.221), channel_id=1, source_target_pairs={{0,2},{1,3},{2,0},{3,1},{4,6},{5,7},{6,4},{7,5},{8,10},{9,11},{10,... | collective-permute-start | bytes 98312 | tf_op jit(solution)/shard_map/ppermute | solution.py:406
  123.0 4.9 %collective-permute-start.32 = (bf16[128,128]{1,0:T(8,128)(2,1)S(1)}, bf16[128,128]{1,0:T(8,128)(2,1)S(1)}, u32[]{:S(2)}, u32[]{:S(2)}) collective-permute-start(bf16[128,128]{1,0:T(8,128)(2,1)S(1)} %bitcast.220), channel_id=1, source_target_pairs={{0,4},{1,5},{2,6},{3,7},{4,0},{5,1},{6,2},{7,3},{8,12},{9,13},{10,... | collective-permute-start | bytes 98312 | tf_op jit(solution)/shard_map/ppermute | solution.py:406
  125.9 5.7 %collective-permute-start.33 = (bf16[128,128]{1,0:T(8,128)(2,1)S(1)}, bf16[128,128]{1,0:T(8,128)(2,1)S(1)}, u32[]{:S(2)}, u32[]{:S(2)}) collective-permute-start(bf16[128,128]{1,0:T(8,128)(2,1)S(1)} %bitcast.219), channel_id=1, source_target_pairs={{0,6},{1,7},{2,4},{3,5},{4,2},{5,3},{6,0},{7,1},{8,14},{9,15},{10,... | collective-permute-start | bytes 98312 | tf_op jit(solution)/shard_map/ppermute | solution.py:406
  132.2 5.2 %collective-permute-start.35 = (bf16[1,4,64,128]{3,2,1,0:T(8,128)(2,1)S(1)}, bf16[1,4,64,128]{3,2,1,0:T(8,128)(2,1)S(1)}, u32[]{:S(2)}, u32[]{:S(2)}) collective-permute-start(bf16[1,4,64,128]{3,2,1,0:T(8,128)(2,1)S(1)} %get-tuple-element.64), channel_id=1, source_target_pairs={{0,24},{8,16},{16,8},{24,0},{1,25},{9,17},{17,9},{25,1},{2,26},{10... | collective-permute-start | bytes 196616 | tf_op jit(solution)/shard_map/ppermute | solution.py:344
  (12 other events, 94.3 us)

commit v3 on v2

v3 whole, which is shorter than its diff:
```python
import functools

import jax
import jax.numpy as jnp
from jax import lax
from jax.experimental import pallas as pl
from jax.experimental.pallas import tpu as pltpu
from jax.sharding import PartitionSpec as P


FORGET_BIAS = 1.0
NT = (((1,), (1,)), ((), ()))
NN = (((1,), (0,)), ((), ()))


def place_columns(dst, row0, pieces, group, cols, masked):
    count, width = pieces[0].shape
    groups = len(pieces)
    place = lax.rem(lax.broadcasted_iota(jnp.int32, (count, width), 0), cols)

    def shifts(piece):
        wide = piece.astype(jnp.float32)
        low = pltpu.roll(wide, 1, 0)
        high = pltpu.roll(wide, count - 1, 0)
        if masked:
            low = jnp.where(place == 0, 0.0, low)
            high = jnp.where(place == cols - 1, 0.0, high)
        return (low.astype(dst.dtype), wide.astype(dst.dtype), high.astype(dst.dtype))

    shifted = [shifts(piece) for piece in pieces]
    rows = pl.ds(row0, count)
    if width % 128 == 0:
        for k in range(groups):
            lanes = pl.ds(pl.multiple_of(lax.bitwise_xor(group, k) * width, width), width)
            for q in range(3):
                dst[q, rows, lanes] = shifted[k][q]
    else:
        for j in range(groups):

            @pl.when(group == j)
            def _():
                for q in range(3):
                    dst[q, rows, :] = jnp.concatenate(
                        [shifted[j ^ i][q] for i in range(groups)], axis=1
                    )


def halo_pieces(a_ref, b_ref, index):
    patch = lax.axis_index("patch")
    even = lax.rem(patch, 2) == 0
    above = patch > 0
    below = patch < lax.axis_size("patch") - 1
    top, bottom = [], []
    for k in range(a_ref.shape[1]):
        a = a_ref[index, k].astype(jnp.float32)
        b = b_ref[index, k].astype(jnp.float32)
        top.append(jnp.where(above, jnp.where(even, b, a), 0.0))
        bottom.append(jnp.where(below, jnp.where(even, a, b), 0.0))
    return top, bottom


def stage_kernel(*refs):
    sources, target, semaphores = refs[:-2], refs[-2], refs[-1]
    copies = []
    for p in range(3):
        for q in range(3):
            for i, source in enumerate(sources):
                copy = pltpu.make_async_copy(source.at[p, q], target.at[p, q, i], semaphores.at[p, q, i])
                copy.start()
                copies.append(copy)
    for copy in copies:
        copy.wait()


def tap(weight_ref, p, q):
    weight = weight_ref[p, q]
    return weight.reshape(-1, weight.shape[-1])


def conv_kernel(groups, cols, index, halo, *refs):
    refs = list(refs)
    parts = [refs.pop(0) for _ in range(groups)]
    if halo:
        edge_a, edge_b = refs.pop(0), refs.pop(0)
    weight_ref, init_ref, out_ref, held = refs
    count = out_ref.shape[1]
    group = lax.axis_index("hid") // 2

    place_columns(held, cols, [part[index] for part in parts], group, cols, True)
    if halo:
        top, bottom = halo_pieces(edge_a, edge_b, index)
        place_columns(held, 0, top, group, cols, True)
        place_columns(held, cols + count, bottom, group, cols, True)
    else:
        zero = jnp.zeros((cols, held.shape[2]), held.dtype)
        for q in range(3):
            held[q, pl.ds(0, cols), :] = zero
            held[q, pl.ds(cols + count, cols), :] = zero
    if init_ref.shape == out_ref.shape:
        total = init_ref[...]
    else:
        column = jnp.broadcast_to(init_ref[...], (8, out_ref.shape[0])).T
        total = jnp.broadcast_to(column[:, :1], out_ref.shape)
    for p in range(3):
        for q in range(3):
            window = held[q, p * cols : p * cols + count, :]
            total = total + lax.dot_general(
                tap(weight_ref, p, q), window, NT, preferred_element_type=jnp.float32
            )
    out_ref[...] = total


def gate_kernel(cols, indices, turn_in, turn_out, *refs):
    refs = list(refs)
    sides = [(refs.pop(0), refs.pop(0), refs.pop(0), index) for index in indices]
    total_ref = refs.pop(0)
    cells = [refs.pop(0), refs.pop(0)]
    hidden_ref = refs.pop(0)
    cells_out = [refs.pop(0), refs.pop(0)]
    held, turned, summed = refs
    group = lax.axis_index("hid") // 2
    core = lax.rem(lax.axis_index("hid"), 2)
    count = total_ref.shape[1]
    channels = total_ref.shape[0] // 8
    side = 2 * cols

    summed[...] = total_ref[...]
    zero = jnp.zeros((cols, held.shape[2]), held.dtype)
    for q in range(3):
        held[q, pl.ds(cols, cols), :] = zero
        held[q, pl.ds(2 * cols, cols), :] = zero
    for edge_a, edge_b, weight_ref, index in sides:
        top, bottom = halo_pieces(edge_a, edge_b, index)
        place_columns(held, 0, top, group, cols, True)
        place_columns(held, 3 * cols, bottom, group, cols, True)
        for p, row0, lane0 in ((0, 0, 0), (2, side, count - side)):
            total = summed[:, lane0 : lane0 + side]
            for q in range(3):
                window = held[q, row0 : row0 + side, :]
                total = total + lax.dot_general(
                    tap(weight_ref, p, q), window, NT, preferred_element_type=jnp.float32
                )
            summed[:, lane0 : lane0 + side] = total
    for half in range(2):
        base = half * 4 * channels
        z0, z1, z2, z3 = (summed[base + i * channels : base + (i + 1) * channels, :] for i in range(4))
        cell = cells[half][...].T if turn_in else cells[half][...]
        cell = jax.nn.sigmoid(z1 + FORGET_BIAS) * cell + jax.nn.sigmoid(z0) * jnp.tanh(z2)
        cells_out[half][...] = cell.T if turn_out else cell
        rows = pl.ds(pl.multiple_of(lax.bitwise_xor(core, half) * channels, channels), channels)
        turned[rows, :] = jax.nn.sigmoid(z3) * jnp.tanh(cell)
    hidden_ref[0] = turned[...].T.astype(hidden_ref.dtype)


def decoder_kernel(groups, rows, width, margin, inner, *refs):
    parts = refs[:groups]
    edge_a, edge_b, first_ref, bias1_ref, second_ref, bias2_ref, out_ref, held, middle = refs[groups:]
    group = lax.axis_index("hid") // 2
    patch = lax.axis_index("patch")
    image_rows = rows * lax.axis_size("patch")
    image_cols = inner * groups

    def conv(source, weight_ref, bias_ref, count):
        total = jnp.broadcast_to(bias_ref[...], (count * width, bias_ref.shape[1]))
        for p in range(3):
            for q in range(3):
                window = source[q, p * width : (p + count) * width, :]
                total = total + lax.dot_general(
                    window, tap(weight_ref, p, q), NN, preferred_element_type=jnp.float32
                )
        return total

    top, bottom = halo_pieces(edge_a, edge_b, 0)
    place_columns(held, 0, top, group, width, False)
    place_columns(held, 2 * width, [part[...] for part in parts], group, width, False)
    place_columns(held, (2 + rows) * width, bottom, group, width, False)
    value = conv(held, first_ref, bias1_ref, rows + 2)
    place = lax.broadcasted_iota(jnp.int32, value.shape, 0)
    row = patch * rows + place // width - 1
    col = group * inner - margin + lax.rem(place, width)
    inside = (row >= 0) & (row < image_rows) & (col >= 0) & (col < image_cols)
    value = jnp.where(inside, value * jax.nn.sigmoid(value), 0.0)
    value = value.astype(middle.dtype).astype(jnp.float32)
    middle[0] = pltpu.roll(value, 1, 0).astype(middle.dtype)
    middle[1] = value.astype(middle.dtype)
    middle[2] = pltpu.roll(value, value.shape[0] - 1, 0).astype(middle.dtype)
    out_ref[...] = conv(middle, second_ref, bias2_ref, rows).astype(out_ref.dtype)


WHOLE = pl.BlockSpec(memory_space=pltpu.VMEM)
VMEM_LIMIT = 10 * 1024 * 1024


def params():
    return pltpu.CompilerParams(vmem_limit_bytes=VMEM_LIMIT)


def cost(flops, size):
    return pl.CostEstimate(flops=flops, bytes_accessed=size, transcendentals=0)


def stage_call(*sources):
    shape = sources[0].shape[:2] + (len(sources),) + sources[0].shape[2:]
    size = 2 * sources[0].size * len(sources)
    return pl.pallas_call(
        stage_kernel,
        in_specs=[pl.BlockSpec(memory_space=pltpu.HBM)] * len(sources),
        out_specs=WHOLE,
        out_shape=pltpu.VMEM(shape, sources[0].dtype),
        scratch_shapes=[pltpu.SemaphoreType.DMA((3, 3, len(sources)))],
        compiler_params=params(),
        cost_estimate=cost(100 * size, size),
    )(*(pltpu.with_memory_space_constraint(source, pltpu.HBM) for source in sources))


def conv_call(parts, index, edges, weight, init, cols):
    groups = len(parts)
    count = parts[0].shape[1]
    channels = weight.shape[-1]
    outs = 2 * weight.shape[3]
    operands = list(parts) + ([] if edges is None else list(edges)) + [weight, init]
    return pl.pallas_call(
        functools.partial(conv_kernel, groups, cols, index, edges is not None),
        in_specs=[WHOLE] * len(operands),
        out_specs=WHOLE,
        out_shape=jax.ShapeDtypeStruct((outs, count), jnp.float32),
        scratch_shapes=[pltpu.VMEM((3, count + 2 * cols, channels), jnp.bfloat16)],
        compiler_params=params(),
        cost_estimate=cost(2 * outs * count * 9 * channels, 18 * outs * channels),
    )(*operands)


def gate_call(sides, total, cells, cols, turn_in, turn_out):
    outs, count = total.shape
    channels = sides[0][2].shape[-1]
    share = outs // 8
    width = 2 * share
    cell_shape = (count, share) if turn_out else (share, count)
    operands = []
    for edges, _, weight in sides:
        operands += [edges[0], edges[1], weight]
    operands += [total, *cells]
    return pl.pallas_call(
        functools.partial(gate_kernel, cols, [index for _, index, _ in sides], turn_in, turn_out),
        in_specs=[WHOLE] * len(operands),
        out_specs=[WHOLE] * 3,
        out_shape=[jax.ShapeDtypeStruct((1, count, width), jnp.bfloat16)]
        + [jax.ShapeDtypeStruct(cell_shape, jnp.float32)] * 2,
        scratch_shapes=[
            pltpu.VMEM((3, 4 * cols, channels), jnp.bfloat16),
            pltpu.VMEM((width, count), jnp.float32),
            pltpu.VMEM((outs, count), jnp.float32),
        ],
        compiler_params=params(),
        cost_estimate=cost(2 * outs * count * 6 * channels, 12 * outs * channels),
    )(*operands)


def decoder_call(parts, edges, first, first_bias, second, second_bias, rows, width, margin, inner):
    groups = len(parts)
    channels = first.shape[3]
    outs = second.shape[4]
    operands = [*parts, *edges, first, first_bias.reshape(1, -1), second, second_bias.reshape(1, -1)]
    return pl.pallas_call(
        functools.partial(decoder_kernel, groups, rows, width, margin, inner),
        in_specs=[WHOLE] * len(operands),
        out_specs=WHOLE,
        out_shape=jax.ShapeDtypeStruct((rows * width, outs), jnp.bfloat16),
        scratch_shapes=[
            pltpu.VMEM((3, (rows + 4) * width, channels), jnp.bfloat16),
            pltpu.VMEM((3, (rows + 2) * width, first.shape[4]), jnp.bfloat16),
        ],
        compiler_params=params(),
        cost_estimate=cost(18 * channels * outs * (2 * rows + 2) * width, 36 * channels * outs),
    )(*operands)


def program(
    frames,
    hidden_start,
    cell_start,
    input_weight,
    hidden_weight,
    gate_bias,
    first_weight,
    first_bias,
    second_weight,
    second_bias,
):
    steps, batch, rows, cols, share = frames.shape
    groups = lax.axis_size("hid") // 2
    patches = lax.axis_size("patch")
    assert batch == 2 and groups & (groups - 1) == 0 and patches % 2 == 0
    hid = lax.axis_index("hid")
    core = lax.rem(hid, 2)
    group = hid // 2
    even = lax.rem(lax.axis_index("patch"), 2) == 0
    count = rows * cols
    width = 2 * share

    pairs = [(i, i ^ 1) for i in range(2 * groups)]
    inner_pairs = [(i, i ^ 1) for i in range(patches)]
    outer_pairs = [(i, (i - 1) % patches if i % 2 == 0 else (i + 1) % patches) for i in range(patches)]

    def swap(value):
        return lax.ppermute(value, "hid", pairs)

    def own_batch(value, axis):
        mine = lax.dynamic_index_in_dim(value, core, axis, keepdims=False, allow_negative_indices=False)
        other = lax.dynamic_index_in_dim(value, 1 - core, axis, keepdims=False, allow_negative_indices=False)
        return mine, swap(other)

    def joined(value, axis):
        mine, other = own_batch(value, axis)
        return jnp.where(core == 0, jnp.concatenate([mine, other], -1), jnp.concatenate([other, mine], -1))

    def gathered(value):
        return [value] + [
            lax.ppermute(value, "hid", [(i, i ^ (2 * k)) for i in range(2 * groups)]) for k in range(1, groups)
        ]

    def swapped_edges(top, bottom):
        first = lax.ppermute(jnp.where(even, bottom, top), "patch", inner_pairs)
        second = lax.ppermute(jnp.where(even, top, bottom), "patch", outer_pairs)
        return first, second

    def edges_of(parts):
        top = jnp.stack([part[:, :cols] for part in parts], 1)
        bottom = jnp.stack([part[:, count - cols :] for part in parts], 1)
        return swapped_edges(top, bottom)

    def gate_major(weight):
        turned = jnp.transpose(weight, (0, 1, 3, 4, 2))
        return turned.reshape(turned.shape[:2] + (-1,) + turned.shape[-1:])

    def ordered(mine, other, axis):
        return jnp.where(core == 0, jnp.concatenate([mine, other], axis), jnp.concatenate([other, mine], axis))

    def of_batch(index):
        return jnp.stack(
            [
                lax.dynamic_index_in_dim(frames[0], index, 0, keepdims=False, allow_negative_indices=False),
                lax.dynamic_index_in_dim(hidden_start, index, 0, keepdims=False, allow_negative_indices=False),
            ]
        )

    lead = ordered(of_batch(core), swap(of_batch(1 - core)), -1).reshape(2, count, width)
    inner = cols // groups
    tile = -(-(inner + 4) // 16) * 16
    margin = (tile - inner) // 2
    starts = [lax.bitwise_xor(group, k) * inner for k in range(groups)]
    out_starts = [margin + core * (inner // 2), margin + (1 - core) * (inner // 2)]
    (lead, starts, out_starts), frames, cell_start, gate_bias, input_own, hidden_own, first_weight, second_weight = (
        lax.optimization_barrier(
            (
                (lead, starts, out_starts),
                frames,
                cell_start,
                gate_bias,
                gate_major(input_weight),
                gate_major(hidden_weight),
                first_weight,
                second_weight,
            )
        )
    )
    lead_parts = gathered(lead)
    input_pair, hidden_pair = swap(input_own), swap(hidden_own)
    first_weight, second_weight = stage_call(first_weight), stage_call(second_weight)
    input_both = stage_call(input_own, input_pair)
    hidden_both = stage_call(hidden_own, hidden_pair)
    rest = joined(frames[1:], 1).reshape(steps - 1, count, width)
    cell_mine, cell_other = own_batch(cell_start, 0)
    cells = [cell_mine.reshape(count, share), cell_other.reshape(count, share)]
    bias_own = gate_bias.reshape(-1)
    bias = jnp.concatenate([bias_own, swap(bias_own)]).reshape(1, -1)

    lead_parts, rest, cells, bias = lax.optimization_barrier((lead_parts, rest, cells, bias))
    lead_edges = edges_of(lead_parts)
    rest_parts = gathered(rest)
    rest_edges = edges_of(rest_parts)

    for time_index in range(steps):
        if time_index == 0:
            total = conv_call(lead_parts, 0, None, input_both, bias, cols)
            parts, part_index, edges = lead_parts, 1, lead_edges
            sides = [(lead_edges, 0, input_both)]
        else:
            late = time_index > 1
            total = conv_call(
                rest_parts, time_index - 1, rest_edges if late else None, input_both, bias, cols
            )
            parts, part_index = gathered(hidden), 0
            edges = edges_of(parts)
            sides = [] if late else [(rest_edges, time_index - 1, input_both)]
        sides.append((edges, part_index, hidden_both))
        total = conv_call(parts, part_index, None, hidden_both, total, cols)
        hidden, *cells = gate_call(sides, total, cells, cols, time_index == 0, time_index == steps - 1)

    image = jnp.pad(hidden.reshape(rows, cols, width), ((0, 0), (margin, margin), (0, 0)))

    def columns_for(k):
        piece = lax.dynamic_slice_in_dim(image, starts[k], tile, axis=1, allow_negative_indices=False)
        return piece.reshape(rows * tile, width)

    tiles = [columns_for(0)] + [
        lax.ppermute(columns_for(k), "hid", [(i, i ^ (2 * k)) for i in range(2 * groups)]) for k in range(1, groups)
    ]
    rim = 2 * tile
    tile_edges = swapped_edges(
        jnp.stack([part[:rim] for part in tiles])[None],
        jnp.stack([part[rows * tile - rim :] for part in tiles])[None],
    )
    decoded = decoder_call(
        tiles, tile_edges, first_weight, first_bias, second_weight, second_bias, rows, tile, margin, inner
    )
    decoded = decoded.reshape(rows, tile, -1)
    mine, other = (
        lax.dynamic_slice_in_dim(decoded, start, inner // 2, axis=1, allow_negative_indices=False)
        for start in out_starts
    )
    other = swap(other)
    decoded = jnp.where(core == 0, jnp.stack([mine, other]), jnp.stack([other, mine]))

    cell_mine = cells[0].reshape(rows, cols, share)
    cell_other = swap(cells[1]).reshape(rows, cols, share)
    cell_final = jnp.where(core == 0, jnp.stack([cell_mine, cell_other]), jnp.stack([cell_other, cell_mine]))
    return decoded, cell_final


def solution(mesh):
    return jax.shard_map(
        program,
        mesh=mesh,
        in_specs=(
            P(None, None, "patch", None, "hid"),
            P(None, "patch", None, "hid"),
            P(None, "patch", None, "hid"),
            P(None, None, None, None, "hid"),
            P(None, None, None, None, "hid"),
            P(None, "hid"),
            P(),
            P(),
            P(),
            P(),
        ),
        out_specs=(P(None, "patch", "hid", None), P(None, "patch", None, "hid")),
        check_vma=False,
    )
```

time: 147 us -> 134 us (0.912)
  Pallas kernels: 50.1 us -> 32.4 us
  waiting for transfers between devices: 36.4 us -> 43.9 us
    pallas_call x12 -> x16, Pallas kernels: 43.1 us -> 30.2 us  [the longest x8 13.7 us: conv_call(): pl.pallas_call(functools.partial(conv_kernel, groups, cols, index, edges...]
    ppermute x15, waiting for transfers between devices: 21.8 us -> 30.1 us  [gathered(): lax.ppermute(value, 'hid', [(i, i ^ 2 * k) for i in range(2 * groups)])]
    pallas_call x1, Pallas kernels: 7.07 us -> 2.15 us  [decoder_call(): pl.pallas_call(functools.partial(decoder_kernel, groups, rows, width, mar...]
    ppermute x6, waiting for transfers between devices: 4.78 us -> 0.02 us  [swapped_edges(): first = lax.ppermute(jnp.where(even, bottom, top), 'patch', inner_pairs)]
    ppermute x8, waiting for transfers between devices: 1.47 us -> 5.39 us  [swap(): return lax.ppermute(value, 'hid', pairs)]
    ppermute x6, starting transfers between devices: 7.82 us -> 11.5 us  [swapped_edges(): second = lax.ppermute(jnp.where(even, top, bottom), 'patch', outer_pairs)]
    ppermute x15, starting transfers between devices: 26.9 us -> 23.3 us  [gathered(): lax.ppermute(value, 'hid', [(i, i ^ 2 * k) for i in range(2 * groups)])]
    dynamic_slice x5 -> x4, local copies, waits for them, and re-layouts: 3.38 us -> 1.02 us  [the longest x1 0.89 us: of_batch(): lax.dynamic_index_in_dim(hidden_start, index, 0, keepdims=False, allow_ne...]
  transfers between devices with their start and end apart: 38 -> 38, of which waited for: 16 -> 15; matrix products, arithmetic and copies ran while one was open for 5% -> 3% of each run, Pallas kernels for 24% -> 21%
where the time goes in v3:
time: 134 us
  starting transfers between devices  48.2 us (36%)
  waiting for transfers between devices  43.9 us (33%)
  Pallas kernels  32.4 us (24%)
  local copies, waits for them, and re-layouts  6.26 us (5%)
  other arithmetic  1.96 us (1%)
    ppermute x15, waiting for transfers between devices, gathered(): lax.ppermute(value, 'hid', [(i, i ^ 2 * k) for i in range(2 * groups)])  30.1 us
    ppermute x15, starting transfers between devices, gathered(): lax.ppermute(value, 'hid', [(i, i ^ 2 * k) for i in range(2 * groups)])  23.3 us
    pallas_call x8, Pallas kernels, conv_call(): pl.pallas_call(functools.partial(conv_kernel, groups, cols, index, edges...  13.7 us
    ppermute x6, starting transfers between devices, swapped_edges(): second = lax.ppermute(jnp.where(even, top, bottom), 'patch', outer_pairs)  11.5 us
    pallas_call x4, Pallas kernels, stage_call(): pl.pallas_call(stage_kernel, in_specs=[pl.BlockSpec(memory_space=pltpu.HB...  9.66 us
    pallas_call x4, Pallas kernels, gate_call(): pl.pallas_call(functools.partial(gate_kernel, cols, [index for _, index,...  6.8 us
    ppermute x6, starting transfers between devices, swapped_edges(): first = lax.ppermute(jnp.where(even, bottom, top), 'patch', inner_pairs)  6.17 us
    ppermute x8, waiting for transfers between devices, swap(): return lax.ppermute(value, 'hid', pairs)  5.39 us
  transfers between devices with their start and end apart: 38, of which 15 were waited for; matrix products, arithmetic and copies ran while one was open for 3% of the time, Pallas kernels for 21%

profile of v3, /device:TPU:0, one launch (start us, length us, event | category | flops | bytes accessed | tf_op | source)
XLA Modules:
  0.0 133.8 jit_solution(13288878003034366320)
XLA Ops:
  8.6 4.3 %collective-permute-done.6 = f32[256]{0:T(256)S(1)} collective-permute-done((f32[256]{0:T(256)S(1)}, f32[256]{0:T(256)S(1)}, u32[]{:S(2)}, u32[]{:S(2)}) %collective-permute-start.6) | collective-permute-done | bytes 1056 | tf_op jit(solution)/shard_map/ppermute | solution.py:306
  12.9 2.9 %collective-permute-start.1 = (bf16[2,256,128]{2,1,0:T(8,128)(2,1)S(1)}, bf16[2,256,128]{2,1,0:T(8,128)(2,1)S(1)}, u32[]{:S(2)}, u32[]{:S(2)}) collective-permute-start(bf16[2,256,128]{2,1,0:T(8,128)(2,1)S(1)} %maximum_select_fusion.2.refs_0_), channel_id=1, source_target_pairs={{0,2},{1,3},{2,0},{3,1},{4,6},{5,7},{6,4},{7,5},{8,10},{9,11},{10,... | collective-permute-start | bytes 393224 | tf_op jit(solution)/shard_map/ppermute | solution.py:319
  15.8 2.6 %collective-permute-start.2 = (bf16[2,256,128]{2,1,0:T(8,128)(2,1)S(1)}, bf16[2,256,128]{2,1,0:T(8,128)(2,1)S(1)}, u32[]{:S(2)}, u32[]{:S(2)}) collective-permute-start(bf16[2,256,128]{2,1,0:T(8,128)(2,1)S(1)} %maximum_select_fusion.2.refs_0_), channel_id=1, source_target_pairs={{0,4},{1,5},{2,6},{3,7},{4,0},{5,1},{6,2},{7,3},{8,12},{9,13},{10,... | collective-permute-start | bytes 393224 | tf_op jit(solution)/shard_map/ppermute | solution.py:319
  18.6 2.9 %collective-permute-done.1.refs_1_ = bf16[2,256,128]{2,1,0:T(8,128)(2,1)S(1)} collective-permute-done((bf16[2,256,128]{2,1,0:T(8,128)(2,1)S(1)}, bf16[2,256,128]{2,1,0:T(8,128)(2,1)S(1)}, u32[]{:S(2)}, u32[]{:S(2)}) %collective-permute-start.1) | collective-permute-done | bytes 131104 | tf_op jit(solution)/shard_map/ppermute | solution.py:319
  21.5 7.2 %collective-permute-done.2.refs_2_ = bf16[2,256,128]{2,1,0:T(8,128)(2,1)S(1)} collective-permute-done((bf16[2,256,128]{2,1,0:T(8,128)(2,1)S(1)}, bf16[2,256,128]{2,1,0:T(8,128)(2,1)S(1)}, u32[]{:S(2)}, u32[]{:S(2)}) %collective-permute-start.2) | collective-permute-done | bytes 131104 | tf_op jit(solution)/shard_map/ppermute | solution.py:319
  28.7 2.4 %collective-permute-start.9 = (bf16[3,256,128]{2,1,0:T(8,128)(2,1)S(1)}, bf16[3,256,128]{2,1,0:T(8,128)(2,1)S(1)}, u32[]{:S(2)}, u32[]{:S(2)}) collective-permute-start(bf16[3,256,128]{2,1,0:T(8,128)(2,1)S(1)} %maximum_select_fusion.1.refs_0_), channel_id=1, source_target_pairs={{0,6},{1,7},{2,4},{3,5},{4,2},{5,3},{6,0},{7,1},{8,14},{9,15},{10,... | collective-permute-start | bytes 589832 | tf_op jit(solution)/shard_map/ppermute | solution.py:319
  33.2 4.9 %collective-permute-done.9.refs_3_ = bf16[3,256,128]{2,1,0:T(8,128)(2,1)S(1)} collective-permute-done((bf16[3,256,128]{2,1,0:T(8,128)(2,1)S(1)}, bf16[3,256,128]{2,1,0:T(8,128)(2,1)S(1)}, u32[]{:S(2)}, u32[]{:S(2)}) %collective-permute-start.9) | collective-permute-done | bytes 196640 | tf_op jit(solution)/shard_map/ppermute | solution.py:319
  39.6 8.4 %collective-permute-done.8.refs_2_ = bf16[3,256,128]{2,1,0:T(8,128)(2,1)S(1)} collective-permute-done((bf16[3,256,128]{2,1,0:T(8,128)(2,1)S(1)}, bf16[3,256,128]{2,1,0:T(8,128)(2,1)S(1)}, u32[]{:S(2)}, u32[]{:S(2)}) %collective-permute-start.8) | collective-permute-done | bytes 196640 | tf_op jit(solution)/shard_map/ppermute | solution.py:319
  48.0 2.4 %collective-permute-start.14 = (bf16[2,4,64,128]{3,2,1,0:T(8,128)(2,1)S(1)}, bf16[2,4,64,128]{3,2,1,0:T(8,128)(2,1)S(1)}, u32[]{:S(2)}, u32[]{:S(2)}) collective-permute-start(bf16[2,4,64,128]{3,2,1,0:T(8,128)(2,1)S(1)} %get-tuple-element.74), channel_id=1, source_target_pairs={{0,24},{8,16},{16,8},{24,0},{1,25},{9,17},{17,9},{25,1},{2,26},{10... | collective-permute-start | bytes 393224 | tf_op jit(solution)/shard_map/ppermute | solution.py:324
  52.6 2.4 %shard_map.113.refs_4_.refs_2_.refs_6_ = bf16[3,3,2,256,512]{4,3,2,1,0:T(8,128)(2,1)S(1)} custom-call(bf16[3,3,256,512]{3,2,1,0:T(8,128)(2,1)} %bitcast.169, bf16[3,3,256,512]{3,2,1,0:T(8,128)(2,1)} %collective-permute-done.12.refs_1_), custom_call_target="tpu_custom_call" | custom-call | flops 471859200 | bytes 4718592 | tf_op jit(solution)/shard_map/pallas_call | solution.py:205
  55.0 1.7 %shard_map.115.refs_5_ = f32[512,256]{1,0:T(8,128)S(1)} custom-call(bf16[2,256,128]{2,1,0:T(8,128)(2,1)S(1)} %maximum_select_fusion.2.refs_0_, bf16[2,256,128]{2,1,0:T(8,128)(2,1)S(1)} %collective-permute-done.1.refs_1_, bf16[2,256,128]{2,1,0:T(8,128)(2,1)S(1)} %collective-permute-done.2.refs_2_, bf16[2,256,128]{2,1,0:T(8,128)(2,1)S(1)} %collective-permute-done.3.refs_3_, ...), custom_call_target="tpu_custom_call" | custom-call | flops 1207959552 | bytes 4718592 | tf_op jit(solution)/shard_map/pallas_call | solution.py:222
  58.1 2.4 %shard_map.114.refs_4_.refs_5_.refs_2_ = bf16[3,3,2,256,512]{4,3,2,1,0:T(8,128)(2,1)S(1)} custom-call(bf16[3,3,256,512]{3,2,1,0:T(8,128)(2,1)} %bitcast.171, bf16[3,3,256,512]{3,2,1,0:T(8,128)(2,1)} %copy-done.2), custom_call_target="tpu_custom_call" | custom-call | flops 471859200 | bytes 4718592 | tf_op jit(solution)/shard_map/pallas_call | solution.py:205
  62.3 2.1 %shard_map.117 = (bf16[1,256,128]{2,1,0:T(8,128)(2,1)S(1)}, f32[64,256]{1,0:T(8,128)S(1)}, f32[64,256]{1,0:T(8,128)S(1)}) custom-call(bf16[2,4,64,128]{3,2,1,0:T(8,128)(2,1)S(1)} %collective-permute-done.13.refs_0_.refs_3_, bf16[2,4,64,128]{3,2,1,0:T(8,128)(2,1)S(1)} %collective-permute-done.14.refs_1_.refs_4_, ...), custom_call_target="tpu_custom_call" | custom-call | flops 805306368 | bytes 3145728 | tf_op jit(solution)/shard_map/pallas_call | solution.py:243
  64.4 2.5 %collective-permute-start.18 = (bf16[1,256,128]{2,1,0:T(8,128)(2,1)S(1)}, bf16[1,256,128]{2,1,0:T(8,128)(2,1)S(1)}, u32[]{:S(2)}, u32[]{:S(2)}) collective-permute-start(bf16[1,256,128]{2,1,0:T(8,128)(2,1)S(1)} %get-tuple-element.50.refs_0_), channel_id=1, source_target_pairs={{0,6},{1,7},{2,4},{3,5},{4,2},{5,3},{6,0},{7,1},{8,14},{9,15},{10,... | collective-permute-start | bytes 196616 | tf_op jit(solution)/shard_map/ppermute | solution.py:319
  66.9 1.9 %collective-permute-start.16 = (bf16[1,256,128]{2,1,0:T(8,128)(2,1)S(1)}, bf16[1,256,128]{2,1,0:T(8,128)(2,1)S(1)}, u32[]{:S(2)}, u32[]{:S(2)}) collective-permute-start(bf16[1,256,128]{2,1,0:T(8,128)(2,1)S(1)} %get-tuple-element.50.refs_0_), channel_id=1, source_target_pairs={{0,2},{1,3},{2,0},{3,1},{4,6},{5,7},{6,4},{7,5},{8,10},{9,11},{10,... | collective-permute-start | bytes 196616 | tf_op jit(solution)/shard_map/ppermute | solution.py:319
  70.6 1.8 %shard_map.121.refs_5_ = f32[512,256]{1,0:T(8,128)S(1)} custom-call(bf16[3,256,128]{2,1,0:T(8,128)(2,1)S(1)} %maximum_select_fusion.1.refs_0_, bf16[3,256,128]{2,1,0:T(8,128)(2,1)S(1)} %collective-permute-done.7.refs_1_, bf16[3,256,128]{2,1,0:T(8,128)(2,1)S(1)} %collective-permute-done.8.refs_2_, bf16[3,256,128]{2,1,0:T(8,128)(2,1)S(1)} %collective-permute-done.9.refs_3_, ...), custom_call_target="tpu_custom_call" | custom-call | flops 1207959552 | bytes 4718592 | tf_op jit(solution)/shard_map/pallas_call | solution.py:222
  72.4 1.8 %shard_map.124.refs_5_ = f32[512,256]{1,0:T(8,128)S(1)} custom-call(bf16[3,256,128]{2,1,0:T(8,128)(2,1)S(1)} %maximum_select_fusion.1.refs_0_, bf16[3,256,128]{2,1,0:T(8,128)(2,1)S(1)} %collective-permute-done.7.refs_1_, bf16[3,256,128]{2,1,0:T(8,128)(2,1)S(1)} %collective-permute-done.8.refs_2_, bf16[3,256,128]{2,1,0:T(8,128)(2,1)S(1)} %collective-permute-done.9.refs_3_, ...), custom_call_target="tpu_custom_call" | custom-call | flops 1207959552 | bytes 4718592 | tf_op jit(solution)/shard_map/pallas_call | solution.py:222
  75.0 2.5 %collective-permute-start.20 = (bf16[1,4,64,128]{3,2,1,0:T(8,128)(2,1)S(1)}, bf16[1,4,64,128]{3,2,1,0:T(8,128)(2,1)S(1)}, u32[]{:S(2)}, u32[]{:S(2)}) collective-permute-start(bf16[1,4,64,128]{3,2,1,0:T(8,128)(2,1)S(1)} %get-tuple-element.94), channel_id=1, source_target_pairs={{0,24},{8,16},{16,8},{24,0},{1,25},{9,17},{17,9},{25,1},{2,26},{10... | collective-permute-start | bytes 196616 | tf_op jit(solution)/shard_map/ppermute | solution.py:324
  80.3 2.3 %shard_map.120 = (bf16[1,256,128]{2,1,0:T(8,128)(2,1)S(1)}, f32[64,256]{1,0:T(8,128)S(1)}, f32[64,256]{1,0:T(8,128)S(1)}) custom-call(bf16[3,4,64,128]{3,2,1,0:T(8,128)(2,1)S(1)} %collective-permute-done.10.refs_0_.refs_4_, bf16[3,4,64,128]{3,2,1,0:T(8,128)(2,1)S(1)} %collective-permute-done.11.refs_1_.refs_5_, ...), custom_call_target="tpu_custom_call" | custom-call | flops 805306368 | bytes 3145728 | tf_op jit(solution)/shard_map/pallas_call | solution.py:243
  82.6 2.5 %collective-permute-start.23 = (bf16[1,256,128]{2,1,0:T(8,128)(2,1)S(1)}, bf16[1,256,128]{2,1,0:T(8,128)(2,1)S(1)}, u32[]{:S(2)}, u32[]{:S(2)}) collective-permute-start(bf16[1,256,128]{2,1,0:T(8,128)(2,1)S(1)} %get-tuple-element.53.refs_0_), channel_id=1, source_target_pairs={{0,6},{1,7},{2,4},{3,5},{4,2},{5,3},{6,0},{7,1},{8,14},{9,15},{10,... | collective-permute-start | bytes 196616 | tf_op jit(solution)/shard_map/ppermute | solution.py:319
  85.2 1.9 %collective-permute-start.21 = (bf16[1,256,128]{2,1,0:T(8,128)(2,1)S(1)}, bf16[1,256,128]{2,1,0:T(8,128)(2,1)S(1)}, u32[]{:S(2)}, u32[]{:S(2)}) collective-permute-start(bf16[1,256,128]{2,1,0:T(8,128)(2,1)S(1)} %get-tuple-element.53.refs_0_), channel_id=1, source_target_pairs={{0,2},{1,3},{2,0},{3,1},{4,6},{5,7},{6,4},{7,5},{8,10},{9,11},{10,... | collective-permute-start | bytes 196616 | tf_op jit(solution)/shard_map/ppermute | solution.py:319
  94.9 2.0 %collective-permute-done.25.refs_1_ = bf16[1,4,64,128]{3,2,1,0:T(8,128)(2,1)S(1)} collective-permute-done((bf16[1,4,64,128]{3,2,1,0:T(8,128)(2,1)S(1)}, bf16[1,4,64,128]{3,2,1,0:T(8,128)(2,1)S(1)}, u32[]{:S(2)}, u32[]{:S(2)}) %collective-permute-start.25) | collective-permute-done | bytes 65568 | tf_op jit(solution)/shard_map/ppermute | solution.py:324
  98.1 2.4 %collective-permute-start.28 = (bf16[1,256,128]{2,1,0:T(8,128)(2,1)S(1)}, bf16[1,256,128]{2,1,0:T(8,128)(2,1)S(1)}, u32[]{:S(2)}, u32[]{:S(2)}) collective-permute-start(bf16[1,256,128]{2,1,0:T(8,128)(2,1)S(1)} %get-tuple-element.56.refs_0_), channel_id=1, source_target_pairs={{0,6},{1,7},{2,4},{3,5},{4,2},{5,3},{6,0},{7,1},{8,14},{9,15},{10,... | collective-permute-start | bytes 196616 | tf_op jit(solution)/shard_map/ppermute | solution.py:319
  100.6 1.9 %collective-permute-start.26 = (bf16[1,256,128]{2,1,0:T(8,128)(2,1)S(1)}, bf16[1,256,128]{2,1,0:T(8,128)(2,1)S(1)}, u32[]{:S(2)}, u32[]{:S(2)}) collective-permute-start(bf16[1,256,128]{2,1,0:T(8,128)(2,1)S(1)} %get-tuple-element.56.refs_0_), channel_id=1, source_target_pairs={{0,2},{1,3},{2,0},{3,1},{4,6},{5,7},{6,4},{7,5},{8,10},{9,11},{10,... | collective-permute-start | bytes 196616 | tf_op jit(solution)/shard_map/ppermute | solution.py:319
  104.2 1.8 %collective-permute-done.27.refs_2_ = bf16[1,256,128]{2,1,0:T(8,128)(2,1)S(1)} collective-permute-done((bf16[1,256,128]{2,1,0:T(8,128)(2,1)S(1)}, bf16[1,256,128]{2,1,0:T(8,128)(2,1)S(1)}, u32[]{:S(2)}, u32[]{:S(2)}) %collective-permute-start.27) | collective-permute-done | bytes 65568 | tf_op jit(solution)/shard_map/ppermute | solution.py:319
  106.9 2.2 %collective-permute-start.30 = (bf16[1,4,64,128]{3,2,1,0:T(8,128)(2,1)S(1)}, bf16[1,4,64,128]{3,2,1,0:T(8,128)(2,1)S(1)}, u32[]{:S(2)}, u32[]{:S(2)}) collective-permute-start(bf16[1,4,64,128]{3,2,1,0:T(8,128)(2,1)S(1)} %get-tuple-element.90), channel_id=1, source_target_pairs={{0,24},{8,16},{16,8},{24,0},{1,25},{9,17},{17,9},{25,1},{2,26},{10... | collective-permute-start | bytes 196616 | tf_op jit(solution)/shard_map/ppermute | solution.py:324
  114.2 1.8 %collective-permute-start.32 = (bf16[128,128]{1,0:T(8,128)(2,1)S(1)}, bf16[128,128]{1,0:T(8,128)(2,1)S(1)}, u32[]{:S(2)}, u32[]{:S(2)}) collective-permute-start(bf16[128,128]{1,0:T(8,128)(2,1)S(1)} %bitcast.181), channel_id=1, source_target_pairs={{0,4},{1,5},{2,6},{3,7},{4,0},{5,1},{6,2},{7,3},{8,12},{9,13},{10,... | collective-permute-start | bytes 98312 | tf_op jit(solution)/shard_map/ppermute | solution.py:407
  116.0 1.8 %collective-permute-start.33 = (bf16[128,128]{1,0:T(8,128)(2,1)S(1)}, bf16[128,128]{1,0:T(8,128)(2,1)S(1)}, u32[]{:S(2)}, u32[]{:S(2)}) collective-permute-start(bf16[128,128]{1,0:T(8,128)(2,1)S(1)} %bitcast.182), channel_id=1, source_target_pairs={{0,6},{1,7},{2,4},{3,5},{4,2},{5,3},{6,0},{7,1},{8,14},{9,15},{10,... | collective-permute-start | bytes 98312 | tf_op jit(solution)/shard_map/ppermute | solution.py:407
  117.9 3.9 %collective-permute-done.33.refs_3_ = bf16[128,128]{1,0:T(8,128)(2,1)S(1)} collective-permute-done((bf16[128,128]{1,0:T(8,128)(2,1)S(1)}, bf16[128,128]{1,0:T(8,128)(2,1)S(1)}, u32[]{:S(2)}, u32[]{:S(2)}) %collective-permute-start.33) | collective-permute-done | bytes 32800 | tf_op jit(solution)/shard_map/ppermute | solution.py:407
  124.6 2.4 %shard_map.127.refs_6_ = bf16[3,3,1,512,512]{4,3,2,1,0:T(8,128)(2,1)S(1)} custom-call(bf16[3,3,512,512]{3,2,1,0:T(8,128)(2,1)} %refs_0_), custom_call_target="tpu_custom_call" | custom-call | flops 471859200 | bytes 4718592 | tf_op jit(solution)/shard_map/pallas_call | solution.py:205
  127.0 2.4 %shard_map.128.refs_8_ = bf16[3,3,1,512,512]{4,3,2,1,0:T(8,128)(2,1)S(1)} custom-call(bf16[3,3,512,512]{3,2,1,0:T(8,128)(2,1)} %refs_0_.1), custom_call_target="tpu_custom_call" | custom-call | flops 471859200 | bytes 4718592 | tf_op jit(solution)/shard_map/pallas_call | solution.py:205
  129.5 2.1 %shard_map.129 = bf16[128,512]{1,0:T(8,128)(2,1)S(1)} custom-call(bf16[128,128]{1,0:T(8,128)(2,1)S(1)} %bitcast.160, bf16[128,128]{1,0:T(8,128)(2,1)S(1)} %collective-permute-done.31.refs_1_, bf16[128,128]{1,0:T(8,128)(2,1)S(1)} %collective-permute-done.32.refs_2_, bf16[128,128]{1,0:T(8,128)(2,1)S(1)} %collective-permute-done.33.refs_3_, ...), custom_call_target="tpu_custom_call" | custom-call | flops 1509949440 | bytes 9437184 | tf_op jit(solution)/shard_map/pallas_call | solution.py:264
  (110 shorter events, 43.9 us)
Async XLA Ops:
  4.2 46.9 %collective-permute-start.12 = (bf16[3,3,256,512]{3,2,1,0:T(8,128)(2,1)}, bf16[3,3,256,512]{3,2,1,0:T(8,128)(2,1)}, u32[]{:S(2)}, u32[]{:S(2)}) collective-permute-start(bf16[3,3,256,512]{3,2,1,0:T(8,128)(2,1)} %bitcast.168), channel_id=1, source_target_pairs={{0,1},{1,0},{2,3},{3,2},{4,5},{5,4},{6,7},{7,6},{8,9},{9,8},{10,11... | collective-permute-start | bytes 7077896 | tf_op jit(solution)/shard_map/ppermute | solution.py:306
  4.6 52.1 %collective-permute-start.15 = (bf16[3,3,256,512]{3,2,1,0:T(8,128)(2,1)}, bf16[3,3,256,512]{3,2,1,0:T(8,128)(2,1)S(1)}, u32[]{:S(2)}, u32[]{:S(2)}) collective-permute-start(bf16[3,3,256,512]{3,2,1,0:T(8,128)(2,1)} %bitcast.170), channel_id=1, source_target_pairs={{0,1},{1,0},{2,3},{3,2},{4,5},{5,4},{6,7},{7,6},{8,9},{9,8},{10,11... | collective-permute-start | bytes 7077896 | tf_op jit(solution)/shard_map/ppermute | solution.py:306
  5.8 12.5 %collective-permute-start.4 = (bf16[3,4,64,64]{3,2,1,0:T(8,128)(2,1)S(1)}, bf16[3,4,64,64]{3,2,1,0:T(8,128)(2,1)S(1)}, u32[]{:S(2)}, u32[]{:S(2)}) collective-permute-start(bf16[3,4,64,64]{3,2,1,0:T(8,128)(2,1)S(1)} %get-tuple-element.73), channel_id=1, source_target_pairs={{0,1},{1,0},{2,3},{3,2},{4,5},{5,4},{6,7},{7,6},{8,9},{9,8},{10,11... | collective-permute-start | bytes 294920 | tf_op jit(solution)/shard_map/ppermute | solution.py:306
  7.3 8.5 %collective-permute-start.5 = (f32[4,64,64]{2,1,0:T(8,128)S(1)}, f32[4,64,64]{2,1,0:T(8,128)S(1)}, u32[]{:S(2)}, u32[]{:S(2)}) collective-permute-start(f32[4,64,64]{2,1,0:T(8,128)S(1)} %get-tuple-element.76), channel_id=1, source_target_pairs={{0,1},{1,0},{2,3},{3,2},{4,5},{5,4},{6,7},{7,6},{8,9},{9,8},{10,11... | collective-permute-start | bytes 196616 | tf_op jit(solution)/shard_map/ppermute | solution.py:306
  12.9 8.6 %collective-permute-start.1 = (bf16[2,256,128]{2,1,0:T(8,128)(2,1)S(1)}, bf16[2,256,128]{2,1,0:T(8,128)(2,1)S(1)}, u32[]{:S(2)}, u32[]{:S(2)}) collective-permute-start(bf16[2,256,128]{2,1,0:T(8,128)(2,1)S(1)} %maximum_select_fusion.2.refs_0_), channel_id=1, source_target_pairs={{0,2},{1,3},{2,0},{3,1},{4,6},{5,7},{6,4},{7,5},{8,10},{9,11},{10,... | collective-permute-start | bytes 393224 | tf_op jit(solution)/shard_map/ppermute | solution.py:319
  15.8 12.9 %collective-permute-start.2 = (bf16[2,256,128]{2,1,0:T(8,128)(2,1)S(1)}, bf16[2,256,128]{2,1,0:T(8,128)(2,1)S(1)}, u32[]{:S(2)}, u32[]{:S(2)}) collective-permute-start(bf16[2,256,128]{2,1,0:T(8,128)(2,1)S(1)} %maximum_select_fusion.2.refs_0_), channel_id=1, source_target_pairs={{0,4},{1,5},{2,6},{3,7},{4,0},{5,1},{6,2},{7,3},{8,12},{9,13},{10,... | collective-permute-start | bytes 393224 | tf_op jit(solution)/shard_map/ppermute | solution.py:319
  18.4 10.3 %collective-permute-start.3 = (bf16[2,256,128]{2,1,0:T(8,128)(2,1)S(1)}, bf16[2,256,128]{2,1,0:T(8,128)(2,1)S(1)}, u32[]{:S(2)}, u32[]{:S(2)}) collective-permute-start(bf16[2,256,128]{2,1,0:T(8,128)(2,1)S(1)} %maximum_select_fusion.2.refs_0_), channel_id=1, source_target_pairs={{0,6},{1,7},{2,4},{3,5},{4,2},{5,3},{6,0},{7,1},{8,14},{9,15},{10,... | collective-permute-start | bytes 393224 | tf_op jit(solution)/shard_map/ppermute | solution.py:319
  28.7 9.4 %collective-permute-start.9 = (bf16[3,256,128]{2,1,0:T(8,128)(2,1)S(1)}, bf16[3,256,128]{2,1,0:T(8,128)(2,1)S(1)}, u32[]{:S(2)}, u32[]{:S(2)}) collective-permute-start(bf16[3,256,128]{2,1,0:T(8,128)(2,1)S(1)} %maximum_select_fusion.1.refs_0_), channel_id=1, source_target_pairs={{0,6},{1,7},{2,4},{3,5},{4,2},{5,3},{6,0},{7,1},{8,14},{9,15},{10,... | collective-permute-start | bytes 589832 | tf_op jit(solution)/shard_map/ppermute | solution.py:319
  31.1 16.9 %collective-permute-start.8 = (bf16[3,256,128]{2,1,0:T(8,128)(2,1)S(1)}, bf16[3,256,128]{2,1,0:T(8,128)(2,1)S(1)}, u32[]{:S(2)}, u32[]{:S(2)}) collective-permute-start(bf16[3,256,128]{2,1,0:T(8,128)(2,1)S(1)} %maximum_select_fusion.1.refs_0_), channel_id=1, source_target_pairs={{0,4},{1,5},{2,6},{3,7},{4,0},{5,1},{6,2},{7,3},{8,12},{9,13},{10,... | collective-permute-start | bytes 589832 | tf_op jit(solution)/shard_map/ppermute | solution.py:319
  32.5 18.0 %collective-permute-start.7 = (bf16[3,256,128]{2,1,0:T(8,128)(2,1)S(1)}, bf16[3,256,128]{2,1,0:T(8,128)(2,1)S(1)}, u32[]{:S(2)}, u32[]{:S(2)}) collective-permute-start(bf16[3,256,128]{2,1,0:T(8,128)(2,1)S(1)} %maximum_select_fusion.1.refs_0_), channel_id=1, source_target_pairs={{0,2},{1,3},{2,0},{3,1},{4,6},{5,7},{6,4},{7,5},{8,10},{9,11},{10,... | collective-permute-start | bytes 589832 | tf_op jit(solution)/shard_map/ppermute | solution.py:319
  38.1 24.2 %collective-permute-start.13 = (bf16[2,4,64,128]{3,2,1,0:T(8,128)(2,1)S(1)}, bf16[2,4,64,128]{3,2,1,0:T(8,128)(2,1)S(1)}, u32[]{:S(2)}, u32[]{:S(2)}) collective-permute-start(bf16[2,4,64,128]{3,2,1,0:T(8,128)(2,1)S(1)} %get-tuple-element.75), channel_id=1, source_target_pairs={{0,8},{8,0},{16,24},{24,16},{1,9},{9,1},{17,25},{25,17},{2,10},{10... | collective-permute-start | bytes 393224 | tf_op jit(solution)/shard_map/ppermute | solution.py:323
  48.0 14.3 %collective-permute-start.14 = (bf16[2,4,64,128]{3,2,1,0:T(8,128)(2,1)S(1)}, bf16[2,4,64,128]{3,2,1,0:T(8,128)(2,1)S(1)}, u32[]{:S(2)}, u32[]{:S(2)}) collective-permute-start(bf16[2,4,64,128]{3,2,1,0:T(8,128)(2,1)S(1)} %get-tuple-element.74), channel_id=1, source_target_pairs={{0,24},{8,16},{16,8},{24,0},{1,25},{9,17},{17,9},{25,1},{2,26},{10... | collective-permute-start | bytes 393224 | tf_op jit(solution)/shard_map/ppermute | solution.py:324
  50.5 20.1 %collective-permute-start.10 = (bf16[3,4,64,128]{3,2,1,0:T(8,128)(2,1)S(1)}, bf16[3,4,64,128]{3,2,1,0:T(8,128)(2,1)S(1)}, u32[]{:S(2)}, u32[]{:S(2)}) collective-permute-start(bf16[3,4,64,128]{3,2,1,0:T(8,128)(2,1)S(1)} %get-tuple-element.71), channel_id=1, source_target_pairs={{0,8},{8,0},{16,24},{24,16},{1,9},{9,1},{17,25},{25,17},{2,10},{10... | collective-permute-start | bytes 589832 | tf_op jit(solution)/shard_map/ppermute | solution.py:323
  51.1 19.5 %collective-permute-start.11 = (bf16[3,4,64,128]{3,2,1,0:T(8,128)(2,1)S(1)}, bf16[3,4,64,128]{3,2,1,0:T(8,128)(2,1)S(1)}, u32[]{:S(2)}, u32[]{:S(2)}) collective-permute-start(bf16[3,4,64,128]{3,2,1,0:T(8,128)(2,1)S(1)} %get-tuple-element.70), channel_id=1, source_target_pairs={{0,24},{8,16},{16,8},{24,0},{1,25},{9,17},{17,9},{25,1},{2,26},{10... | collective-permute-start | bytes 589832 | tf_op jit(solution)/shard_map/ppermute | solution.py:324
  64.4 9.9 %collective-permute-start.18 = (bf16[1,256,128]{2,1,0:T(8,128)(2,1)S(1)}, bf16[1,256,128]{2,1,0:T(8,128)(2,1)S(1)}, u32[]{:S(2)}, u32[]{:S(2)}) collective-permute-start(bf16[1,256,128]{2,1,0:T(8,128)(2,1)S(1)} %get-tuple-element.50.refs_0_), channel_id=1, source_target_pairs={{0,6},{1,7},{2,4},{3,5},{4,2},{5,3},{6,0},{7,1},{8,14},{9,15},{10,... | collective-permute-start | bytes 196616 | tf_op jit(solution)/shard_map/ppermute | solution.py:319
  66.9 7.4 %collective-permute-start.17 = (bf16[1,256,128]{2,1,0:T(8,128)(2,1)S(1)}, bf16[1,256,128]{2,1,0:T(8,128)(2,1)S(1)}, u32[]{:S(2)}, u32[]{:S(2)}) collective-permute-start(bf16[1,256,128]{2,1,0:T(8,128)(2,1)S(1)} %get-tuple-element.50.refs_0_), channel_id=1, source_target_pairs={{0,4},{1,5},{2,6},{3,7},{4,0},{5,1},{6,2},{7,3},{8,12},{9,13},{10,... | collective-permute-start | bytes 196616 | tf_op jit(solution)/shard_map/ppermute | solution.py:319
  66.9 7.4 %collective-permute-start.16 = (bf16[1,256,128]{2,1,0:T(8,128)(2,1)S(1)}, bf16[1,256,128]{2,1,0:T(8,128)(2,1)S(1)}, u32[]{:S(2)}, u32[]{:S(2)}) collective-permute-start(bf16[1,256,128]{2,1,0:T(8,128)(2,1)S(1)} %get-tuple-element.50.refs_0_), channel_id=1, source_target_pairs={{0,2},{1,3},{2,0},{3,1},{4,6},{5,7},{6,4},{7,5},{8,10},{9,11},{10,... | collective-permute-start | bytes 196616 | tf_op jit(solution)/shard_map/ppermute | solution.py:319
  74.4 4.7 %collective-permute-start.19 = (bf16[1,4,64,128]{3,2,1,0:T(8,128)(2,1)S(1)}, bf16[1,4,64,128]{3,2,1,0:T(8,128)(2,1)S(1)}, u32[]{:S(2)}, u32[]{:S(2)}) collective-permute-start(bf16[1,4,64,128]{3,2,1,0:T(8,128)(2,1)S(1)} %get-tuple-element.95), channel_id=1, source_target_pairs={{0,8},{8,0},{16,24},{24,16},{1,9},{9,1},{17,25},{25,17},{2,10},{10... | collective-permute-start | bytes 196616 | tf_op jit(solution)/shard_map/ppermute | solution.py:323
  75.0 5.4 %collective-permute-start.20 = (bf16[1,4,64,128]{3,2,1,0:T(8,128)(2,1)S(1)}, bf16[1,4,64,128]{3,2,1,0:T(8,128)(2,1)S(1)}, u32[]{:S(2)}, u32[]{:S(2)}) collective-permute-start(bf16[1,4,64,128]{3,2,1,0:T(8,128)(2,1)S(1)} %get-tuple-element.94), channel_id=1, source_target_pairs={{0,24},{8,16},{16,8},{24,0},{1,25},{9,17},{17,9},{25,1},{2,26},{10... | collective-permute-start | bytes 196616 | tf_op jit(solution)/shard_map/ppermute | solution.py:324
  82.6 6.1 %collective-permute-start.23 = (bf16[1,256,128]{2,1,0:T(8,128)(2,1)S(1)}, bf16[1,256,128]{2,1,0:T(8,128)(2,1)S(1)}, u32[]{:S(2)}, u32[]{:S(2)}) collective-permute-start(bf16[1,256,128]{2,1,0:T(8,128)(2,1)S(1)} %get-tuple-element.53.refs_0_), channel_id=1, source_target_pairs={{0,6},{1,7},{2,4},{3,5},{4,2},{5,3},{6,0},{7,1},{8,14},{9,15},{10,... | collective-permute-start | bytes 196616 | tf_op jit(solution)/shard_map/ppermute | solution.py:319
  85.2 5.2 %collective-permute-start.22 = (bf16[1,256,128]{2,1,0:T(8,128)(2,1)S(1)}, bf16[1,256,128]{2,1,0:T(8,128)(2,1)S(1)}, u32[]{:S(2)}, u32[]{:S(2)}) collective-permute-start(bf16[1,256,128]{2,1,0:T(8,128)(2,1)S(1)} %get-tuple-element.53.refs_0_), channel_id=1, source_target_pairs={{0,4},{1,5},{2,6},{3,7},{4,0},{5,1},{6,2},{7,3},{8,12},{9,13},{10,... | collective-permute-start | bytes 196616 | tf_op jit(solution)/shard_map/ppermute | solution.py:319
  85.2 5.2 %collective-permute-start.21 = (bf16[1,256,128]{2,1,0:T(8,128)(2,1)S(1)}, bf16[1,256,128]{2,1,0:T(8,128)(2,1)S(1)}, u32[]{:S(2)}, u32[]{:S(2)}) collective-permute-start(bf16[1,256,128]{2,1,0:T(8,128)(2,1)S(1)} %get-tuple-element.53.refs_0_), channel_id=1, source_target_pairs={{0,2},{1,3},{2,0},{3,1},{4,6},{5,7},{6,4},{7,5},{8,10},{9,11},{10,... | collective-permute-start | bytes 196616 | tf_op jit(solution)/shard_map/ppermute | solution.py:319
  91.7 5.2 %collective-permute-start.25 = (bf16[1,4,64,128]{3,2,1,0:T(8,128)(2,1)S(1)}, bf16[1,4,64,128]{3,2,1,0:T(8,128)(2,1)S(1)}, u32[]{:S(2)}, u32[]{:S(2)}) collective-permute-start(bf16[1,4,64,128]{3,2,1,0:T(8,128)(2,1)S(1)} %get-tuple-element.92), channel_id=1, source_target_pairs={{0,24},{8,16},{16,8},{24,0},{1,25},{9,17},{17,9},{25,1},{2,26},{10... | collective-permute-start | bytes 196616 | tf_op jit(solution)/shard_map/ppermute | solution.py:324
  98.1 6.1 %collective-permute-start.28 = (bf16[1,256,128]{2,1,0:T(8,128)(2,1)S(1)}, bf16[1,256,128]{2,1,0:T(8,128)(2,1)S(1)}, u32[]{:S(2)}, u32[]{:S(2)}) collective-permute-start(bf16[1,256,128]{2,1,0:T(8,128)(2,1)S(1)} %get-tuple-element.56.refs_0_), channel_id=1, source_target_pairs={{0,6},{1,7},{2,4},{3,5},{4,2},{5,3},{6,0},{7,1},{8,14},{9,15},{10,... | collective-permute-start | bytes 196616 | tf_op jit(solution)/shard_map/ppermute | solution.py:319
  100.5 5.6 %collective-permute-start.27 = (bf16[1,256,128]{2,1,0:T(8,128)(2,1)S(1)}, bf16[1,256,128]{2,1,0:T(8,128)(2,1)S(1)}, u32[]{:S(2)}, u32[]{:S(2)}) collective-permute-start(bf16[1,256,128]{2,1,0:T(8,128)(2,1)S(1)} %get-tuple-element.56.refs_0_), channel_id=1, source_target_pairs={{0,4},{1,5},{2,6},{3,7},{4,0},{5,1},{6,2},{7,3},{8,12},{9,13},{10,... | collective-permute-start | bytes 196616 | tf_op jit(solution)/shard_map/ppermute | solution.py:319
  100.6 5.4 %collective-permute-start.26 = (bf16[1,256,128]{2,1,0:T(8,128)(2,1)S(1)}, bf16[1,256,128]{2,1,0:T(8,128)(2,1)S(1)}, u32[]{:S(2)}, u32[]{:S(2)}) collective-permute-start(bf16[1,256,128]{2,1,0:T(8,128)(2,1)S(1)} %get-tuple-element.56.refs_0_), channel_id=1, source_target_pairs={{0,2},{1,3},{2,0},{3,1},{4,6},{5,7},{6,4},{7,5},{8,10},{9,11},{10,... | collective-permute-start | bytes 196616 | tf_op jit(solution)/shard_map/ppermute | solution.py:319
  106.9 5.2 %collective-permute-start.30 = (bf16[1,4,64,128]{3,2,1,0:T(8,128)(2,1)S(1)}, bf16[1,4,64,128]{3,2,1,0:T(8,128)(2,1)S(1)}, u32[]{:S(2)}, u32[]{:S(2)}) collective-permute-start(bf16[1,4,64,128]{3,2,1,0:T(8,128)(2,1)S(1)} %get-tuple-element.90), channel_id=1, source_target_pairs={{0,24},{8,16},{16,8},{24,0},{1,25},{9,17},{17,9},{25,1},{2,26},{10... | collective-permute-start | bytes 196616 | tf_op jit(solution)/shard_map/ppermute | solution.py:324
  113.4 8.4 %collective-permute-start.31 = (bf16[128,128]{1,0:T(8,128)(2,1)S(1)}, bf16[128,128]{1,0:T(8,128)(2,1)S(1)}, u32[]{:S(2)}, u32[]{:S(2)}) collective-permute-start(bf16[128,128]{1,0:T(8,128)(2,1)S(1)} %bitcast.180), channel_id=1, source_target_pairs={{0,2},{1,3},{2,0},{3,1},{4,6},{5,7},{6,4},{7,5},{8,10},{9,11},{10,... | collective-permute-start | bytes 98312 | tf_op jit(solution)/shard_map/ppermute | solution.py:407
  114.2 7.5 %collective-permute-start.32 = (bf16[128,128]{1,0:T(8,128)(2,1)S(1)}, bf16[128,128]{1,0:T(8,128)(2,1)S(1)}, u32[]{:S(2)}, u32[]{:S(2)}) collective-permute-start(bf16[128,128]{1,0:T(8,128)(2,1)S(1)} %bitcast.181), channel_id=1, source_target_pairs={{0,4},{1,5},{2,6},{3,7},{4,0},{5,1},{6,2},{7,3},{8,12},{9,13},{10,... | collective-permute-start | bytes 98312 | tf_op jit(solution)/shard_map/ppermute | solution.py:407
  116.0 5.7 %collective-permute-start.33 = (bf16[128,128]{1,0:T(8,128)(2,1)S(1)}, bf16[128,128]{1,0:T(8,128)(2,1)S(1)}, u32[]{:S(2)}, u32[]{:S(2)}) collective-permute-start(bf16[128,128]{1,0:T(8,128)(2,1)S(1)} %bitcast.182), channel_id=1, source_target_pairs={{0,6},{1,7},{2,4},{3,5},{4,2},{5,3},{6,0},{7,1},{8,14},{9,15},{10,... | collective-permute-start | bytes 98312 | tf_op jit(solution)/shard_map/ppermute | solution.py:407
  121.8 7.7 %collective-permute-start.34 = (bf16[1,4,64,128]{3,2,1,0:T(8,128)(2,1)S(1)}, bf16[1,4,64,128]{3,2,1,0:T(8,128)(2,1)S(1)}, u32[]{:S(2)}, u32[]{:S(2)}) collective-permute-start(bf16[1,4,64,128]{3,2,1,0:T(8,128)(2,1)S(1)} %get-tuple-element.89), channel_id=1, source_target_pairs={{0,8},{8,0},{16,24},{24,16},{1,9},{9,1},{17,25},{25,17},{2,10},{10... | collective-permute-start | bytes 196616 | tf_op jit(solution)/shard_map/ppermute | solution.py:323
  123.1 6.4 %collective-permute-start.35 = (bf16[1,4,64,128]{3,2,1,0:T(8,128)(2,1)S(1)}, bf16[1,4,64,128]{3,2,1,0:T(8,128)(2,1)S(1)}, u32[]{:S(2)}, u32[]{:S(2)}) collective-permute-start(bf16[1,4,64,128]{3,2,1,0:T(8,128)(2,1)S(1)} %get-tuple-element.88), channel_id=1, source_target_pairs={{0,24},{8,16},{16,8},{24,0},{1,25},{9,17},{17,9},{25,1},{2,26},{10... | collective-permute-start | bytes 196616 | tf_op jit(solution)/shard_map/ppermute | solution.py:324
  (9 other events, 26.1 us)

commit v4 on v3

--- a/solution.py
+++ b/solution.py
@@ -59,22 +59,19 @@
     return top, bottom
 
 
-def stage_kernel(*refs):
-    sources, target, semaphores = refs[:-2], refs[-2], refs[-1]
+def stage_kernel(source, target, semaphores):
     copies = []
     for p in range(3):
         for q in range(3):
-            for i, source in enumerate(sources):
-                copy = pltpu.make_async_copy(source.at[p, q], target.at[p, q, i], semaphores.at[p, q, i])
-                copy.start()
-                copies.append(copy)
+            copy = pltpu.make_async_copy(source.at[p, q], target.at[p, q], semaphores.at[p, q])
+            copy.start()
+            copies.append(copy)
     for copy in copies:
         copy.wait()
 
 
-def tap(weight_ref, p, q):
-    weight = weight_ref[p, q]
-    return weight.reshape(-1, weight.shape[-1])
+def tap(weight_refs, p, q):
+    return jnp.concatenate([weight_ref[p, q] for weight_ref in weight_refs], axis=0)
 
 
 def conv_kernel(groups, cols, index, halo, *refs):
@@ -82,7 +79,7 @@
     parts = [refs.pop(0) for _ in range(groups)]
     if halo:
         edge_a, edge_b = refs.pop(0), refs.pop(0)
-    weight_ref, init_ref, out_ref, held = refs
+    own_ref, pair_ref, init_ref, out_ref, held = refs
     count = out_ref.shape[1]
     group = lax.axis_index("hid") // 2
 
@@ -105,14 +102,14 @@
         for q in range(3):
             window = held[q, p * cols : p * cols + count, :]
             total = total + lax.dot_general(
-                tap(weight_ref, p, q), window, NT, preferred_element_type=jnp.float32
+                tap((own_ref, pair_ref), p, q), window, NT, preferred_element_type=jnp.float32
             )
     out_ref[...] = total
 
 
 def gate_kernel(cols, indices, turn_in, turn_out, *refs):
     refs = list(refs)
-    sides = [(refs.pop(0), refs.pop(0), refs.pop(0), index) for index in indices]
+    sides = [(refs.pop(0), refs.pop(0), (refs.pop(0), refs.pop(0)), index) for index in indices]
     total_ref = refs.pop(0)
     cells = [refs.pop(0), refs.pop(0)]
     hidden_ref = refs.pop(0)
@@ -129,7 +126,7 @@
     for q in range(3):
         held[q, pl.ds(cols, cols), :] = zero
         held[q, pl.ds(2 * cols, cols), :] = zero
-    for edge_a, edge_b, weight_ref, index in sides:
+    for edge_a, edge_b, weight_refs, index in sides:
         top, bottom = halo_pieces(edge_a, edge_b, index)
         place_columns(held, 0, top, group, cols, True)
         place_columns(held, 3 * cols, bottom, group, cols, True)
@@ -138,7 +135,7 @@
             for q in range(3):
                 window = held[q, row0 : row0 + side, :]
                 total = total + lax.dot_general(
-                    tap(weight_ref, p, q), window, NT, preferred_element_type=jnp.float32
+                    tap(weight_refs, p, q), window, NT, preferred_element_type=jnp.float32
                 )
             summed[:, lane0 : lane0 + side] = total
     for half in range(2):
@@ -166,7 +163,7 @@
             for q in range(3):
                 window = source[q, p * width : (p + count) * width, :]
                 total = total + lax.dot_general(
-                    window, tap(weight_ref, p, q), NN, preferred_element_type=jnp.float32
+                    window, weight_ref[p, q], NN, preferred_element_type=jnp.float32
                 )
         return total
 
@@ -199,26 +196,25 @@
     return pl.CostEstimate(flops=flops, bytes_accessed=size, transcendentals=0)
 
 
-def stage_call(*sources):
-    shape = sources[0].shape[:2] + (len(sources),) + sources[0].shape[2:]
-    size = 2 * sources[0].size * len(sources)
+def stage_call(source):
+    size = 2 * source.size
     return pl.pallas_call(
         stage_kernel,
-        in_specs=[pl.BlockSpec(memory_space=pltpu.HBM)] * len(sources),
+        in_specs=[pl.BlockSpec(memory_space=pltpu.HBM)],
         out_specs=WHOLE,
-        out_shape=pltpu.VMEM(shape, sources[0].dtype),
-        scratch_shapes=[pltpu.SemaphoreType.DMA((3, 3, len(sources)))],
+        out_shape=pltpu.VMEM(source.shape, source.dtype),
+        scratch_shapes=[pltpu.SemaphoreType.DMA((3, 3))],
         compiler_params=params(),
         cost_estimate=cost(100 * size, size),
-    )(*(pltpu.with_memory_space_constraint(source, pltpu.HBM) for source in sources))
-
-
-def conv_call(parts, index, edges, weight, init, cols):
+    )(pltpu.with_memory_space_constraint(source, pltpu.HBM))
+
+
+def conv_call(parts, index, edges, weights, init, cols):
     groups = len(parts)
     count = parts[0].shape[1]
-    channels = weight.shape[-1]
-    outs = 2 * weight.shape[3]
-    operands = list(parts) + ([] if edges is None else list(edges)) + [weight, init]
+    channels = weights[0].shape[-1]
+    outs = 2 * weights[0].shape[2]
+    operands = list(parts) + ([] if edges is None else list(edges)) + [*weights, init]
     return pl.pallas_call(
         functools.partial(conv_kernel, groups, cols, index, edges is not None),
         in_specs=[WHOLE] * len(operands),
@@ -232,13 +228,13 @@
 
 def gate_call(sides, total, cells, cols, turn_in, turn_out):
     outs, count = total.shape
-    channels = sides[0][2].shape[-1]
+    channels = sides[0][2][0].shape[-1]
     share = outs // 8
     width = 2 * share
     cell_shape = (count, share) if turn_out else (share, count)
     operands = []
-    for edges, _, weight in sides:
-        operands += [edges[0], edges[1], weight]
+    for edges, _, weights in sides:
+        operands += [*edges, *weights]
     operands += [total, *cells]
     return pl.pallas_call(
         functools.partial(gate_kernel, cols, [index for _, index, _ in sides], turn_in, turn_out),
@@ -258,8 +254,8 @@
 
 def decoder_call(parts, edges, first, first_bias, second, second_bias, rows, width, margin, inner):
     groups = len(parts)
-    channels = first.shape[3]
-    outs = second.shape[4]
+    channels = first.shape[2]
+    outs = second.shape[3]
     operands = [*parts, *edges, first, first_bias.reshape(1, -1), second, second_bias.reshape(1, -1)]
     return pl.pallas_call(
         functools.partial(decoder_kernel, groups, rows, width, margin, inner),
@@ -268,7 +264,7 @@
         out_shape=jax.ShapeDtypeStruct((rows * width, outs), jnp.bfloat16),
         scratch_shapes=[
             pltpu.VMEM((3, (rows + 4) * width, channels), jnp.bfloat16),
-            pltpu.VMEM((3, (rows + 2) * width, first.shape[4]), jnp.bfloat16),
+            pltpu.VMEM((3, (rows + 2) * width, first.shape[3]), jnp.bfloat16),
         ],
         compiler_params=params(),
         cost_estimate=cost(18 * channels * outs * (2 * rows + 2) * width, 36 * channels * outs),
@@ -310,10 +306,6 @@
         other = lax.dynamic_index_in_dim(value, 1 - core, axis, keepdims=False, allow_negative_indices=False)
         return mine, swap(other)
 
-    def joined(value, axis):
-        mine, other = own_batch(value, axis)
-        return jnp.where(core == 0, jnp.concatenate([mine, other], -1), jnp.concatenate([other, mine], -1))
-
     def gathered(value):
         return [value] + [
             lax.ppermute(value, "hid", [(i, i ^ (2 * k)) for i in range(2 * groups)]) for k in range(1, groups)
@@ -336,13 +328,13 @@
     def ordered(mine, other, axis):
         return jnp.where(core == 0, jnp.concatenate([mine, other], axis), jnp.concatenate([other, mine], axis))
 
+    def frames_of(index, first):
+        size = (steps - 1 if first else 1, 1) + frames.shape[2:]
+        return lax.dynamic_slice(frames, (first, index, 0, 0, 0), size, allow_negative_indices=False)[:, 0]
+
     def of_batch(index):
-        return jnp.stack(
-            [
-                lax.dynamic_index_in_dim(frames[0], index, 0, keepdims=False, allow_negative_indices=False),
-                lax.dynamic_index_in_dim(hidden_start, index, 0, keepdims=False, allow_negative_indices=False),
-            ]
-        )
+        state = lax.dynamic_slice_in_dim(hidden_start, index, 1, 0, allow_negative_indices=False)
+        return jnp.concatenate([frames_of(index, 0), state], 0)
 
     lead = ordered(of_batch(core), swap(of_batch(1 - core)), -1).reshape(2, count, width)
     inner = cols // groups
@@ -366,16 +358,15 @@
     )
     lead_parts = gathered(lead)
     input_pair, hidden_pair = swap(input_own), swap(hidden_own)
+    input_both, hidden_both = (input_own, input_pair), (hidden_own, hidden_pair)
     first_weight, second_weight = stage_call(first_weight), stage_call(second_weight)
-    input_both = stage_call(input_own, input_pair)
-    hidden_both = stage_call(hidden_own, hidden_pair)
-    rest = joined(frames[1:], 1).reshape(steps - 1, count, width)
+    rest = ordered(frames_of(core, 1), swap(frames_of(1 - core, 1)), -1).reshape(steps - 1, count, width)
     cell_mine, cell_other = own_batch(cell_start, 0)
     cells = [cell_mine.reshape(count, share), cell_other.reshape(count, share)]
     bias_own = gate_bias.reshape(-1)
     bias = jnp.concatenate([bias_own, swap(bias_own)]).reshape(1, -1)
 
-    lead_parts, rest, cells, bias = lax.optimization_barrier((lead_parts, rest, cells, bias))
+    lead_parts, cells, bias = lax.optimization_barrier((lead_parts, cells, bias))
     lead_edges = edges_of(lead_parts)
     rest_parts = gathered(rest)
     rest_edges = edges_of(rest_parts)

time: 134 us -> 127 us (0.948)
  waiting for transfers between devices: 43.9 us -> 34.6 us
  Pallas kernels: 32.4 us -> 37.5 us
  starting transfers between devices: 48.2 us -> 46.1 us
    ppermute x15, waiting for transfers between devices: 30.1 us -> 22.2 us  [gathered(): lax.ppermute(value, 'hid', [(i, i ^ 2 * k) for i in range(2 * groups)])]
    pallas_call x8, Pallas kernels: 13.7 us -> 20.4 us  [conv_call(): pl.pallas_call(functools.partial(conv_kernel, groups, cols, index, edges...]
    pallas_call x4 -> x2, Pallas kernels: 9.66 us -> 4.77 us  [stage_call(): pl.pallas_call(stage_kernel, in_specs=[pl.BlockSpec(memory_space=pltpu.HB...]
    pallas_call x4, Pallas kernels: 6.8 us -> 10.2 us  [gate_call(): pl.pallas_call(functools.partial(gate_kernel, cols, [index for _, index,...]
    ppermute x8, waiting for transfers between devices: 5.39 us -> 2.95 us  [swap(): return lax.ppermute(value, 'hid', pairs)]
    dynamic_slice x3, local copies, waits for them, and re-layouts: 0.94 us -> 2.97 us  [the longest x2 2.09 us: frames_of(): lax.dynamic_slice(frames, (first, index, 0, 0, 0), size, allow_negative_i...]
    slice x2 -> x0, local copies, waits for them, and re-layouts: 1.94 us -> none  [the longest x1 1.02 us: program(): rest = joined(frames[1:], 1).reshape(steps - 1, count, width)]
    ppermute x6, starting transfers between devices: 11.5 us -> 9.74 us  [swapped_edges(): second = lax.ppermute(jnp.where(even, top, bottom), 'patch', outer_pairs)]
  transfers between devices with their start and end apart: 38 -> 38, of which waited for: 15 -> 19; matrix products, arithmetic and copies ran while one was open for 3% -> 3% of each run, Pallas kernels for 21% -> 25%
where the time goes in v4:
time: 127 us; the launch traced here: 126 us
  starting transfers between devices  46.1 us (36%)
  Pallas kernels  37.5 us (30%)
  waiting for transfers between devices  34.6 us (27%)
  local copies, waits for them, and re-layouts  5.15 us (4%)
  other arithmetic  1.95 us (2%)
    ppermute x15, starting transfers between devices, gathered(): lax.ppermute(value, 'hid', [(i, i ^ 2 * k) for i in range(2 * groups)])  23.2 us
    ppermute x15, waiting for transfers between devices, gathered(): lax.ppermute(value, 'hid', [(i, i ^ 2 * k) for i in range(2 * groups)])  22.2 us
    pallas_call x8, Pallas kernels, conv_call(): pl.pallas_call(functools.partial(conv_kernel, groups, cols, index, edges...  20.4 us
    pallas_call x4, Pallas kernels, gate_call(): pl.pallas_call(functools.partial(gate_kernel, cols, [index for _, index,...  10.2 us
    ppermute x6, starting transfers between devices, swapped_edges(): second = lax.ppermute(jnp.where(even, top, bottom), 'patch', outer_pairs)  9.74 us
    ppermute x6, starting transfers between devices, swapped_edges(): first = lax.ppermute(jnp.where(even, bottom, top), 'patch', inner_pairs)  6.92 us
    pallas_call x2, Pallas kernels, stage_call(): pl.pallas_call(stage_kernel, in_specs=[pl.BlockSpec(memory_space=pltpu.HB...  4.77 us
    ppermute x3, waiting for transfers between devices, program(): lax.ppermute(columns_for(k), 'hid', [(i, i ^ 2 * k) for i in range(2 * gr...  4.56 us
  transfers between devices with their start and end apart: 38, of which 19 were waited for; matrix products, arithmetic and copies ran while one was open for 3% of the time, Pallas kernels for 25%

profile of v4, /device:TPU:0, one launch (start us, length us, event | category | flops | bytes accessed | tf_op | source)
XLA Modules:
  0.0 126.3 jit_solution(4693499128558398607)
XLA Ops:
  4.7 4.9 %collective-permute-start.10 = (bf16[2,256,128]{2,1,0:T(8,128)(2,1)S(1)}, bf16[2,256,128]{2,1,0:T(8,128)(2,1)S(1)}, u32[]{:S(2)}, u32[]{:S(2)}) collective-permute-start(bf16[2,256,128]{2,1,0:T(8,128)(2,1)S(1)} %maximum_select_fusion.2.refs_0_), channel_id=1, source_target_pairs={{0,6},{1,7},{2,4},{3,5},{4,2},{5,3},{6,0},{7,1},{8,14},{9,15},{10,... | collective-permute-start | bytes 393224 | tf_op jit(solution)/shard_map/ppermute | solution.py:311
  15.7 2.3 %collective-permute-start.8 = (bf16[2,256,128]{2,1,0:T(8,128)(2,1)S(1)}, bf16[2,256,128]{2,1,0:T(8,128)(2,1)S(1)}, u32[]{:S(2)}, u32[]{:S(2)}) collective-permute-start(bf16[2,256,128]{2,1,0:T(8,128)(2,1)S(1)} %maximum_select_fusion.2.refs_0_), channel_id=1, source_target_pairs={{0,2},{1,3},{2,0},{3,1},{4,6},{5,7},{6,4},{7,5},{8,10},{9,11},{10,... | collective-permute-start | bytes 393224 | tf_op jit(solution)/shard_map/ppermute | solution.py:311
  18.1 2.5 %collective-permute-start.4 = (bf16[3,256,128]{2,1,0:T(8,128)(2,1)S(1)}, bf16[3,256,128]{2,1,0:T(8,128)(2,1)S(1)}, u32[]{:S(2)}, u32[]{:S(2)}) collective-permute-start(bf16[3,256,128]{2,1,0:T(8,128)(2,1)S(1)} %maximum_select_fusion.1.refs_0_), channel_id=1, source_target_pairs={{0,6},{1,7},{2,4},{3,5},{4,2},{5,3},{6,0},{7,1},{8,14},{9,15},{10,... | collective-permute-start | bytes 589832 | tf_op jit(solution)/shard_map/ppermute | solution.py:311
  21.2 3.3 %collective-permute-done.8.refs_1_ = bf16[2,256,128]{2,1,0:T(8,128)(2,1)S(1)} collective-permute-done((bf16[2,256,128]{2,1,0:T(8,128)(2,1)S(1)}, bf16[2,256,128]{2,1,0:T(8,128)(2,1)S(1)}, u32[]{:S(2)}, u32[]{:S(2)}) %collective-permute-start.8) | collective-permute-done | bytes 131104 | tf_op jit(solution)/shard_map/ppermute | solution.py:311
  24.6 4.6 %collective-permute-done.4.refs_3_ = bf16[3,256,128]{2,1,0:T(8,128)(2,1)S(1)} collective-permute-done((bf16[3,256,128]{2,1,0:T(8,128)(2,1)S(1)}, bf16[3,256,128]{2,1,0:T(8,128)(2,1)S(1)}, u32[]{:S(2)}, u32[]{:S(2)}) %collective-permute-start.4) | collective-permute-done | bytes 196640 | tf_op jit(solution)/shard_map/ppermute | solution.py:311
  29.2 2.4 %collective-permute-start.14 = (bf16[2,4,64,128]{3,2,1,0:T(8,128)(2,1)S(1)}, bf16[2,4,64,128]{3,2,1,0:T(8,128)(2,1)S(1)}, u32[]{:S(2)}, u32[]{:S(2)}) collective-permute-start(bf16[2,4,64,128]{3,2,1,0:T(8,128)(2,1)S(1)} %get-tuple-element.74), channel_id=1, source_target_pairs={{0,24},{8,16},{16,8},{24,0},{1,25},{9,17},{17,9},{25,1},{2,26},{10... | collective-permute-start | bytes 393224 | tf_op jit(solution)/shard_map/ppermute | solution.py:316
  31.6 6.7 %collective-permute-done.3.refs_2_ = bf16[3,256,128]{2,1,0:T(8,128)(2,1)S(1)} collective-permute-done((bf16[3,256,128]{2,1,0:T(8,128)(2,1)S(1)}, bf16[3,256,128]{2,1,0:T(8,128)(2,1)S(1)}, u32[]{:S(2)}, u32[]{:S(2)}) %collective-permute-start.3) | collective-permute-done | bytes 196640 | tf_op jit(solution)/shard_map/ppermute | solution.py:311
  42.9 3.4 %shard_map.113.refs_6_ = f32[512,256]{1,0:T(8,128)S(1)} custom-call(bf16[2,256,128]{2,1,0:T(8,128)(2,1)S(1)} %maximum_select_fusion.2.refs_0_, bf16[2,256,128]{2,1,0:T(8,128)(2,1)S(1)} %collective-permute-done.8.refs_1_, bf16[2,256,128]{2,1,0:T(8,128)(2,1)S(1)} %collective-permute-done.9.refs_2_, bf16[2,256,128]{2,1,0:T(8,128)(2,1)S(1)} %collective-permute-done.10.refs_3_, ...), custom_call_target="tpu_custom_call" | custom-call | flops 1207959552 | bytes 4718592 | tf_op jit(solution)/shard_map/pallas_call | solution.py:218
  46.3 1.7 %shard_map.114.refs_8_ = f32[512,256]{1,0:T(8,128)S(1)} custom-call(bf16[2,256,128]{2,1,0:T(8,128)(2,1)S(1)} %maximum_select_fusion.2.refs_0_, bf16[2,256,128]{2,1,0:T(8,128)(2,1)S(1)} %collective-permute-done.8.refs_1_, bf16[2,256,128]{2,1,0:T(8,128)(2,1)S(1)} %collective-permute-done.9.refs_2_, bf16[2,256,128]{2,1,0:T(8,128)(2,1)S(1)} %collective-permute-done.10.refs_3_, ...), custom_call_target="tpu_custom_call" | custom-call | flops 1207959552 | bytes 4718592 | tf_op jit(solution)/shard_map/pallas_call | solution.py:218
  48.0 3.8 %shard_map.115 = (bf16[1,256,128]{2,1,0:T(8,128)(2,1)S(1)}, f32[64,256]{1,0:T(8,128)S(1)}, f32[64,256]{1,0:T(8,128)S(1)}) custom-call(bf16[2,4,64,128]{3,2,1,0:T(8,128)(2,1)S(1)} %collective-permute-done.13.refs_0_.refs_4_, bf16[2,4,64,128]{3,2,1,0:T(8,128)(2,1)S(1)} %collective-permute-done.14.refs_1_.refs_5_, bf16[3,3,256,512]{3,2,1,0:T(8,128)(2,1)S(1)} %bitcast.166, ...), custom_call_target="tpu_custom_call" | custom-call | flops 805306368 | bytes 3145728 | tf_op jit(solution)/shard_map/pallas_call | solution.py:239
  51.8 2.8 %collective-permute-start.18 = (bf16[1,256,128]{2,1,0:T(8,128)(2,1)S(1)}, bf16[1,256,128]{2,1,0:T(8,128)(2,1)S(1)}, u32[]{:S(2)}, u32[]{:S(2)}) collective-permute-start(bf16[1,256,128]{2,1,0:T(8,128)(2,1)S(1)} %get-tuple-element.48.refs_0_), channel_id=1, source_target_pairs={{0,6},{1,7},{2,4},{3,5},{4,2},{5,3},{6,0},{7,1},{8,14},{9,15},{10,... | collective-permute-start | bytes 196616 | tf_op jit(solution)/shard_map/ppermute | solution.py:311
  56.3 3.5 %shard_map.122.refs_6_ = f32[512,256]{1,0:T(8,128)S(1)} custom-call(bf16[3,256,128]{2,1,0:T(8,128)(2,1)S(1)} %maximum_select_fusion.1.refs_0_, bf16[3,256,128]{2,1,0:T(8,128)(2,1)S(1)} %collective-permute-done.2.refs_1_, bf16[3,256,128]{2,1,0:T(8,128)(2,1)S(1)} %collective-permute-done.3.refs_2_, bf16[3,256,128]{2,1,0:T(8,128)(2,1)S(1)} %collective-permute-done.4.refs_3_, ...), custom_call_target="tpu_custom_call" | custom-call | flops 1207959552 | bytes 4718592 | tf_op jit(solution)/shard_map/pallas_call | solution.py:218
  59.8 3.5 %shard_map.119.refs_6_ = f32[512,256]{1,0:T(8,128)S(1)} custom-call(bf16[3,256,128]{2,1,0:T(8,128)(2,1)S(1)} %maximum_select_fusion.1.refs_0_, bf16[3,256,128]{2,1,0:T(8,128)(2,1)S(1)} %collective-permute-done.2.refs_1_, bf16[3,256,128]{2,1,0:T(8,128)(2,1)S(1)} %collective-permute-done.3.refs_2_, bf16[3,256,128]{2,1,0:T(8,128)(2,1)S(1)} %collective-permute-done.4.refs_3_, ...), custom_call_target="tpu_custom_call" | custom-call | flops 1207959552 | bytes 4718592 | tf_op jit(solution)/shard_map/pallas_call | solution.py:218
  63.3 3.4 %shard_map.116.refs_6_ = f32[512,256]{1,0:T(8,128)S(1)} custom-call(bf16[3,256,128]{2,1,0:T(8,128)(2,1)S(1)} %maximum_select_fusion.1.refs_0_, bf16[3,256,128]{2,1,0:T(8,128)(2,1)S(1)} %collective-permute-done.2.refs_1_, bf16[3,256,128]{2,1,0:T(8,128)(2,1)S(1)} %collective-permute-done.3.refs_2_, bf16[3,256,128]{2,1,0:T(8,128)(2,1)S(1)} %collective-permute-done.4.refs_3_, ...), custom_call_target="tpu_custom_call" | custom-call | flops 1207959552 | bytes 4718592 | tf_op jit(solution)/shard_map/pallas_call | solution.py:218
  68.8 1.7 %shard_map.117.refs_8_ = f32[512,256]{1,0:T(8,128)S(1)} custom-call(bf16[1,256,128]{2,1,0:T(8,128)(2,1)S(1)} %get-tuple-element.48.refs_0_, bf16[1,256,128]{2,1,0:T(8,128)(2,1)S(1)} %collective-permute-done.16.refs_1_, bf16[1,256,128]{2,1,0:T(8,128)(2,1)S(1)} %collective-permute-done.17.refs_2_, bf16[1,256,128]{2,1,0:T(8,128)(2,1)S(1)} %collective-permute-done.18.refs_3_, ...), custom_call_target="tpu_custom_call" | custom-call | flops 1207959552 | bytes 4718592 | tf_op jit(solution)/shard_map/pallas_call | solution.py:218
  72.0 4.0 %shard_map.118 = (bf16[1,256,128]{2,1,0:T(8,128)(2,1)S(1)}, f32[64,256]{1,0:T(8,128)S(1)}, f32[64,256]{1,0:T(8,128)S(1)}) custom-call(bf16[3,4,64,128]{3,2,1,0:T(8,128)(2,1)S(1)} %collective-permute-done.5.refs_0_.refs_4_, bf16[3,4,64,128]{3,2,1,0:T(8,128)(2,1)S(1)} %collective-permute-done.6.refs_1_.refs_5_, bf16[3,3,256,512]{3,2,1,0:T(8,128)(2,1)S(1)} %bitcast.170, ...), custom_call_target="tpu_custom_call" | custom-call | flops 805306368 | bytes 3145728 | tf_op jit(solution)/shard_map/pallas_call | solution.py:239
  76.0 2.8 %collective-permute-start.23 = (bf16[1,256,128]{2,1,0:T(8,128)(2,1)S(1)}, bf16[1,256,128]{2,1,0:T(8,128)(2,1)S(1)}, u32[]{:S(2)}, u32[]{:S(2)}) collective-permute-start(bf16[1,256,128]{2,1,0:T(8,128)(2,1)S(1)} %get-tuple-element.51.refs_0_), channel_id=1, source_target_pairs={{0,6},{1,7},{2,4},{3,5},{4,2},{5,3},{6,0},{7,1},{8,14},{9,15},{10,... | collective-permute-start | bytes 196616 | tf_op jit(solution)/shard_map/ppermute | solution.py:311
  80.4 1.7 %collective-permute-done.23.refs_3_ = bf16[1,256,128]{2,1,0:T(8,128)(2,1)S(1)} collective-permute-done((bf16[1,256,128]{2,1,0:T(8,128)(2,1)S(1)}, bf16[1,256,128]{2,1,0:T(8,128)(2,1)S(1)}, u32[]{:S(2)}, u32[]{:S(2)}) %collective-permute-start.23) | collective-permute-done | bytes 65568 | tf_op jit(solution)/shard_map/ppermute | solution.py:311
  82.1 1.8 %collective-permute-done.22.refs_2_ = bf16[1,256,128]{2,1,0:T(8,128)(2,1)S(1)} collective-permute-done((bf16[1,256,128]{2,1,0:T(8,128)(2,1)S(1)}, bf16[1,256,128]{2,1,0:T(8,128)(2,1)S(1)}, u32[]{:S(2)}, u32[]{:S(2)}) %collective-permute-start.22) | collective-permute-done | bytes 65568 | tf_op jit(solution)/shard_map/ppermute | solution.py:311
  84.0 2.1 %collective-permute-start.25 = (bf16[1,4,64,128]{3,2,1,0:T(8,128)(2,1)S(1)}, bf16[1,4,64,128]{3,2,1,0:T(8,128)(2,1)S(1)}, u32[]{:S(2)}, u32[]{:S(2)}) collective-permute-start(bf16[1,4,64,128]{3,2,1,0:T(8,128)(2,1)S(1)} %get-tuple-element.92), channel_id=1, source_target_pairs={{0,24},{8,16},{16,8},{24,0},{1,25},{9,17},{17,9},{25,1},{2,26},{10... | collective-permute-start | bytes 196616 | tf_op jit(solution)/shard_map/ppermute | solution.py:316
  86.8 1.7 %shard_map.120.refs_4_ = f32[512,256]{1,0:T(8,128)S(1)} custom-call(bf16[1,256,128]{2,1,0:T(8,128)(2,1)S(1)} %get-tuple-element.51.refs_0_, bf16[1,256,128]{2,1,0:T(8,128)(2,1)S(1)} %collective-permute-done.21.refs_1_, bf16[1,256,128]{2,1,0:T(8,128)(2,1)S(1)} %collective-permute-done.22.refs_2_, bf16[1,256,128]{2,1,0:T(8,128)(2,1)S(1)} %collective-permute-done.23.refs_3_, ...), custom_call_target="tpu_custom_call" | custom-call | flops 1207959552 | bytes 4718592 | tf_op jit(solution)/shard_map/pallas_call | solution.py:218
  91.6 2.4 %collective-permute-start.28 = (bf16[1,256,128]{2,1,0:T(8,128)(2,1)S(1)}, bf16[1,256,128]{2,1,0:T(8,128)(2,1)S(1)}, u32[]{:S(2)}, u32[]{:S(2)}) collective-permute-start(bf16[1,256,128]{2,1,0:T(8,128)(2,1)S(1)} %get-tuple-element.54.refs_0_), channel_id=1, source_target_pairs={{0,6},{1,7},{2,4},{3,5},{4,2},{5,3},{6,0},{7,1},{8,14},{9,15},{10,... | collective-permute-start | bytes 196616 | tf_op jit(solution)/shard_map/ppermute | solution.py:311
  93.9 2.1 %collective-permute-start.26 = (bf16[1,256,128]{2,1,0:T(8,128)(2,1)S(1)}, bf16[1,256,128]{2,1,0:T(8,128)(2,1)S(1)}, u32[]{:S(2)}, u32[]{:S(2)}) collective-permute-start(bf16[1,256,128]{2,1,0:T(8,128)(2,1)S(1)} %get-tuple-element.54.refs_0_), channel_id=1, source_target_pairs={{0,2},{1,3},{2,0},{3,1},{4,6},{5,7},{6,4},{7,5},{8,10},{9,11},{10,... | collective-permute-start | bytes 196616 | tf_op jit(solution)/shard_map/ppermute | solution.py:311
  96.0 1.7 %collective-permute-done.28.refs_3_ = bf16[1,256,128]{2,1,0:T(8,128)(2,1)S(1)} collective-permute-done((bf16[1,256,128]{2,1,0:T(8,128)(2,1)S(1)}, bf16[1,256,128]{2,1,0:T(8,128)(2,1)S(1)}, u32[]{:S(2)}, u32[]{:S(2)}) %collective-permute-start.28) | collective-permute-done | bytes 65568 | tf_op jit(solution)/shard_map/ppermute | solution.py:311
  97.7 1.8 %collective-permute-done.27.refs_2_ = bf16[1,256,128]{2,1,0:T(8,128)(2,1)S(1)} collective-permute-done((bf16[1,256,128]{2,1,0:T(8,128)(2,1)S(1)}, bf16[1,256,128]{2,1,0:T(8,128)(2,1)S(1)}, u32[]{:S(2)}, u32[]{:S(2)}) %collective-permute-start.27) | collective-permute-done | bytes 65568 | tf_op jit(solution)/shard_map/ppermute | solution.py:311
  101.6 1.7 %shard_map.123.refs_4_ = f32[512,256]{1,0:T(8,128)S(1)} custom-call(bf16[1,256,128]{2,1,0:T(8,128)(2,1)S(1)} %get-tuple-element.54.refs_0_, bf16[1,256,128]{2,1,0:T(8,128)(2,1)S(1)} %collective-permute-done.26.refs_1_, bf16[1,256,128]{2,1,0:T(8,128)(2,1)S(1)} %collective-permute-done.27.refs_2_, bf16[1,256,128]{2,1,0:T(8,128)(2,1)S(1)} %collective-permute-done.28.refs_3_, ...), custom_call_target="tpu_custom_call" | custom-call | flops 1207959552 | bytes 4718592 | tf_op jit(solution)/shard_map/pallas_call | solution.py:218
  107.0 2.5 %collective-permute-start.33 = (bf16[128,128]{1,0:T(8,128)(2,1)S(1)}, bf16[128,128]{1,0:T(8,128)(2,1)S(1)}, u32[]{:S(2)}, u32[]{:S(2)}) collective-permute-start(bf16[128,128]{1,0:T(8,128)(2,1)S(1)} %bitcast.193), channel_id=1, source_target_pairs={{0,6},{1,7},{2,4},{3,5},{4,2},{5,3},{6,0},{7,1},{8,14},{9,15},{10,... | collective-permute-start | bytes 98312 | tf_op jit(solution)/shard_map/ppermute | solution.py:398
  110.1 2.6 %collective-permute-done.33.refs_3_ = bf16[128,128]{1,0:T(8,128)(2,1)S(1)} collective-permute-done((bf16[128,128]{1,0:T(8,128)(2,1)S(1)}, bf16[128,128]{1,0:T(8,128)(2,1)S(1)}, u32[]{:S(2)}, u32[]{:S(2)}) %collective-permute-start.33) | collective-permute-done | bytes 32800 | tf_op jit(solution)/shard_map/ppermute | solution.py:398
  114.4 2.1 %collective-permute-start.35 = (bf16[1,4,64,128]{3,2,1,0:T(8,128)(2,1)S(1)}, bf16[1,4,64,128]{3,2,1,0:T(8,128)(2,1)S(1)}, u32[]{:S(2)}, u32[]{:S(2)}) collective-permute-start(bf16[1,4,64,128]{3,2,1,0:T(8,128)(2,1)S(1)} %get-tuple-element.88), channel_id=1, source_target_pairs={{0,24},{8,16},{16,8},{24,0},{1,25},{9,17},{17,9},{25,1},{2,26},{10... | collective-permute-start | bytes 196616 | tf_op jit(solution)/shard_map/ppermute | solution.py:316
  117.2 2.4 %shard_map.125.refs_6_ = bf16[3,3,512,512]{3,2,1,0:T(8,128)(2,1)S(1)} custom-call(bf16[3,3,512,512]{3,2,1,0:T(8,128)(2,1)} %source), custom_call_target="tpu_custom_call" | custom-call | flops 471859200 | bytes 4718592 | tf_op jit(solution)/shard_map/pallas_call | solution.py:201
  119.6 2.4 %shard_map.126.refs_8_ = bf16[3,3,512,512]{3,2,1,0:T(8,128)(2,1)S(1)} custom-call(bf16[3,3,512,512]{3,2,1,0:T(8,128)(2,1)} %source.1), custom_call_target="tpu_custom_call" | custom-call | flops 471859200 | bytes 4718592 | tf_op jit(solution)/shard_map/pallas_call | solution.py:201
  122.1 2.1 %shard_map.127 = bf16[128,512]{1,0:T(8,128)(2,1)S(1)} custom-call(bf16[128,128]{1,0:T(8,128)(2,1)S(1)} %bitcast.176, bf16[128,128]{1,0:T(8,128)(2,1)S(1)} %collective-permute-done.31.refs_1_, bf16[128,128]{1,0:T(8,128)(2,1)S(1)} %collective-permute-done.32.refs_2_, bf16[128,128]{1,0:T(8,128)(2,1)S(1)} %collective-permute-done.33.refs_3_, ...), custom_call_target="tpu_custom_call" | custom-call | flops 1509949440 | bytes 9437184 | tf_op jit(solution)/shard_map/pallas_call | solution.py:260
  (108 shorter events, 36.9 us)
Async XLA Ops:
  4.1 37.3 %collective-permute-start.7 = (bf16[3,3,256,512]{3,2,1,0:T(8,128)(2,1)}, bf16[3,3,256,512]{3,2,1,0:T(8,128)(2,1)}, u32[]{:S(2)}, u32[]{:S(2)}) collective-permute-start(bf16[3,3,256,512]{3,2,1,0:T(8,128)(2,1)} %bitcast.164), channel_id=1, source_target_pairs={{0,1},{1,0},{2,3},{3,2},{4,5},{5,4},{6,7},{7,6},{8,9},{9,8},{10,11... | collective-permute-start | bytes 7077896 | tf_op jit(solution)/shard_map/ppermute | solution.py:302
  4.6 41.7 %collective-permute-start.15 = (bf16[3,3,256,512]{3,2,1,0:T(8,128)(2,1)}, bf16[3,3,256,512]{3,2,1,0:T(8,128)(2,1)S(1)}, u32[]{:S(2)}, u32[]{:S(2)}) collective-permute-start(bf16[3,3,256,512]{3,2,1,0:T(8,128)(2,1)} %bitcast.155), channel_id=1, source_target_pairs={{0,1},{1,0},{2,3},{3,2},{4,5},{5,4},{6,7},{7,6},{8,9},{9,8},{10,11... | collective-permute-start | bytes 7077896 | tf_op jit(solution)/shard_map/ppermute | solution.py:302
  4.7 13.3 %collective-permute-start.10 = (bf16[2,256,128]{2,1,0:T(8,128)(2,1)S(1)}, bf16[2,256,128]{2,1,0:T(8,128)(2,1)S(1)}, u32[]{:S(2)}, u32[]{:S(2)}) collective-permute-start(bf16[2,256,128]{2,1,0:T(8,128)(2,1)S(1)} %maximum_select_fusion.2.refs_0_), channel_id=1, source_target_pairs={{0,6},{1,7},{2,4},{3,5},{4,2},{5,3},{6,0},{7,1},{8,14},{9,15},{10,... | collective-permute-start | bytes 393224 | tf_op jit(solution)/shard_map/ppermute | solution.py:311
  9.7 11.5 %collective-permute-start.9 = (bf16[2,256,128]{2,1,0:T(8,128)(2,1)S(1)}, bf16[2,256,128]{2,1,0:T(8,128)(2,1)S(1)}, u32[]{:S(2)}, u32[]{:S(2)}) collective-permute-start(bf16[2,256,128]{2,1,0:T(8,128)(2,1)S(1)} %maximum_select_fusion.2.refs_0_), channel_id=1, source_target_pairs={{0,4},{1,5},{2,6},{3,7},{4,0},{5,1},{6,2},{7,3},{8,12},{9,13},{10,... | collective-permute-start | bytes 393224 | tf_op jit(solution)/shard_map/ppermute | solution.py:311
  15.7 8.7 %collective-permute-start.8 = (bf16[2,256,128]{2,1,0:T(8,128)(2,1)S(1)}, bf16[2,256,128]{2,1,0:T(8,128)(2,1)S(1)}, u32[]{:S(2)}, u32[]{:S(2)}) collective-permute-start(bf16[2,256,128]{2,1,0:T(8,128)(2,1)S(1)} %maximum_select_fusion.2.refs_0_), channel_id=1, source_target_pairs={{0,2},{1,3},{2,0},{3,1},{4,6},{5,7},{6,4},{7,5},{8,10},{9,11},{10,... | collective-permute-start | bytes 393224 | tf_op jit(solution)/shard_map/ppermute | solution.py:311
  18.1 11.1 %collective-permute-start.4 = (bf16[3,256,128]{2,1,0:T(8,128)(2,1)S(1)}, bf16[3,256,128]{2,1,0:T(8,128)(2,1)S(1)}, u32[]{:S(2)}, u32[]{:S(2)}) collective-permute-start(bf16[3,256,128]{2,1,0:T(8,128)(2,1)S(1)} %maximum_select_fusion.1.refs_0_), channel_id=1, source_target_pairs={{0,6},{1,7},{2,4},{3,5},{4,2},{5,3},{6,0},{7,1},{8,14},{9,15},{10,... | collective-permute-start | bytes 589832 | tf_op jit(solution)/shard_map/ppermute | solution.py:311
  21.2 17.1 %collective-permute-start.3 = (bf16[3,256,128]{2,1,0:T(8,128)(2,1)S(1)}, bf16[3,256,128]{2,1,0:T(8,128)(2,1)S(1)}, u32[]{:S(2)}, u32[]{:S(2)}) collective-permute-start(bf16[3,256,128]{2,1,0:T(8,128)(2,1)S(1)} %maximum_select_fusion.1.refs_0_), channel_id=1, source_target_pairs={{0,4},{1,5},{2,6},{3,7},{4,0},{5,1},{6,2},{7,3},{8,12},{9,13},{10,... | collective-permute-start | bytes 589832 | tf_op jit(solution)/shard_map/ppermute | solution.py:311
  24.5 15.3 %collective-permute-start.2 = (bf16[3,256,128]{2,1,0:T(8,128)(2,1)S(1)}, bf16[3,256,128]{2,1,0:T(8,128)(2,1)S(1)}, u32[]{:S(2)}, u32[]{:S(2)}) collective-permute-start(bf16[3,256,128]{2,1,0:T(8,128)(2,1)S(1)} %maximum_select_fusion.1.refs_0_), channel_id=1, source_target_pairs={{0,2},{1,3},{2,0},{3,1},{4,6},{5,7},{6,4},{7,5},{8,10},{9,11},{10,... | collective-permute-start | bytes 589832 | tf_op jit(solution)/shard_map/ppermute | solution.py:311
  29.2 18.8 %collective-permute-start.14 = (bf16[2,4,64,128]{3,2,1,0:T(8,128)(2,1)S(1)}, bf16[2,4,64,128]{3,2,1,0:T(8,128)(2,1)S(1)}, u32[]{:S(2)}, u32[]{:S(2)}) collective-permute-start(bf16[2,4,64,128]{3,2,1,0:T(8,128)(2,1)S(1)} %get-tuple-element.74), channel_id=1, source_target_pairs={{0,24},{8,16},{16,8},{24,0},{1,25},{9,17},{17,9},{25,1},{2,26},{10... | collective-permute-start | bytes 393224 | tf_op jit(solution)/shard_map/ppermute | solution.py:316
  38.3 9.7 %collective-permute-start.13 = (bf16[2,4,64,128]{3,2,1,0:T(8,128)(2,1)S(1)}, bf16[2,4,64,128]{3,2,1,0:T(8,128)(2,1)S(1)}, u32[]{:S(2)}, u32[]{:S(2)}) collective-permute-start(bf16[2,4,64,128]{3,2,1,0:T(8,128)(2,1)S(1)} %get-tuple-element.75), channel_id=1, source_target_pairs={{0,8},{8,0},{16,24},{24,16},{1,9},{9,1},{17,25},{25,17},{2,10},{10... | collective-permute-start | bytes 393224 | tf_op jit(solution)/shard_map/ppermute | solution.py:315
  39.9 16.4 %collective-permute-start.6 = (bf16[3,4,64,128]{3,2,1,0:T(8,128)(2,1)S(1)}, bf16[3,4,64,128]{3,2,1,0:T(8,128)(2,1)S(1)}, u32[]{:S(2)}, u32[]{:S(2)}) collective-permute-start(bf16[3,4,64,128]{3,2,1,0:T(8,128)(2,1)S(1)} %get-tuple-element.72), channel_id=1, source_target_pairs={{0,24},{8,16},{16,8},{24,0},{1,25},{9,17},{17,9},{25,1},{2,26},{10... | collective-permute-start | bytes 589832 | tf_op jit(solution)/shard_map/ppermute | solution.py:316
  41.4 14.9 %collective-permute-start.5 = (bf16[3,4,64,128]{3,2,1,0:T(8,128)(2,1)S(1)}, bf16[3,4,64,128]{3,2,1,0:T(8,128)(2,1)S(1)}, u32[]{:S(2)}, u32[]{:S(2)}) collective-permute-start(bf16[3,4,64,128]{3,2,1,0:T(8,128)(2,1)S(1)} %get-tuple-element.73), channel_id=1, source_target_pairs={{0,8},{8,0},{16,24},{24,16},{1,9},{9,1},{17,25},{25,17},{2,10},{10... | collective-permute-start | bytes 589832 | tf_op jit(solution)/shard_map/ppermute | solution.py:315
  51.8 14.9 %collective-permute-start.18 = (bf16[1,256,128]{2,1,0:T(8,128)(2,1)S(1)}, bf16[1,256,128]{2,1,0:T(8,128)(2,1)S(1)}, u32[]{:S(2)}, u32[]{:S(2)}) collective-permute-start(bf16[1,256,128]{2,1,0:T(8,128)(2,1)S(1)} %get-tuple-element.48.refs_0_), channel_id=1, source_target_pairs={{0,6},{1,7},{2,4},{3,5},{4,2},{5,3},{6,0},{7,1},{8,14},{9,15},{10,... | collective-permute-start | bytes 196616 | tf_op jit(solution)/shard_map/ppermute | solution.py:311
  54.6 12.1 %collective-permute-start.17 = (bf16[1,256,128]{2,1,0:T(8,128)(2,1)S(1)}, bf16[1,256,128]{2,1,0:T(8,128)(2,1)S(1)}, u32[]{:S(2)}, u32[]{:S(2)}) collective-permute-start(bf16[1,256,128]{2,1,0:T(8,128)(2,1)S(1)} %get-tuple-element.48.refs_0_), channel_id=1, source_target_pairs={{0,4},{1,5},{2,6},{3,7},{4,0},{5,1},{6,2},{7,3},{8,12},{9,13},{10,... | collective-permute-start | bytes 196616 | tf_op jit(solution)/shard_map/ppermute | solution.py:311
  54.6 12.1 %collective-permute-start.16 = (bf16[1,256,128]{2,1,0:T(8,128)(2,1)S(1)}, bf16[1,256,128]{2,1,0:T(8,128)(2,1)S(1)}, u32[]{:S(2)}, u32[]{:S(2)}) collective-permute-start(bf16[1,256,128]{2,1,0:T(8,128)(2,1)S(1)} %get-tuple-element.48.refs_0_), channel_id=1, source_target_pairs={{0,2},{1,3},{2,0},{3,1},{4,6},{5,7},{6,4},{7,5},{8,10},{9,11},{10,... | collective-permute-start | bytes 196616 | tf_op jit(solution)/shard_map/ppermute | solution.py:311
  66.8 5.2 %collective-permute-start.20 = (bf16[1,4,64,128]{3,2,1,0:T(8,128)(2,1)S(1)}, bf16[1,4,64,128]{3,2,1,0:T(8,128)(2,1)S(1)}, u32[]{:S(2)}, u32[]{:S(2)}) collective-permute-start(bf16[1,4,64,128]{3,2,1,0:T(8,128)(2,1)S(1)} %get-tuple-element.94), channel_id=1, source_target_pairs={{0,24},{8,16},{16,8},{24,0},{1,25},{9,17},{17,9},{25,1},{2,26},{10... | collective-permute-start | bytes 196616 | tf_op jit(solution)/shard_map/ppermute | solution.py:316
  67.3 4.7 %collective-permute-start.19 = (bf16[1,4,64,128]{3,2,1,0:T(8,128)(2,1)S(1)}, bf16[1,4,64,128]{3,2,1,0:T(8,128)(2,1)S(1)}, u32[]{:S(2)}, u32[]{:S(2)}) collective-permute-start(bf16[1,4,64,128]{3,2,1,0:T(8,128)(2,1)S(1)} %get-tuple-element.95), channel_id=1, source_target_pairs={{0,8},{8,0},{16,24},{24,16},{1,9},{9,1},{17,25},{25,17},{2,10},{10... | collective-permute-start | bytes 196616 | tf_op jit(solution)/shard_map/ppermute | solution.py:315
  76.0 6.1 %collective-permute-start.23 = (bf16[1,256,128]{2,1,0:T(8,128)(2,1)S(1)}, bf16[1,256,128]{2,1,0:T(8,128)(2,1)S(1)}, u32[]{:S(2)}, u32[]{:S(2)}) collective-permute-start(bf16[1,256,128]{2,1,0:T(8,128)(2,1)S(1)} %get-tuple-element.51.refs_0_), channel_id=1, source_target_pairs={{0,6},{1,7},{2,4},{3,5},{4,2},{5,3},{6,0},{7,1},{8,14},{9,15},{10,... | collective-permute-start | bytes 196616 | tf_op jit(solution)/shard_map/ppermute | solution.py:311
  78.8 5.2 %collective-permute-start.22 = (bf16[1,256,128]{2,1,0:T(8,128)(2,1)S(1)}, bf16[1,256,128]{2,1,0:T(8,128)(2,1)S(1)}, u32[]{:S(2)}, u32[]{:S(2)}) collective-permute-start(bf16[1,256,128]{2,1,0:T(8,128)(2,1)S(1)} %get-tuple-element.51.refs_0_), channel_id=1, source_target_pairs={{0,4},{1,5},{2,6},{3,7},{4,0},{5,1},{6,2},{7,3},{8,12},{9,13},{10,... | collective-permute-start | bytes 196616 | tf_op jit(solution)/shard_map/ppermute | solution.py:311
  78.8 5.2 %collective-permute-start.21 = (bf16[1,256,128]{2,1,0:T(8,128)(2,1)S(1)}, bf16[1,256,128]{2,1,0:T(8,128)(2,1)S(1)}, u32[]{:S(2)}, u32[]{:S(2)}) collective-permute-start(bf16[1,256,128]{2,1,0:T(8,128)(2,1)S(1)} %get-tuple-element.51.refs_0_), channel_id=1, source_target_pairs={{0,2},{1,3},{2,0},{3,1},{4,6},{5,7},{6,4},{7,5},{8,10},{9,11},{10,... | collective-permute-start | bytes 196616 | tf_op jit(solution)/shard_map/ppermute | solution.py:311
  84.0 5.2 %collective-permute-start.25 = (bf16[1,4,64,128]{3,2,1,0:T(8,128)(2,1)S(1)}, bf16[1,4,64,128]{3,2,1,0:T(8,128)(2,1)S(1)}, u32[]{:S(2)}, u32[]{:S(2)}) collective-permute-start(bf16[1,4,64,128]{3,2,1,0:T(8,128)(2,1)S(1)} %get-tuple-element.92), channel_id=1, source_target_pairs={{0,24},{8,16},{16,8},{24,0},{1,25},{9,17},{17,9},{25,1},{2,26},{10... | collective-permute-start | bytes 196616 | tf_op jit(solution)/shard_map/ppermute | solution.py:316
  86.1 4.3 %collective-permute-start.24 = (bf16[1,4,64,128]{3,2,1,0:T(8,128)(2,1)S(1)}, bf16[1,4,64,128]{3,2,1,0:T(8,128)(2,1)S(1)}, u32[]{:S(2)}, u32[]{:S(2)}) collective-permute-start(bf16[1,4,64,128]{3,2,1,0:T(8,128)(2,1)S(1)} %get-tuple-element.93), channel_id=1, source_target_pairs={{0,8},{8,0},{16,24},{24,16},{1,9},{9,1},{17,25},{25,17},{2,10},{10... | collective-permute-start | bytes 196616 | tf_op jit(solution)/shard_map/ppermute | solution.py:315
  91.6 6.1 %collective-permute-start.28 = (bf16[1,256,128]{2,1,0:T(8,128)(2,1)S(1)}, bf16[1,256,128]{2,1,0:T(8,128)(2,1)S(1)}, u32[]{:S(2)}, u32[]{:S(2)}) collective-permute-start(bf16[1,256,128]{2,1,0:T(8,128)(2,1)S(1)} %get-tuple-element.54.refs_0_), channel_id=1, source_target_pairs={{0,6},{1,7},{2,4},{3,5},{4,2},{5,3},{6,0},{7,1},{8,14},{9,15},{10,... | collective-permute-start | bytes 196616 | tf_op jit(solution)/shard_map/ppermute | solution.py:311
  93.9 5.6 %collective-permute-start.27 = (bf16[1,256,128]{2,1,0:T(8,128)(2,1)S(1)}, bf16[1,256,128]{2,1,0:T(8,128)(2,1)S(1)}, u32[]{:S(2)}, u32[]{:S(2)}) collective-permute-start(bf16[1,256,128]{2,1,0:T(8,128)(2,1)S(1)} %get-tuple-element.54.refs_0_), channel_id=1, source_target_pairs={{0,4},{1,5},{2,6},{3,7},{4,0},{5,1},{6,2},{7,3},{8,12},{9,13},{10,... | collective-permute-start | bytes 196616 | tf_op jit(solution)/shard_map/ppermute | solution.py:311
  93.9 5.6 %collective-permute-start.26 = (bf16[1,256,128]{2,1,0:T(8,128)(2,1)S(1)}, bf16[1,256,128]{2,1,0:T(8,128)(2,1)S(1)}, u32[]{:S(2)}, u32[]{:S(2)}) collective-permute-start(bf16[1,256,128]{2,1,0:T(8,128)(2,1)S(1)} %get-tuple-element.54.refs_0_), channel_id=1, source_target_pairs={{0,2},{1,3},{2,0},{3,1},{4,6},{5,7},{6,4},{7,5},{8,10},{9,11},{10,... | collective-permute-start | bytes 196616 | tf_op jit(solution)/shard_map/ppermute | solution.py:311
  99.6 5.2 %collective-permute-start.30 = (bf16[1,4,64,128]{3,2,1,0:T(8,128)(2,1)S(1)}, bf16[1,4,64,128]{3,2,1,0:T(8,128)(2,1)S(1)}, u32[]{:S(2)}, u32[]{:S(2)}) collective-permute-start(bf16[1,4,64,128]{3,2,1,0:T(8,128)(2,1)S(1)} %get-tuple-element.90), channel_id=1, source_target_pairs={{0,24},{8,16},{16,8},{24,0},{1,25},{9,17},{17,9},{25,1},{2,26},{10... | collective-permute-start | bytes 196616 | tf_op jit(solution)/shard_map/ppermute | solution.py:316
  100.5 4.3 %collective-permute-start.29 = (bf16[1,4,64,128]{3,2,1,0:T(8,128)(2,1)S(1)}, bf16[1,4,64,128]{3,2,1,0:T(8,128)(2,1)S(1)}, u32[]{:S(2)}, u32[]{:S(2)}) collective-permute-start(bf16[1,4,64,128]{3,2,1,0:T(8,128)(2,1)S(1)} %get-tuple-element.91), channel_id=1, source_target_pairs={{0,8},{8,0},{16,24},{24,16},{1,9},{9,1},{17,25},{25,17},{2,10},{10... | collective-permute-start | bytes 196616 | tf_op jit(solution)/shard_map/ppermute | solution.py:315
  106.1 4.0 %collective-permute-start.31 = (bf16[128,128]{1,0:T(8,128)(2,1)S(1)}, bf16[128,128]{1,0:T(8,128)(2,1)S(1)}, u32[]{:S(2)}, u32[]{:S(2)}) collective-permute-start(bf16[128,128]{1,0:T(8,128)(2,1)S(1)} %bitcast.194), channel_id=1, source_target_pairs={{0,2},{1,3},{2,0},{3,1},{4,6},{5,7},{6,4},{7,5},{8,10},{9,11},{10,... | collective-permute-start | bytes 98312 | tf_op jit(solution)/shard_map/ppermute | solution.py:398
  107.0 5.8 %collective-permute-start.33 = (bf16[128,128]{1,0:T(8,128)(2,1)S(1)}, bf16[128,128]{1,0:T(8,128)(2,1)S(1)}, u32[]{:S(2)}, u32[]{:S(2)}) collective-permute-start(bf16[128,128]{1,0:T(8,128)(2,1)S(1)} %bitcast.193), channel_id=1, source_target_pairs={{0,6},{1,7},{2,4},{3,5},{4,2},{5,3},{6,0},{7,1},{8,14},{9,15},{10,... | collective-permute-start | bytes 98312 | tf_op jit(solution)/shard_map/ppermute | solution.py:398
  109.5 4.8 %collective-permute-start.32 = (bf16[128,128]{1,0:T(8,128)(2,1)S(1)}, bf16[128,128]{1,0:T(8,128)(2,1)S(1)}, u32[]{:S(2)}, u32[]{:S(2)}) collective-permute-start(bf16[128,128]{1,0:T(8,128)(2,1)S(1)} %bitcast.192), channel_id=1, source_target_pairs={{0,4},{1,5},{2,6},{3,7},{4,0},{5,1},{6,2},{7,3},{8,12},{9,13},{10,... | collective-permute-start | bytes 98312 | tf_op jit(solution)/shard_map/ppermute | solution.py:398
  114.4 7.7 %collective-permute-start.35 = (bf16[1,4,64,128]{3,2,1,0:T(8,128)(2,1)S(1)}, bf16[1,4,64,128]{3,2,1,0:T(8,128)(2,1)S(1)}, u32[]{:S(2)}, u32[]{:S(2)}) collective-permute-start(bf16[1,4,64,128]{3,2,1,0:T(8,128)(2,1)S(1)} %get-tuple-element.88), channel_id=1, source_target_pairs={{0,24},{8,16},{16,8},{24,0},{1,25},{9,17},{17,9},{25,1},{2,26},{10... | collective-permute-start | bytes 196616 | tf_op jit(solution)/shard_map/ppermute | solution.py:316
  116.5 5.6 %collective-permute-start.34 = (bf16[1,4,64,128]{3,2,1,0:T(8,128)(2,1)S(1)}, bf16[1,4,64,128]{3,2,1,0:T(8,128)(2,1)S(1)}, u32[]{:S(2)}, u32[]{:S(2)}) collective-permute-start(bf16[1,4,64,128]{3,2,1,0:T(8,128)(2,1)S(1)} %get-tuple-element.89), channel_id=1, source_target_pairs={{0,8},{8,0},{16,24},{24,16},{1,9},{9,1},{17,25},{25,17},{2,10},{10... | collective-permute-start | bytes 196616 | tf_op jit(solution)/shard_map/ppermute | solution.py:315
  (10 other events, 83.3 us)

commit v5 on v3

--- a/solution.py
+++ b/solution.py
@@ -238,7 +238,7 @@
     cell_shape = (count, share) if turn_out else (share, count)
     operands = []
     for edges, _, weight in sides:
-        operands += [edges[0], edges[1], weight]
+        operands += [*edges, weight]
     operands += [total, *cells]
     return pl.pallas_call(
         functools.partial(gate_kernel, cols, [index for _, index, _ in sides], turn_in, turn_out),
@@ -310,10 +310,6 @@
         other = lax.dynamic_index_in_dim(value, 1 - core, axis, keepdims=False, allow_negative_indices=False)
         return mine, swap(other)
 
-    def joined(value, axis):
-        mine, other = own_batch(value, axis)
-        return jnp.where(core == 0, jnp.concatenate([mine, other], -1), jnp.concatenate([other, mine], -1))
-
     def gathered(value):
         return [value] + [
             lax.ppermute(value, "hid", [(i, i ^ (2 * k)) for i in range(2 * groups)]) for k in range(1, groups)
@@ -336,13 +332,13 @@
     def ordered(mine, other, axis):
         return jnp.where(core == 0, jnp.concatenate([mine, other], axis), jnp.concatenate([other, mine], axis))
 
+    def frames_of(index, first):
+        size = (steps - 1 if first else 1, 1) + frames.shape[2:]
+        return lax.dynamic_slice(frames, (first, index, 0, 0, 0), size, allow_negative_indices=False)[:, 0]
+
     def of_batch(index):
-        return jnp.stack(
-            [
-                lax.dynamic_index_in_dim(frames[0], index, 0, keepdims=False, allow_negative_indices=False),
-                lax.dynamic_index_in_dim(hidden_start, index, 0, keepdims=False, allow_negative_indices=False),
-            ]
-        )
+        state = lax.dynamic_slice_in_dim(hidden_start, index, 1, 0, allow_negative_indices=False)
+        return jnp.concatenate([frames_of(index, 0), state], 0)
 
     lead = ordered(of_batch(core), swap(of_batch(1 - core)), -1).reshape(2, count, width)
     inner = cols // groups
@@ -366,16 +362,17 @@
     )
     lead_parts = gathered(lead)
     input_pair, hidden_pair = swap(input_own), swap(hidden_own)
-    first_weight, second_weight = stage_call(first_weight), stage_call(second_weight)
     input_both = stage_call(input_own, input_pair)
     hidden_both = stage_call(hidden_own, hidden_pair)
-    rest = joined(frames[1:], 1).reshape(steps - 1, count, width)
+    first_weight = stage_call(first_weight)
+    second_weight = stage_call(second_weight)
+    rest = ordered(frames_of(core, 1), swap(frames_of(1 - core, 1)), -1).reshape(steps - 1, count, width)
     cell_mine, cell_other = own_batch(cell_start, 0)
     cells = [cell_mine.reshape(count, share), cell_other.reshape(count, share)]
     bias_own = gate_bias.reshape(-1)
     bias = jnp.concatenate([bias_own, swap(bias_own)]).reshape(1, -1)
 
-    lead_parts, rest, cells, bias = lax.optimization_barrier((lead_parts, rest, cells, bias))
+    lead_parts, cells, bias = lax.optimization_barrier((lead_parts, cells, bias))
     lead_edges = edges_of(lead_parts)
     rest_parts = gathered(rest)
     rest_edges = edges_of(rest_parts)
@@ -404,7 +401,8 @@
         return piece.reshape(rows * tile, width)
 
     tiles = [columns_for(0)] + [
-        lax.ppermute(columns_for(k), "hid", [(i, i ^ (2 * k)) for i in range(2 * groups)]) for k in range(1, groups)
+        lax.ppermute(columns_for(k), "hid", [(i, i ^ (2 * k)) for i in range(2 * groups)])
+        for k in range(1, groups)
     ]
     rim = 2 * tile
     tile_edges = swapped_edges(

time: 134 us -> 129 us (0.963)
  waiting for transfers between devices: 43.9 us -> 26.4 us
  starting transfers between devices: 48.2 us -> 60.5 us
    ppermute x15, waiting for transfers between devices: 30.1 us -> 15.1 us  [gathered(): lax.ppermute(value, 'hid', [(i, i ^ 2 * k) for i in range(2 * groups)])]
    ppermute x15, starting transfers between devices: 23.3 us -> 35.6 us  [gathered(): lax.ppermute(value, 'hid', [(i, i ^ 2 * k) for i in range(2 * groups)])]
    ppermute x8, waiting for transfers between devices: 5.39 us -> 2.96 us  [swap(): return lax.ppermute(value, 'hid', pairs)]
    slice x2 -> x0, local copies, waits for them, and re-layouts: 1.94 us -> none  [the longest x1 1.02 us: program(): rest = joined(frames[1:], 1).reshape(steps - 1, count, width)]
    dynamic_slice x3, local copies, waits for them, and re-layouts: 0.94 us -> 2.82 us  [the longest x2 1.94 us: frames_of(): lax.dynamic_slice(frames, (first, index, 0, 0, 0), size, allow_negative_i...]
  transfers between devices with their start and end apart: 38 -> 38, of which waited for: 15 -> 14; matrix products, arithmetic and copies ran while one was open for 3% -> 3% of each run, Pallas kernels for 21% -> 21%
where the time goes in v5:
time: 129 us
  starting transfers between devices  60.5 us (47%)
  Pallas kernels  32.3 us (25%)
  waiting for transfers between devices  26.4 us (20%)
  local copies, waits for them, and re-layouts  6.21 us (5%)
  other arithmetic  1.96 us (2%)
    ppermute x15, starting transfers between devices, gathered(): lax.ppermute(value, 'hid', [(i, i ^ 2 * k) for i in range(2 * groups)])  35.6 us
    ppermute x15, waiting for transfers between devices, gathered(): lax.ppermute(value, 'hid', [(i, i ^ 2 * k) for i in range(2 * groups)])  15.1 us
    pallas_call x8, Pallas kernels, conv_call(): pl.pallas_call(functools.partial(conv_kernel, groups, cols, index, edges...  13.7 us
    ppermute x6, starting transfers between devices, swapped_edges(): second = lax.ppermute(jnp.where(even, top, bottom), 'patch', outer_pairs)  11.3 us
    pallas_call x4, Pallas kernels, stage_call(): pl.pallas_call(stage_kernel, in_specs=[pl.BlockSpec(memory_space=pltpu.HB...  9.66 us
    pallas_call x4, Pallas kernels, gate_call(): pl.pallas_call(functools.partial(gate_kernel, cols, [index for _, index,...  6.81 us
    ppermute x6, starting transfers between devices, swapped_edges(): first = lax.ppermute(jnp.where(even, bottom, top), 'patch', inner_pairs)  6.47 us
    ppermute x6, waiting for transfers between devices, swapped_edges(): second = lax.ppermute(jnp.where(even, top, bottom), 'patch', outer_pairs)  4.51 us
  transfers between devices with their start and end apart: 38, of which 14 were waited for; matrix products, arithmetic and copies ran while one was open for 3% of the time, Pallas kernels for 21%

profile of v5, /device:TPU:0, one launch (start us, length us, event | category | flops | bytes accessed | tf_op | source)
XLA Modules:
  0.0 128.6 jit_solution(3968133411758916274)
XLA Ops:
  4.7 2.9 %collective-permute-start.8 = (bf16[2,256,128]{2,1,0:T(8,128)(2,1)S(1)}, bf16[2,256,128]{2,1,0:T(8,128)(2,1)S(1)}, u32[]{:S(2)}, u32[]{:S(2)}) collective-permute-start(bf16[2,256,128]{2,1,0:T(8,128)(2,1)S(1)} %maximum_select_fusion.2.refs_0_), channel_id=1, source_target_pairs={{0,2},{1,3},{2,0},{3,1},{4,6},{5,7},{6,4},{7,5},{8,10},{9,11},{10,... | collective-permute-start | bytes 393224 | tf_op jit(solution)/shard_map/ppermute | solution.py:315
  7.6 2.6 %collective-permute-start.9 = (bf16[2,256,128]{2,1,0:T(8,128)(2,1)S(1)}, bf16[2,256,128]{2,1,0:T(8,128)(2,1)S(1)}, u32[]{:S(2)}, u32[]{:S(2)}) collective-permute-start(bf16[2,256,128]{2,1,0:T(8,128)(2,1)S(1)} %maximum_select_fusion.2.refs_0_), channel_id=1, source_target_pairs={{0,4},{1,5},{2,6},{3,7},{4,0},{5,1},{6,2},{7,3},{8,12},{9,13},{10,... | collective-permute-start | bytes 393224 | tf_op jit(solution)/shard_map/ppermute | solution.py:315
  16.1 4.0 %collective-permute-start.10 = (bf16[2,256,128]{2,1,0:T(8,128)(2,1)S(1)}, bf16[2,256,128]{2,1,0:T(8,128)(2,1)S(1)}, u32[]{:S(2)}, u32[]{:S(2)}) collective-permute-start(bf16[2,256,128]{2,1,0:T(8,128)(2,1)S(1)} %maximum_select_fusion.2.refs_0_), channel_id=1, source_target_pairs={{0,6},{1,7},{2,4},{3,5},{4,2},{5,3},{6,0},{7,1},{8,14},{9,15},{10,... | collective-permute-start | bytes 393224 | tf_op jit(solution)/shard_map/ppermute | solution.py:315
  21.2 2.8 %collective-permute-done.10.refs_3_ = bf16[2,256,128]{2,1,0:T(8,128)(2,1)S(1)} collective-permute-done((bf16[2,256,128]{2,1,0:T(8,128)(2,1)S(1)}, bf16[2,256,128]{2,1,0:T(8,128)(2,1)S(1)}, u32[]{:S(2)}, u32[]{:S(2)}) %collective-permute-start.10) | collective-permute-done | bytes 131104 | tf_op jit(solution)/shard_map/ppermute | solution.py:315
  24.0 11.6 %collective-permute-start.2 = (bf16[3,256,128]{2,1,0:T(8,128)(2,1)S(1)}, bf16[3,256,128]{2,1,0:T(8,128)(2,1)S(1)}, u32[]{:S(2)}, u32[]{:S(2)}) collective-permute-start(bf16[3,256,128]{2,1,0:T(8,128)(2,1)S(1)} %maximum_select_fusion.1.refs_0_), channel_id=1, source_target_pairs={{0,2},{1,3},{2,0},{3,1},{4,6},{5,7},{6,4},{7,5},{8,10},{9,11},{10,... | collective-permute-start | bytes 589832 | tf_op jit(solution)/shard_map/ppermute | solution.py:315
  37.3 5.5 %collective-permute-done.3.refs_2_ = bf16[3,256,128]{2,1,0:T(8,128)(2,1)S(1)} collective-permute-done((bf16[3,256,128]{2,1,0:T(8,128)(2,1)S(1)}, bf16[3,256,128]{2,1,0:T(8,128)(2,1)S(1)}, u32[]{:S(2)}, u32[]{:S(2)}) %collective-permute-start.3) | collective-permute-done | bytes 196640 | tf_op jit(solution)/shard_map/ppermute | solution.py:315
  42.8 2.4 %collective-permute-start.14 = (bf16[2,4,64,128]{3,2,1,0:T(8,128)(2,1)S(1)}, bf16[2,4,64,128]{3,2,1,0:T(8,128)(2,1)S(1)}, u32[]{:S(2)}, u32[]{:S(2)}) collective-permute-start(bf16[2,4,64,128]{3,2,1,0:T(8,128)(2,1)S(1)} %get-tuple-element.74), channel_id=1, source_target_pairs={{0,24},{8,16},{16,8},{24,0},{1,25},{9,17},{17,9},{25,1},{2,26},{10... | collective-permute-start | bytes 393224 | tf_op jit(solution)/shard_map/ppermute | solution.py:320
  47.4 2.4 %shard_map.113.refs_4_.refs_2_.refs_6_ = bf16[3,3,2,256,512]{4,3,2,1,0:T(8,128)(2,1)S(1)} custom-call(bf16[3,3,256,512]{3,2,1,0:T(8,128)(2,1)} %bitcast.169, bf16[3,3,256,512]{3,2,1,0:T(8,128)(2,1)} %collective-permute-done.7.refs_1_), custom_call_target="tpu_custom_call" | custom-call | flops 471859200 | bytes 4718592 | tf_op jit(solution)/shard_map/pallas_call | solution.py:205
  49.8 1.7 %shard_map.115.refs_5_ = f32[512,256]{1,0:T(8,128)S(1)} custom-call(bf16[2,256,128]{2,1,0:T(8,128)(2,1)S(1)} %maximum_select_fusion.2.refs_0_, bf16[2,256,128]{2,1,0:T(8,128)(2,1)S(1)} %collective-permute-done.8.refs_1_, bf16[2,256,128]{2,1,0:T(8,128)(2,1)S(1)} %collective-permute-done.9.refs_2_, bf16[2,256,128]{2,1,0:T(8,128)(2,1)S(1)} %collective-permute-done.10.refs_3_, ...), custom_call_target="tpu_custom_call" | custom-call | flops 1207959552 | bytes 4718592 | tf_op jit(solution)/shard_map/pallas_call | solution.py:222
  52.9 2.4 %shard_map.114.refs_4_.refs_5_.refs_2_ = bf16[3,3,2,256,512]{4,3,2,1,0:T(8,128)(2,1)S(1)} custom-call(bf16[3,3,256,512]{3,2,1,0:T(8,128)(2,1)} %bitcast.171, bf16[3,3,256,512]{3,2,1,0:T(8,128)(2,1)} %copy-done.2), custom_call_target="tpu_custom_call" | custom-call | flops 471859200 | bytes 4718592 | tf_op jit(solution)/shard_map/pallas_call | solution.py:205
  57.1 2.1 %shard_map.117 = (bf16[1,256,128]{2,1,0:T(8,128)(2,1)S(1)}, f32[64,256]{1,0:T(8,128)S(1)}, f32[64,256]{1,0:T(8,128)S(1)}) custom-call(bf16[2,4,64,128]{3,2,1,0:T(8,128)(2,1)S(1)} %collective-permute-done.13.refs_0_.refs_3_, bf16[2,4,64,128]{3,2,1,0:T(8,128)(2,1)S(1)} %collective-permute-done.14.refs_1_.refs_4_, ...), custom_call_target="tpu_custom_call" | custom-call | flops 805306368 | bytes 3145728 | tf_op jit(solution)/shard_map/pallas_call | solution.py:243
  59.2 2.5 %collective-permute-start.18 = (bf16[1,256,128]{2,1,0:T(8,128)(2,1)S(1)}, bf16[1,256,128]{2,1,0:T(8,128)(2,1)S(1)}, u32[]{:S(2)}, u32[]{:S(2)}) collective-permute-start(bf16[1,256,128]{2,1,0:T(8,128)(2,1)S(1)} %get-tuple-element.48.refs_0_), channel_id=1, source_target_pairs={{0,6},{1,7},{2,4},{3,5},{4,2},{5,3},{6,0},{7,1},{8,14},{9,15},{10,... | collective-permute-start | bytes 196616 | tf_op jit(solution)/shard_map/ppermute | solution.py:315
  61.8 1.9 %collective-permute-start.16 = (bf16[1,256,128]{2,1,0:T(8,128)(2,1)S(1)}, bf16[1,256,128]{2,1,0:T(8,128)(2,1)S(1)}, u32[]{:S(2)}, u32[]{:S(2)}) collective-permute-start(bf16[1,256,128]{2,1,0:T(8,128)(2,1)S(1)} %get-tuple-element.48.refs_0_), channel_id=1, source_target_pairs={{0,2},{1,3},{2,0},{3,1},{4,6},{5,7},{6,4},{7,5},{8,10},{9,11},{10,... | collective-permute-start | bytes 196616 | tf_op jit(solution)/shard_map/ppermute | solution.py:315
  63.7 1.7 %shard_map.118.refs_5_ = f32[512,256]{1,0:T(8,128)S(1)} custom-call(bf16[3,256,128]{2,1,0:T(8,128)(2,1)S(1)} %maximum_select_fusion.1.refs_0_, bf16[3,256,128]{2,1,0:T(8,128)(2,1)S(1)} %collective-permute-done.2.refs_1_, bf16[3,256,128]{2,1,0:T(8,128)(2,1)S(1)} %collective-permute-done.3.refs_2_, bf16[3,256,128]{2,1,0:T(8,128)(2,1)S(1)} %collective-permute-done.4.refs_3_, ...), custom_call_target="tpu_custom_call" | custom-call | flops 1207959552 | bytes 4718592 | tf_op jit(solution)/shard_map/pallas_call | solution.py:222
  65.4 1.8 %shard_map.121.refs_5_ = f32[512,256]{1,0:T(8,128)S(1)} custom-call(bf16[3,256,128]{2,1,0:T(8,128)(2,1)S(1)} %maximum_select_fusion.1.refs_0_, bf16[3,256,128]{2,1,0:T(8,128)(2,1)S(1)} %collective-permute-done.2.refs_1_, bf16[3,256,128]{2,1,0:T(8,128)(2,1)S(1)} %collective-permute-done.3.refs_2_, bf16[3,256,128]{2,1,0:T(8,128)(2,1)S(1)} %collective-permute-done.4.refs_3_, ...), custom_call_target="tpu_custom_call" | custom-call | flops 1207959552 | bytes 4718592 | tf_op jit(solution)/shard_map/pallas_call | solution.py:222
  67.2 1.8 %shard_map.124.refs_5_ = f32[512,256]{1,0:T(8,128)S(1)} custom-call(bf16[3,256,128]{2,1,0:T(8,128)(2,1)S(1)} %maximum_select_fusion.1.refs_0_, bf16[3,256,128]{2,1,0:T(8,128)(2,1)S(1)} %collective-permute-done.2.refs_1_, bf16[3,256,128]{2,1,0:T(8,128)(2,1)S(1)} %collective-permute-done.3.refs_2_, bf16[3,256,128]{2,1,0:T(8,128)(2,1)S(1)} %collective-permute-done.4.refs_3_, ...), custom_call_target="tpu_custom_call" | custom-call | flops 1207959552 | bytes 4718592 | tf_op jit(solution)/shard_map/pallas_call | solution.py:222
  70.0 2.2 %collective-permute-start.20 = (bf16[1,4,64,128]{3,2,1,0:T(8,128)(2,1)S(1)}, bf16[1,4,64,128]{3,2,1,0:T(8,128)(2,1)S(1)}, u32[]{:S(2)}, u32[]{:S(2)}) collective-permute-start(bf16[1,4,64,128]{3,2,1,0:T(8,128)(2,1)S(1)} %get-tuple-element.94), channel_id=1, source_target_pairs={{0,24},{8,16},{16,8},{24,0},{1,25},{9,17},{17,9},{25,1},{2,26},{10... | collective-permute-start | bytes 196616 | tf_op jit(solution)/shard_map/ppermute | solution.py:320
  75.2 2.3 %shard_map.120 = (bf16[1,256,128]{2,1,0:T(8,128)(2,1)S(1)}, f32[64,256]{1,0:T(8,128)S(1)}, f32[64,256]{1,0:T(8,128)S(1)}) custom-call(bf16[3,4,64,128]{3,2,1,0:T(8,128)(2,1)S(1)} %collective-permute-done.5.refs_0_.refs_4_, bf16[3,4,64,128]{3,2,1,0:T(8,128)(2,1)S(1)} %collective-permute-done.6.refs_1_.refs_5_, ...), custom_call_target="tpu_custom_call" | custom-call | flops 805306368 | bytes 3145728 | tf_op jit(solution)/shard_map/pallas_call | solution.py:243
  77.4 2.5 %collective-permute-start.23 = (bf16[1,256,128]{2,1,0:T(8,128)(2,1)S(1)}, bf16[1,256,128]{2,1,0:T(8,128)(2,1)S(1)}, u32[]{:S(2)}, u32[]{:S(2)}) collective-permute-start(bf16[1,256,128]{2,1,0:T(8,128)(2,1)S(1)} %get-tuple-element.51.refs_0_), channel_id=1, source_target_pairs={{0,6},{1,7},{2,4},{3,5},{4,2},{5,3},{6,0},{7,1},{8,14},{9,15},{10,... | collective-permute-start | bytes 196616 | tf_op jit(solution)/shard_map/ppermute | solution.py:315
  80.0 1.9 %collective-permute-start.21 = (bf16[1,256,128]{2,1,0:T(8,128)(2,1)S(1)}, bf16[1,256,128]{2,1,0:T(8,128)(2,1)S(1)}, u32[]{:S(2)}, u32[]{:S(2)}) collective-permute-start(bf16[1,256,128]{2,1,0:T(8,128)(2,1)S(1)} %get-tuple-element.51.refs_0_), channel_id=1, source_target_pairs={{0,2},{1,3},{2,0},{3,1},{4,6},{5,7},{6,4},{7,5},{8,10},{9,11},{10,... | collective-permute-start | bytes 196616 | tf_op jit(solution)/shard_map/ppermute | solution.py:315
  81.9 1.7 %collective-permute-done.23.refs_3_ = bf16[1,256,128]{2,1,0:T(8,128)(2,1)S(1)} collective-permute-done((bf16[1,256,128]{2,1,0:T(8,128)(2,1)S(1)}, bf16[1,256,128]{2,1,0:T(8,128)(2,1)S(1)}, u32[]{:S(2)}, u32[]{:S(2)}) %collective-permute-start.23) | collective-permute-done | bytes 65568 | tf_op jit(solution)/shard_map/ppermute | solution.py:315
  89.7 2.0 %collective-permute-done.25.refs_1_ = bf16[1,4,64,128]{3,2,1,0:T(8,128)(2,1)S(1)} collective-permute-done((bf16[1,4,64,128]{3,2,1,0:T(8,128)(2,1)S(1)}, bf16[1,4,64,128]{3,2,1,0:T(8,128)(2,1)S(1)}, u32[]{:S(2)}, u32[]{:S(2)}) %collective-permute-start.25) | collective-permute-done | bytes 65568 | tf_op jit(solution)/shard_map/ppermute | solution.py:320
  92.9 2.4 %collective-permute-start.28 = (bf16[1,256,128]{2,1,0:T(8,128)(2,1)S(1)}, bf16[1,256,128]{2,1,0:T(8,128)(2,1)S(1)}, u32[]{:S(2)}, u32[]{:S(2)}) collective-permute-start(bf16[1,256,128]{2,1,0:T(8,128)(2,1)S(1)} %get-tuple-element.54.refs_0_), channel_id=1, source_target_pairs={{0,6},{1,7},{2,4},{3,5},{4,2},{5,3},{6,0},{7,1},{8,14},{9,15},{10,... | collective-permute-start | bytes 196616 | tf_op jit(solution)/shard_map/ppermute | solution.py:315
  95.4 1.9 %collective-permute-start.26 = (bf16[1,256,128]{2,1,0:T(8,128)(2,1)S(1)}, bf16[1,256,128]{2,1,0:T(8,128)(2,1)S(1)}, u32[]{:S(2)}, u32[]{:S(2)}) collective-permute-start(bf16[1,256,128]{2,1,0:T(8,128)(2,1)S(1)} %get-tuple-element.54.refs_0_), channel_id=1, source_target_pairs={{0,2},{1,3},{2,0},{3,1},{4,6},{5,7},{6,4},{7,5},{8,10},{9,11},{10,... | collective-permute-start | bytes 196616 | tf_op jit(solution)/shard_map/ppermute | solution.py:315
  99.0 1.8 %collective-permute-done.27.refs_2_ = bf16[1,256,128]{2,1,0:T(8,128)(2,1)S(1)} collective-permute-done((bf16[1,256,128]{2,1,0:T(8,128)(2,1)S(1)}, bf16[1,256,128]{2,1,0:T(8,128)(2,1)S(1)}, u32[]{:S(2)}, u32[]{:S(2)}) %collective-permute-start.27) | collective-permute-done | bytes 65568 | tf_op jit(solution)/shard_map/ppermute | solution.py:315
  101.7 2.2 %collective-permute-start.30 = (bf16[1,4,64,128]{3,2,1,0:T(8,128)(2,1)S(1)}, bf16[1,4,64,128]{3,2,1,0:T(8,128)(2,1)S(1)}, u32[]{:S(2)}, u32[]{:S(2)}) collective-permute-start(bf16[1,4,64,128]{3,2,1,0:T(8,128)(2,1)S(1)} %get-tuple-element.90), channel_id=1, source_target_pairs={{0,24},{8,16},{16,8},{24,0},{1,25},{9,17},{17,9},{25,1},{2,26},{10... | collective-permute-start | bytes 196616 | tf_op jit(solution)/shard_map/ppermute | solution.py:320
  109.0 1.8 %collective-permute-start.32 = (bf16[128,128]{1,0:T(8,128)(2,1)S(1)}, bf16[128,128]{1,0:T(8,128)(2,1)S(1)}, u32[]{:S(2)}, u32[]{:S(2)}) collective-permute-start(bf16[128,128]{1,0:T(8,128)(2,1)S(1)} %bitcast.181), channel_id=1, source_target_pairs={{0,4},{1,5},{2,6},{3,7},{4,0},{5,1},{6,2},{7,3},{8,12},{9,13},{10,... | collective-permute-start | bytes 98312 | tf_op jit(solution)/shard_map/ppermute | solution.py:404
  110.8 1.8 %collective-permute-start.33 = (bf16[128,128]{1,0:T(8,128)(2,1)S(1)}, bf16[128,128]{1,0:T(8,128)(2,1)S(1)}, u32[]{:S(2)}, u32[]{:S(2)}) collective-permute-start(bf16[128,128]{1,0:T(8,128)(2,1)S(1)} %bitcast.182), channel_id=1, source_target_pairs={{0,6},{1,7},{2,4},{3,5},{4,2},{5,3},{6,0},{7,1},{8,14},{9,15},{10,... | collective-permute-start | bytes 98312 | tf_op jit(solution)/shard_map/ppermute | solution.py:404
  112.7 3.9 %collective-permute-done.33.refs_3_ = bf16[128,128]{1,0:T(8,128)(2,1)S(1)} collective-permute-done((bf16[128,128]{1,0:T(8,128)(2,1)S(1)}, bf16[128,128]{1,0:T(8,128)(2,1)S(1)}, u32[]{:S(2)}, u32[]{:S(2)}) %collective-permute-start.33) | collective-permute-done | bytes 32800 | tf_op jit(solution)/shard_map/ppermute | solution.py:404
  119.4 2.4 %shard_map.127.refs_6_ = bf16[3,3,1,512,512]{4,3,2,1,0:T(8,128)(2,1)S(1)} custom-call(bf16[3,3,512,512]{3,2,1,0:T(8,128)(2,1)} %refs_0_), custom_call_target="tpu_custom_call" | custom-call | flops 471859200 | bytes 4718592 | tf_op jit(solution)/shard_map/pallas_call | solution.py:205
  121.8 2.4 %shard_map.128.refs_8_ = bf16[3,3,1,512,512]{4,3,2,1,0:T(8,128)(2,1)S(1)} custom-call(bf16[3,3,512,512]{3,2,1,0:T(8,128)(2,1)} %refs_0_.1), custom_call_target="tpu_custom_call" | custom-call | flops 471859200 | bytes 4718592 | tf_op jit(solution)/shard_map/pallas_call | solution.py:205
  124.4 2.1 %shard_map.129 = bf16[128,512]{1,0:T(8,128)(2,1)S(1)} custom-call(bf16[128,128]{1,0:T(8,128)(2,1)S(1)} %bitcast.160, bf16[128,128]{1,0:T(8,128)(2,1)S(1)} %collective-permute-done.31.refs_1_, bf16[128,128]{1,0:T(8,128)(2,1)S(1)} %collective-permute-done.32.refs_2_, bf16[128,128]{1,0:T(8,128)(2,1)S(1)} %collective-permute-done.33.refs_3_, ...), custom_call_target="tpu_custom_call" | custom-call | flops 1509949440 | bytes 9437184 | tf_op jit(solution)/shard_map/pallas_call | solution.py:264
  (108 shorter events, 41.7 us)
Async XLA Ops:
  4.1 41.8 %collective-permute-start.7 = (bf16[3,3,256,512]{3,2,1,0:T(8,128)(2,1)}, bf16[3,3,256,512]{3,2,1,0:T(8,128)(2,1)}, u32[]{:S(2)}, u32[]{:S(2)}) collective-permute-start(bf16[3,3,256,512]{3,2,1,0:T(8,128)(2,1)} %bitcast.168), channel_id=1, source_target_pairs={{0,1},{1,0},{2,3},{3,2},{4,5},{5,4},{6,7},{7,6},{8,9},{9,8},{10,11... | collective-permute-start | bytes 7077896 | tf_op jit(solution)/shard_map/ppermute | solution.py:306
  4.6 47.0 %collective-permute-start.15 = (bf16[3,3,256,512]{3,2,1,0:T(8,128)(2,1)}, bf16[3,3,256,512]{3,2,1,0:T(8,128)(2,1)S(1)}, u32[]{:S(2)}, u32[]{:S(2)}) collective-permute-start(bf16[3,3,256,512]{3,2,1,0:T(8,128)(2,1)} %bitcast.170), channel_id=1, source_target_pairs={{0,1},{1,0},{2,3},{3,2},{4,5},{5,4},{6,7},{7,6},{8,9},{9,8},{10,11... | collective-permute-start | bytes 7077896 | tf_op jit(solution)/shard_map/ppermute | solution.py:306
  4.7 15.4 %collective-permute-start.8 = (bf16[2,256,128]{2,1,0:T(8,128)(2,1)S(1)}, bf16[2,256,128]{2,1,0:T(8,128)(2,1)S(1)}, u32[]{:S(2)}, u32[]{:S(2)}) collective-permute-start(bf16[2,256,128]{2,1,0:T(8,128)(2,1)S(1)} %maximum_select_fusion.2.refs_0_), channel_id=1, source_target_pairs={{0,2},{1,3},{2,0},{3,1},{4,6},{5,7},{6,4},{7,5},{8,10},{9,11},{10,... | collective-permute-start | bytes 393224 | tf_op jit(solution)/shard_map/ppermute | solution.py:315
  7.6 12.5 %collective-permute-start.9 = (bf16[2,256,128]{2,1,0:T(8,128)(2,1)S(1)}, bf16[2,256,128]{2,1,0:T(8,128)(2,1)S(1)}, u32[]{:S(2)}, u32[]{:S(2)}) collective-permute-start(bf16[2,256,128]{2,1,0:T(8,128)(2,1)S(1)} %maximum_select_fusion.2.refs_0_), channel_id=1, source_target_pairs={{0,4},{1,5},{2,6},{3,7},{4,0},{5,1},{6,2},{7,3},{8,12},{9,13},{10,... | collective-permute-start | bytes 393224 | tf_op jit(solution)/shard_map/ppermute | solution.py:315
  16.1 7.9 %collective-permute-start.10 = (bf16[2,256,128]{2,1,0:T(8,128)(2,1)S(1)}, bf16[2,256,128]{2,1,0:T(8,128)(2,1)S(1)}, u32[]{:S(2)}, u32[]{:S(2)}) collective-permute-start(bf16[2,256,128]{2,1,0:T(8,128)(2,1)S(1)} %maximum_select_fusion.2.refs_0_), channel_id=1, source_target_pairs={{0,6},{1,7},{2,4},{3,5},{4,2},{5,3},{6,0},{7,1},{8,14},{9,15},{10,... | collective-permute-start | bytes 393224 | tf_op jit(solution)/shard_map/ppermute | solution.py:315
  20.1 15.6 %collective-permute-start.4 = (bf16[3,256,128]{2,1,0:T(8,128)(2,1)S(1)}, bf16[3,256,128]{2,1,0:T(8,128)(2,1)S(1)}, u32[]{:S(2)}, u32[]{:S(2)}) collective-permute-start(bf16[3,256,128]{2,1,0:T(8,128)(2,1)S(1)} %maximum_select_fusion.1.refs_0_), channel_id=1, source_target_pairs={{0,6},{1,7},{2,4},{3,5},{4,2},{5,3},{6,0},{7,1},{8,14},{9,15},{10,... | collective-permute-start | bytes 589832 | tf_op jit(solution)/shard_map/ppermute | solution.py:315
  20.2 22.6 %collective-permute-start.3 = (bf16[3,256,128]{2,1,0:T(8,128)(2,1)S(1)}, bf16[3,256,128]{2,1,0:T(8,128)(2,1)S(1)}, u32[]{:S(2)}, u32[]{:S(2)}) collective-permute-start(bf16[3,256,128]{2,1,0:T(8,128)(2,1)S(1)} %maximum_select_fusion.1.refs_0_), channel_id=1, source_target_pairs={{0,4},{1,5},{2,6},{3,7},{4,0},{5,1},{6,2},{7,3},{8,12},{9,13},{10,... | collective-permute-start | bytes 589832 | tf_op jit(solution)/shard_map/ppermute | solution.py:315
  24.0 21.3 %collective-permute-start.2 = (bf16[3,256,128]{2,1,0:T(8,128)(2,1)S(1)}, bf16[3,256,128]{2,1,0:T(8,128)(2,1)S(1)}, u32[]{:S(2)}, u32[]{:S(2)}) collective-permute-start(bf16[3,256,128]{2,1,0:T(8,128)(2,1)S(1)} %maximum_select_fusion.1.refs_0_), channel_id=1, source_target_pairs={{0,2},{1,3},{2,0},{3,1},{4,6},{5,7},{6,4},{7,5},{8,10},{9,11},{10,... | collective-permute-start | bytes 589832 | tf_op jit(solution)/shard_map/ppermute | solution.py:315
  35.7 21.3 %collective-permute-start.13 = (bf16[2,4,64,128]{3,2,1,0:T(8,128)(2,1)S(1)}, bf16[2,4,64,128]{3,2,1,0:T(8,128)(2,1)S(1)}, u32[]{:S(2)}, u32[]{:S(2)}) collective-permute-start(bf16[2,4,64,128]{3,2,1,0:T(8,128)(2,1)S(1)} %get-tuple-element.75), channel_id=1, source_target_pairs={{0,8},{8,0},{16,24},{24,16},{1,9},{9,1},{17,25},{25,17},{2,10},{10... | collective-permute-start | bytes 393224 | tf_op jit(solution)/shard_map/ppermute | solution.py:319
  42.8 14.3 %collective-permute-start.14 = (bf16[2,4,64,128]{3,2,1,0:T(8,128)(2,1)S(1)}, bf16[2,4,64,128]{3,2,1,0:T(8,128)(2,1)S(1)}, u32[]{:S(2)}, u32[]{:S(2)}) collective-permute-start(bf16[2,4,64,128]{3,2,1,0:T(8,128)(2,1)S(1)} %get-tuple-element.74), channel_id=1, source_target_pairs={{0,24},{8,16},{16,8},{24,0},{1,25},{9,17},{17,9},{25,1},{2,26},{10... | collective-permute-start | bytes 393224 | tf_op jit(solution)/shard_map/ppermute | solution.py:320
  45.3 20.1 %collective-permute-start.5 = (bf16[3,4,64,128]{3,2,1,0:T(8,128)(2,1)S(1)}, bf16[3,4,64,128]{3,2,1,0:T(8,128)(2,1)S(1)}, u32[]{:S(2)}, u32[]{:S(2)}) collective-permute-start(bf16[3,4,64,128]{3,2,1,0:T(8,128)(2,1)S(1)} %get-tuple-element.73), channel_id=1, source_target_pairs={{0,8},{8,0},{16,24},{24,16},{1,9},{9,1},{17,25},{25,17},{2,10},{10... | collective-permute-start | bytes 589832 | tf_op jit(solution)/shard_map/ppermute | solution.py:319
  45.9 19.5 %collective-permute-start.6 = (bf16[3,4,64,128]{3,2,1,0:T(8,128)(2,1)S(1)}, bf16[3,4,64,128]{3,2,1,0:T(8,128)(2,1)S(1)}, u32[]{:S(2)}, u32[]{:S(2)}) collective-permute-start(bf16[3,4,64,128]{3,2,1,0:T(8,128)(2,1)S(1)} %get-tuple-element.72), channel_id=1, source_target_pairs={{0,24},{8,16},{16,8},{24,0},{1,25},{9,17},{17,9},{25,1},{2,26},{10... | collective-permute-start | bytes 589832 | tf_op jit(solution)/shard_map/ppermute | solution.py:320
  59.2 9.9 %collective-permute-start.18 = (bf16[1,256,128]{2,1,0:T(8,128)(2,1)S(1)}, bf16[1,256,128]{2,1,0:T(8,128)(2,1)S(1)}, u32[]{:S(2)}, u32[]{:S(2)}) collective-permute-start(bf16[1,256,128]{2,1,0:T(8,128)(2,1)S(1)} %get-tuple-element.48.refs_0_), channel_id=1, source_target_pairs={{0,6},{1,7},{2,4},{3,5},{4,2},{5,3},{6,0},{7,1},{8,14},{9,15},{10,... | collective-permute-start | bytes 196616 | tf_op jit(solution)/shard_map/ppermute | solution.py:315
  61.8 7.3 %collective-permute-start.17 = (bf16[1,256,128]{2,1,0:T(8,128)(2,1)S(1)}, bf16[1,256,128]{2,1,0:T(8,128)(2,1)S(1)}, u32[]{:S(2)}, u32[]{:S(2)}) collective-permute-start(bf16[1,256,128]{2,1,0:T(8,128)(2,1)S(1)} %get-tuple-element.48.refs_0_), channel_id=1, source_target_pairs={{0,4},{1,5},{2,6},{3,7},{4,0},{5,1},{6,2},{7,3},{8,12},{9,13},{10,... | collective-permute-start | bytes 196616 | tf_op jit(solution)/shard_map/ppermute | solution.py:315
  61.8 7.4 %collective-permute-start.16 = (bf16[1,256,128]{2,1,0:T(8,128)(2,1)S(1)}, bf16[1,256,128]{2,1,0:T(8,128)(2,1)S(1)}, u32[]{:S(2)}, u32[]{:S(2)}) collective-permute-start(bf16[1,256,128]{2,1,0:T(8,128)(2,1)S(1)} %get-tuple-element.48.refs_0_), channel_id=1, source_target_pairs={{0,2},{1,3},{2,0},{3,1},{4,6},{5,7},{6,4},{7,5},{8,10},{9,11},{10,... | collective-permute-start | bytes 196616 | tf_op jit(solution)/shard_map/ppermute | solution.py:315
  69.2 4.7 %collective-permute-start.19 = (bf16[1,4,64,128]{3,2,1,0:T(8,128)(2,1)S(1)}, bf16[1,4,64,128]{3,2,1,0:T(8,128)(2,1)S(1)}, u32[]{:S(2)}, u32[]{:S(2)}) collective-permute-start(bf16[1,4,64,128]{3,2,1,0:T(8,128)(2,1)S(1)} %get-tuple-element.95), channel_id=1, source_target_pairs={{0,8},{8,0},{16,24},{24,16},{1,9},{9,1},{17,25},{25,17},{2,10},{10... | collective-permute-start | bytes 196616 | tf_op jit(solution)/shard_map/ppermute | solution.py:319
  70.0 5.2 %collective-permute-start.20 = (bf16[1,4,64,128]{3,2,1,0:T(8,128)(2,1)S(1)}, bf16[1,4,64,128]{3,2,1,0:T(8,128)(2,1)S(1)}, u32[]{:S(2)}, u32[]{:S(2)}) collective-permute-start(bf16[1,4,64,128]{3,2,1,0:T(8,128)(2,1)S(1)} %get-tuple-element.94), channel_id=1, source_target_pairs={{0,24},{8,16},{16,8},{24,0},{1,25},{9,17},{17,9},{25,1},{2,26},{10... | collective-permute-start | bytes 196616 | tf_op jit(solution)/shard_map/ppermute | solution.py:320
  77.4 6.1 %collective-permute-start.23 = (bf16[1,256,128]{2,1,0:T(8,128)(2,1)S(1)}, bf16[1,256,128]{2,1,0:T(8,128)(2,1)S(1)}, u32[]{:S(2)}, u32[]{:S(2)}) collective-permute-start(bf16[1,256,128]{2,1,0:T(8,128)(2,1)S(1)} %get-tuple-element.51.refs_0_), channel_id=1, source_target_pairs={{0,6},{1,7},{2,4},{3,5},{4,2},{5,3},{6,0},{7,1},{8,14},{9,15},{10,... | collective-permute-start | bytes 196616 | tf_op jit(solution)/shard_map/ppermute | solution.py:315
  80.0 5.2 %collective-permute-start.22 = (bf16[1,256,128]{2,1,0:T(8,128)(2,1)S(1)}, bf16[1,256,128]{2,1,0:T(8,128)(2,1)S(1)}, u32[]{:S(2)}, u32[]{:S(2)}) collective-permute-start(bf16[1,256,128]{2,1,0:T(8,128)(2,1)S(1)} %get-tuple-element.51.refs_0_), channel_id=1, source_target_pairs={{0,4},{1,5},{2,6},{3,7},{4,0},{5,1},{6,2},{7,3},{8,12},{9,13},{10,... | collective-permute-start | bytes 196616 | tf_op jit(solution)/shard_map/ppermute | solution.py:315
  80.0 5.2 %collective-permute-start.21 = (bf16[1,256,128]{2,1,0:T(8,128)(2,1)S(1)}, bf16[1,256,128]{2,1,0:T(8,128)(2,1)S(1)}, u32[]{:S(2)}, u32[]{:S(2)}) collective-permute-start(bf16[1,256,128]{2,1,0:T(8,128)(2,1)S(1)} %get-tuple-element.51.refs_0_), channel_id=1, source_target_pairs={{0,2},{1,3},{2,0},{3,1},{4,6},{5,7},{6,4},{7,5},{8,10},{9,11},{10,... | collective-permute-start | bytes 196616 | tf_op jit(solution)/shard_map/ppermute | solution.py:315
  85.2 4.5 %collective-permute-start.24 = (bf16[1,4,64,128]{3,2,1,0:T(8,128)(2,1)S(1)}, bf16[1,4,64,128]{3,2,1,0:T(8,128)(2,1)S(1)}, u32[]{:S(2)}, u32[]{:S(2)}) collective-permute-start(bf16[1,4,64,128]{3,2,1,0:T(8,128)(2,1)S(1)} %get-tuple-element.93), channel_id=1, source_target_pairs={{0,8},{8,0},{16,24},{24,16},{1,9},{9,1},{17,25},{25,17},{2,10},{10... | collective-permute-start | bytes 196616 | tf_op jit(solution)/shard_map/ppermute | solution.py:319
  86.5 5.2 %collective-permute-start.25 = (bf16[1,4,64,128]{3,2,1,0:T(8,128)(2,1)S(1)}, bf16[1,4,64,128]{3,2,1,0:T(8,128)(2,1)S(1)}, u32[]{:S(2)}, u32[]{:S(2)}) collective-permute-start(bf16[1,4,64,128]{3,2,1,0:T(8,128)(2,1)S(1)} %get-tuple-element.92), channel_id=1, source_target_pairs={{0,24},{8,16},{16,8},{24,0},{1,25},{9,17},{17,9},{25,1},{2,26},{10... | collective-permute-start | bytes 196616 | tf_op jit(solution)/shard_map/ppermute | solution.py:320
  92.9 6.1 %collective-permute-start.28 = (bf16[1,256,128]{2,1,0:T(8,128)(2,1)S(1)}, bf16[1,256,128]{2,1,0:T(8,128)(2,1)S(1)}, u32[]{:S(2)}, u32[]{:S(2)}) collective-permute-start(bf16[1,256,128]{2,1,0:T(8,128)(2,1)S(1)} %get-tuple-element.54.refs_0_), channel_id=1, source_target_pairs={{0,6},{1,7},{2,4},{3,5},{4,2},{5,3},{6,0},{7,1},{8,14},{9,15},{10,... | collective-permute-start | bytes 196616 | tf_op jit(solution)/shard_map/ppermute | solution.py:315
  95.3 5.6 %collective-permute-start.27 = (bf16[1,256,128]{2,1,0:T(8,128)(2,1)S(1)}, bf16[1,256,128]{2,1,0:T(8,128)(2,1)S(1)}, u32[]{:S(2)}, u32[]{:S(2)}) collective-permute-start(bf16[1,256,128]{2,1,0:T(8,128)(2,1)S(1)} %get-tuple-element.54.refs_0_), channel_id=1, source_target_pairs={{0,4},{1,5},{2,6},{3,7},{4,0},{5,1},{6,2},{7,3},{8,12},{9,13},{10,... | collective-permute-start | bytes 196616 | tf_op jit(solution)/shard_map/ppermute | solution.py:315
  95.4 5.4 %collective-permute-start.26 = (bf16[1,256,128]{2,1,0:T(8,128)(2,1)S(1)}, bf16[1,256,128]{2,1,0:T(8,128)(2,1)S(1)}, u32[]{:S(2)}, u32[]{:S(2)}) collective-permute-start(bf16[1,256,128]{2,1,0:T(8,128)(2,1)S(1)} %get-tuple-element.54.refs_0_), channel_id=1, source_target_pairs={{0,2},{1,3},{2,0},{3,1},{4,6},{5,7},{6,4},{7,5},{8,10},{9,11},{10,... | collective-permute-start | bytes 196616 | tf_op jit(solution)/shard_map/ppermute | solution.py:315
  100.9 4.7 %collective-permute-start.29 = (bf16[1,4,64,128]{3,2,1,0:T(8,128)(2,1)S(1)}, bf16[1,4,64,128]{3,2,1,0:T(8,128)(2,1)S(1)}, u32[]{:S(2)}, u32[]{:S(2)}) collective-permute-start(bf16[1,4,64,128]{3,2,1,0:T(8,128)(2,1)S(1)} %get-tuple-element.91), channel_id=1, source_target_pairs={{0,8},{8,0},{16,24},{24,16},{1,9},{9,1},{17,25},{25,17},{2,10},{10... | collective-permute-start | bytes 196616 | tf_op jit(solution)/shard_map/ppermute | solution.py:319
  101.7 5.2 %collective-permute-start.30 = (bf16[1,4,64,128]{3,2,1,0:T(8,128)(2,1)S(1)}, bf16[1,4,64,128]{3,2,1,0:T(8,128)(2,1)S(1)}, u32[]{:S(2)}, u32[]{:S(2)}) collective-permute-start(bf16[1,4,64,128]{3,2,1,0:T(8,128)(2,1)S(1)} %get-tuple-element.90), channel_id=1, source_target_pairs={{0,24},{8,16},{16,8},{24,0},{1,25},{9,17},{17,9},{25,1},{2,26},{10... | collective-permute-start | bytes 196616 | tf_op jit(solution)/shard_map/ppermute | solution.py:320
  108.2 8.4 %collective-permute-start.31 = (bf16[128,128]{1,0:T(8,128)(2,1)S(1)}, bf16[128,128]{1,0:T(8,128)(2,1)S(1)}, u32[]{:S(2)}, u32[]{:S(2)}) collective-permute-start(bf16[128,128]{1,0:T(8,128)(2,1)S(1)} %bitcast.180), channel_id=1, source_target_pairs={{0,2},{1,3},{2,0},{3,1},{4,6},{5,7},{6,4},{7,5},{8,10},{9,11},{10,... | collective-permute-start | bytes 98312 | tf_op jit(solution)/shard_map/ppermute | solution.py:404
  109.0 7.5 %collective-permute-start.32 = (bf16[128,128]{1,0:T(8,128)(2,1)S(1)}, bf16[128,128]{1,0:T(8,128)(2,1)S(1)}, u32[]{:S(2)}, u32[]{:S(2)}) collective-permute-start(bf16[128,128]{1,0:T(8,128)(2,1)S(1)} %bitcast.181), channel_id=1, source_target_pairs={{0,4},{1,5},{2,6},{3,7},{4,0},{5,1},{6,2},{7,3},{8,12},{9,13},{10,... | collective-permute-start | bytes 98312 | tf_op jit(solution)/shard_map/ppermute | solution.py:404
  110.8 5.7 %collective-permute-start.33 = (bf16[128,128]{1,0:T(8,128)(2,1)S(1)}, bf16[128,128]{1,0:T(8,128)(2,1)S(1)}, u32[]{:S(2)}, u32[]{:S(2)}) collective-permute-start(bf16[128,128]{1,0:T(8,128)(2,1)S(1)} %bitcast.182), channel_id=1, source_target_pairs={{0,6},{1,7},{2,4},{3,5},{4,2},{5,3},{6,0},{7,1},{8,14},{9,15},{10,... | collective-permute-start | bytes 98312 | tf_op jit(solution)/shard_map/ppermute | solution.py:404
  116.6 7.7 %collective-permute-start.34 = (bf16[1,4,64,128]{3,2,1,0:T(8,128)(2,1)S(1)}, bf16[1,4,64,128]{3,2,1,0:T(8,128)(2,1)S(1)}, u32[]{:S(2)}, u32[]{:S(2)}) collective-permute-start(bf16[1,4,64,128]{3,2,1,0:T(8,128)(2,1)S(1)} %get-tuple-element.89), channel_id=1, source_target_pairs={{0,8},{8,0},{16,24},{24,16},{1,9},{9,1},{17,25},{25,17},{2,10},{10... | collective-permute-start | bytes 196616 | tf_op jit(solution)/shard_map/ppermute | solution.py:319
  117.9 6.4 %collective-permute-start.35 = (bf16[1,4,64,128]{3,2,1,0:T(8,128)(2,1)S(1)}, bf16[1,4,64,128]{3,2,1,0:T(8,128)(2,1)S(1)}, u32[]{:S(2)}, u32[]{:S(2)}) collective-permute-start(bf16[1,4,64,128]{3,2,1,0:T(8,128)(2,1)S(1)} %get-tuple-element.88), channel_id=1, source_target_pairs={{0,24},{8,16},{16,8},{24,0},{1,25},{9,17},{17,9},{25,1},{2,26},{10... | collective-permute-start | bytes 196616 | tf_op jit(solution)/shard_map/ppermute | solution.py:320
  (9 other events, 17.3 us)

commit v6 on v5

--- a/solution.py
+++ b/solution.py
@@ -314,6 +314,17 @@
         return [value] + [
             lax.ppermute(value, "hid", [(i, i ^ (2 * k)) for i in range(2 * groups)]) for k in range(1, groups)
         ]
+
+    def across(value, k):
+        return lax.ppermute(value, "hid", [(i, i ^ (2 * k)) for i in range(2 * groups)])
+
+    def forwarded(value):
+        parts = [value]
+        parts += [across(value, k) for k in range(1, groups) if k == 1 or k % 2 == 0]
+        near = dict(zip([0, 1] + [k for k in range(2, groups, 2)], parts))
+        for k in range(3, groups, 2):
+            near[k] = across(near[k - 1], 1)
+        return [near[k] for k in range(groups)]
 
     def swapped_edges(top, bottom):
         first = lax.ppermute(jnp.where(even, bottom, top), "patch", inner_pairs)
@@ -374,7 +385,7 @@
 
     lead_parts, cells, bias = lax.optimization_barrier((lead_parts, cells, bias))
     lead_edges = edges_of(lead_parts)
-    rest_parts = gathered(rest)
+    rest_parts = forwarded(rest)
     rest_edges = edges_of(rest_parts)
 
     for time_index in range(steps):

time: 129 us -> 126 us (0.977)
  starting transfers between devices: 60.5 us -> 48.6 us
  waiting for transfers between devices: 26.4 us -> 35.7 us
    ppermute x0 -> x3, waiting for transfers between devices: none -> 13.7 us  [across(): lax.ppermute(value, 'hid', [(i, i ^ 2 * k) for i in range(2 * groups)])]
    ppermute x15 -> x12, starting transfers between devices: 35.6 us -> 22.9 us  [gathered(): lax.ppermute(value, 'hid', [(i, i ^ 2 * k) for i in range(2 * groups)])]
    ppermute x15 -> x12, waiting for transfers between devices: 15.1 us -> 10.6 us  [gathered(): lax.ppermute(value, 'hid', [(i, i ^ 2 * k) for i in range(2 * groups)])]
  transfers between devices with their start and end apart: 38 -> 38, of which waited for: 14 -> 15; matrix products, arithmetic and copies ran while one was open for 3% -> 3% of each run, Pallas kernels for 21% -> 22%
where the time goes in v6:
time: 126 us
  starting transfers between devices  48.6 us (39%)
  waiting for transfers between devices  35.7 us (28%)
  Pallas kernels  32.3 us (26%)
  local copies, waits for them, and re-layouts  6.21 us (5%)
  other arithmetic  1.96 us (2%)
    ppermute x12, starting transfers between devices, gathered(): lax.ppermute(value, 'hid', [(i, i ^ 2 * k) for i in range(2 * groups)])  22.9 us
    pallas_call x8, Pallas kernels, conv_call(): pl.pallas_call(functools.partial(conv_kernel, groups, cols, index, edges...  13.7 us
    ppermute x3, waiting for transfers between devices, across(): lax.ppermute(value, 'hid', [(i, i ^ 2 * k) for i in range(2 * groups)])  13.7 us
    ppermute x6, starting transfers between devices, swapped_edges(): second = lax.ppermute(jnp.where(even, top, bottom), 'patch', outer_pairs)  11.6 us
    ppermute x12, waiting for transfers between devices, gathered(): lax.ppermute(value, 'hid', [(i, i ^ 2 * k) for i in range(2 * groups)])  10.6 us
    pallas_call x4, Pallas kernels, stage_call(): pl.pallas_call(stage_kernel, in_specs=[pl.BlockSpec(memory_space=pltpu.HB...  9.66 us
    pallas_call x4, Pallas kernels, gate_call(): pl.pallas_call(functools.partial(gate_kernel, cols, [index for _, index,...  6.81 us
    ppermute x6, starting transfers between devices, swapped_edges(): first = lax.ppermute(jnp.where(even, bottom, top), 'patch', inner_pairs)  6.26 us
  transfers between devices with their start and end apart: 38, of which 15 were waited for; matrix products, arithmetic and copies ran while one was open for 3% of the time, Pallas kernels for 22%

profile of v6, /device:TPU:0, one launch (start us, length us, event | category | flops | bytes accessed | tf_op | source)
XLA Modules:
  0.0 126.0 jit_solution(11120357971936107562)
XLA Ops:
  4.7 2.9 %collective-permute-start.8 = (bf16[2,256,128]{2,1,0:T(8,128)(2,1)S(1)}, bf16[2,256,128]{2,1,0:T(8,128)(2,1)S(1)}, u32[]{:S(2)}, u32[]{:S(2)}) collective-permute-start(bf16[2,256,128]{2,1,0:T(8,128)(2,1)S(1)} %maximum_select_fusion.2.refs_0_), channel_id=1, source_target_pairs={{0,2},{1,3},{2,0},{3,1},{4,6},{5,7},{6,4},{7,5},{8,10},{9,11},{10,... | collective-permute-start | bytes 393224 | tf_op jit(solution)/shard_map/ppermute | solution.py:315
  7.6 2.6 %collective-permute-start.9 = (bf16[2,256,128]{2,1,0:T(8,128)(2,1)S(1)}, bf16[2,256,128]{2,1,0:T(8,128)(2,1)S(1)}, u32[]{:S(2)}, u32[]{:S(2)}) collective-permute-start(bf16[2,256,128]{2,1,0:T(8,128)(2,1)S(1)} %maximum_select_fusion.2.refs_0_), channel_id=1, source_target_pairs={{0,4},{1,5},{2,6},{3,7},{4,0},{5,1},{6,2},{7,3},{8,12},{9,13},{10,... | collective-permute-start | bytes 393224 | tf_op jit(solution)/shard_map/ppermute | solution.py:315
  16.1 4.0 %collective-permute-start.10 = (bf16[2,256,128]{2,1,0:T(8,128)(2,1)S(1)}, bf16[2,256,128]{2,1,0:T(8,128)(2,1)S(1)}, u32[]{:S(2)}, u32[]{:S(2)}) collective-permute-start(bf16[2,256,128]{2,1,0:T(8,128)(2,1)S(1)} %maximum_select_fusion.2.refs_0_), channel_id=1, source_target_pairs={{0,6},{1,7},{2,4},{3,5},{4,2},{5,3},{6,0},{7,1},{8,14},{9,15},{10,... | collective-permute-start | bytes 393224 | tf_op jit(solution)/shard_map/ppermute | solution.py:315
  20.7 3.8 %collective-permute-done.10.refs_3_ = bf16[2,256,128]{2,1,0:T(8,128)(2,1)S(1)} collective-permute-done((bf16[2,256,128]{2,1,0:T(8,128)(2,1)S(1)}, bf16[2,256,128]{2,1,0:T(8,128)(2,1)S(1)}, u32[]{:S(2)}, u32[]{:S(2)}) %collective-permute-start.10) | collective-permute-done | bytes 131104 | tf_op jit(solution)/shard_map/ppermute | solution.py:315
  24.6 1.8 %collective-permute-start.13 = (bf16[2,4,64,128]{3,2,1,0:T(8,128)(2,1)S(1)}, bf16[2,4,64,128]{3,2,1,0:T(8,128)(2,1)S(1)}, u32[]{:S(2)}, u32[]{:S(2)}) collective-permute-start(bf16[2,4,64,128]{3,2,1,0:T(8,128)(2,1)S(1)} %get-tuple-element.75), channel_id=1, source_target_pairs={{0,8},{8,0},{16,24},{24,16},{1,9},{9,1},{17,25},{25,17},{2,10},{10... | collective-permute-start | bytes 393224 | tf_op jit(solution)/shard_map/ppermute | solution.py:330
  26.4 7.9 %collective-permute-done.3.refs_2_ = bf16[3,256,128]{2,1,0:T(8,128)(2,1)S(1)} collective-permute-done((bf16[3,256,128]{2,1,0:T(8,128)(2,1)S(1)}, bf16[3,256,128]{2,1,0:T(8,128)(2,1)S(1)}, u32[]{:S(2)}, u32[]{:S(2)}) %collective-permute-start.3) | collective-permute-done | bytes 196640 | tf_op jit(solution)/shard_map/ppermute | solution.py:319
  34.3 2.4 %collective-permute-start.14 = (bf16[2,4,64,128]{3,2,1,0:T(8,128)(2,1)S(1)}, bf16[2,4,64,128]{3,2,1,0:T(8,128)(2,1)S(1)}, u32[]{:S(2)}, u32[]{:S(2)}) collective-permute-start(bf16[2,4,64,128]{3,2,1,0:T(8,128)(2,1)S(1)} %get-tuple-element.74), channel_id=1, source_target_pairs={{0,24},{8,16},{16,8},{24,0},{1,25},{9,17},{17,9},{25,1},{2,26},{10... | collective-permute-start | bytes 393224 | tf_op jit(solution)/shard_map/ppermute | solution.py:331
  36.8 5.8 %collective-permute-done.4.refs_3_ = bf16[3,256,128]{2,1,0:T(8,128)(2,1)S(1)} collective-permute-done((bf16[3,256,128]{2,1,0:T(8,128)(2,1)S(1)}, bf16[3,256,128]{2,1,0:T(8,128)(2,1)S(1)}, u32[]{:S(2)}, u32[]{:S(2)}) %collective-permute-start.4) | collective-permute-done | bytes 196640 | tf_op jit(solution)/shard_map/ppermute | solution.py:319
  44.7 2.4 %shard_map.113.refs_4_.refs_2_.refs_6_ = bf16[3,3,2,256,512]{4,3,2,1,0:T(8,128)(2,1)S(1)} custom-call(bf16[3,3,256,512]{3,2,1,0:T(8,128)(2,1)} %bitcast.169, bf16[3,3,256,512]{3,2,1,0:T(8,128)(2,1)} %collective-permute-done.7.refs_1_), custom_call_target="tpu_custom_call" | custom-call | flops 471859200 | bytes 4718592 | tf_op jit(solution)/shard_map/pallas_call | solution.py:205
  47.2 1.7 %shard_map.115.refs_5_ = f32[512,256]{1,0:T(8,128)S(1)} custom-call(bf16[2,256,128]{2,1,0:T(8,128)(2,1)S(1)} %maximum_select_fusion.2.refs_0_, bf16[2,256,128]{2,1,0:T(8,128)(2,1)S(1)} %collective-permute-done.8.refs_1_, bf16[2,256,128]{2,1,0:T(8,128)(2,1)S(1)} %collective-permute-done.9.refs_2_, bf16[2,256,128]{2,1,0:T(8,128)(2,1)S(1)} %collective-permute-done.10.refs_3_, ...), custom_call_target="tpu_custom_call" | custom-call | flops 1207959552 | bytes 4718592 | tf_op jit(solution)/shard_map/pallas_call | solution.py:222
  50.3 2.4 %shard_map.114.refs_4_.refs_5_.refs_2_ = bf16[3,3,2,256,512]{4,3,2,1,0:T(8,128)(2,1)S(1)} custom-call(bf16[3,3,256,512]{3,2,1,0:T(8,128)(2,1)} %bitcast.171, bf16[3,3,256,512]{3,2,1,0:T(8,128)(2,1)} %copy-done.2), custom_call_target="tpu_custom_call" | custom-call | flops 471859200 | bytes 4718592 | tf_op jit(solution)/shard_map/pallas_call | solution.py:205
  54.4 2.1 %shard_map.117 = (bf16[1,256,128]{2,1,0:T(8,128)(2,1)S(1)}, f32[64,256]{1,0:T(8,128)S(1)}, f32[64,256]{1,0:T(8,128)S(1)}) custom-call(bf16[2,4,64,128]{3,2,1,0:T(8,128)(2,1)S(1)} %collective-permute-done.13.refs_0_.refs_3_, bf16[2,4,64,128]{3,2,1,0:T(8,128)(2,1)S(1)} %collective-permute-done.14.refs_1_.refs_4_, ...), custom_call_target="tpu_custom_call" | custom-call | flops 805306368 | bytes 3145728 | tf_op jit(solution)/shard_map/pallas_call | solution.py:243
  56.6 2.6 %collective-permute-start.18 = (bf16[1,256,128]{2,1,0:T(8,128)(2,1)S(1)}, bf16[1,256,128]{2,1,0:T(8,128)(2,1)S(1)}, u32[]{:S(2)}, u32[]{:S(2)}) collective-permute-start(bf16[1,256,128]{2,1,0:T(8,128)(2,1)S(1)} %get-tuple-element.48.refs_0_), channel_id=1, source_target_pairs={{0,6},{1,7},{2,4},{3,5},{4,2},{5,3},{6,0},{7,1},{8,14},{9,15},{10,... | collective-permute-start | bytes 196616 | tf_op jit(solution)/shard_map/ppermute | solution.py:315
  59.1 1.9 %collective-permute-start.16 = (bf16[1,256,128]{2,1,0:T(8,128)(2,1)S(1)}, bf16[1,256,128]{2,1,0:T(8,128)(2,1)S(1)}, u32[]{:S(2)}, u32[]{:S(2)}) collective-permute-start(bf16[1,256,128]{2,1,0:T(8,128)(2,1)S(1)} %get-tuple-element.48.refs_0_), channel_id=1, source_target_pairs={{0,2},{1,3},{2,0},{3,1},{4,6},{5,7},{6,4},{7,5},{8,10},{9,11},{10,... | collective-permute-start | bytes 196616 | tf_op jit(solution)/shard_map/ppermute | solution.py:315
  61.0 1.7 %shard_map.118.refs_5_ = f32[512,256]{1,0:T(8,128)S(1)} custom-call(bf16[3,256,128]{2,1,0:T(8,128)(2,1)S(1)} %maximum_select_fusion.1.refs_0_, bf16[3,256,128]{2,1,0:T(8,128)(2,1)S(1)} %collective-permute-done.2.refs_1_, bf16[3,256,128]{2,1,0:T(8,128)(2,1)S(1)} %collective-permute-done.3.refs_2_, bf16[3,256,128]{2,1,0:T(8,128)(2,1)S(1)} %collective-permute-done.4.refs_3_, ...), custom_call_target="tpu_custom_call" | custom-call | flops 1207959552 | bytes 4718592 | tf_op jit(solution)/shard_map/pallas_call | solution.py:222
  62.8 1.8 %shard_map.121.refs_5_ = f32[512,256]{1,0:T(8,128)S(1)} custom-call(bf16[3,256,128]{2,1,0:T(8,128)(2,1)S(1)} %maximum_select_fusion.1.refs_0_, bf16[3,256,128]{2,1,0:T(8,128)(2,1)S(1)} %collective-permute-done.2.refs_1_, bf16[3,256,128]{2,1,0:T(8,128)(2,1)S(1)} %collective-permute-done.3.refs_2_, bf16[3,256,128]{2,1,0:T(8,128)(2,1)S(1)} %collective-permute-done.4.refs_3_, ...), custom_call_target="tpu_custom_call" | custom-call | flops 1207959552 | bytes 4718592 | tf_op jit(solution)/shard_map/pallas_call | solution.py:222
  64.6 1.8 %shard_map.124.refs_5_ = f32[512,256]{1,0:T(8,128)S(1)} custom-call(bf16[3,256,128]{2,1,0:T(8,128)(2,1)S(1)} %maximum_select_fusion.1.refs_0_, bf16[3,256,128]{2,1,0:T(8,128)(2,1)S(1)} %collective-permute-done.2.refs_1_, bf16[3,256,128]{2,1,0:T(8,128)(2,1)S(1)} %collective-permute-done.3.refs_2_, bf16[3,256,128]{2,1,0:T(8,128)(2,1)S(1)} %collective-permute-done.4.refs_3_, ...), custom_call_target="tpu_custom_call" | custom-call | flops 1207959552 | bytes 4718592 | tf_op jit(solution)/shard_map/pallas_call | solution.py:222
  67.1 2.5 %collective-permute-start.20 = (bf16[1,4,64,128]{3,2,1,0:T(8,128)(2,1)S(1)}, bf16[1,4,64,128]{3,2,1,0:T(8,128)(2,1)S(1)}, u32[]{:S(2)}, u32[]{:S(2)}) collective-permute-start(bf16[1,4,64,128]{3,2,1,0:T(8,128)(2,1)S(1)} %get-tuple-element.94), channel_id=1, source_target_pairs={{0,24},{8,16},{16,8},{24,0},{1,25},{9,17},{17,9},{25,1},{2,26},{10... | collective-permute-start | bytes 196616 | tf_op jit(solution)/shard_map/ppermute | solution.py:331
  72.5 2.3 %shard_map.120 = (bf16[1,256,128]{2,1,0:T(8,128)(2,1)S(1)}, f32[64,256]{1,0:T(8,128)S(1)}, f32[64,256]{1,0:T(8,128)S(1)}) custom-call(bf16[3,4,64,128]{3,2,1,0:T(8,128)(2,1)S(1)} %collective-permute-done.5.refs_0_.refs_4_, bf16[3,4,64,128]{3,2,1,0:T(8,128)(2,1)S(1)} %collective-permute-done.6.refs_1_.refs_5_, ...), custom_call_target="tpu_custom_call" | custom-call | flops 805306368 | bytes 3145728 | tf_op jit(solution)/shard_map/pallas_call | solution.py:243
  74.8 2.6 %collective-permute-start.23 = (bf16[1,256,128]{2,1,0:T(8,128)(2,1)S(1)}, bf16[1,256,128]{2,1,0:T(8,128)(2,1)S(1)}, u32[]{:S(2)}, u32[]{:S(2)}) collective-permute-start(bf16[1,256,128]{2,1,0:T(8,128)(2,1)S(1)} %get-tuple-element.51.refs_0_), channel_id=1, source_target_pairs={{0,6},{1,7},{2,4},{3,5},{4,2},{5,3},{6,0},{7,1},{8,14},{9,15},{10,... | collective-permute-start | bytes 196616 | tf_op jit(solution)/shard_map/ppermute | solution.py:315
  77.4 1.9 %collective-permute-start.21 = (bf16[1,256,128]{2,1,0:T(8,128)(2,1)S(1)}, bf16[1,256,128]{2,1,0:T(8,128)(2,1)S(1)}, u32[]{:S(2)}, u32[]{:S(2)}) collective-permute-start(bf16[1,256,128]{2,1,0:T(8,128)(2,1)S(1)} %get-tuple-element.51.refs_0_), channel_id=1, source_target_pairs={{0,2},{1,3},{2,0},{3,1},{4,6},{5,7},{6,4},{7,5},{8,10},{9,11},{10,... | collective-permute-start | bytes 196616 | tf_op jit(solution)/shard_map/ppermute | solution.py:315
  79.3 1.7 %collective-permute-done.23.refs_3_ = bf16[1,256,128]{2,1,0:T(8,128)(2,1)S(1)} collective-permute-done((bf16[1,256,128]{2,1,0:T(8,128)(2,1)S(1)}, bf16[1,256,128]{2,1,0:T(8,128)(2,1)S(1)}, u32[]{:S(2)}, u32[]{:S(2)}) %collective-permute-start.23) | collective-permute-done | bytes 65568 | tf_op jit(solution)/shard_map/ppermute | solution.py:315
  87.1 2.0 %collective-permute-done.25.refs_1_ = bf16[1,4,64,128]{3,2,1,0:T(8,128)(2,1)S(1)} collective-permute-done((bf16[1,4,64,128]{3,2,1,0:T(8,128)(2,1)S(1)}, bf16[1,4,64,128]{3,2,1,0:T(8,128)(2,1)S(1)}, u32[]{:S(2)}, u32[]{:S(2)}) %collective-permute-start.25) | collective-permute-done | bytes 65568 | tf_op jit(solution)/shard_map/ppermute | solution.py:331
  90.3 2.4 %collective-permute-start.28 = (bf16[1,256,128]{2,1,0:T(8,128)(2,1)S(1)}, bf16[1,256,128]{2,1,0:T(8,128)(2,1)S(1)}, u32[]{:S(2)}, u32[]{:S(2)}) collective-permute-start(bf16[1,256,128]{2,1,0:T(8,128)(2,1)S(1)} %get-tuple-element.54.refs_0_), channel_id=1, source_target_pairs={{0,6},{1,7},{2,4},{3,5},{4,2},{5,3},{6,0},{7,1},{8,14},{9,15},{10,... | collective-permute-start | bytes 196616 | tf_op jit(solution)/shard_map/ppermute | solution.py:315
  92.8 2.0 %collective-permute-start.26 = (bf16[1,256,128]{2,1,0:T(8,128)(2,1)S(1)}, bf16[1,256,128]{2,1,0:T(8,128)(2,1)S(1)}, u32[]{:S(2)}, u32[]{:S(2)}) collective-permute-start(bf16[1,256,128]{2,1,0:T(8,128)(2,1)S(1)} %get-tuple-element.54.refs_0_), channel_id=1, source_target_pairs={{0,2},{1,3},{2,0},{3,1},{4,6},{5,7},{6,4},{7,5},{8,10},{9,11},{10,... | collective-permute-start | bytes 196616 | tf_op jit(solution)/shard_map/ppermute | solution.py:315
  94.7 1.7 %collective-permute-done.28.refs_3_ = bf16[1,256,128]{2,1,0:T(8,128)(2,1)S(1)} collective-permute-done((bf16[1,256,128]{2,1,0:T(8,128)(2,1)S(1)}, bf16[1,256,128]{2,1,0:T(8,128)(2,1)S(1)}, u32[]{:S(2)}, u32[]{:S(2)}) %collective-permute-start.28) | collective-permute-done | bytes 65568 | tf_op jit(solution)/shard_map/ppermute | solution.py:315
  96.4 1.8 %collective-permute-done.27.refs_2_ = bf16[1,256,128]{2,1,0:T(8,128)(2,1)S(1)} collective-permute-done((bf16[1,256,128]{2,1,0:T(8,128)(2,1)S(1)}, bf16[1,256,128]{2,1,0:T(8,128)(2,1)S(1)}, u32[]{:S(2)}, u32[]{:S(2)}) %collective-permute-start.27) | collective-permute-done | bytes 65568 | tf_op jit(solution)/shard_map/ppermute | solution.py:315
  99.1 2.3 %collective-permute-start.30 = (bf16[1,4,64,128]{3,2,1,0:T(8,128)(2,1)S(1)}, bf16[1,4,64,128]{3,2,1,0:T(8,128)(2,1)S(1)}, u32[]{:S(2)}, u32[]{:S(2)}) collective-permute-start(bf16[1,4,64,128]{3,2,1,0:T(8,128)(2,1)S(1)} %get-tuple-element.90), channel_id=1, source_target_pairs={{0,24},{8,16},{16,8},{24,0},{1,25},{9,17},{17,9},{25,1},{2,26},{10... | collective-permute-start | bytes 196616 | tf_op jit(solution)/shard_map/ppermute | solution.py:331
  110.1 4.0 %collective-permute-done.33.refs_3_ = bf16[128,128]{1,0:T(8,128)(2,1)S(1)} collective-permute-done((bf16[128,128]{1,0:T(8,128)(2,1)S(1)}, bf16[128,128]{1,0:T(8,128)(2,1)S(1)}, u32[]{:S(2)}, u32[]{:S(2)}) %collective-permute-start.33) | collective-permute-done | bytes 32800 | tf_op jit(solution)/shard_map/ppermute | solution.py:415
  116.8 2.4 %shard_map.127.refs_6_ = bf16[3,3,1,512,512]{4,3,2,1,0:T(8,128)(2,1)S(1)} custom-call(bf16[3,3,512,512]{3,2,1,0:T(8,128)(2,1)} %refs_0_), custom_call_target="tpu_custom_call" | custom-call | flops 471859200 | bytes 4718592 | tf_op jit(solution)/shard_map/pallas_call | solution.py:205
  119.2 2.4 %shard_map.128.refs_8_ = bf16[3,3,1,512,512]{4,3,2,1,0:T(8,128)(2,1)S(1)} custom-call(bf16[3,3,512,512]{3,2,1,0:T(8,128)(2,1)} %refs_0_.1), custom_call_target="tpu_custom_call" | custom-call | flops 471859200 | bytes 4718592 | tf_op jit(solution)/shard_map/pallas_call | solution.py:205
  121.7 2.1 %shard_map.129 = bf16[128,512]{1,0:T(8,128)(2,1)S(1)} custom-call(bf16[128,128]{1,0:T(8,128)(2,1)S(1)} %bitcast.160, bf16[128,128]{1,0:T(8,128)(2,1)S(1)} %collective-permute-done.31.refs_1_, bf16[128,128]{1,0:T(8,128)(2,1)S(1)} %collective-permute-done.32.refs_2_, bf16[128,128]{1,0:T(8,128)(2,1)S(1)} %collective-permute-done.33.refs_3_, ...), custom_call_target="tpu_custom_call" | custom-call | flops 1509949440 | bytes 9437184 | tf_op jit(solution)/shard_map/pallas_call | solution.py:264
  (108 shorter events, 41.3 us)
Async XLA Ops:
  4.1 39.1 %collective-permute-start.7 = (bf16[3,3,256,512]{3,2,1,0:T(8,128)(2,1)}, bf16[3,3,256,512]{3,2,1,0:T(8,128)(2,1)}, u32[]{:S(2)}, u32[]{:S(2)}) collective-permute-start(bf16[3,3,256,512]{3,2,1,0:T(8,128)(2,1)} %bitcast.168), channel_id=1, source_target_pairs={{0,1},{1,0},{2,3},{3,2},{4,5},{5,4},{6,7},{7,6},{8,9},{9,8},{10,11... | collective-permute-start | bytes 7077896 | tf_op jit(solution)/shard_map/ppermute | solution.py:306
  4.6 44.3 %collective-permute-start.15 = (bf16[3,3,256,512]{3,2,1,0:T(8,128)(2,1)}, bf16[3,3,256,512]{3,2,1,0:T(8,128)(2,1)S(1)}, u32[]{:S(2)}, u32[]{:S(2)}) collective-permute-start(bf16[3,3,256,512]{3,2,1,0:T(8,128)(2,1)} %bitcast.170), channel_id=1, source_target_pairs={{0,1},{1,0},{2,3},{3,2},{4,5},{5,4},{6,7},{7,6},{8,9},{9,8},{10,11... | collective-permute-start | bytes 7077896 | tf_op jit(solution)/shard_map/ppermute | solution.py:306
  4.7 15.4 %collective-permute-start.8 = (bf16[2,256,128]{2,1,0:T(8,128)(2,1)S(1)}, bf16[2,256,128]{2,1,0:T(8,128)(2,1)S(1)}, u32[]{:S(2)}, u32[]{:S(2)}) collective-permute-start(bf16[2,256,128]{2,1,0:T(8,128)(2,1)S(1)} %maximum_select_fusion.2.refs_0_), channel_id=1, source_target_pairs={{0,2},{1,3},{2,0},{3,1},{4,6},{5,7},{6,4},{7,5},{8,10},{9,11},{10,... | collective-permute-start | bytes 393224 | tf_op jit(solution)/shard_map/ppermute | solution.py:315
  7.6 12.5 %collective-permute-start.9 = (bf16[2,256,128]{2,1,0:T(8,128)(2,1)S(1)}, bf16[2,256,128]{2,1,0:T(8,128)(2,1)S(1)}, u32[]{:S(2)}, u32[]{:S(2)}) collective-permute-start(bf16[2,256,128]{2,1,0:T(8,128)(2,1)S(1)} %maximum_select_fusion.2.refs_0_), channel_id=1, source_target_pairs={{0,4},{1,5},{2,6},{3,7},{4,0},{5,1},{6,2},{7,3},{8,12},{9,13},{10,... | collective-permute-start | bytes 393224 | tf_op jit(solution)/shard_map/ppermute | solution.py:315
  16.1 8.5 %collective-permute-start.10 = (bf16[2,256,128]{2,1,0:T(8,128)(2,1)S(1)}, bf16[2,256,128]{2,1,0:T(8,128)(2,1)S(1)}, u32[]{:S(2)}, u32[]{:S(2)}) collective-permute-start(bf16[2,256,128]{2,1,0:T(8,128)(2,1)S(1)} %maximum_select_fusion.2.refs_0_), channel_id=1, source_target_pairs={{0,6},{1,7},{2,4},{3,5},{4,2},{5,3},{6,0},{7,1},{8,14},{9,15},{10,... | collective-permute-start | bytes 393224 | tf_op jit(solution)/shard_map/ppermute | solution.py:315
  20.1 14.2 %collective-permute-start.3 = (bf16[3,256,128]{2,1,0:T(8,128)(2,1)S(1)}, bf16[3,256,128]{2,1,0:T(8,128)(2,1)S(1)}, u32[]{:S(2)}, u32[]{:S(2)}) collective-permute-start(bf16[3,256,128]{2,1,0:T(8,128)(2,1)S(1)} %maximum_select_fusion.1.refs_0_), channel_id=1, source_target_pairs={{0,4},{1,5},{2,6},{3,7},{4,0},{5,1},{6,2},{7,3},{8,12},{9,13},{10,... | collective-permute-start | bytes 589832 | tf_op jit(solution)/shard_map/ppermute | solution.py:319
  20.2 16.6 %collective-permute-start.2 = (bf16[3,256,128]{2,1,0:T(8,128)(2,1)S(1)}, bf16[3,256,128]{2,1,0:T(8,128)(2,1)S(1)}, u32[]{:S(2)}, u32[]{:S(2)}) collective-permute-start(bf16[3,256,128]{2,1,0:T(8,128)(2,1)S(1)} %maximum_select_fusion.1.refs_0_), channel_id=1, source_target_pairs={{0,2},{1,3},{2,0},{3,1},{4,6},{5,7},{6,4},{7,5},{8,10},{9,11},{10,... | collective-permute-start | bytes 589832 | tf_op jit(solution)/shard_map/ppermute | solution.py:319
  24.6 29.8 %collective-permute-start.13 = (bf16[2,4,64,128]{3,2,1,0:T(8,128)(2,1)S(1)}, bf16[2,4,64,128]{3,2,1,0:T(8,128)(2,1)S(1)}, u32[]{:S(2)}, u32[]{:S(2)}) collective-permute-start(bf16[2,4,64,128]{3,2,1,0:T(8,128)(2,1)S(1)} %get-tuple-element.75), channel_id=1, source_target_pairs={{0,8},{8,0},{16,24},{24,16},{1,9},{9,1},{17,25},{25,17},{2,10},{10... | collective-permute-start | bytes 393224 | tf_op jit(solution)/shard_map/ppermute | solution.py:330
  34.3 20.2 %collective-permute-start.14 = (bf16[2,4,64,128]{3,2,1,0:T(8,128)(2,1)S(1)}, bf16[2,4,64,128]{3,2,1,0:T(8,128)(2,1)S(1)}, u32[]{:S(2)}, u32[]{:S(2)}) collective-permute-start(bf16[2,4,64,128]{3,2,1,0:T(8,128)(2,1)S(1)} %get-tuple-element.74), channel_id=1, source_target_pairs={{0,24},{8,16},{16,8},{24,0},{1,25},{9,17},{17,9},{25,1},{2,26},{10... | collective-permute-start | bytes 393224 | tf_op jit(solution)/shard_map/ppermute | solution.py:331
  36.7 5.9 %collective-permute-start.4 = (bf16[3,256,128]{2,1,0:T(8,128)(2,1)S(1)}, bf16[3,256,128]{2,1,0:T(8,128)(2,1)S(1)}, u32[]{:S(2)}, u32[]{:S(2)}) collective-permute-start(bf16[3,256,128]{2,1,0:T(8,128)(2,1)S(1)} %collective-permute-done.3.refs_2_), channel_id=1, source_target_pairs={{0,2},{1,3},{2,0},{3,1},{4,6},{5,7},{6,4},{7,5},{8,10},{9,11},{10,... | collective-permute-start | bytes 589832 | tf_op jit(solution)/shard_map/ppermute | solution.py:319
  42.7 20.1 %collective-permute-start.5 = (bf16[3,4,64,128]{3,2,1,0:T(8,128)(2,1)S(1)}, bf16[3,4,64,128]{3,2,1,0:T(8,128)(2,1)S(1)}, u32[]{:S(2)}, u32[]{:S(2)}) collective-permute-start(bf16[3,4,64,128]{3,2,1,0:T(8,128)(2,1)S(1)} %get-tuple-element.73), channel_id=1, source_target_pairs={{0,8},{8,0},{16,24},{24,16},{1,9},{9,1},{17,25},{25,17},{2,10},{10... | collective-permute-start | bytes 589832 | tf_op jit(solution)/shard_map/ppermute | solution.py:330
  43.3 19.5 %collective-permute-start.6 = (bf16[3,4,64,128]{3,2,1,0:T(8,128)(2,1)S(1)}, bf16[3,4,64,128]{3,2,1,0:T(8,128)(2,1)S(1)}, u32[]{:S(2)}, u32[]{:S(2)}) collective-permute-start(bf16[3,4,64,128]{3,2,1,0:T(8,128)(2,1)S(1)} %get-tuple-element.72), channel_id=1, source_target_pairs={{0,24},{8,16},{16,8},{24,0},{1,25},{9,17},{17,9},{25,1},{2,26},{10... | collective-permute-start | bytes 589832 | tf_op jit(solution)/shard_map/ppermute | solution.py:331
  56.6 9.9 %collective-permute-start.18 = (bf16[1,256,128]{2,1,0:T(8,128)(2,1)S(1)}, bf16[1,256,128]{2,1,0:T(8,128)(2,1)S(1)}, u32[]{:S(2)}, u32[]{:S(2)}) collective-permute-start(bf16[1,256,128]{2,1,0:T(8,128)(2,1)S(1)} %get-tuple-element.48.refs_0_), channel_id=1, source_target_pairs={{0,6},{1,7},{2,4},{3,5},{4,2},{5,3},{6,0},{7,1},{8,14},{9,15},{10,... | collective-permute-start | bytes 196616 | tf_op jit(solution)/shard_map/ppermute | solution.py:315
  59.1 7.3 %collective-permute-start.17 = (bf16[1,256,128]{2,1,0:T(8,128)(2,1)S(1)}, bf16[1,256,128]{2,1,0:T(8,128)(2,1)S(1)}, u32[]{:S(2)}, u32[]{:S(2)}) collective-permute-start(bf16[1,256,128]{2,1,0:T(8,128)(2,1)S(1)} %get-tuple-element.48.refs_0_), channel_id=1, source_target_pairs={{0,4},{1,5},{2,6},{3,7},{4,0},{5,1},{6,2},{7,3},{8,12},{9,13},{10,... | collective-permute-start | bytes 196616 | tf_op jit(solution)/shard_map/ppermute | solution.py:315
  59.1 7.3 %collective-permute-start.16 = (bf16[1,256,128]{2,1,0:T(8,128)(2,1)S(1)}, bf16[1,256,128]{2,1,0:T(8,128)(2,1)S(1)}, u32[]{:S(2)}, u32[]{:S(2)}) collective-permute-start(bf16[1,256,128]{2,1,0:T(8,128)(2,1)S(1)} %get-tuple-element.48.refs_0_), channel_id=1, source_target_pairs={{0,2},{1,3},{2,0},{3,1},{4,6},{5,7},{6,4},{7,5},{8,10},{9,11},{10,... | collective-permute-start | bytes 196616 | tf_op jit(solution)/shard_map/ppermute | solution.py:315
  66.5 4.7 %collective-permute-start.19 = (bf16[1,4,64,128]{3,2,1,0:T(8,128)(2,1)S(1)}, bf16[1,4,64,128]{3,2,1,0:T(8,128)(2,1)S(1)}, u32[]{:S(2)}, u32[]{:S(2)}) collective-permute-start(bf16[1,4,64,128]{3,2,1,0:T(8,128)(2,1)S(1)} %get-tuple-element.95), channel_id=1, source_target_pairs={{0,8},{8,0},{16,24},{24,16},{1,9},{9,1},{17,25},{25,17},{2,10},{10... | collective-permute-start | bytes 196616 | tf_op jit(solution)/shard_map/ppermute | solution.py:330
  67.1 5.4 %collective-permute-start.20 = (bf16[1,4,64,128]{3,2,1,0:T(8,128)(2,1)S(1)}, bf16[1,4,64,128]{3,2,1,0:T(8,128)(2,1)S(1)}, u32[]{:S(2)}, u32[]{:S(2)}) collective-permute-start(bf16[1,4,64,128]{3,2,1,0:T(8,128)(2,1)S(1)} %get-tuple-element.94), channel_id=1, source_target_pairs={{0,24},{8,16},{16,8},{24,0},{1,25},{9,17},{17,9},{25,1},{2,26},{10... | collective-permute-start | bytes 196616 | tf_op jit(solution)/shard_map/ppermute | solution.py:331
  74.8 6.1 %collective-permute-start.23 = (bf16[1,256,128]{2,1,0:T(8,128)(2,1)S(1)}, bf16[1,256,128]{2,1,0:T(8,128)(2,1)S(1)}, u32[]{:S(2)}, u32[]{:S(2)}) collective-permute-start(bf16[1,256,128]{2,1,0:T(8,128)(2,1)S(1)} %get-tuple-element.51.refs_0_), channel_id=1, source_target_pairs={{0,6},{1,7},{2,4},{3,5},{4,2},{5,3},{6,0},{7,1},{8,14},{9,15},{10,... | collective-permute-start | bytes 196616 | tf_op jit(solution)/shard_map/ppermute | solution.py:315
  77.4 5.2 %collective-permute-start.22 = (bf16[1,256,128]{2,1,0:T(8,128)(2,1)S(1)}, bf16[1,256,128]{2,1,0:T(8,128)(2,1)S(1)}, u32[]{:S(2)}, u32[]{:S(2)}) collective-permute-start(bf16[1,256,128]{2,1,0:T(8,128)(2,1)S(1)} %get-tuple-element.51.refs_0_), channel_id=1, source_target_pairs={{0,4},{1,5},{2,6},{3,7},{4,0},{5,1},{6,2},{7,3},{8,12},{9,13},{10,... | collective-permute-start | bytes 196616 | tf_op jit(solution)/shard_map/ppermute | solution.py:315
  77.4 5.2 %collective-permute-start.21 = (bf16[1,256,128]{2,1,0:T(8,128)(2,1)S(1)}, bf16[1,256,128]{2,1,0:T(8,128)(2,1)S(1)}, u32[]{:S(2)}, u32[]{:S(2)}) collective-permute-start(bf16[1,256,128]{2,1,0:T(8,128)(2,1)S(1)} %get-tuple-element.51.refs_0_), channel_id=1, source_target_pairs={{0,2},{1,3},{2,0},{3,1},{4,6},{5,7},{6,4},{7,5},{8,10},{9,11},{10,... | collective-permute-start | bytes 196616 | tf_op jit(solution)/shard_map/ppermute | solution.py:315
  82.6 4.5 %collective-permute-start.24 = (bf16[1,4,64,128]{3,2,1,0:T(8,128)(2,1)S(1)}, bf16[1,4,64,128]{3,2,1,0:T(8,128)(2,1)S(1)}, u32[]{:S(2)}, u32[]{:S(2)}) collective-permute-start(bf16[1,4,64,128]{3,2,1,0:T(8,128)(2,1)S(1)} %get-tuple-element.93), channel_id=1, source_target_pairs={{0,8},{8,0},{16,24},{24,16},{1,9},{9,1},{17,25},{25,17},{2,10},{10... | collective-permute-start | bytes 196616 | tf_op jit(solution)/shard_map/ppermute | solution.py:330
  83.9 5.2 %collective-permute-start.25 = (bf16[1,4,64,128]{3,2,1,0:T(8,128)(2,1)S(1)}, bf16[1,4,64,128]{3,2,1,0:T(8,128)(2,1)S(1)}, u32[]{:S(2)}, u32[]{:S(2)}) collective-permute-start(bf16[1,4,64,128]{3,2,1,0:T(8,128)(2,1)S(1)} %get-tuple-element.92), channel_id=1, source_target_pairs={{0,24},{8,16},{16,8},{24,0},{1,25},{9,17},{17,9},{25,1},{2,26},{10... | collective-permute-start | bytes 196616 | tf_op jit(solution)/shard_map/ppermute | solution.py:331
  90.3 6.1 %collective-permute-start.28 = (bf16[1,256,128]{2,1,0:T(8,128)(2,1)S(1)}, bf16[1,256,128]{2,1,0:T(8,128)(2,1)S(1)}, u32[]{:S(2)}, u32[]{:S(2)}) collective-permute-start(bf16[1,256,128]{2,1,0:T(8,128)(2,1)S(1)} %get-tuple-element.54.refs_0_), channel_id=1, source_target_pairs={{0,6},{1,7},{2,4},{3,5},{4,2},{5,3},{6,0},{7,1},{8,14},{9,15},{10,... | collective-permute-start | bytes 196616 | tf_op jit(solution)/shard_map/ppermute | solution.py:315
  92.6 5.6 %collective-permute-start.27 = (bf16[1,256,128]{2,1,0:T(8,128)(2,1)S(1)}, bf16[1,256,128]{2,1,0:T(8,128)(2,1)S(1)}, u32[]{:S(2)}, u32[]{:S(2)}) collective-permute-start(bf16[1,256,128]{2,1,0:T(8,128)(2,1)S(1)} %get-tuple-element.54.refs_0_), channel_id=1, source_target_pairs={{0,4},{1,5},{2,6},{3,7},{4,0},{5,1},{6,2},{7,3},{8,12},{9,13},{10,... | collective-permute-start | bytes 196616 | tf_op jit(solution)/shard_map/ppermute | solution.py:315
  92.8 5.5 %collective-permute-start.26 = (bf16[1,256,128]{2,1,0:T(8,128)(2,1)S(1)}, bf16[1,256,128]{2,1,0:T(8,128)(2,1)S(1)}, u32[]{:S(2)}, u32[]{:S(2)}) collective-permute-start(bf16[1,256,128]{2,1,0:T(8,128)(2,1)S(1)} %get-tuple-element.54.refs_0_), channel_id=1, source_target_pairs={{0,2},{1,3},{2,0},{3,1},{4,6},{5,7},{6,4},{7,5},{8,10},{9,11},{10,... | collective-permute-start | bytes 196616 | tf_op jit(solution)/shard_map/ppermute | solution.py:315
  98.3 4.8 %collective-permute-start.29 = (bf16[1,4,64,128]{3,2,1,0:T(8,128)(2,1)S(1)}, bf16[1,4,64,128]{3,2,1,0:T(8,128)(2,1)S(1)}, u32[]{:S(2)}, u32[]{:S(2)}) collective-permute-start(bf16[1,4,64,128]{3,2,1,0:T(8,128)(2,1)S(1)} %get-tuple-element.91), channel_id=1, source_target_pairs={{0,8},{8,0},{16,24},{24,16},{1,9},{9,1},{17,25},{25,17},{2,10},{10... | collective-permute-start | bytes 196616 | tf_op jit(solution)/shard_map/ppermute | solution.py:330
  99.1 5.2 %collective-permute-start.30 = (bf16[1,4,64,128]{3,2,1,0:T(8,128)(2,1)S(1)}, bf16[1,4,64,128]{3,2,1,0:T(8,128)(2,1)S(1)}, u32[]{:S(2)}, u32[]{:S(2)}) collective-permute-start(bf16[1,4,64,128]{3,2,1,0:T(8,128)(2,1)S(1)} %get-tuple-element.90), channel_id=1, source_target_pairs={{0,24},{8,16},{16,8},{24,0},{1,25},{9,17},{17,9},{25,1},{2,26},{10... | collective-permute-start | bytes 196616 | tf_op jit(solution)/shard_map/ppermute | solution.py:331
  105.6 8.5 %collective-permute-start.31 = (bf16[128,128]{1,0:T(8,128)(2,1)S(1)}, bf16[128,128]{1,0:T(8,128)(2,1)S(1)}, u32[]{:S(2)}, u32[]{:S(2)}) collective-permute-start(bf16[128,128]{1,0:T(8,128)(2,1)S(1)} %bitcast.180), channel_id=1, source_target_pairs={{0,2},{1,3},{2,0},{3,1},{4,6},{5,7},{6,4},{7,5},{8,10},{9,11},{10,... | collective-permute-start | bytes 98312 | tf_op jit(solution)/shard_map/ppermute | solution.py:415
  107.3 6.8 %collective-permute-start.32 = (bf16[128,128]{1,0:T(8,128)(2,1)S(1)}, bf16[128,128]{1,0:T(8,128)(2,1)S(1)}, u32[]{:S(2)}, u32[]{:S(2)}) collective-permute-start(bf16[128,128]{1,0:T(8,128)(2,1)S(1)} %bitcast.181), channel_id=1, source_target_pairs={{0,4},{1,5},{2,6},{3,7},{4,0},{5,1},{6,2},{7,3},{8,12},{9,13},{10,... | collective-permute-start | bytes 98312 | tf_op jit(solution)/shard_map/ppermute | solution.py:415
  108.4 5.7 %collective-permute-start.33 = (bf16[128,128]{1,0:T(8,128)(2,1)S(1)}, bf16[128,128]{1,0:T(8,128)(2,1)S(1)}, u32[]{:S(2)}, u32[]{:S(2)}) collective-permute-start(bf16[128,128]{1,0:T(8,128)(2,1)S(1)} %bitcast.182), channel_id=1, source_target_pairs={{0,6},{1,7},{2,4},{3,5},{4,2},{5,3},{6,0},{7,1},{8,14},{9,15},{10,... | collective-permute-start | bytes 98312 | tf_op jit(solution)/shard_map/ppermute | solution.py:415
  114.2 7.5 %collective-permute-start.34 = (bf16[1,4,64,128]{3,2,1,0:T(8,128)(2,1)S(1)}, bf16[1,4,64,128]{3,2,1,0:T(8,128)(2,1)S(1)}, u32[]{:S(2)}, u32[]{:S(2)}) collective-permute-start(bf16[1,4,64,128]{3,2,1,0:T(8,128)(2,1)S(1)} %get-tuple-element.89), channel_id=1, source_target_pairs={{0,8},{8,0},{16,24},{24,16},{1,9},{9,1},{17,25},{25,17},{2,10},{10... | collective-permute-start | bytes 196616 | tf_op jit(solution)/shard_map/ppermute | solution.py:330
  115.3 6.4 %collective-permute-start.35 = (bf16[1,4,64,128]{3,2,1,0:T(8,128)(2,1)S(1)}, bf16[1,4,64,128]{3,2,1,0:T(8,128)(2,1)S(1)}, u32[]{:S(2)}, u32[]{:S(2)}) collective-permute-start(bf16[1,4,64,128]{3,2,1,0:T(8,128)(2,1)S(1)} %get-tuple-element.88), channel_id=1, source_target_pairs={{0,24},{8,16},{16,8},{24,0},{1,25},{9,17},{17,9},{25,1},{2,26},{10... | collective-permute-start | bytes 196616 | tf_op jit(solution)/shard_map/ppermute | solution.py:331
  (9 other events, 17.3 us)

commit v7 on v6

--- a/solution.py
+++ b/solution.py
@@ -51,9 +51,9 @@
     above = patch > 0
     below = patch < lax.axis_size("patch") - 1
     top, bottom = [], []
-    for k in range(a_ref.shape[1]):
-        a = a_ref[index, k].astype(jnp.float32)
-        b = b_ref[index, k].astype(jnp.float32)
+    for k in range(a_ref.shape[0]):
+        a = a_ref[k, index].astype(jnp.float32)
+        b = b_ref[k, index].astype(jnp.float32)
         top.append(jnp.where(above, jnp.where(even, b, a), 0.0))
         bottom.append(jnp.where(below, jnp.where(even, a, b), 0.0))
     return top, bottom
@@ -72,23 +72,25 @@
         copy.wait()
 
 
-def tap(weight_ref, p, q):
-    weight = weight_ref[p, q]
-    return weight.reshape(-1, weight.shape[-1])
-
-
-def conv_kernel(groups, cols, index, halo, *refs):
+def tap(weight_refs, p, q):
+    weights = [weight_ref[p, q] for weight_ref in weight_refs]
+    weights = [weight.reshape(-1, weight.shape[-1]) for weight in weights]
+    return weights[0] if len(weights) == 1 else jnp.concatenate(weights, axis=0)
+
+
+def conv_kernel(groups, cols, index, edge_index, *refs):
     refs = list(refs)
+    halo = edge_index is not None
     parts = [refs.pop(0) for _ in range(groups)]
     if halo:
         edge_a, edge_b = refs.pop(0), refs.pop(0)
-    weight_ref, init_ref, out_ref, held = refs
+    *weight_refs, init_ref, out_ref, held = refs
     count = out_ref.shape[1]
     group = lax.axis_index("hid") // 2
 
     place_columns(held, cols, [part[index] for part in parts], group, cols, True)
     if halo:
-        top, bottom = halo_pieces(edge_a, edge_b, index)
+        top, bottom = halo_pieces(edge_a, edge_b, edge_index)
         place_columns(held, 0, top, group, cols, True)
         place_columns(held, cols + count, bottom, group, cols, True)
     else:
@@ -105,14 +107,16 @@
         for q in range(3):
             window = held[q, p * cols : p * cols + count, :]
             total = total + lax.dot_general(
-                tap(weight_ref, p, q), window, NT, preferred_element_type=jnp.float32
+                tap(weight_refs, p, q), window, NT, preferred_element_type=jnp.float32
             )
     out_ref[...] = total
 
 
 def gate_kernel(cols, indices, turn_in, turn_out, *refs):
     refs = list(refs)
-    sides = [(refs.pop(0), refs.pop(0), refs.pop(0), index) for index in indices]
+    sides = []
+    for index, pieces in indices:
+        sides.append((refs.pop(0), refs.pop(0), [refs.pop(0) for _ in range(pieces)], index))
     total_ref = refs.pop(0)
     cells = [refs.pop(0), refs.pop(0)]
     hidden_ref = refs.pop(0)
@@ -129,7 +133,7 @@
     for q in range(3):
         held[q, pl.ds(cols, cols), :] = zero
         held[q, pl.ds(2 * cols, cols), :] = zero
-    for edge_a, edge_b, weight_ref, index in sides:
+    for edge_a, edge_b, weight_refs, index in sides:
         top, bottom = halo_pieces(edge_a, edge_b, index)
         place_columns(held, 0, top, group, cols, True)
         place_columns(held, 3 * cols, bottom, group, cols, True)
@@ -138,7 +142,7 @@
             for q in range(3):
                 window = held[q, row0 : row0 + side, :]
                 total = total + lax.dot_general(
-                    tap(weight_ref, p, q), window, NT, preferred_element_type=jnp.float32
+                    tap(weight_refs, p, q), window, NT, preferred_element_type=jnp.float32
                 )
             summed[:, lane0 : lane0 + side] = total
     for half in range(2):
@@ -166,7 +170,7 @@
             for q in range(3):
                 window = source[q, p * width : (p + count) * width, :]
                 total = total + lax.dot_general(
-                    window, tap(weight_ref, p, q), NN, preferred_element_type=jnp.float32
+                    window, tap([weight_ref], p, q), NN, preferred_element_type=jnp.float32
                 )
         return total
 
@@ -213,14 +217,14 @@
     )(*(pltpu.with_memory_space_constraint(source, pltpu.HBM) for source in sources))
 
 
-def conv_call(parts, index, edges, weight, init, cols):
+def conv_call(parts, index, edges, edge_index, weights, init, cols):
     groups = len(parts)
     count = parts[0].shape[1]
-    channels = weight.shape[-1]
-    outs = 2 * weight.shape[3]
-    operands = list(parts) + ([] if edges is None else list(edges)) + [weight, init]
+    channels = weights[0].shape[-1]
+    outs = 2 * weights[0].shape[3]
+    operands = [*parts, *edges, *weights, init]
     return pl.pallas_call(
-        functools.partial(conv_kernel, groups, cols, index, edges is not None),
+        functools.partial(conv_kernel, groups, cols, index, edge_index if edges else None),
         in_specs=[WHOLE] * len(operands),
         out_specs=WHOLE,
         out_shape=jax.ShapeDtypeStruct((outs, count), jnp.float32),
@@ -232,16 +236,16 @@
 
 def gate_call(sides, total, cells, cols, turn_in, turn_out):
     outs, count = total.shape
-    channels = sides[0][2].shape[-1]
+    channels = sides[0][2][0].shape[-1]
     share = outs // 8
     width = 2 * share
     cell_shape = (count, share) if turn_out else (share, count)
     operands = []
-    for edges, _, weight in sides:
-        operands += [*edges, weight]
+    for edges, _, weights in sides:
+        operands += [*edges, *weights]
     operands += [total, *cells]
     return pl.pallas_call(
-        functools.partial(gate_kernel, cols, [index for _, index, _ in sides], turn_in, turn_out),
+        functools.partial(gate_kernel, cols, [(index, len(weights)) for _, index, weights in sides], turn_in, turn_out),
         in_specs=[WHOLE] * len(operands),
         out_specs=[WHOLE] * 3,
         out_shape=[jax.ShapeDtypeStruct((1, count, width), jnp.bfloat16)]
@@ -332,8 +336,8 @@
         return first, second
 
     def edges_of(parts):
-        top = jnp.stack([part[:, :cols] for part in parts], 1)
-        bottom = jnp.stack([part[:, count - cols :] for part in parts], 1)
+        top = jnp.stack([part[:, :cols] for part in parts])
+        bottom = jnp.stack([part[:, count - cols :] for part in parts])
         return swapped_edges(top, bottom)
 
     def gate_major(weight):
@@ -357,24 +361,16 @@
     margin = (tile - inner) // 2
     starts = [lax.bitwise_xor(group, k) * inner for k in range(groups)]
     out_starts = [margin + core * (inner // 2), margin + (1 - core) * (inner // 2)]
-    (lead, starts, out_starts), frames, cell_start, gate_bias, input_own, hidden_own, first_weight, second_weight = (
+    input_own, hidden_own = gate_major(input_weight), gate_major(hidden_weight)
+    input_pair, hidden_pair = swap(input_own), swap(hidden_own)
+    (lead, starts, out_starts), frames, cell_start, gate_bias, first_weight, second_weight = (
         lax.optimization_barrier(
-            (
-                (lead, starts, out_starts),
-                frames,
-                cell_start,
-                gate_bias,
-                gate_major(input_weight),
-                gate_major(hidden_weight),
-                first_weight,
-                second_weight,
-            )
+            ((lead, starts, out_starts), frames, cell_start, gate_bias, first_weight, second_weight)
         )
     )
     lead_parts = gathered(lead)
-    input_pair, hidden_pair = swap(input_own), swap(hidden_own)
-    input_both = stage_call(input_own, input_pair)
-    hidden_both = stage_call(hidden_own, hidden_pair)
+    input_both = (stage_call(input_own, input_pair),)
+    hidden_both = (stage_call(hidden_own), hidden_pair[:, :, None])
     first_weight = stage_call(first_weight)
     second_weight = stage_call(second_weight)
     rest = ordered(frames_of(core, 1), swap(frames_of(1 - core, 1)), -1).reshape(steps - 1, count, width)
@@ -386,23 +382,23 @@
     lead_parts, cells, bias = lax.optimization_barrier((lead_parts, cells, bias))
     lead_edges = edges_of(lead_parts)
     rest_parts = forwarded(rest)
-    rest_edges = edges_of(rest_parts)
+    next_edges = edges_of([part[:1] for part in rest_parts])
+    later_edges = edges_of([part[1:] for part in rest_parts])
 
     for time_index in range(steps):
         if time_index == 0:
-            total = conv_call(lead_parts, 0, None, input_both, bias, cols)
             parts, part_index, edges = lead_parts, 1, lead_edges
-            sides = [(lead_edges, 0, input_both)]
+            image_parts, image_index, image_edges, edge_index = lead_parts, 0, lead_edges, 0
         else:
-            late = time_index > 1
-            total = conv_call(
-                rest_parts, time_index - 1, rest_edges if late else None, input_both, bias, cols
-            )
             parts, part_index = gathered(hidden), 0
             edges = edges_of(parts)
-            sides = [] if late else [(rest_edges, time_index - 1, input_both)]
+            image_parts, image_index = rest_parts, time_index - 1
+            image_edges, edge_index = (next_edges, 0) if time_index == 1 else (later_edges, time_index - 2)
+        late = time_index > 2
+        total = conv_call(image_parts, image_index, image_edges if late else (), edge_index, input_both, bias, cols)
+        sides = [] if late else [(image_edges, edge_index, input_both)]
         sides.append((edges, part_index, hidden_both))
-        total = conv_call(parts, part_index, None, hidden_both, total, cols)
+        total = conv_call(parts, part_index, (), 0, hidden_both, total, cols)
         hidden, *cells = gate_call(sides, total, cells, cols, time_index == 0, time_index == steps - 1)
 
     image = jnp.pad(hidden.reshape(rows, cols, width), ((0, 0), (margin, margin), (0, 0)))
@@ -417,8 +413,8 @@
     ]
     rim = 2 * tile
     tile_edges = swapped_edges(
-        jnp.stack([part[:rim] for part in tiles])[None],
-        jnp.stack([part[rows * tile - rim :] for part in tiles])[None],
+        jnp.stack([part[:rim] for part in tiles])[:, None],
+        jnp.stack([part[rows * tile - rim :] for part in tiles])[:, None],
     )
     decoded = decoder_call(
         tiles, tile_edges, first_weight, first_bias, second_weight, second_bias, rows, tile, margin, inner

time: 126 us -> 126 us (level)
  local copies, waits for them, and re-layouts: 6.21 us -> 2.24 us
  waiting for transfers between devices: 35.7 us -> 38.5 us
    ppermute x12, waiting for transfers between devices: 10.6 us -> 16.2 us  [gathered(): lax.ppermute(value, 'hid', [(i, i ^ 2 * k) for i in range(2 * groups)])]
    ppermute x12, starting transfers between devices: 22.9 us -> 19.1 us  [gathered(): lax.ppermute(value, 'hid', [(i, i ^ 2 * k) for i in range(2 * groups)])]
    ppermute x3, waiting for transfers between devices: 13.7 us -> 9.99 us  [across(): lax.ppermute(value, 'hid', [(i, i ^ 2 * k) for i in range(2 * groups)])]
    ppermute x6 -> x7, starting transfers between devices: 6.26 us -> 9.36 us  [swapped_edges(): first = lax.ppermute(jnp.where(even, bottom, top), 'patch', inner_pairs)]
    unnamed x6 -> x10, local copies, waits for them, and re-layouts: 1.39 us -> 0.02 us
    ppermute x3, starting transfers between devices: 0.7 us -> 2.05 us  [across(): lax.ppermute(value, 'hid', [(i, i ^ 2 * k) for i in range(2 * groups)])]
    ppermute x6 -> x7, starting transfers between devices: 11.6 us -> 12.3 us  [swapped_edges(): second = lax.ppermute(jnp.where(even, top, bottom), 'patch', outer_pairs)]
    ppermute x6 -> x7, waiting for transfers between devices: 4.51 us -> 4.66 us  [swapped_edges(): second = lax.ppermute(jnp.where(even, top, bottom), 'patch', outer_pairs)]
  transfers between devices with their start and end apart: 38 -> 40, of which waited for: 15 -> 18; matrix products, arithmetic and copies ran while one was open for 3% -> 1% of each run, Pallas kernels for 22% -> 21%
where the time goes in v7:
time: 126 us
  starting transfers between devices  49 us (39%)
  waiting for transfers between devices  38.5 us (31%)
  Pallas kernels  32.4 us (26%)
  local copies, waits for them, and re-layouts  2.24 us (2%)
  other arithmetic  2.18 us (2%)
    ppermute x12, starting transfers between devices, gathered(): lax.ppermute(value, 'hid', [(i, i ^ 2 * k) for i in range(2 * groups)])  19.1 us
    ppermute x12, waiting for transfers between devices, gathered(): lax.ppermute(value, 'hid', [(i, i ^ 2 * k) for i in range(2 * groups)])  16.2 us
    pallas_call x8, Pallas kernels, conv_call(): pl.pallas_call(functools.partial(conv_kernel, groups, cols, index, edge_i...  13.6 us
    ppermute x7, starting transfers between devices, swapped_edges(): second = lax.ppermute(jnp.where(even, top, bottom), 'patch', outer_pairs)  12.3 us
    ppermute x3, waiting for transfers between devices, across(): lax.ppermute(value, 'hid', [(i, i ^ 2 * k) for i in range(2 * groups)])  9.99 us
    ppermute x7, starting transfers between devices, swapped_edges(): first = lax.ppermute(jnp.where(even, bottom, top), 'patch', inner_pairs)  9.36 us
    pallas_call x4, Pallas kernels, stage_call(): pl.pallas_call(stage_kernel, in_specs=[pl.BlockSpec(memory_space=pltpu.HB...  8.93 us
    pallas_call x4, Pallas kernels, gate_call(): pl.pallas_call(functools.partial(gate_kernel, cols, [(index, len(weights)...  7.68 us
  transfers between devices with their start and end apart: 40, of which 18 were waited for; matrix products, arithmetic and copies ran while one was open for 1% of the time, Pallas kernels for 21%

profile of v7, /device:TPU:0, one launch (start us, length us, event | category | flops | bytes accessed | tf_op | source)
XLA Modules:
  0.0 125.5 jit_solution(15397930755765370656)
XLA Ops:
  3.2 1.7 %shard_map.114.refs_4_.refs_5_.refs_2_ = bf16[3,3,1,256,512]{4,3,2,1,0:T(8,128)(2,1)S(1)} custom-call(bf16[3,3,256,512]{3,2,1,0:T(8,128)(2,1)} %bitcast.168), custom_call_target="tpu_custom_call" | custom-call | flops 235929600 | bytes 2359296 | tf_op jit(solution)/shard_map/pallas_call | solution.py:209
  5.0 3.1 %collective-permute-start.10 = (bf16[2,256,128]{2,1,0:T(8,128)(2,1)S(1)}, bf16[2,256,128]{2,1,0:T(8,128)(2,1)S(1)}, u32[]{:S(2)}, u32[]{:S(2)}) collective-permute-start(bf16[2,256,128]{2,1,0:T(8,128)(2,1)S(1)} %maximum_select_fusion.3.refs_0_), channel_id=1, source_target_pairs={{0,2},{1,3},{2,0},{3,1},{4,6},{5,7},{6,4},{7,5},{8,10},{9,11},{10,... | collective-permute-start | bytes 393224 | tf_op jit(solution)/shard_map/ppermute | solution.py:319
  8.1 2.6 %collective-permute-start.11 = (bf16[2,256,128]{2,1,0:T(8,128)(2,1)S(1)}, bf16[2,256,128]{2,1,0:T(8,128)(2,1)S(1)}, u32[]{:S(2)}, u32[]{:S(2)}) collective-permute-start(bf16[2,256,128]{2,1,0:T(8,128)(2,1)S(1)} %maximum_select_fusion.3.refs_0_), channel_id=1, source_target_pairs={{0,4},{1,5},{2,6},{3,7},{4,0},{5,1},{6,2},{7,3},{8,12},{9,13},{10,... | collective-permute-start | bytes 393224 | tf_op jit(solution)/shard_map/ppermute | solution.py:319
  15.2 2.0 %collective-permute-start.3 = (bf16[3,256,128]{2,1,0:T(8,128)(2,1)S(1)}, bf16[3,256,128]{2,1,0:T(8,128)(2,1)S(1)}, u32[]{:S(2)}, u32[]{:S(2)}) collective-permute-start(bf16[3,256,128]{2,1,0:T(8,128)(2,1)S(1)} %maximum_select_fusion.2.refs_0_), channel_id=1, source_target_pairs={{0,4},{1,5},{2,6},{3,7},{4,0},{5,1},{6,2},{7,3},{8,12},{9,13},{10,... | collective-permute-start | bytes 589832 | tf_op jit(solution)/shard_map/ppermute | solution.py:323
  17.2 8.0 %collective-permute-done.11.refs_2_ = bf16[2,256,128]{2,1,0:T(8,128)(2,1)S(1)} collective-permute-done((bf16[2,256,128]{2,1,0:T(8,128)(2,1)S(1)}, bf16[2,256,128]{2,1,0:T(8,128)(2,1)S(1)}, u32[]{:S(2)}, u32[]{:S(2)}) %collective-permute-start.11) | collective-permute-done | bytes 131104 | tf_op jit(solution)/shard_map/ppermute | solution.py:319
  26.8 4.4 %collective-permute-done.3.refs_2_ = bf16[3,256,128]{2,1,0:T(8,128)(2,1)S(1)} collective-permute-done((bf16[3,256,128]{2,1,0:T(8,128)(2,1)S(1)}, bf16[3,256,128]{2,1,0:T(8,128)(2,1)S(1)}, u32[]{:S(2)}, u32[]{:S(2)}) %collective-permute-start.3) | collective-permute-done | bytes 196640 | tf_op jit(solution)/shard_map/ppermute | solution.py:323
  31.2 2.4 %collective-permute-start.16 = (bf16[4,2,64,128]{3,2,1,0:T(8,128)(2,1)S(1)}, bf16[4,2,64,128]{3,2,1,0:T(8,128)(2,1)S(1)}, u32[]{:S(2)}, u32[]{:S(2)}) collective-permute-start(bf16[4,2,64,128]{3,2,1,0:T(8,128)(2,1)S(1)} %get-tuple-element.68), channel_id=1, source_target_pairs={{0,24},{8,16},{16,8},{24,0},{1,25},{9,17},{17,9},{25,1},{2,26},{10... | collective-permute-start | bytes 393224 | tf_op jit(solution)/shard_map/ppermute | solution.py:335
  33.8 5.6 %collective-permute-done.4.refs_3_ = bf16[3,256,128]{2,1,0:T(8,128)(2,1)S(1)} collective-permute-done((bf16[3,256,128]{2,1,0:T(8,128)(2,1)S(1)}, bf16[3,256,128]{2,1,0:T(8,128)(2,1)S(1)}, u32[]{:S(2)}, u32[]{:S(2)}) %collective-permute-start.4) | collective-permute-done | bytes 196640 | tf_op jit(solution)/shard_map/ppermute | solution.py:323
  42.1 2.4 %shard_map.113.refs_4_.refs_2_.refs_6_ = bf16[3,3,2,256,512]{4,3,2,1,0:T(8,128)(2,1)S(1)} custom-call(bf16[3,3,256,512]{3,2,1,0:T(8,128)(2,1)} %bitcast.171, bf16[3,3,256,512]{3,2,1,0:T(8,128)(2,1)} %collective-permute-done.7.refs_1_), custom_call_target="tpu_custom_call" | custom-call | flops 471859200 | bytes 4718592 | tf_op jit(solution)/shard_map/pallas_call | solution.py:209
  44.5 1.7 %shard_map.115.refs_6_ = f32[512,256]{1,0:T(8,128)S(1)} custom-call(bf16[2,256,128]{2,1,0:T(8,128)(2,1)S(1)} %maximum_select_fusion.3.refs_0_, bf16[2,256,128]{2,1,0:T(8,128)(2,1)S(1)} %collective-permute-done.10.refs_1_, bf16[2,256,128]{2,1,0:T(8,128)(2,1)S(1)} %collective-permute-done.11.refs_2_, bf16[2,256,128]{2,1,0:T(8,128)(2,1)S(1)} %collective-permute-done.12.refs_3_, ...), custom_call_target="tpu_custom_call" | custom-call | flops 1207959552 | bytes 4718592 | tf_op jit(solution)/shard_map/pallas_call | solution.py:226
  46.3 1.8 %collective-permute-start.8 = (bf16[4,1,64,128]{3,2,1,0:T(8,128)(2,1)S(1)}, bf16[4,1,64,128]{3,2,1,0:T(8,128)(2,1)S(1)}, u32[]{:S(2)}, u32[]{:S(2)}) collective-permute-start(bf16[4,1,64,128]{3,2,1,0:T(8,128)(2,1)S(1)} %get-tuple-element.105), channel_id=1, source_target_pairs={{0,8},{8,0},{16,24},{24,16},{1,9},{9,1},{17,25},{25,17},{2,10},{10... | collective-permute-start | bytes 196616 | tf_op jit(solution)/shard_map/ppermute | solution.py:334
  50.6 2.1 %shard_map.117 = (bf16[1,256,128]{2,1,0:T(8,128)(2,1)S(1)}, f32[64,256]{1,0:T(8,128)S(1)}, f32[64,256]{1,0:T(8,128)S(1)}) custom-call(bf16[4,2,64,128]{3,2,1,0:T(8,128)(2,1)S(1)} %collective-permute-done.15.refs_0_.refs_3_, bf16[4,2,64,128]{3,2,1,0:T(8,128)(2,1)S(1)} %collective-permute-done.16.refs_1_.refs_4_, ...), custom_call_target="tpu_custom_call" | custom-call | flops 805306368 | bytes 3145728 | tf_op jit(solution)/shard_map/pallas_call | solution.py:247
  52.7 2.5 %collective-permute-start.20 = (bf16[1,256,128]{2,1,0:T(8,128)(2,1)S(1)}, bf16[1,256,128]{2,1,0:T(8,128)(2,1)S(1)}, u32[]{:S(2)}, u32[]{:S(2)}) collective-permute-start(bf16[1,256,128]{2,1,0:T(8,128)(2,1)S(1)} %get-tuple-element.44.refs_0_), channel_id=1, source_target_pairs={{0,6},{1,7},{2,4},{3,5},{4,2},{5,3},{6,0},{7,1},{8,14},{9,15},{10,... | collective-permute-start | bytes 196616 | tf_op jit(solution)/shard_map/ppermute | solution.py:319
  56.9 1.7 %shard_map.121.refs_6_ = f32[512,256]{1,0:T(8,128)S(1)} custom-call(bf16[3,256,128]{2,1,0:T(8,128)(2,1)S(1)} %maximum_select_fusion.2.refs_0_, bf16[3,256,128]{2,1,0:T(8,128)(2,1)S(1)} %collective-permute-done.2.refs_1_, bf16[3,256,128]{2,1,0:T(8,128)(2,1)S(1)} %collective-permute-done.3.refs_2_, bf16[3,256,128]{2,1,0:T(8,128)(2,1)S(1)} %collective-permute-done.4.refs_3_, ...), custom_call_target="tpu_custom_call" | custom-call | flops 1207959552 | bytes 4718592 | tf_op jit(solution)/shard_map/pallas_call | solution.py:226
  58.8 1.9 %collective-permute-start.18 = (bf16[1,256,128]{2,1,0:T(8,128)(2,1)S(1)}, bf16[1,256,128]{2,1,0:T(8,128)(2,1)S(1)}, u32[]{:S(2)}, u32[]{:S(2)}) collective-permute-start(bf16[1,256,128]{2,1,0:T(8,128)(2,1)S(1)} %get-tuple-element.44.refs_0_), channel_id=1, source_target_pairs={{0,2},{1,3},{2,0},{3,1},{4,6},{5,7},{6,4},{7,5},{8,10},{9,11},{10,... | collective-permute-start | bytes 196616 | tf_op jit(solution)/shard_map/ppermute | solution.py:319
  60.7 1.8 %shard_map.124.refs_6_ = f32[512,256]{1,0:T(8,128)S(1)} custom-call(bf16[3,256,128]{2,1,0:T(8,128)(2,1)S(1)} %maximum_select_fusion.2.refs_0_, bf16[3,256,128]{2,1,0:T(8,128)(2,1)S(1)} %collective-permute-done.2.refs_1_, bf16[3,256,128]{2,1,0:T(8,128)(2,1)S(1)} %collective-permute-done.3.refs_2_, bf16[3,256,128]{2,1,0:T(8,128)(2,1)S(1)} %collective-permute-done.4.refs_3_, ...), custom_call_target="tpu_custom_call" | custom-call | flops 1207959552 | bytes 4718592 | tf_op jit(solution)/shard_map/pallas_call | solution.py:226
  68.3 1.9 %collective-permute-done.22.refs_4_ = bf16[4,1,64,128]{3,2,1,0:T(8,128)(2,1)S(1)} collective-permute-done((bf16[4,1,64,128]{3,2,1,0:T(8,128)(2,1)S(1)}, bf16[4,1,64,128]{3,2,1,0:T(8,128)(2,1)S(1)}, u32[]{:S(2)}, u32[]{:S(2)}) %collective-permute-start.22) | collective-permute-done | bytes 65568 | tf_op jit(solution)/shard_map/ppermute | solution.py:335
  70.1 2.3 %shard_map.120 = (bf16[1,256,128]{2,1,0:T(8,128)(2,1)S(1)}, f32[64,256]{1,0:T(8,128)S(1)}, f32[64,256]{1,0:T(8,128)S(1)}) custom-call(bf16[4,1,64,128]{3,2,1,0:T(8,128)(2,1)S(1)} %collective-permute-done.8.refs_0_, bf16[4,1,64,128]{3,2,1,0:T(8,128)(2,1)S(1)} %collective-permute-done.9.refs_1_, ...), custom_call_target="tpu_custom_call" | custom-call | flops 805306368 | bytes 3145728 | tf_op jit(solution)/shard_map/pallas_call | solution.py:247
  72.4 2.2 %collective-permute-start.25 = (bf16[1,256,128]{2,1,0:T(8,128)(2,1)S(1)}, bf16[1,256,128]{2,1,0:T(8,128)(2,1)S(1)}, u32[]{:S(2)}, u32[]{:S(2)}) collective-permute-start(bf16[1,256,128]{2,1,0:T(8,128)(2,1)S(1)} %get-tuple-element.47.refs_0_), channel_id=1, source_target_pairs={{0,6},{1,7},{2,4},{3,5},{4,2},{5,3},{6,0},{7,1},{8,14},{9,15},{10,... | collective-permute-start | bytes 196616 | tf_op jit(solution)/shard_map/ppermute | solution.py:319
  75.0 1.9 %collective-permute-start.23 = (bf16[1,256,128]{2,1,0:T(8,128)(2,1)S(1)}, bf16[1,256,128]{2,1,0:T(8,128)(2,1)S(1)}, u32[]{:S(2)}, u32[]{:S(2)}) collective-permute-start(bf16[1,256,128]{2,1,0:T(8,128)(2,1)S(1)} %get-tuple-element.47.refs_0_), channel_id=1, source_target_pairs={{0,2},{1,3},{2,0},{3,1},{4,6},{5,7},{6,4},{7,5},{8,10},{9,11},{10,... | collective-permute-start | bytes 196616 | tf_op jit(solution)/shard_map/ppermute | solution.py:319
  78.6 1.8 %collective-permute-done.24.refs_2_ = bf16[1,256,128]{2,1,0:T(8,128)(2,1)S(1)} collective-permute-done((bf16[1,256,128]{2,1,0:T(8,128)(2,1)S(1)}, bf16[1,256,128]{2,1,0:T(8,128)(2,1)S(1)}, u32[]{:S(2)}, u32[]{:S(2)}) %collective-permute-start.24) | collective-permute-done | bytes 65568 | tf_op jit(solution)/shard_map/ppermute | solution.py:319
  81.5 2.1 %collective-permute-start.27 = (bf16[4,1,64,128]{3,2,1,0:T(8,128)(2,1)S(1)}, bf16[4,1,64,128]{3,2,1,0:T(8,128)(2,1)S(1)}, u32[]{:S(2)}, u32[]{:S(2)}) collective-permute-start(bf16[4,1,64,128]{3,2,1,0:T(8,128)(2,1)S(1)} %get-tuple-element.92), channel_id=1, source_target_pairs={{0,24},{8,16},{16,8},{24,0},{1,25},{9,17},{17,9},{25,1},{2,26},{10... | collective-permute-start | bytes 196616 | tf_op jit(solution)/shard_map/ppermute | solution.py:335
  86.7 2.1 %shard_map.123 = (bf16[1,256,128]{2,1,0:T(8,128)(2,1)S(1)}, f32[64,256]{1,0:T(8,128)S(1)}, f32[64,256]{1,0:T(8,128)S(1)}) custom-call(bf16[4,2,64,128]{3,2,1,0:T(8,128)(2,1)S(1)} %collective-permute-done.5.refs_0_.refs_4_, bf16[4,2,64,128]{3,2,1,0:T(8,128)(2,1)S(1)} %collective-permute-done.6.refs_1_.refs_5_, ...), custom_call_target="tpu_custom_call" | custom-call | flops 805306368 | bytes 3145728 | tf_op jit(solution)/shard_map/pallas_call | solution.py:247
  88.8 2.1 %collective-permute-start.30 = (bf16[1,256,128]{2,1,0:T(8,128)(2,1)S(1)}, bf16[1,256,128]{2,1,0:T(8,128)(2,1)S(1)}, u32[]{:S(2)}, u32[]{:S(2)}) collective-permute-start(bf16[1,256,128]{2,1,0:T(8,128)(2,1)S(1)} %get-tuple-element.50.refs_0_), channel_id=1, source_target_pairs={{0,6},{1,7},{2,4},{3,5},{4,2},{5,3},{6,0},{7,1},{8,14},{9,15},{10,... | collective-permute-start | bytes 196616 | tf_op jit(solution)/shard_map/ppermute | solution.py:319
  91.1 2.2 %collective-permute-start.28 = (bf16[1,256,128]{2,1,0:T(8,128)(2,1)S(1)}, bf16[1,256,128]{2,1,0:T(8,128)(2,1)S(1)}, u32[]{:S(2)}, u32[]{:S(2)}) collective-permute-start(bf16[1,256,128]{2,1,0:T(8,128)(2,1)S(1)} %get-tuple-element.50.refs_0_), channel_id=1, source_target_pairs={{0,2},{1,3},{2,0},{3,1},{4,6},{5,7},{6,4},{7,5},{8,10},{9,11},{10,... | collective-permute-start | bytes 196616 | tf_op jit(solution)/shard_map/ppermute | solution.py:319
  97.5 2.1 %collective-permute-start.32 = (bf16[4,1,64,128]{3,2,1,0:T(8,128)(2,1)S(1)}, bf16[4,1,64,128]{3,2,1,0:T(8,128)(2,1)S(1)}, u32[]{:S(2)}, u32[]{:S(2)}) collective-permute-start(bf16[4,1,64,128]{3,2,1,0:T(8,128)(2,1)S(1)} %get-tuple-element.90), channel_id=1, source_target_pairs={{0,24},{8,16},{16,8},{24,0},{1,25},{9,17},{17,9},{25,1},{2,26},{10... | collective-permute-start | bytes 196616 | tf_op jit(solution)/shard_map/ppermute | solution.py:335
  108.4 4.2 %collective-permute-done.35.refs_3_ = bf16[128,128]{1,0:T(8,128)(2,1)S(1)} collective-permute-done((bf16[128,128]{1,0:T(8,128)(2,1)S(1)}, bf16[128,128]{1,0:T(8,128)(2,1)S(1)}, u32[]{:S(2)}, u32[]{:S(2)}) %collective-permute-start.35) | collective-permute-done | bytes 32800 | tf_op jit(solution)/shard_map/ppermute | solution.py:411
  112.7 1.9 %collective-permute-start.36 = (bf16[4,1,64,128]{3,2,1,0:T(8,128)(2,1)S(1)}, bf16[4,1,64,128]{3,2,1,0:T(8,128)(2,1)S(1)}, u32[]{:S(2)}, u32[]{:S(2)}) collective-permute-start(bf16[4,1,64,128]{3,2,1,0:T(8,128)(2,1)S(1)} %get-tuple-element.89), channel_id=1, source_target_pairs={{0,8},{8,0},{16,24},{24,16},{1,9},{9,1},{17,25},{25,17},{2,10},{10... | collective-permute-start | bytes 196616 | tf_op jit(solution)/shard_map/ppermute | solution.py:334
  114.6 1.8 %collective-permute-start.37 = (bf16[4,1,64,128]{3,2,1,0:T(8,128)(2,1)S(1)}, bf16[4,1,64,128]{3,2,1,0:T(8,128)(2,1)S(1)}, u32[]{:S(2)}, u32[]{:S(2)}) collective-permute-start(bf16[4,1,64,128]{3,2,1,0:T(8,128)(2,1)S(1)} %get-tuple-element.88), channel_id=1, source_target_pairs={{0,24},{8,16},{16,8},{24,0},{1,25},{9,17},{17,9},{25,1},{2,26},{10... | collective-permute-start | bytes 196616 | tf_op jit(solution)/shard_map/ppermute | solution.py:335
  116.4 2.4 %shard_map.127.refs_6_ = bf16[3,3,1,512,512]{4,3,2,1,0:T(8,128)(2,1)S(1)} custom-call(bf16[3,3,512,512]{3,2,1,0:T(8,128)(2,1)} %refs_0_), custom_call_target="tpu_custom_call" | custom-call | flops 471859200 | bytes 4718592 | tf_op jit(solution)/shard_map/pallas_call | solution.py:209
  118.8 2.4 %shard_map.128.refs_8_ = bf16[3,3,1,512,512]{4,3,2,1,0:T(8,128)(2,1)S(1)} custom-call(bf16[3,3,512,512]{3,2,1,0:T(8,128)(2,1)} %refs_0_.1), custom_call_target="tpu_custom_call" | custom-call | flops 471859200 | bytes 4718592 | tf_op jit(solution)/shard_map/pallas_call | solution.py:209
  121.3 2.2 %shard_map.129 = bf16[128,512]{1,0:T(8,128)(2,1)S(1)} custom-call(bf16[128,128]{1,0:T(8,128)(2,1)S(1)} %bitcast.160, bf16[128,128]{1,0:T(8,128)(2,1)S(1)} %collective-permute-done.33.refs_1_, bf16[128,128]{1,0:T(8,128)(2,1)S(1)} %collective-permute-done.34.refs_2_, bf16[128,128]{1,0:T(8,128)(2,1)S(1)} %collective-permute-done.35.refs_3_, ...), custom_call_target="tpu_custom_call" | custom-call | flops 1509949440 | bytes 9437184 | tf_op jit(solution)/shard_map/pallas_call | solution.py:268
  (124 shorter events, 43.1 us)
Async XLA Ops:
  3.1 37.4 %collective-permute-start.7 = (bf16[3,3,256,512]{3,2,1,0:T(8,128)(2,1)}, bf16[3,3,256,512]{3,2,1,0:T(8,128)(2,1)}, u32[]{:S(2)}, u32[]{:S(2)}) collective-permute-start(bf16[3,3,256,512]{3,2,1,0:T(8,128)(2,1)} %bitcast.170), channel_id=1, source_target_pairs={{0,1},{1,0},{2,3},{3,2},{4,5},{5,4},{6,7},{7,6},{8,9},{9,8},{10,11... | collective-permute-start | bytes 7077896 | tf_op jit(solution)/shard_map/ppermute | solution.py:310
  5.0 10.1 %collective-permute-start.10 = (bf16[2,256,128]{2,1,0:T(8,128)(2,1)S(1)}, bf16[2,256,128]{2,1,0:T(8,128)(2,1)S(1)}, u32[]{:S(2)}, u32[]{:S(2)}) collective-permute-start(bf16[2,256,128]{2,1,0:T(8,128)(2,1)S(1)} %maximum_select_fusion.3.refs_0_), channel_id=1, source_target_pairs={{0,2},{1,3},{2,0},{3,1},{4,6},{5,7},{6,4},{7,5},{8,10},{9,11},{10,... | collective-permute-start | bytes 393224 | tf_op jit(solution)/shard_map/ppermute | solution.py:319
  8.1 17.1 %collective-permute-start.11 = (bf16[2,256,128]{2,1,0:T(8,128)(2,1)S(1)}, bf16[2,256,128]{2,1,0:T(8,128)(2,1)S(1)}, u32[]{:S(2)}, u32[]{:S(2)}) collective-permute-start(bf16[2,256,128]{2,1,0:T(8,128)(2,1)S(1)} %maximum_select_fusion.3.refs_0_), channel_id=1, source_target_pairs={{0,4},{1,5},{2,6},{3,7},{4,0},{5,1},{6,2},{7,3},{8,12},{9,13},{10,... | collective-permute-start | bytes 393224 | tf_op jit(solution)/shard_map/ppermute | solution.py:319
  10.7 14.5 %collective-permute-start.12 = (bf16[2,256,128]{2,1,0:T(8,128)(2,1)S(1)}, bf16[2,256,128]{2,1,0:T(8,128)(2,1)S(1)}, u32[]{:S(2)}, u32[]{:S(2)}) collective-permute-start(bf16[2,256,128]{2,1,0:T(8,128)(2,1)S(1)} %maximum_select_fusion.3.refs_0_), channel_id=1, source_target_pairs={{0,6},{1,7},{2,4},{3,5},{4,2},{5,3},{6,0},{7,1},{8,14},{9,15},{10,... | collective-permute-start | bytes 393224 | tf_op jit(solution)/shard_map/ppermute | solution.py:319
  14.8 31.5 %collective-permute-start.17 = (bf16[3,3,256,512]{3,2,1,0:T(8,128)(2,1)}, bf16[3,3,256,512]{3,2,1,0:T(8,128)(2,1)S(1)}, u32[]{:S(2)}, u32[]{:S(2)}) collective-permute-start(bf16[3,3,256,512]{3,2,1,0:T(8,128)(2,1)} %bitcast.169), channel_id=1, source_target_pairs={{0,1},{1,0},{2,3},{3,2},{4,5},{5,4},{6,7},{7,6},{8,9},{9,8},{10,11... | collective-permute-start | bytes 7077896 | tf_op jit(solution)/shard_map/ppermute | solution.py:310
  15.2 16.0 %collective-permute-start.3 = (bf16[3,256,128]{2,1,0:T(8,128)(2,1)S(1)}, bf16[3,256,128]{2,1,0:T(8,128)(2,1)S(1)}, u32[]{:S(2)}, u32[]{:S(2)}) collective-permute-start(bf16[3,256,128]{2,1,0:T(8,128)(2,1)S(1)} %maximum_select_fusion.2.refs_0_), channel_id=1, source_target_pairs={{0,4},{1,5},{2,6},{3,7},{4,0},{5,1},{6,2},{7,3},{8,12},{9,13},{10,... | collective-permute-start | bytes 589832 | tf_op jit(solution)/shard_map/ppermute | solution.py:323
  25.2 8.5 %collective-permute-start.2 = (bf16[3,256,128]{2,1,0:T(8,128)(2,1)S(1)}, bf16[3,256,128]{2,1,0:T(8,128)(2,1)S(1)}, u32[]{:S(2)}, u32[]{:S(2)}) collective-permute-start(bf16[3,256,128]{2,1,0:T(8,128)(2,1)S(1)} %maximum_select_fusion.2.refs_0_), channel_id=1, source_target_pairs={{0,2},{1,3},{2,0},{3,1},{4,6},{5,7},{6,4},{7,5},{8,10},{9,11},{10,... | collective-permute-start | bytes 589832 | tf_op jit(solution)/shard_map/ppermute | solution.py:323
  25.3 24.4 %collective-permute-start.15 = (bf16[4,2,64,128]{3,2,1,0:T(8,128)(2,1)S(1)}, bf16[4,2,64,128]{3,2,1,0:T(8,128)(2,1)S(1)}, u32[]{:S(2)}, u32[]{:S(2)}) collective-permute-start(bf16[4,2,64,128]{3,2,1,0:T(8,128)(2,1)S(1)} %get-tuple-element.69), channel_id=1, source_target_pairs={{0,8},{8,0},{16,24},{24,16},{1,9},{9,1},{17,25},{25,17},{2,10},{10... | collective-permute-start | bytes 393224 | tf_op jit(solution)/shard_map/ppermute | solution.py:334
  31.2 19.4 %collective-permute-start.16 = (bf16[4,2,64,128]{3,2,1,0:T(8,128)(2,1)S(1)}, bf16[4,2,64,128]{3,2,1,0:T(8,128)(2,1)S(1)}, u32[]{:S(2)}, u32[]{:S(2)}) collective-permute-start(bf16[4,2,64,128]{3,2,1,0:T(8,128)(2,1)S(1)} %get-tuple-element.68), channel_id=1, source_target_pairs={{0,24},{8,16},{16,8},{24,0},{1,25},{9,17},{17,9},{25,1},{2,26},{10... | collective-permute-start | bytes 393224 | tf_op jit(solution)/shard_map/ppermute | solution.py:335
  33.7 5.7 %collective-permute-start.4 = (bf16[3,256,128]{2,1,0:T(8,128)(2,1)S(1)}, bf16[3,256,128]{2,1,0:T(8,128)(2,1)S(1)}, u32[]{:S(2)}, u32[]{:S(2)}) collective-permute-start(bf16[3,256,128]{2,1,0:T(8,128)(2,1)S(1)} %collective-permute-done.3.refs_2_), channel_id=1, source_target_pairs={{0,2},{1,3},{2,0},{3,1},{4,6},{5,7},{6,4},{7,5},{8,10},{9,11},{10,... | collective-permute-start | bytes 589832 | tf_op jit(solution)/shard_map/ppermute | solution.py:323
  39.5 19.2 %collective-permute-start.5 = (bf16[4,2,64,128]{3,2,1,0:T(8,128)(2,1)S(1)}, bf16[4,2,64,128]{3,2,1,0:T(8,128)(2,1)S(1)}, u32[]{:S(2)}, u32[]{:S(2)}) collective-permute-start(bf16[4,2,64,128]{3,2,1,0:T(8,128)(2,1)S(1)} %get-tuple-element.73), channel_id=1, source_target_pairs={{0,8},{8,0},{16,24},{24,16},{1,9},{9,1},{17,25},{25,17},{2,10},{10... | collective-permute-start | bytes 393224 | tf_op jit(solution)/shard_map/ppermute | solution.py:334
  40.5 18.2 %collective-permute-start.6 = (bf16[4,2,64,128]{3,2,1,0:T(8,128)(2,1)S(1)}, bf16[4,2,64,128]{3,2,1,0:T(8,128)(2,1)S(1)}, u32[]{:S(2)}, u32[]{:S(2)}) collective-permute-start(bf16[4,2,64,128]{3,2,1,0:T(8,128)(2,1)S(1)} %get-tuple-element.72), channel_id=1, source_target_pairs={{0,24},{8,16},{16,8},{24,0},{1,25},{9,17},{17,9},{25,1},{2,26},{10... | collective-permute-start | bytes 393224 | tf_op jit(solution)/shard_map/ppermute | solution.py:335
  46.3 21.9 %collective-permute-start.8 = (bf16[4,1,64,128]{3,2,1,0:T(8,128)(2,1)S(1)}, bf16[4,1,64,128]{3,2,1,0:T(8,128)(2,1)S(1)}, u32[]{:S(2)}, u32[]{:S(2)}) collective-permute-start(bf16[4,1,64,128]{3,2,1,0:T(8,128)(2,1)S(1)} %get-tuple-element.105), channel_id=1, source_target_pairs={{0,8},{8,0},{16,24},{24,16},{1,9},{9,1},{17,25},{25,17},{2,10},{10... | collective-permute-start | bytes 196616 | tf_op jit(solution)/shard_map/ppermute | solution.py:334
  49.7 18.4 %collective-permute-start.9 = (bf16[4,1,64,128]{3,2,1,0:T(8,128)(2,1)S(1)}, bf16[4,1,64,128]{3,2,1,0:T(8,128)(2,1)S(1)}, u32[]{:S(2)}, u32[]{:S(2)}) collective-permute-start(bf16[4,1,64,128]{3,2,1,0:T(8,128)(2,1)S(1)} %get-tuple-element.104), channel_id=1, source_target_pairs={{0,24},{8,16},{16,8},{24,0},{1,25},{9,17},{17,9},{25,1},{2,26},{10... | collective-permute-start | bytes 196616 | tf_op jit(solution)/shard_map/ppermute | solution.py:335
  52.7 9.8 %collective-permute-start.20 = (bf16[1,256,128]{2,1,0:T(8,128)(2,1)S(1)}, bf16[1,256,128]{2,1,0:T(8,128)(2,1)S(1)}, u32[]{:S(2)}, u32[]{:S(2)}) collective-permute-start(bf16[1,256,128]{2,1,0:T(8,128)(2,1)S(1)} %get-tuple-element.44.refs_0_), channel_id=1, source_target_pairs={{0,6},{1,7},{2,4},{3,5},{4,2},{5,3},{6,0},{7,1},{8,14},{9,15},{10,... | collective-permute-start | bytes 196616 | tf_op jit(solution)/shard_map/ppermute | solution.py:319
  58.7 5.2 %collective-permute-start.19 = (bf16[1,256,128]{2,1,0:T(8,128)(2,1)S(1)}, bf16[1,256,128]{2,1,0:T(8,128)(2,1)S(1)}, u32[]{:S(2)}, u32[]{:S(2)}) collective-permute-start(bf16[1,256,128]{2,1,0:T(8,128)(2,1)S(1)} %get-tuple-element.44.refs_0_), channel_id=1, source_target_pairs={{0,4},{1,5},{2,6},{3,7},{4,0},{5,1},{6,2},{7,3},{8,12},{9,13},{10,... | collective-permute-start | bytes 196616 | tf_op jit(solution)/shard_map/ppermute | solution.py:319
  58.8 5.1 %collective-permute-start.18 = (bf16[1,256,128]{2,1,0:T(8,128)(2,1)S(1)}, bf16[1,256,128]{2,1,0:T(8,128)(2,1)S(1)}, u32[]{:S(2)}, u32[]{:S(2)}) collective-permute-start(bf16[1,256,128]{2,1,0:T(8,128)(2,1)S(1)} %get-tuple-element.44.refs_0_), channel_id=1, source_target_pairs={{0,2},{1,3},{2,0},{3,1},{4,6},{5,7},{6,4},{7,5},{8,10},{9,11},{10,... | collective-permute-start | bytes 196616 | tf_op jit(solution)/shard_map/ppermute | solution.py:319
  65.0 5.2 %collective-permute-start.22 = (bf16[4,1,64,128]{3,2,1,0:T(8,128)(2,1)S(1)}, bf16[4,1,64,128]{3,2,1,0:T(8,128)(2,1)S(1)}, u32[]{:S(2)}, u32[]{:S(2)}) collective-permute-start(bf16[4,1,64,128]{3,2,1,0:T(8,128)(2,1)S(1)} %get-tuple-element.94), channel_id=1, source_target_pairs={{0,24},{8,16},{16,8},{24,0},{1,25},{9,17},{17,9},{25,1},{2,26},{10... | collective-permute-start | bytes 196616 | tf_op jit(solution)/shard_map/ppermute | solution.py:335
  72.4 6.1 %collective-permute-start.25 = (bf16[1,256,128]{2,1,0:T(8,128)(2,1)S(1)}, bf16[1,256,128]{2,1,0:T(8,128)(2,1)S(1)}, u32[]{:S(2)}, u32[]{:S(2)}) collective-permute-start(bf16[1,256,128]{2,1,0:T(8,128)(2,1)S(1)} %get-tuple-element.47.refs_0_), channel_id=1, source_target_pairs={{0,6},{1,7},{2,4},{3,5},{4,2},{5,3},{6,0},{7,1},{8,14},{9,15},{10,... | collective-permute-start | bytes 196616 | tf_op jit(solution)/shard_map/ppermute | solution.py:319
  74.6 5.7 %collective-permute-start.24 = (bf16[1,256,128]{2,1,0:T(8,128)(2,1)S(1)}, bf16[1,256,128]{2,1,0:T(8,128)(2,1)S(1)}, u32[]{:S(2)}, u32[]{:S(2)}) collective-permute-start(bf16[1,256,128]{2,1,0:T(8,128)(2,1)S(1)} %get-tuple-element.47.refs_0_), channel_id=1, source_target_pairs={{0,4},{1,5},{2,6},{3,7},{4,0},{5,1},{6,2},{7,3},{8,12},{9,13},{10,... | collective-permute-start | bytes 196616 | tf_op jit(solution)/shard_map/ppermute | solution.py:319
  75.0 5.4 %collective-permute-start.23 = (bf16[1,256,128]{2,1,0:T(8,128)(2,1)S(1)}, bf16[1,256,128]{2,1,0:T(8,128)(2,1)S(1)}, u32[]{:S(2)}, u32[]{:S(2)}) collective-permute-start(bf16[1,256,128]{2,1,0:T(8,128)(2,1)S(1)} %get-tuple-element.47.refs_0_), channel_id=1, source_target_pairs={{0,2},{1,3},{2,0},{3,1},{4,6},{5,7},{6,4},{7,5},{8,10},{9,11},{10,... | collective-permute-start | bytes 196616 | tf_op jit(solution)/shard_map/ppermute | solution.py:319
  80.4 4.9 %collective-permute-start.26 = (bf16[4,1,64,128]{3,2,1,0:T(8,128)(2,1)S(1)}, bf16[4,1,64,128]{3,2,1,0:T(8,128)(2,1)S(1)}, u32[]{:S(2)}, u32[]{:S(2)}) collective-permute-start(bf16[4,1,64,128]{3,2,1,0:T(8,128)(2,1)S(1)} %get-tuple-element.93), channel_id=1, source_target_pairs={{0,8},{8,0},{16,24},{24,16},{1,9},{9,1},{17,25},{25,17},{2,10},{10... | collective-permute-start | bytes 196616 | tf_op jit(solution)/shard_map/ppermute | solution.py:334
  81.5 5.2 %collective-permute-start.27 = (bf16[4,1,64,128]{3,2,1,0:T(8,128)(2,1)S(1)}, bf16[4,1,64,128]{3,2,1,0:T(8,128)(2,1)S(1)}, u32[]{:S(2)}, u32[]{:S(2)}) collective-permute-start(bf16[4,1,64,128]{3,2,1,0:T(8,128)(2,1)S(1)} %get-tuple-element.92), channel_id=1, source_target_pairs={{0,24},{8,16},{16,8},{24,0},{1,25},{9,17},{17,9},{25,1},{2,26},{10... | collective-permute-start | bytes 196616 | tf_op jit(solution)/shard_map/ppermute | solution.py:335
  88.8 6.1 %collective-permute-start.30 = (bf16[1,256,128]{2,1,0:T(8,128)(2,1)S(1)}, bf16[1,256,128]{2,1,0:T(8,128)(2,1)S(1)}, u32[]{:S(2)}, u32[]{:S(2)}) collective-permute-start(bf16[1,256,128]{2,1,0:T(8,128)(2,1)S(1)} %get-tuple-element.50.refs_0_), channel_id=1, source_target_pairs={{0,6},{1,7},{2,4},{3,5},{4,2},{5,3},{6,0},{7,1},{8,14},{9,15},{10,... | collective-permute-start | bytes 196616 | tf_op jit(solution)/shard_map/ppermute | solution.py:319
  90.9 5.5 %collective-permute-start.29 = (bf16[1,256,128]{2,1,0:T(8,128)(2,1)S(1)}, bf16[1,256,128]{2,1,0:T(8,128)(2,1)S(1)}, u32[]{:S(2)}, u32[]{:S(2)}) collective-permute-start(bf16[1,256,128]{2,1,0:T(8,128)(2,1)S(1)} %get-tuple-element.50.refs_0_), channel_id=1, source_target_pairs={{0,4},{1,5},{2,6},{3,7},{4,0},{5,1},{6,2},{7,3},{8,12},{9,13},{10,... | collective-permute-start | bytes 196616 | tf_op jit(solution)/shard_map/ppermute | solution.py:319
  91.1 5.4 %collective-permute-start.28 = (bf16[1,256,128]{2,1,0:T(8,128)(2,1)S(1)}, bf16[1,256,128]{2,1,0:T(8,128)(2,1)S(1)}, u32[]{:S(2)}, u32[]{:S(2)}) collective-permute-start(bf16[1,256,128]{2,1,0:T(8,128)(2,1)S(1)} %get-tuple-element.50.refs_0_), channel_id=1, source_target_pairs={{0,2},{1,3},{2,0},{3,1},{4,6},{5,7},{6,4},{7,5},{8,10},{9,11},{10,... | collective-permute-start | bytes 196616 | tf_op jit(solution)/shard_map/ppermute | solution.py:319
  97.5 5.2 %collective-permute-start.32 = (bf16[4,1,64,128]{3,2,1,0:T(8,128)(2,1)S(1)}, bf16[4,1,64,128]{3,2,1,0:T(8,128)(2,1)S(1)}, u32[]{:S(2)}, u32[]{:S(2)}) collective-permute-start(bf16[4,1,64,128]{3,2,1,0:T(8,128)(2,1)S(1)} %get-tuple-element.90), channel_id=1, source_target_pairs={{0,24},{8,16},{16,8},{24,0},{1,25},{9,17},{17,9},{25,1},{2,26},{10... | collective-permute-start | bytes 196616 | tf_op jit(solution)/shard_map/ppermute | solution.py:335
  104.0 8.7 %collective-permute-start.33 = (bf16[128,128]{1,0:T(8,128)(2,1)S(1)}, bf16[128,128]{1,0:T(8,128)(2,1)S(1)}, u32[]{:S(2)}, u32[]{:S(2)}) collective-permute-start(bf16[128,128]{1,0:T(8,128)(2,1)S(1)} %bitcast.183), channel_id=1, source_target_pairs={{0,2},{1,3},{2,0},{3,1},{4,6},{5,7},{6,4},{7,5},{8,10},{9,11},{10,... | collective-permute-start | bytes 98312 | tf_op jit(solution)/shard_map/ppermute | solution.py:411
  105.6 7.0 %collective-permute-start.34 = (bf16[128,128]{1,0:T(8,128)(2,1)S(1)}, bf16[128,128]{1,0:T(8,128)(2,1)S(1)}, u32[]{:S(2)}, u32[]{:S(2)}) collective-permute-start(bf16[128,128]{1,0:T(8,128)(2,1)S(1)} %bitcast.184), channel_id=1, source_target_pairs={{0,4},{1,5},{2,6},{3,7},{4,0},{5,1},{6,2},{7,3},{8,12},{9,13},{10,... | collective-permute-start | bytes 98312 | tf_op jit(solution)/shard_map/ppermute | solution.py:411
  106.9 5.7 %collective-permute-start.35 = (bf16[128,128]{1,0:T(8,128)(2,1)S(1)}, bf16[128,128]{1,0:T(8,128)(2,1)S(1)}, u32[]{:S(2)}, u32[]{:S(2)}) collective-permute-start(bf16[128,128]{1,0:T(8,128)(2,1)S(1)} %bitcast.185), channel_id=1, source_target_pairs={{0,6},{1,7},{2,4},{3,5},{4,2},{5,3},{6,0},{7,1},{8,14},{9,15},{10,... | collective-permute-start | bytes 98312 | tf_op jit(solution)/shard_map/ppermute | solution.py:411
  112.7 8.6 %collective-permute-start.36 = (bf16[4,1,64,128]{3,2,1,0:T(8,128)(2,1)S(1)}, bf16[4,1,64,128]{3,2,1,0:T(8,128)(2,1)S(1)}, u32[]{:S(2)}, u32[]{:S(2)}) collective-permute-start(bf16[4,1,64,128]{3,2,1,0:T(8,128)(2,1)S(1)} %get-tuple-element.89), channel_id=1, source_target_pairs={{0,8},{8,0},{16,24},{24,16},{1,9},{9,1},{17,25},{25,17},{2,10},{10... | collective-permute-start | bytes 196616 | tf_op jit(solution)/shard_map/ppermute | solution.py:334
  114.6 6.7 %collective-permute-start.37 = (bf16[4,1,64,128]{3,2,1,0:T(8,128)(2,1)S(1)}, bf16[4,1,64,128]{3,2,1,0:T(8,128)(2,1)S(1)}, u32[]{:S(2)}, u32[]{:S(2)}) collective-permute-start(bf16[4,1,64,128]{3,2,1,0:T(8,128)(2,1)S(1)} %get-tuple-element.88), channel_id=1, source_target_pairs={{0,24},{8,16},{16,8},{24,0},{1,25},{9,17},{17,9},{25,1},{2,26},{10... | collective-permute-start | bytes 196616 | tf_op jit(solution)/shard_map/ppermute | solution.py:335
  (13 other events, 52.5 us)

commit v8 on v7

--- a/solution.py
+++ b/solution.py
@@ -72,6 +72,24 @@
         copy.wait()
 
 
+def fetch_kernel(frames, hidden, cell, lead0, lead1, rest0, rest1, cell0, cell1, semaphores):
+    core = lax.rem(lax.axis_index("hid"), 2)
+    steps = frames.shape[0]
+    copies = []
+    for side, (lead, rest, kept) in enumerate(((lead0, rest0, cell0), (lead1, rest1, cell1))):
+        index = core if side == 0 else 1 - core
+        moves = [(frames.at[0, index], lead.at[0]), (hidden.at[index], lead.at[1])]
+        moves += [(frames.at[t, index], rest.at[t - 1]) for t in range(1, steps)]
+        moves += [(cell.at[index], kept)]
+        copies += [
+            pltpu.make_async_copy(source, target, semaphores.at[side, i]) for i, (source, target) in enumerate(moves)
+        ]
+    for copy in copies:
+        copy.start()
+    for copy in copies:
+        copy.wait()
+
+
 def tap(weight_refs, p, q):
     weights = [weight_ref[p, q] for weight_ref in weight_refs]
     weights = [weight.reshape(-1, weight.shape[-1]) for weight in weights]
@@ -84,7 +102,10 @@
     parts = [refs.pop(0) for _ in range(groups)]
     if halo:
         edge_a, edge_b = refs.pop(0), refs.pop(0)
-    *weight_refs, init_ref, out_ref, held = refs
+    *weight_refs, out_ref, held = refs
+    inits = [weight_refs.pop()]
+    if inits[0].shape != out_ref.shape:
+        inits.append(weight_refs.pop())
     count = out_ref.shape[1]
     group = lax.axis_index("hid") // 2
 
@@ -98,11 +119,13 @@
         for q in range(3):
             held[q, pl.ds(0, cols), :] = zero
             held[q, pl.ds(cols + count, cols), :] = zero
-    if init_ref.shape == out_ref.shape:
-        total = init_ref[...]
+    if len(inits) == 1:
+        total = inits[0][...]
     else:
-        column = jnp.broadcast_to(init_ref[...], (8, out_ref.shape[0])).T
-        total = jnp.broadcast_to(column[:, :1], out_ref.shape)
+        turned = jnp.concatenate([inits[1][...], inits[0][...]]).T
+        total = jnp.concatenate(
+            [jnp.broadcast_to(turned[:, i : i + 1], (turned.shape[0], count)) for i in range(turned.shape[1])]
+        )
     for p in range(3):
         for q in range(3):
             window = held[q, p * cols : p * cols + count, :]
@@ -112,23 +135,10 @@
     out_ref[...] = total
 
 
-def gate_kernel(cols, indices, turn_in, turn_out, *refs):
-    refs = list(refs)
-    sides = []
-    for index, pieces in indices:
-        sides.append((refs.pop(0), refs.pop(0), [refs.pop(0) for _ in range(pieces)], index))
-    total_ref = refs.pop(0)
-    cells = [refs.pop(0), refs.pop(0)]
-    hidden_ref = refs.pop(0)
-    cells_out = [refs.pop(0), refs.pop(0)]
-    held, turned, summed = refs
+def add_edges(sides, summed, held, cols):
     group = lax.axis_index("hid") // 2
-    core = lax.rem(lax.axis_index("hid"), 2)
-    count = total_ref.shape[1]
-    channels = total_ref.shape[0] // 8
+    count = summed.shape[1]
     side = 2 * cols
-
-    summed[...] = total_ref[...]
     zero = jnp.zeros((cols, held.shape[2]), held.dtype)
     for q in range(3):
         held[q, pl.ds(cols, cols), :] = zero
@@ -145,6 +155,29 @@
                     tap(weight_refs, p, q), window, NT, preferred_element_type=jnp.float32
                 )
             summed[:, lane0 : lane0 + side] = total
+
+
+def side_kernel(cols, index, edge_a, edge_b, *refs):
+    *weight_refs, total_ref, out_ref, held = refs
+    out_ref[...] = total_ref[...]
+    add_edges([(edge_a, edge_b, weight_refs, index)], out_ref, held, cols)
+
+
+def gate_kernel(cols, indices, turn_in, turn_out, *refs):
+    refs = list(refs)
+    sides = []
+    for index, pieces in indices:
+        sides.append((refs.pop(0), refs.pop(0), [refs.pop(0) for _ in range(pieces)], index))
+    total_ref = refs.pop(0)
+    cells = [refs.pop(0), refs.pop(0)]
+    hidden_ref = refs.pop(0)
+    cells_out = [refs.pop(0), refs.pop(0)]
+    held, turned, summed = refs
+    core = lax.rem(lax.axis_index("hid"), 2)
+    channels = total_ref.shape[0] // 8
+
+    summed[...] = total_ref[...]
+    add_edges(sides, summed, held, cols)
     for half in range(2):
         base = half * 4 * channels
         z0, z1, z2, z3 = (summed[base + i * channels : base + (i + 1) * channels, :] for i in range(4))
@@ -217,12 +250,41 @@
     )(*(pltpu.with_memory_space_constraint(source, pltpu.HBM) for source in sources))
 
 
-def conv_call(parts, index, edges, edge_index, weights, init, cols):
+def fetch_call(frames, hidden, cell):
+    steps, _, *block = frames.shape
+    pair = [pltpu.VMEM((2, *block), frames.dtype)] * 2
+    pair += [pltpu.VMEM((steps - 1, *block), frames.dtype)] * 2
+    pair += [pltpu.VMEM(tuple(block), cell.dtype)] * 2
+    return pl.pallas_call(
+        fetch_kernel,
+        in_specs=[pl.BlockSpec(memory_space=pltpu.HBM)] * 3,
+        out_specs=[WHOLE] * 6,
+        out_shape=pair,
+        scratch_shapes=[pltpu.SemaphoreType.DMA((2, steps + 2))],
+        compiler_params=params(),
+        cost_estimate=cost(1000, 4 * frames.size),
+    )(*(pltpu.with_memory_space_constraint(source, pltpu.HBM) for source in (frames, hidden, cell)))
+
+
+def side_call(edges, index, weights, total, cols):
+    operands = [*edges, *weights, total]
+    return pl.pallas_call(
+        functools.partial(side_kernel, cols, index),
+        in_specs=[WHOLE] * len(operands),
+        out_specs=WHOLE,
+        out_shape=jax.ShapeDtypeStruct(total.shape, total.dtype),
+        scratch_shapes=[pltpu.VMEM((3, 4 * cols, weights[0].shape[-1]), jnp.bfloat16)],
+        compiler_params=params(),
+        cost_estimate=cost(3 * total.size * weights[0].shape[-1], 4 * total.size),
+    )(*operands)
+
+
+def conv_call(parts, index, edges, edge_index, weights, inits, cols):
     groups = len(parts)
     count = parts[0].shape[1]
     channels = weights[0].shape[-1]
     outs = 2 * weights[0].shape[3]
-    operands = [*parts, *edges, *weights, init]
+    operands = [*parts, *edges, *weights, *inits]
     return pl.pallas_call(
         functools.partial(conv_kernel, groups, cols, index, edge_index if edges else None),
         in_specs=[WHOLE] * len(operands),
@@ -309,11 +371,6 @@
     def swap(value):
         return lax.ppermute(value, "hid", pairs)
 
-    def own_batch(value, axis):
-        mine = lax.dynamic_index_in_dim(value, core, axis, keepdims=False, allow_negative_indices=False)
-        other = lax.dynamic_index_in_dim(value, 1 - core, axis, keepdims=False, allow_negative_indices=False)
-        return mine, swap(other)
-
     def gathered(value):
         return [value] + [
             lax.ppermute(value, "hid", [(i, i ^ (2 * k)) for i in range(2 * groups)]) for k in range(1, groups)
@@ -347,15 +404,8 @@
     def ordered(mine, other, axis):
         return jnp.where(core == 0, jnp.concatenate([mine, other], axis), jnp.concatenate([other, mine], axis))
 
-    def frames_of(index, first):
-        size = (steps - 1 if first else 1, 1) + frames.shape[2:]
-        return lax.dynamic_slice(frames, (first, index, 0, 0, 0), size, allow_negative_indices=False)[:, 0]
-
-    def of_batch(index):
-        state = lax.dynamic_slice_in_dim(hidden_start, index, 1, 0, allow_negative_indices=False)
-        return jnp.concatenate([frames_of(index, 0), state], 0)
-
-    lead = ordered(of_batch(core), swap(of_batch(1 - core)), -1).reshape(2, count, width)
+    lead_mine, lead_other, rest_mine, rest_other, cell_mine, cell_other = fetch_call(frames, hidden_start, cell_start)
+    lead = ordered(lead_mine, swap(lead_other), -1).reshape(2, count, width)
     inner = cols // groups
     tile = -(-(inner + 4) // 16) * 16
     margin = (tile - inner) // 2
@@ -363,9 +413,9 @@
     out_starts = [margin + core * (inner // 2), margin + (1 - core) * (inner // 2)]
     input_own, hidden_own = gate_major(input_weight), gate_major(hidden_weight)
     input_pair, hidden_pair = swap(input_own), swap(hidden_own)
-    (lead, starts, out_starts), frames, cell_start, gate_bias, first_weight, second_weight = (
+    (lead, starts, out_starts), rest_other, cell_other, gate_bias, first_weight, second_weight = (
         lax.optimization_barrier(
-            ((lead, starts, out_starts), frames, cell_start, gate_bias, first_weight, second_weight)
+            ((lead, starts, out_starts), rest_other, cell_other, gate_bias, first_weight, second_weight)
         )
     )
     lead_parts = gathered(lead)
@@ -373,11 +423,10 @@
     hidden_both = (stage_call(hidden_own), hidden_pair[:, :, None])
     first_weight = stage_call(first_weight)
     second_weight = stage_call(second_weight)
-    rest = ordered(frames_of(core, 1), swap(frames_of(1 - core, 1)), -1).reshape(steps - 1, count, width)
-    cell_mine, cell_other = own_batch(cell_start, 0)
-    cells = [cell_mine.reshape(count, share), cell_other.reshape(count, share)]
-    bias_own = gate_bias.reshape(-1)
-    bias = jnp.concatenate([bias_own, swap(bias_own)]).reshape(1, -1)
+    rest = ordered(rest_mine, swap(rest_other), -1).reshape(steps - 1, count, width)
+    rest = lax.optimization_barrier(rest)
+    cells = [cell.reshape(count, share) for cell in (cell_mine, swap(cell_other))]
+    bias = [gate_bias, swap(gate_bias)]
 
     lead_parts, cells, bias = lax.optimization_barrier((lead_parts, cells, bias))
     lead_edges = edges_of(lead_parts)
@@ -396,9 +445,11 @@
             image_edges, edge_index = (next_edges, 0) if time_index == 1 else (later_edges, time_index - 2)
         late = time_index > 2
         total = conv_call(image_parts, image_index, image_edges if late else (), edge_index, input_both, bias, cols)
-        sides = [] if late else [(image_edges, edge_index, input_both)]
+        sides = [(image_edges, edge_index, input_both)] if time_index == 0 else []
         sides.append((edges, part_index, hidden_both))
-        total = conv_call(parts, part_index, (), 0, hidden_both, total, cols)
+        total = conv_call(parts, part_index, (), 0, hidden_both, [total], cols)
+        if 0 < time_index and not late:
+            total = side_call(image_edges, edge_index, input_both, total, cols)
         hidden, *cells = gate_call(sides, total, cells, cols, time_index == 0, time_index == steps - 1)
 
     image = jnp.pad(hidden.reshape(rows, cols, width), ((0, 0), (margin, margin), (0, 0)))

time: 126 us -> 133 us (1.056)
  waiting for transfers between devices: 38.5 us -> 43.5 us
  starting transfers between devices: 49 us -> 51.8 us
  local copies, waits for them, and re-layouts: 2.24 us -> 0.27 us
  Pallas kernels: 32.4 us -> 34 us
    ppermute x12, waiting for transfers between devices: 16.2 us -> 20.2 us  [gathered(): lax.ppermute(value, 'hid', [(i, i ^ 2 * k) for i in range(2 * groups)])]
    pallas_call x0 -> x3, Pallas kernels: none -> 3.57 us  [the longest x2 2.2 us: side_call(): pl.pallas_call(functools.partial(side_kernel, cols, index), in_specs=[WHO...]
    ppermute x12, starting transfers between devices: 19.1 us -> 21.5 us  [gathered(): lax.ppermute(value, 'hid', [(i, i ^ 2 * k) for i in range(2 * groups)])]
    ppermute x3, waiting for transfers between devices: 9.99 us -> 12.2 us  [across(): lax.ppermute(value, 'hid', [(i, i ^ 2 * k) for i in range(2 * groups)])]
    dynamic_slice x3 -> x0, local copies, waits for them, and re-layouts: 1.84 us -> none  [the longest x1 0.92 us: of_batch(): lax.dynamic_slice_in_dim(hidden_start, index, 1, 0, allow_negative_indice...]
    pallas_call x4, Pallas kernels: 7.68 us -> 5.9 us  [gate_call(): pl.pallas_call(functools.partial(gate_kernel, cols, [(index, len(weights)...]
    ppermute x7, waiting for transfers between devices: 4.66 us -> 3.03 us  [swapped_edges(): second = lax.ppermute(jnp.where(even, top, bottom), 'patch', outer_pairs)]
  transfers between devices with their start and end apart: 40 -> 40, of which waited for: 18 -> 16; matrix products, arithmetic and copies ran while one was open for 1% -> 1% of each run, Pallas kernels for 21% -> 22%
where the time goes in v8:
time: 133 us
  starting transfers between devices  51.8 us (39%)
  waiting for transfers between devices  43.5 us (33%)
  Pallas kernels  34 us (26%)
  other arithmetic  1.93 us (1%)
    ppermute x12, starting transfers between devices, gathered(): lax.ppermute(value, 'hid', [(i, i ^ 2 * k) for i in range(2 * groups)])  21.5 us
    ppermute x12, waiting for transfers between devices, gathered(): lax.ppermute(value, 'hid', [(i, i ^ 2 * k) for i in range(2 * groups)])  20.2 us
    pallas_call x8, Pallas kernels, conv_call(): pl.pallas_call(functools.partial(conv_kernel, groups, cols, index, edge_i...  13.5 us
    ppermute x7, starting transfers between devices, swapped_edges(): second = lax.ppermute(jnp.where(even, top, bottom), 'patch', outer_pairs)  12.2 us
    ppermute x3, waiting for transfers between devices, across(): lax.ppermute(value, 'hid', [(i, i ^ 2 * k) for i in range(2 * groups)])  12.2 us
    pallas_call x4, Pallas kernels, stage_call(): pl.pallas_call(stage_kernel, in_specs=[pl.BlockSpec(memory_space=pltpu.HB...  8.87 us
    ppermute x7, starting transfers between devices, swapped_edges(): first = lax.ppermute(jnp.where(even, bottom, top), 'patch', inner_pairs)  8.74 us
    pallas_call x4, Pallas kernels, gate_call(): pl.pallas_call(functools.partial(gate_kernel, cols, [(index, len(weights)...  5.9 us
  transfers between devices with their start and end apart: 40, of which 16 were waited for; matrix products, arithmetic and copies ran while one was open for 1% of the time, Pallas kernels for 22%

profile of v8, /device:TPU:0, one launch (start us, length us, event | category | flops | bytes accessed | tf_op | source)
XLA Modules:
  0.0 132.6 jit_solution(11617379426911548858)
XLA Ops:
  6.3 2.8 %collective-permute-start.1 = (bf16[2,256,128]{2,1,0:T(8,128)(2,1)S(1)}, bf16[2,256,128]{2,1,0:T(8,128)(2,1)S(1)}, u32[]{:S(2)}, u32[]{:S(2)}) collective-permute-start(bf16[2,256,128]{2,1,0:T(8,128)(2,1)S(1)} %maximum_select_fusion.2.refs_0_), channel_id=1, source_target_pairs={{0,2},{1,3},{2,0},{3,1},{4,6},{5,7},{6,4},{7,5},{8,10},{9,11},{10,... | collective-permute-start | bytes 393224 | tf_op jit(solution)/shard_map/ppermute | solution.py:376
  9.8 2.6 %collective-permute-done.5.refs_6_.refs_8_ = f32[4,64]{1,0:T(4,128)S(1)} collective-permute-done((f32[4,64]{1,0:T(4,128)S(1)}, f32[4,64]{1,0:T(4,128)S(1)}, u32[]{:S(2)}, u32[]{:S(2)}) %collective-permute-start.5) | collective-permute-done | bytes 1056 | tf_op jit(solution)/shard_map/ppermute | solution.py:372
  12.4 3.7 %collective-permute-start.2 = (bf16[2,256,128]{2,1,0:T(8,128)(2,1)S(1)}, bf16[2,256,128]{2,1,0:T(8,128)(2,1)S(1)}, u32[]{:S(2)}, u32[]{:S(2)}) collective-permute-start(bf16[2,256,128]{2,1,0:T(8,128)(2,1)S(1)} %maximum_select_fusion.2.refs_0_), channel_id=1, source_target_pairs={{0,4},{1,5},{2,6},{3,7},{4,0},{5,1},{6,2},{7,3},{8,12},{9,13},{10,... | collective-permute-start | bytes 393224 | tf_op jit(solution)/shard_map/ppermute | solution.py:376
  17.5 1.7 %collective-permute-start.17 = (bf16[3,256,128]{2,1,0:T(8,128)(2,1)S(1)}, bf16[3,256,128]{2,1,0:T(8,128)(2,1)S(1)}, u32[]{:S(2)}, u32[]{:S(2)}) collective-permute-start(bf16[3,256,128]{2,1,0:T(8,128)(2,1)S(1)} %maximum_select_fusion.1.refs_0_), channel_id=1, source_target_pairs={{0,4},{1,5},{2,6},{3,7},{4,0},{5,1},{6,2},{7,3},{8,12},{9,13},{10,... | collective-permute-start | bytes 589832 | tf_op jit(solution)/shard_map/ppermute | solution.py:380
  19.2 11.1 %collective-permute-done.2.refs_2_ = bf16[2,256,128]{2,1,0:T(8,128)(2,1)S(1)} collective-permute-done((bf16[2,256,128]{2,1,0:T(8,128)(2,1)S(1)}, bf16[2,256,128]{2,1,0:T(8,128)(2,1)S(1)}, u32[]{:S(2)}, u32[]{:S(2)}) %collective-permute-start.2) | collective-permute-done | bytes 131104 | tf_op jit(solution)/shard_map/ppermute | solution.py:376
  32.4 4.7 %collective-permute-done.17.refs_2_ = bf16[3,256,128]{2,1,0:T(8,128)(2,1)S(1)} collective-permute-done((bf16[3,256,128]{2,1,0:T(8,128)(2,1)S(1)}, bf16[3,256,128]{2,1,0:T(8,128)(2,1)S(1)}, u32[]{:S(2)}, u32[]{:S(2)}) %collective-permute-start.17) | collective-permute-done | bytes 196640 | tf_op jit(solution)/shard_map/ppermute | solution.py:380
  37.1 2.5 %collective-permute-start.7 = (bf16[4,2,64,128]{3,2,1,0:T(8,128)(2,1)S(1)}, bf16[4,2,64,128]{3,2,1,0:T(8,128)(2,1)S(1)}, u32[]{:S(2)}, u32[]{:S(2)}) collective-permute-start(bf16[4,2,64,128]{3,2,1,0:T(8,128)(2,1)S(1)} %get-tuple-element.80), channel_id=1, source_target_pairs={{0,24},{8,16},{16,8},{24,0},{1,25},{9,17},{17,9},{25,1},{2,26},{10... | collective-permute-start | bytes 393224 | tf_op jit(solution)/shard_map/ppermute | solution.py:392
  40.9 6.4 %collective-permute-done.18.refs_3_ = bf16[3,256,128]{2,1,0:T(8,128)(2,1)S(1)} collective-permute-done((bf16[3,256,128]{2,1,0:T(8,128)(2,1)S(1)}, bf16[3,256,128]{2,1,0:T(8,128)(2,1)S(1)}, u32[]{:S(2)}, u32[]{:S(2)}) %collective-permute-start.18) | collective-permute-done | bytes 196640 | tf_op jit(solution)/shard_map/ppermute | solution.py:380
  49.9 2.4 %shard_map.114.refs_4_.refs_2_.refs_0_.refs_6_ = bf16[3,3,2,256,512]{4,3,2,1,0:T(8,128)(2,1)S(1)} custom-call(bf16[3,3,256,512]{3,2,1,0:T(8,128)(2,1)} %bitcast.158, bf16[3,3,256,512]{3,2,1,0:T(8,128)(2,1)} %collective-permute-done.8.refs_1_), custom_call_target="tpu_custom_call" | custom-call | flops 471859200 | bytes 4718592 | tf_op jit(solution)/shard_map/pallas_call | solution.py:242
  52.4 1.7 %shard_map.116.refs_6_ = f32[512,256]{1,0:T(8,128)S(1)} custom-call(bf16[2,256,128]{2,1,0:T(8,128)(2,1)S(1)} %maximum_select_fusion.2.refs_0_, bf16[2,256,128]{2,1,0:T(8,128)(2,1)S(1)} %collective-permute-done.1.refs_1_, bf16[2,256,128]{2,1,0:T(8,128)(2,1)S(1)} %collective-permute-done.2.refs_2_, bf16[2,256,128]{2,1,0:T(8,128)(2,1)S(1)} %collective-permute-done.3.refs_3_, ...), custom_call_target="tpu_custom_call" | custom-call | flops 1207959552 | bytes 4718592 | tf_op jit(solution)/shard_map/pallas_call | solution.py:288
  58.4 2.1 %shard_map.118 = (bf16[1,256,128]{2,1,0:T(8,128)(2,1)S(1)}, f32[64,256]{1,0:T(8,128)S(1)}, f32[64,256]{1,0:T(8,128)S(1)}) custom-call(bf16[4,2,64,128]{3,2,1,0:T(8,128)(2,1)S(1)} %collective-permute-done.6.refs_0_.refs_3_, bf16[4,2,64,128]{3,2,1,0:T(8,128)(2,1)S(1)} %collective-permute-done.7.refs_1_.refs_4_, ...), custom_call_target="tpu_custom_call" | custom-call | flops 805306368 | bytes 3145728 | tf_op jit(solution)/shard_map/pallas_call | solution.py:309
  60.5 4.2 %collective-permute-start.12 = (bf16[1,256,128]{2,1,0:T(8,128)(2,1)S(1)}, bf16[1,256,128]{2,1,0:T(8,128)(2,1)S(1)}, u32[]{:S(2)}, u32[]{:S(2)}) collective-permute-start(bf16[1,256,128]{2,1,0:T(8,128)(2,1)S(1)} %get-tuple-element.56.refs_0_), channel_id=1, source_target_pairs={{0,6},{1,7},{2,4},{3,5},{4,2},{5,3},{6,0},{7,1},{8,14},{9,15},{10,... | collective-permute-start | bytes 196616 | tf_op jit(solution)/shard_map/ppermute | solution.py:376
  64.6 1.7 %shard_map.119.refs_6_ = f32[512,256]{1,0:T(8,128)S(1)} custom-call(bf16[3,256,128]{2,1,0:T(8,128)(2,1)S(1)} %maximum_select_fusion.1.refs_0_, bf16[3,256,128]{2,1,0:T(8,128)(2,1)S(1)} %collective-permute-done.16.refs_1_, bf16[3,256,128]{2,1,0:T(8,128)(2,1)S(1)} %collective-permute-done.17.refs_2_, bf16[3,256,128]{2,1,0:T(8,128)(2,1)S(1)} %collective-permute-done.18.refs_3_, ...), custom_call_target="tpu_custom_call" | custom-call | flops 1207959552 | bytes 4718592 | tf_op jit(solution)/shard_map/pallas_call | solution.py:288
  66.3 1.7 %shard_map.123.refs_6_ = f32[512,256]{1,0:T(8,128)S(1)} custom-call(bf16[3,256,128]{2,1,0:T(8,128)(2,1)S(1)} %maximum_select_fusion.1.refs_0_, bf16[3,256,128]{2,1,0:T(8,128)(2,1)S(1)} %collective-permute-done.16.refs_1_, bf16[3,256,128]{2,1,0:T(8,128)(2,1)S(1)} %collective-permute-done.17.refs_2_, bf16[3,256,128]{2,1,0:T(8,128)(2,1)S(1)} %collective-permute-done.18.refs_3_, ...), custom_call_target="tpu_custom_call" | custom-call | flops 1207959552 | bytes 4718592 | tf_op jit(solution)/shard_map/pallas_call | solution.py:288
  68.7 1.8 %shard_map.127.refs_6_ = f32[512,256]{1,0:T(8,128)S(1)} custom-call(bf16[3,256,128]{2,1,0:T(8,128)(2,1)S(1)} %maximum_select_fusion.1.refs_0_, bf16[3,256,128]{2,1,0:T(8,128)(2,1)S(1)} %collective-permute-done.16.refs_1_, bf16[3,256,128]{2,1,0:T(8,128)(2,1)S(1)} %collective-permute-done.17.refs_2_, bf16[3,256,128]{2,1,0:T(8,128)(2,1)S(1)} %collective-permute-done.18.refs_3_, ...), custom_call_target="tpu_custom_call" | custom-call | flops 1207959552 | bytes 4718592 | tf_op jit(solution)/shard_map/pallas_call | solution.py:288
  70.5 2.8 %collective-permute-done.11.refs_2_ = bf16[1,256,128]{2,1,0:T(8,128)(2,1)S(1)} collective-permute-done((bf16[1,256,128]{2,1,0:T(8,128)(2,1)S(1)}, bf16[1,256,128]{2,1,0:T(8,128)(2,1)S(1)}, u32[]{:S(2)}, u32[]{:S(2)}) %collective-permute-start.11) | collective-permute-done | bytes 65568 | tf_op jit(solution)/shard_map/ppermute | solution.py:376
  76.3 1.7 %shard_map.120.refs_1_ = f32[512,256]{1,0:T(8,128)S(1)} custom-call(bf16[1,256,128]{2,1,0:T(8,128)(2,1)S(1)} %get-tuple-element.56.refs_0_, bf16[1,256,128]{2,1,0:T(8,128)(2,1)S(1)} %collective-permute-done.10.refs_1_, bf16[1,256,128]{2,1,0:T(8,128)(2,1)S(1)} %collective-permute-done.11.refs_2_, bf16[1,256,128]{2,1,0:T(8,128)(2,1)S(1)} %collective-permute-done.12.refs_3_, ...), custom_call_target="tpu_custom_call" | custom-call | flops 1207959552 | bytes 4718592 | tf_op jit(solution)/shard_map/pallas_call | solution.py:288
  83.6 2.3 %collective-permute-start.21 = (bf16[1,256,128]{2,1,0:T(8,128)(2,1)S(1)}, bf16[1,256,128]{2,1,0:T(8,128)(2,1)S(1)}, u32[]{:S(2)}, u32[]{:S(2)}) collective-permute-start(bf16[1,256,128]{2,1,0:T(8,128)(2,1)S(1)} %get-tuple-element.61.refs_0_), channel_id=1, source_target_pairs={{0,2},{1,3},{2,0},{3,1},{4,6},{5,7},{6,4},{7,5},{8,10},{9,11},{10,... | collective-permute-start | bytes 196616 | tf_op jit(solution)/shard_map/ppermute | solution.py:376
  85.9 1.7 %collective-permute-done.23.refs_3_ = bf16[1,256,128]{2,1,0:T(8,128)(2,1)S(1)} collective-permute-done((bf16[1,256,128]{2,1,0:T(8,128)(2,1)S(1)}, bf16[1,256,128]{2,1,0:T(8,128)(2,1)S(1)}, u32[]{:S(2)}, u32[]{:S(2)}) %collective-permute-start.23) | collective-permute-done | bytes 65568 | tf_op jit(solution)/shard_map/ppermute | solution.py:376
  89.8 2.2 %collective-permute-start.25 = (bf16[4,1,64,128]{3,2,1,0:T(8,128)(2,1)S(1)}, bf16[4,1,64,128]{3,2,1,0:T(8,128)(2,1)S(1)}, u32[]{:S(2)}, u32[]{:S(2)}) collective-permute-start(bf16[4,1,64,128]{3,2,1,0:T(8,128)(2,1)S(1)} %get-tuple-element.104), channel_id=1, source_target_pairs={{0,24},{8,16},{16,8},{24,0},{1,25},{9,17},{17,9},{25,1},{2,26},{10... | collective-permute-start | bytes 196616 | tf_op jit(solution)/shard_map/ppermute | solution.py:392
  92.0 1.7 %shard_map.124.refs_1_ = f32[512,256]{1,0:T(8,128)S(1)} custom-call(bf16[1,256,128]{2,1,0:T(8,128)(2,1)S(1)} %get-tuple-element.61.refs_0_, bf16[1,256,128]{2,1,0:T(8,128)(2,1)S(1)} %collective-permute-done.21.refs_1_, bf16[1,256,128]{2,1,0:T(8,128)(2,1)S(1)} %collective-permute-done.22.refs_2_, bf16[1,256,128]{2,1,0:T(8,128)(2,1)S(1)} %collective-permute-done.23.refs_3_, ...), custom_call_target="tpu_custom_call" | custom-call | flops 1207959552 | bytes 4718592 | tf_op jit(solution)/shard_map/pallas_call | solution.py:288
  96.2 2.5 %collective-permute-start.30 = (bf16[1,256,128]{2,1,0:T(8,128)(2,1)S(1)}, bf16[1,256,128]{2,1,0:T(8,128)(2,1)S(1)}, u32[]{:S(2)}, u32[]{:S(2)}) collective-permute-start(bf16[1,256,128]{2,1,0:T(8,128)(2,1)S(1)} %get-tuple-element.64.refs_0_), channel_id=1, source_target_pairs={{0,6},{1,7},{2,4},{3,5},{4,2},{5,3},{6,0},{7,1},{8,14},{9,15},{10,... | collective-permute-start | bytes 196616 | tf_op jit(solution)/shard_map/ppermute | solution.py:376
  98.9 1.8 %collective-permute-start.28 = (bf16[1,256,128]{2,1,0:T(8,128)(2,1)S(1)}, bf16[1,256,128]{2,1,0:T(8,128)(2,1)S(1)}, u32[]{:S(2)}, u32[]{:S(2)}) collective-permute-start(bf16[1,256,128]{2,1,0:T(8,128)(2,1)S(1)} %get-tuple-element.64.refs_0_), channel_id=1, source_target_pairs={{0,2},{1,3},{2,0},{3,1},{4,6},{5,7},{6,4},{7,5},{8,10},{9,11},{10,... | collective-permute-start | bytes 196616 | tf_op jit(solution)/shard_map/ppermute | solution.py:376
  100.7 1.7 %collective-permute-done.30.refs_3_ = bf16[1,256,128]{2,1,0:T(8,128)(2,1)S(1)} collective-permute-done((bf16[1,256,128]{2,1,0:T(8,128)(2,1)S(1)}, bf16[1,256,128]{2,1,0:T(8,128)(2,1)S(1)}, u32[]{:S(2)}, u32[]{:S(2)}) %collective-permute-start.30) | collective-permute-done | bytes 65568 | tf_op jit(solution)/shard_map/ppermute | solution.py:376
  106.7 1.7 %shard_map.128.refs_4_ = f32[512,256]{1,0:T(8,128)S(1)} custom-call(bf16[1,256,128]{2,1,0:T(8,128)(2,1)S(1)} %get-tuple-element.64.refs_0_, bf16[1,256,128]{2,1,0:T(8,128)(2,1)S(1)} %collective-permute-done.28.refs_1_, bf16[1,256,128]{2,1,0:T(8,128)(2,1)S(1)} %collective-permute-done.29.refs_2_, bf16[1,256,128]{2,1,0:T(8,128)(2,1)S(1)} %collective-permute-done.30.refs_3_, ...), custom_call_target="tpu_custom_call" | custom-call | flops 1207959552 | bytes 4718592 | tf_op jit(solution)/shard_map/pallas_call | solution.py:288
  108.4 2.0 %collective-permute-done.32.refs_1_ = bf16[4,1,64,128]{3,2,1,0:T(8,128)(2,1)S(1)} collective-permute-done((bf16[4,1,64,128]{3,2,1,0:T(8,128)(2,1)S(1)}, bf16[4,1,64,128]{3,2,1,0:T(8,128)(2,1)S(1)}, u32[]{:S(2)}, u32[]{:S(2)}) %collective-permute-start.32) | collective-permute-done | bytes 65568 | tf_op jit(solution)/shard_map/ppermute | solution.py:392
  113.2 1.7 %collective-permute-start.34 = (bf16[128,128]{1,0:T(8,128)(2,1)S(1)}, bf16[128,128]{1,0:T(8,128)(2,1)S(1)}, u32[]{:S(2)}, u32[]{:S(2)}) collective-permute-start(bf16[128,128]{1,0:T(8,128)(2,1)S(1)} %bitcast.165), channel_id=1, source_target_pairs={{0,4},{1,5},{2,6},{3,7},{4,0},{5,1},{6,2},{7,3},{8,12},{9,13},{10,... | collective-permute-start | bytes 98312 | tf_op jit(solution)/shard_map/ppermute | solution.py:462
  116.3 4.3 %collective-permute-done.35.refs_3_ = bf16[128,128]{1,0:T(8,128)(2,1)S(1)} collective-permute-done((bf16[128,128]{1,0:T(8,128)(2,1)S(1)}, bf16[128,128]{1,0:T(8,128)(2,1)S(1)}, u32[]{:S(2)}, u32[]{:S(2)}) %collective-permute-start.35) | collective-permute-done | bytes 32800 | tf_op jit(solution)/shard_map/ppermute | solution.py:462
  121.5 1.9 %collective-permute-start.37 = (bf16[4,1,64,128]{3,2,1,0:T(8,128)(2,1)S(1)}, bf16[4,1,64,128]{3,2,1,0:T(8,128)(2,1)S(1)}, u32[]{:S(2)}, u32[]{:S(2)}) collective-permute-start(bf16[4,1,64,128]{3,2,1,0:T(8,128)(2,1)S(1)} %get-tuple-element.100), channel_id=1, source_target_pairs={{0,24},{8,16},{16,8},{24,0},{1,25},{9,17},{17,9},{25,1},{2,26},{10... | collective-permute-start | bytes 196616 | tf_op jit(solution)/shard_map/ppermute | solution.py:392
  123.5 2.4 %shard_map.130.refs_6_ = bf16[3,3,1,512,512]{4,3,2,1,0:T(8,128)(2,1)S(1)} custom-call(bf16[3,3,512,512]{3,2,1,0:T(8,128)(2,1)} %refs_0_), custom_call_target="tpu_custom_call" | custom-call | flops 471859200 | bytes 4718592 | tf_op jit(solution)/shard_map/pallas_call | solution.py:242
  125.9 2.4 %shard_map.131.refs_8_ = bf16[3,3,1,512,512]{4,3,2,1,0:T(8,128)(2,1)S(1)} custom-call(bf16[3,3,512,512]{3,2,1,0:T(8,128)(2,1)} %refs_0_.1), custom_call_target="tpu_custom_call" | custom-call | flops 471859200 | bytes 4718592 | tf_op jit(solution)/shard_map/pallas_call | solution.py:242
  128.4 2.1 %shard_map.132 = bf16[128,512]{1,0:T(8,128)(2,1)S(1)} custom-call(bf16[128,128]{1,0:T(8,128)(2,1)S(1)} %bitcast.150, bf16[128,128]{1,0:T(8,128)(2,1)S(1)} %collective-permute-done.33.refs_1_, bf16[128,128]{1,0:T(8,128)(2,1)S(1)} %collective-permute-done.34.refs_2_, bf16[128,128]{1,0:T(8,128)(2,1)S(1)} %collective-permute-done.35.refs_3_, ...), custom_call_target="tpu_custom_call" | custom-call | flops 1509949440 | bytes 9437184 | tf_op jit(solution)/shard_map/pallas_call | solution.py:330
  (113 shorter events, 43.8 us)
Async XLA Ops:
  3.7 5.5 %collective-permute-start.15 = (bf16[3,4,64,64]{3,2,1,0:T(8,128)(2,1)S(1)}, bf16[3,4,64,64]{3,2,1,0:T(8,128)(2,1)S(1)}, u32[]{:S(2)}, u32[]{:S(2)}) collective-permute-start(bf16[3,4,64,64]{3,2,1,0:T(8,128)(2,1)S(1)} %get-tuple-element.58), channel_id=1, source_target_pairs={{0,1},{1,0},{2,3},{3,2},{4,5},{5,4},{6,7},{7,6},{8,9},{9,8},{10,11... | collective-permute-start | bytes 294920 | tf_op jit(solution)/shard_map/ppermute | solution.py:372
  4.1 44.2 %collective-permute-start.8 = (bf16[3,3,256,512]{3,2,1,0:T(8,128)(2,1)}, bf16[3,3,256,512]{3,2,1,0:T(8,128)(2,1)}, u32[]{:S(2)}, u32[]{:S(2)}) collective-permute-start(bf16[3,3,256,512]{3,2,1,0:T(8,128)(2,1)} %bitcast.157), channel_id=1, source_target_pairs={{0,1},{1,0},{2,3},{3,2},{4,5},{5,4},{6,7},{7,6},{8,9},{9,8},{10,11... | collective-permute-start | bytes 7077896 | tf_op jit(solution)/shard_map/ppermute | solution.py:372
  4.3 49.8 %collective-permute-start.9 = (bf16[3,3,256,512]{3,2,1,0:T(8,128)(2,1)}, bf16[3,3,256,512]{3,2,1,0:T(8,128)(2,1)S(1)}, u32[]{:S(2)}, u32[]{:S(2)}) collective-permute-start(bf16[3,3,256,512]{3,2,1,0:T(8,128)(2,1)} %bitcast.155), channel_id=1, source_target_pairs={{0,1},{1,0},{2,3},{3,2},{4,5},{5,4},{6,7},{7,6},{8,9},{9,8},{10,11... | collective-permute-start | bytes 7077896 | tf_op jit(solution)/shard_map/ppermute | solution.py:372
  6.3 11.2 %collective-permute-start.1 = (bf16[2,256,128]{2,1,0:T(8,128)(2,1)S(1)}, bf16[2,256,128]{2,1,0:T(8,128)(2,1)S(1)}, u32[]{:S(2)}, u32[]{:S(2)}) collective-permute-start(bf16[2,256,128]{2,1,0:T(8,128)(2,1)S(1)} %maximum_select_fusion.2.refs_0_), channel_id=1, source_target_pairs={{0,2},{1,3},{2,0},{3,1},{4,6},{5,7},{6,4},{7,5},{8,10},{9,11},{10,... | collective-permute-start | bytes 393224 | tf_op jit(solution)/shard_map/ppermute | solution.py:376
  9.1 7.1 %collective-permute-start.4 = (f32[4,64,64]{2,1,0:T(8,128)S(1)}, f32[4,64,64]{2,1,0:T(8,128)S(1)}, u32[]{:S(2)}, u32[]{:S(2)}) collective-permute-start(f32[4,64,64]{2,1,0:T(8,128)S(1)} %get-tuple-element.46), channel_id=1, source_target_pairs={{0,1},{1,0},{2,3},{3,2},{4,5},{5,4},{6,7},{7,6},{8,9},{9,8},{10,11... | collective-permute-start | bytes 196616 | tf_op jit(solution)/shard_map/ppermute | solution.py:372
  12.4 17.9 %collective-permute-start.2 = (bf16[2,256,128]{2,1,0:T(8,128)(2,1)S(1)}, bf16[2,256,128]{2,1,0:T(8,128)(2,1)S(1)}, u32[]{:S(2)}, u32[]{:S(2)}) collective-permute-start(bf16[2,256,128]{2,1,0:T(8,128)(2,1)S(1)} %maximum_select_fusion.2.refs_0_), channel_id=1, source_target_pairs={{0,4},{1,5},{2,6},{3,7},{4,0},{5,1},{6,2},{7,3},{8,12},{9,13},{10,... | collective-permute-start | bytes 393224 | tf_op jit(solution)/shard_map/ppermute | solution.py:376
  16.2 14.6 %collective-permute-start.3 = (bf16[2,256,128]{2,1,0:T(8,128)(2,1)S(1)}, bf16[2,256,128]{2,1,0:T(8,128)(2,1)S(1)}, u32[]{:S(2)}, u32[]{:S(2)}) collective-permute-start(bf16[2,256,128]{2,1,0:T(8,128)(2,1)S(1)} %maximum_select_fusion.2.refs_0_), channel_id=1, source_target_pairs={{0,6},{1,7},{2,4},{3,5},{4,2},{5,3},{6,0},{7,1},{8,14},{9,15},{10,... | collective-permute-start | bytes 393224 | tf_op jit(solution)/shard_map/ppermute | solution.py:376
  17.5 19.6 %collective-permute-start.17 = (bf16[3,256,128]{2,1,0:T(8,128)(2,1)S(1)}, bf16[3,256,128]{2,1,0:T(8,128)(2,1)S(1)}, u32[]{:S(2)}, u32[]{:S(2)}) collective-permute-start(bf16[3,256,128]{2,1,0:T(8,128)(2,1)S(1)} %maximum_select_fusion.1.refs_0_), channel_id=1, source_target_pairs={{0,4},{1,5},{2,6},{3,7},{4,0},{5,1},{6,2},{7,3},{8,12},{9,13},{10,... | collective-permute-start | bytes 589832 | tf_op jit(solution)/shard_map/ppermute | solution.py:380
  30.3 10.5 %collective-permute-start.16 = (bf16[3,256,128]{2,1,0:T(8,128)(2,1)S(1)}, bf16[3,256,128]{2,1,0:T(8,128)(2,1)S(1)}, u32[]{:S(2)}, u32[]{:S(2)}) collective-permute-start(bf16[3,256,128]{2,1,0:T(8,128)(2,1)S(1)} %maximum_select_fusion.1.refs_0_), channel_id=1, source_target_pairs={{0,2},{1,3},{2,0},{3,1},{4,6},{5,7},{6,4},{7,5},{8,10},{9,11},{10,... | collective-permute-start | bytes 589832 | tf_op jit(solution)/shard_map/ppermute | solution.py:380
  30.9 26.4 %collective-permute-start.6 = (bf16[4,2,64,128]{3,2,1,0:T(8,128)(2,1)S(1)}, bf16[4,2,64,128]{3,2,1,0:T(8,128)(2,1)S(1)}, u32[]{:S(2)}, u32[]{:S(2)}) collective-permute-start(bf16[4,2,64,128]{3,2,1,0:T(8,128)(2,1)S(1)} %get-tuple-element.81), channel_id=1, source_target_pairs={{0,8},{8,0},{16,24},{24,16},{1,9},{9,1},{17,25},{25,17},{2,10},{10... | collective-permute-start | bytes 393224 | tf_op jit(solution)/shard_map/ppermute | solution.py:391
  37.1 21.2 %collective-permute-start.7 = (bf16[4,2,64,128]{3,2,1,0:T(8,128)(2,1)S(1)}, bf16[4,2,64,128]{3,2,1,0:T(8,128)(2,1)S(1)}, u32[]{:S(2)}, u32[]{:S(2)}) collective-permute-start(bf16[4,2,64,128]{3,2,1,0:T(8,128)(2,1)S(1)} %get-tuple-element.80), channel_id=1, source_target_pairs={{0,24},{8,16},{16,8},{24,0},{1,25},{9,17},{17,9},{25,1},{2,26},{10... | collective-permute-start | bytes 393224 | tf_op jit(solution)/shard_map/ppermute | solution.py:392
  40.8 6.4 %collective-permute-start.18 = (bf16[3,256,128]{2,1,0:T(8,128)(2,1)S(1)}, bf16[3,256,128]{2,1,0:T(8,128)(2,1)S(1)}, u32[]{:S(2)}, u32[]{:S(2)}) collective-permute-start(bf16[3,256,128]{2,1,0:T(8,128)(2,1)S(1)} %collective-permute-done.17.refs_2_), channel_id=1, source_target_pairs={{0,2},{1,3},{2,0},{3,1},{4,6},{5,7},{6,4},{7,5},{8,10},{9,11},{10,... | collective-permute-start | bytes 589832 | tf_op jit(solution)/shard_map/ppermute | solution.py:380
  47.2 30.8 %collective-permute-start.19 = (bf16[4,1,64,128]{3,2,1,0:T(8,128)(2,1)S(1)}, bf16[4,1,64,128]{3,2,1,0:T(8,128)(2,1)S(1)}, u32[]{:S(2)}, u32[]{:S(2)}) collective-permute-start(bf16[4,1,64,128]{3,2,1,0:T(8,128)(2,1)S(1)} %get-tuple-element.107), channel_id=1, source_target_pairs={{0,8},{8,0},{16,24},{24,16},{1,9},{9,1},{17,25},{25,17},{2,10},{10... | collective-permute-start | bytes 196616 | tf_op jit(solution)/shard_map/ppermute | solution.py:391
  48.4 29.7 %collective-permute-start.20 = (bf16[4,1,64,128]{3,2,1,0:T(8,128)(2,1)S(1)}, bf16[4,1,64,128]{3,2,1,0:T(8,128)(2,1)S(1)}, u32[]{:S(2)}, u32[]{:S(2)}) collective-permute-start(bf16[4,1,64,128]{3,2,1,0:T(8,128)(2,1)S(1)} %get-tuple-element.106), channel_id=1, source_target_pairs={{0,24},{8,16},{16,8},{24,0},{1,25},{9,17},{17,9},{25,1},{2,26},{10... | collective-permute-start | bytes 196616 | tf_op jit(solution)/shard_map/ppermute | solution.py:392
  54.1 13.9 %collective-permute-start.26 = (bf16[4,2,64,128]{3,2,1,0:T(8,128)(2,1)S(1)}, bf16[4,2,64,128]{3,2,1,0:T(8,128)(2,1)S(1)}, u32[]{:S(2)}, u32[]{:S(2)}) collective-permute-start(bf16[4,2,64,128]{3,2,1,0:T(8,128)(2,1)S(1)} %get-tuple-element.79), channel_id=1, source_target_pairs={{0,8},{8,0},{16,24},{24,16},{1,9},{9,1},{17,25},{25,17},{2,10},{10... | collective-permute-start | bytes 393224 | tf_op jit(solution)/shard_map/ppermute | solution.py:391
  57.3 10.8 %collective-permute-start.27 = (bf16[4,2,64,128]{3,2,1,0:T(8,128)(2,1)S(1)}, bf16[4,2,64,128]{3,2,1,0:T(8,128)(2,1)S(1)}, u32[]{:S(2)}, u32[]{:S(2)}) collective-permute-start(bf16[4,2,64,128]{3,2,1,0:T(8,128)(2,1)S(1)} %get-tuple-element.78), channel_id=1, source_target_pairs={{0,24},{8,16},{16,8},{24,0},{1,25},{9,17},{17,9},{25,1},{2,26},{10... | collective-permute-start | bytes 393224 | tf_op jit(solution)/shard_map/ppermute | solution.py:392
  60.5 10.0 %collective-permute-start.12 = (bf16[1,256,128]{2,1,0:T(8,128)(2,1)S(1)}, bf16[1,256,128]{2,1,0:T(8,128)(2,1)S(1)}, u32[]{:S(2)}, u32[]{:S(2)}) collective-permute-start(bf16[1,256,128]{2,1,0:T(8,128)(2,1)S(1)} %get-tuple-element.56.refs_0_), channel_id=1, source_target_pairs={{0,6},{1,7},{2,4},{3,5},{4,2},{5,3},{6,0},{7,1},{8,14},{9,15},{10,... | collective-permute-start | bytes 196616 | tf_op jit(solution)/shard_map/ppermute | solution.py:376
  68.0 5.2 %collective-permute-start.11 = (bf16[1,256,128]{2,1,0:T(8,128)(2,1)S(1)}, bf16[1,256,128]{2,1,0:T(8,128)(2,1)S(1)}, u32[]{:S(2)}, u32[]{:S(2)}) collective-permute-start(bf16[1,256,128]{2,1,0:T(8,128)(2,1)S(1)} %get-tuple-element.56.refs_0_), channel_id=1, source_target_pairs={{0,4},{1,5},{2,6},{3,7},{4,0},{5,1},{6,2},{7,3},{8,12},{9,13},{10,... | collective-permute-start | bytes 196616 | tf_op jit(solution)/shard_map/ppermute | solution.py:376
  73.3 5.8 %collective-permute-start.13 = (bf16[4,1,64,128]{3,2,1,0:T(8,128)(2,1)S(1)}, bf16[4,1,64,128]{3,2,1,0:T(8,128)(2,1)S(1)}, u32[]{:S(2)}, u32[]{:S(2)}) collective-permute-start(bf16[4,1,64,128]{3,2,1,0:T(8,128)(2,1)S(1)} %get-tuple-element.109), channel_id=1, source_target_pairs={{0,8},{8,0},{16,24},{24,16},{1,9},{9,1},{17,25},{25,17},{2,10},{10... | collective-permute-start | bytes 196616 | tf_op jit(solution)/shard_map/ppermute | solution.py:391
  81.4 6.2 %collective-permute-start.23 = (bf16[1,256,128]{2,1,0:T(8,128)(2,1)S(1)}, bf16[1,256,128]{2,1,0:T(8,128)(2,1)S(1)}, u32[]{:S(2)}, u32[]{:S(2)}) collective-permute-start(bf16[1,256,128]{2,1,0:T(8,128)(2,1)S(1)} %get-tuple-element.61.refs_0_), channel_id=1, source_target_pairs={{0,6},{1,7},{2,4},{3,5},{4,2},{5,3},{6,0},{7,1},{8,14},{9,15},{10,... | collective-permute-start | bytes 196616 | tf_op jit(solution)/shard_map/ppermute | solution.py:376
  82.9 6.0 %collective-permute-start.22 = (bf16[1,256,128]{2,1,0:T(8,128)(2,1)S(1)}, bf16[1,256,128]{2,1,0:T(8,128)(2,1)S(1)}, u32[]{:S(2)}, u32[]{:S(2)}) collective-permute-start(bf16[1,256,128]{2,1,0:T(8,128)(2,1)S(1)} %get-tuple-element.61.refs_0_), channel_id=1, source_target_pairs={{0,4},{1,5},{2,6},{3,7},{4,0},{5,1},{6,2},{7,3},{8,12},{9,13},{10,... | collective-permute-start | bytes 196616 | tf_op jit(solution)/shard_map/ppermute | solution.py:376
  83.6 5.4 %collective-permute-start.21 = (bf16[1,256,128]{2,1,0:T(8,128)(2,1)S(1)}, bf16[1,256,128]{2,1,0:T(8,128)(2,1)S(1)}, u32[]{:S(2)}, u32[]{:S(2)}) collective-permute-start(bf16[1,256,128]{2,1,0:T(8,128)(2,1)S(1)} %get-tuple-element.61.refs_0_), channel_id=1, source_target_pairs={{0,2},{1,3},{2,0},{3,1},{4,6},{5,7},{6,4},{7,5},{8,10},{9,11},{10,... | collective-permute-start | bytes 196616 | tf_op jit(solution)/shard_map/ppermute | solution.py:376
  89.0 5.8 %collective-permute-start.24 = (bf16[4,1,64,128]{3,2,1,0:T(8,128)(2,1)S(1)}, bf16[4,1,64,128]{3,2,1,0:T(8,128)(2,1)S(1)}, u32[]{:S(2)}, u32[]{:S(2)}) collective-permute-start(bf16[4,1,64,128]{3,2,1,0:T(8,128)(2,1)S(1)} %get-tuple-element.105), channel_id=1, source_target_pairs={{0,8},{8,0},{16,24},{24,16},{1,9},{9,1},{17,25},{25,17},{2,10},{10... | collective-permute-start | bytes 196616 | tf_op jit(solution)/shard_map/ppermute | solution.py:391
  89.8 5.2 %collective-permute-start.25 = (bf16[4,1,64,128]{3,2,1,0:T(8,128)(2,1)S(1)}, bf16[4,1,64,128]{3,2,1,0:T(8,128)(2,1)S(1)}, u32[]{:S(2)}, u32[]{:S(2)}) collective-permute-start(bf16[4,1,64,128]{3,2,1,0:T(8,128)(2,1)S(1)} %get-tuple-element.104), channel_id=1, source_target_pairs={{0,24},{8,16},{16,8},{24,0},{1,25},{9,17},{17,9},{25,1},{2,26},{10... | collective-permute-start | bytes 196616 | tf_op jit(solution)/shard_map/ppermute | solution.py:392
  96.2 6.1 %collective-permute-start.30 = (bf16[1,256,128]{2,1,0:T(8,128)(2,1)S(1)}, bf16[1,256,128]{2,1,0:T(8,128)(2,1)S(1)}, u32[]{:S(2)}, u32[]{:S(2)}) collective-permute-start(bf16[1,256,128]{2,1,0:T(8,128)(2,1)S(1)} %get-tuple-element.64.refs_0_), channel_id=1, source_target_pairs={{0,6},{1,7},{2,4},{3,5},{4,2},{5,3},{6,0},{7,1},{8,14},{9,15},{10,... | collective-permute-start | bytes 196616 | tf_op jit(solution)/shard_map/ppermute | solution.py:376
  98.7 5.2 %collective-permute-start.29 = (bf16[1,256,128]{2,1,0:T(8,128)(2,1)S(1)}, bf16[1,256,128]{2,1,0:T(8,128)(2,1)S(1)}, u32[]{:S(2)}, u32[]{:S(2)}) collective-permute-start(bf16[1,256,128]{2,1,0:T(8,128)(2,1)S(1)} %get-tuple-element.64.refs_0_), channel_id=1, source_target_pairs={{0,4},{1,5},{2,6},{3,7},{4,0},{5,1},{6,2},{7,3},{8,12},{9,13},{10,... | collective-permute-start | bytes 196616 | tf_op jit(solution)/shard_map/ppermute | solution.py:376
  105.2 5.2 %collective-permute-start.32 = (bf16[4,1,64,128]{3,2,1,0:T(8,128)(2,1)S(1)}, bf16[4,1,64,128]{3,2,1,0:T(8,128)(2,1)S(1)}, u32[]{:S(2)}, u32[]{:S(2)}) collective-permute-start(bf16[4,1,64,128]{3,2,1,0:T(8,128)(2,1)S(1)} %get-tuple-element.102), channel_id=1, source_target_pairs={{0,24},{8,16},{16,8},{24,0},{1,25},{9,17},{17,9},{25,1},{2,26},{10... | collective-permute-start | bytes 196616 | tf_op jit(solution)/shard_map/ppermute | solution.py:392
  111.7 8.9 %collective-permute-start.33 = (bf16[128,128]{1,0:T(8,128)(2,1)S(1)}, bf16[128,128]{1,0:T(8,128)(2,1)S(1)}, u32[]{:S(2)}, u32[]{:S(2)}) collective-permute-start(bf16[128,128]{1,0:T(8,128)(2,1)S(1)} %bitcast.164), channel_id=1, source_target_pairs={{0,2},{1,3},{2,0},{3,1},{4,6},{5,7},{6,4},{7,5},{8,10},{9,11},{10,... | collective-permute-start | bytes 98312 | tf_op jit(solution)/shard_map/ppermute | solution.py:462
  113.2 7.4 %collective-permute-start.34 = (bf16[128,128]{1,0:T(8,128)(2,1)S(1)}, bf16[128,128]{1,0:T(8,128)(2,1)S(1)}, u32[]{:S(2)}, u32[]{:S(2)}) collective-permute-start(bf16[128,128]{1,0:T(8,128)(2,1)S(1)} %bitcast.165), channel_id=1, source_target_pairs={{0,4},{1,5},{2,6},{3,7},{4,0},{5,1},{6,2},{7,3},{8,12},{9,13},{10,... | collective-permute-start | bytes 98312 | tf_op jit(solution)/shard_map/ppermute | solution.py:462
  114.9 5.7 %collective-permute-start.35 = (bf16[128,128]{1,0:T(8,128)(2,1)S(1)}, bf16[128,128]{1,0:T(8,128)(2,1)S(1)}, u32[]{:S(2)}, u32[]{:S(2)}) collective-permute-start(bf16[128,128]{1,0:T(8,128)(2,1)S(1)} %bitcast.166), channel_id=1, source_target_pairs={{0,6},{1,7},{2,4},{3,5},{4,2},{5,3},{6,0},{7,1},{8,14},{9,15},{10,... | collective-permute-start | bytes 98312 | tf_op jit(solution)/shard_map/ppermute | solution.py:462
  120.6 7.7 %collective-permute-start.36 = (bf16[4,1,64,128]{3,2,1,0:T(8,128)(2,1)S(1)}, bf16[4,1,64,128]{3,2,1,0:T(8,128)(2,1)S(1)}, u32[]{:S(2)}, u32[]{:S(2)}) collective-permute-start(bf16[4,1,64,128]{3,2,1,0:T(8,128)(2,1)S(1)} %get-tuple-element.101), channel_id=1, source_target_pairs={{0,8},{8,0},{16,24},{24,16},{1,9},{9,1},{17,25},{25,17},{2,10},{10... | collective-permute-start | bytes 196616 | tf_op jit(solution)/shard_map/ppermute | solution.py:391
  121.5 6.8 %collective-permute-start.37 = (bf16[4,1,64,128]{3,2,1,0:T(8,128)(2,1)S(1)}, bf16[4,1,64,128]{3,2,1,0:T(8,128)(2,1)S(1)}, u32[]{:S(2)}, u32[]{:S(2)}) collective-permute-start(bf16[4,1,64,128]{3,2,1,0:T(8,128)(2,1)S(1)} %get-tuple-element.100), channel_id=1, source_target_pairs={{0,24},{8,16},{16,8},{24,0},{1,25},{9,17},{17,9},{25,1},{2,26},{10... | collective-permute-start | bytes 196616 | tf_op jit(solution)/shard_map/ppermute | solution.py:392
  (11 other events, 42.5 us)

commit v9 on v8

--- a/solution.py
+++ b/solution.py
@@ -458,10 +458,9 @@
         piece = lax.dynamic_slice_in_dim(image, starts[k], tile, axis=1, allow_negative_indices=False)
         return piece.reshape(rows * tile, width)
 
-    tiles = [columns_for(0)] + [
-        lax.ppermute(columns_for(k), "hid", [(i, i ^ (2 * k)) for i in range(2 * groups)])
-        for k in range(1, groups)
-    ]
+    tiles = [columns_for(0)]
+    for k in range(1, groups):
+        tiles.append(lax.ppermute(columns_for(k), "hid", [(i, i ^ (2 * k)) for i in range(2 * groups)]))
     rim = 2 * tile
     tile_edges = swapped_edges(
         jnp.stack([part[:rim] for part in tiles])[:, None],

time: 133 us -> 133 us (level)
  no operation moved by 1% of the time
where the time goes in v9:
time: 133 us
  starting transfers between devices  51.8 us (39%)
  waiting for transfers between devices  43.5 us (33%)
  Pallas kernels  34 us (26%)
  other arithmetic  1.93 us (1%)
    ppermute x12, starting transfers between devices, gathered(): lax.ppermute(value, 'hid', [(i, i ^ 2 * k) for i in range(2 * groups)])  21.5 us
    ppermute x12, waiting for transfers between devices, gathered(): lax.ppermute(value, 'hid', [(i, i ^ 2 * k) for i in range(2 * groups)])  20.2 us
    pallas_call x8, Pallas kernels, conv_call(): pl.pallas_call(functools.partial(conv_kernel, groups, cols, index, edge_i...  13.5 us
    ppermute x7, starting transfers between devices, swapped_edges(): second = lax.ppermute(jnp.where(even, top, bottom), 'patch', outer_pairs)  12.2 us
    ppermute x3, waiting for transfers between devices, across(): lax.ppermute(value, 'hid', [(i, i ^ 2 * k) for i in range(2 * groups)])  12.2 us
    pallas_call x4, Pallas kernels, stage_call(): pl.pallas_call(stage_kernel, in_specs=[pl.BlockSpec(memory_space=pltpu.HB...  8.87 us
    ppermute x7, starting transfers between devices, swapped_edges(): first = lax.ppermute(jnp.where(even, bottom, top), 'patch', inner_pairs)  8.74 us
    pallas_call x4, Pallas kernels, gate_call(): pl.pallas_call(functools.partial(gate_kernel, cols, [(index, len(weights)...  5.9 us
  transfers between devices with their start and end apart: 40, of which 16 were waited for; matrix products, arithmetic and copies ran while one was open for 1% of the time, Pallas kernels for 22%

profile of v9, /device:TPU:0, one launch (start us, length us, event | category | flops | bytes accessed | tf_op | source)
XLA Modules:
  0.0 132.6 jit_solution(11617379426911548858)
XLA Ops:
  6.3 2.8 %collective-permute-start.1 = (bf16[2,256,128]{2,1,0:T(8,128)(2,1)S(1)}, bf16[2,256,128]{2,1,0:T(8,128)(2,1)S(1)}, u32[]{:S(2)}, u32[]{:S(2)}) collective-permute-start(bf16[2,256,128]{2,1,0:T(8,128)(2,1)S(1)} %maximum_select_fusion.2.refs_0_), channel_id=1, source_target_pairs={{0,2},{1,3},{2,0},{3,1},{4,6},{5,7},{6,4},{7,5},{8,10},{9,11},{10,... | collective-permute-start | bytes 393224 | tf_op jit(solution)/shard_map/ppermute | solution.py:376
  9.8 2.6 %collective-permute-done.5.refs_6_.refs_8_ = f32[4,64]{1,0:T(4,128)S(1)} collective-permute-done((f32[4,64]{1,0:T(4,128)S(1)}, f32[4,64]{1,0:T(4,128)S(1)}, u32[]{:S(2)}, u32[]{:S(2)}) %collective-permute-start.5) | collective-permute-done | bytes 1056 | tf_op jit(solution)/shard_map/ppermute | solution.py:372
  12.4 3.7 %collective-permute-start.2 = (bf16[2,256,128]{2,1,0:T(8,128)(2,1)S(1)}, bf16[2,256,128]{2,1,0:T(8,128)(2,1)S(1)}, u32[]{:S(2)}, u32[]{:S(2)}) collective-permute-start(bf16[2,256,128]{2,1,0:T(8,128)(2,1)S(1)} %maximum_select_fusion.2.refs_0_), channel_id=1, source_target_pairs={{0,4},{1,5},{2,6},{3,7},{4,0},{5,1},{6,2},{7,3},{8,12},{9,13},{10,... | collective-permute-start | bytes 393224 | tf_op jit(solution)/shard_map/ppermute | solution.py:376
  17.5 1.7 %collective-permute-start.17 = (bf16[3,256,128]{2,1,0:T(8,128)(2,1)S(1)}, bf16[3,256,128]{2,1,0:T(8,128)(2,1)S(1)}, u32[]{:S(2)}, u32[]{:S(2)}) collective-permute-start(bf16[3,256,128]{2,1,0:T(8,128)(2,1)S(1)} %maximum_select_fusion.1.refs_0_), channel_id=1, source_target_pairs={{0,4},{1,5},{2,6},{3,7},{4,0},{5,1},{6,2},{7,3},{8,12},{9,13},{10,... | collective-permute-start | bytes 589832 | tf_op jit(solution)/shard_map/ppermute | solution.py:380
  19.2 11.1 %collective-permute-done.2.refs_2_ = bf16[2,256,128]{2,1,0:T(8,128)(2,1)S(1)} collective-permute-done((bf16[2,256,128]{2,1,0:T(8,128)(2,1)S(1)}, bf16[2,256,128]{2,1,0:T(8,128)(2,1)S(1)}, u32[]{:S(2)}, u32[]{:S(2)}) %collective-permute-start.2) | collective-permute-done | bytes 131104 | tf_op jit(solution)/shard_map/ppermute | solution.py:376
  32.4 4.7 %collective-permute-done.17.refs_2_ = bf16[3,256,128]{2,1,0:T(8,128)(2,1)S(1)} collective-permute-done((bf16[3,256,128]{2,1,0:T(8,128)(2,1)S(1)}, bf16[3,256,128]{2,1,0:T(8,128)(2,1)S(1)}, u32[]{:S(2)}, u32[]{:S(2)}) %collective-permute-start.17) | collective-permute-done | bytes 196640 | tf_op jit(solution)/shard_map/ppermute | solution.py:380
  37.1 2.5 %collective-permute-start.7 = (bf16[4,2,64,128]{3,2,1,0:T(8,128)(2,1)S(1)}, bf16[4,2,64,128]{3,2,1,0:T(8,128)(2,1)S(1)}, u32[]{:S(2)}, u32[]{:S(2)}) collective-permute-start(bf16[4,2,64,128]{3,2,1,0:T(8,128)(2,1)S(1)} %get-tuple-element.80), channel_id=1, source_target_pairs={{0,24},{8,16},{16,8},{24,0},{1,25},{9,17},{17,9},{25,1},{2,26},{10... | collective-permute-start | bytes 393224 | tf_op jit(solution)/shard_map/ppermute | solution.py:392
  40.9 6.4 %collective-permute-done.18.refs_3_ = bf16[3,256,128]{2,1,0:T(8,128)(2,1)S(1)} collective-permute-done((bf16[3,256,128]{2,1,0:T(8,128)(2,1)S(1)}, bf16[3,256,128]{2,1,0:T(8,128)(2,1)S(1)}, u32[]{:S(2)}, u32[]{:S(2)}) %collective-permute-start.18) | collective-permute-done | bytes 196640 | tf_op jit(solution)/shard_map/ppermute | solution.py:380
  49.9 2.4 %shard_map.114.refs_4_.refs_2_.refs_0_.refs_6_ = bf16[3,3,2,256,512]{4,3,2,1,0:T(8,128)(2,1)S(1)} custom-call(bf16[3,3,256,512]{3,2,1,0:T(8,128)(2,1)} %bitcast.158, bf16[3,3,256,512]{3,2,1,0:T(8,128)(2,1)} %collective-permute-done.8.refs_1_), custom_call_target="tpu_custom_call" | custom-call | flops 471859200 | bytes 4718592 | tf_op jit(solution)/shard_map/pallas_call | solution.py:242
  52.4 1.7 %shard_map.116.refs_6_ = f32[512,256]{1,0:T(8,128)S(1)} custom-call(bf16[2,256,128]{2,1,0:T(8,128)(2,1)S(1)} %maximum_select_fusion.2.refs_0_, bf16[2,256,128]{2,1,0:T(8,128)(2,1)S(1)} %collective-permute-done.1.refs_1_, bf16[2,256,128]{2,1,0:T(8,128)(2,1)S(1)} %collective-permute-done.2.refs_2_, bf16[2,256,128]{2,1,0:T(8,128)(2,1)S(1)} %collective-permute-done.3.refs_3_, ...), custom_call_target="tpu_custom_call" | custom-call | flops 1207959552 | bytes 4718592 | tf_op jit(solution)/shard_map/pallas_call | solution.py:288
  58.4 2.1 %shard_map.118 = (bf16[1,256,128]{2,1,0:T(8,128)(2,1)S(1)}, f32[64,256]{1,0:T(8,128)S(1)}, f32[64,256]{1,0:T(8,128)S(1)}) custom-call(bf16[4,2,64,128]{3,2,1,0:T(8,128)(2,1)S(1)} %collective-permute-done.6.refs_0_.refs_3_, bf16[4,2,64,128]{3,2,1,0:T(8,128)(2,1)S(1)} %collective-permute-done.7.refs_1_.refs_4_, ...), custom_call_target="tpu_custom_call" | custom-call | flops 805306368 | bytes 3145728 | tf_op jit(solution)/shard_map/pallas_call | solution.py:309
  60.5 4.2 %collective-permute-start.12 = (bf16[1,256,128]{2,1,0:T(8,128)(2,1)S(1)}, bf16[1,256,128]{2,1,0:T(8,128)(2,1)S(1)}, u32[]{:S(2)}, u32[]{:S(2)}) collective-permute-start(bf16[1,256,128]{2,1,0:T(8,128)(2,1)S(1)} %get-tuple-element.56.refs_0_), channel_id=1, source_target_pairs={{0,6},{1,7},{2,4},{3,5},{4,2},{5,3},{6,0},{7,1},{8,14},{9,15},{10,... | collective-permute-start | bytes 196616 | tf_op jit(solution)/shard_map/ppermute | solution.py:376
  64.6 1.7 %shard_map.119.refs_6_ = f32[512,256]{1,0:T(8,128)S(1)} custom-call(bf16[3,256,128]{2,1,0:T(8,128)(2,1)S(1)} %maximum_select_fusion.1.refs_0_, bf16[3,256,128]{2,1,0:T(8,128)(2,1)S(1)} %collective-permute-done.16.refs_1_, bf16[3,256,128]{2,1,0:T(8,128)(2,1)S(1)} %collective-permute-done.17.refs_2_, bf16[3,256,128]{2,1,0:T(8,128)(2,1)S(1)} %collective-permute-done.18.refs_3_, ...), custom_call_target="tpu_custom_call" | custom-call | flops 1207959552 | bytes 4718592 | tf_op jit(solution)/shard_map/pallas_call | solution.py:288
  66.3 1.7 %shard_map.123.refs_6_ = f32[512,256]{1,0:T(8,128)S(1)} custom-call(bf16[3,256,128]{2,1,0:T(8,128)(2,1)S(1)} %maximum_select_fusion.1.refs_0_, bf16[3,256,128]{2,1,0:T(8,128)(2,1)S(1)} %collective-permute-done.16.refs_1_, bf16[3,256,128]{2,1,0:T(8,128)(2,1)S(1)} %collective-permute-done.17.refs_2_, bf16[3,256,128]{2,1,0:T(8,128)(2,1)S(1)} %collective-permute-done.18.refs_3_, ...), custom_call_target="tpu_custom_call" | custom-call | flops 1207959552 | bytes 4718592 | tf_op jit(solution)/shard_map/pallas_call | solution.py:288
  68.7 1.8 %shard_map.127.refs_6_ = f32[512,256]{1,0:T(8,128)S(1)} custom-call(bf16[3,256,128]{2,1,0:T(8,128)(2,1)S(1)} %maximum_select_fusion.1.refs_0_, bf16[3,256,128]{2,1,0:T(8,128)(2,1)S(1)} %collective-permute-done.16.refs_1_, bf16[3,256,128]{2,1,0:T(8,128)(2,1)S(1)} %collective-permute-done.17.refs_2_, bf16[3,256,128]{2,1,0:T(8,128)(2,1)S(1)} %collective-permute-done.18.refs_3_, ...), custom_call_target="tpu_custom_call" | custom-call | flops 1207959552 | bytes 4718592 | tf_op jit(solution)/shard_map/pallas_call | solution.py:288
  70.5 2.8 %collective-permute-done.11.refs_2_ = bf16[1,256,128]{2,1,0:T(8,128)(2,1)S(1)} collective-permute-done((bf16[1,256,128]{2,1,0:T(8,128)(2,1)S(1)}, bf16[1,256,128]{2,1,0:T(8,128)(2,1)S(1)}, u32[]{:S(2)}, u32[]{:S(2)}) %collective-permute-start.11) | collective-permute-done | bytes 65568 | tf_op jit(solution)/shard_map/ppermute | solution.py:376
  76.3 1.7 %shard_map.120.refs_1_ = f32[512,256]{1,0:T(8,128)S(1)} custom-call(bf16[1,256,128]{2,1,0:T(8,128)(2,1)S(1)} %get-tuple-element.56.refs_0_, bf16[1,256,128]{2,1,0:T(8,128)(2,1)S(1)} %collective-permute-done.10.refs_1_, bf16[1,256,128]{2,1,0:T(8,128)(2,1)S(1)} %collective-permute-done.11.refs_2_, bf16[1,256,128]{2,1,0:T(8,128)(2,1)S(1)} %collective-permute-done.12.refs_3_, ...), custom_call_target="tpu_custom_call" | custom-call | flops 1207959552 | bytes 4718592 | tf_op jit(solution)/shard_map/pallas_call | solution.py:288
  83.6 2.3 %collective-permute-start.21 = (bf16[1,256,128]{2,1,0:T(8,128)(2,1)S(1)}, bf16[1,256,128]{2,1,0:T(8,128)(2,1)S(1)}, u32[]{:S(2)}, u32[]{:S(2)}) collective-permute-start(bf16[1,256,128]{2,1,0:T(8,128)(2,1)S(1)} %get-tuple-element.61.refs_0_), channel_id=1, source_target_pairs={{0,2},{1,3},{2,0},{3,1},{4,6},{5,7},{6,4},{7,5},{8,10},{9,11},{10,... | collective-permute-start | bytes 196616 | tf_op jit(solution)/shard_map/ppermute | solution.py:376
  85.9 1.7 %collective-permute-done.23.refs_3_ = bf16[1,256,128]{2,1,0:T(8,128)(2,1)S(1)} collective-permute-done((bf16[1,256,128]{2,1,0:T(8,128)(2,1)S(1)}, bf16[1,256,128]{2,1,0:T(8,128)(2,1)S(1)}, u32[]{:S(2)}, u32[]{:S(2)}) %collective-permute-start.23) | collective-permute-done | bytes 65568 | tf_op jit(solution)/shard_map/ppermute | solution.py:376
  89.8 2.2 %collective-permute-start.25 = (bf16[4,1,64,128]{3,2,1,0:T(8,128)(2,1)S(1)}, bf16[4,1,64,128]{3,2,1,0:T(8,128)(2,1)S(1)}, u32[]{:S(2)}, u32[]{:S(2)}) collective-permute-start(bf16[4,1,64,128]{3,2,1,0:T(8,128)(2,1)S(1)} %get-tuple-element.104), channel_id=1, source_target_pairs={{0,24},{8,16},{16,8},{24,0},{1,25},{9,17},{17,9},{25,1},{2,26},{10... | collective-permute-start | bytes 196616 | tf_op jit(solution)/shard_map/ppermute | solution.py:392
  92.0 1.7 %shard_map.124.refs_1_ = f32[512,256]{1,0:T(8,128)S(1)} custom-call(bf16[1,256,128]{2,1,0:T(8,128)(2,1)S(1)} %get-tuple-element.61.refs_0_, bf16[1,256,128]{2,1,0:T(8,128)(2,1)S(1)} %collective-permute-done.21.refs_1_, bf16[1,256,128]{2,1,0:T(8,128)(2,1)S(1)} %collective-permute-done.22.refs_2_, bf16[1,256,128]{2,1,0:T(8,128)(2,1)S(1)} %collective-permute-done.23.refs_3_, ...), custom_call_target="tpu_custom_call" | custom-call | flops 1207959552 | bytes 4718592 | tf_op jit(solution)/shard_map/pallas_call | solution.py:288
  96.2 2.5 %collective-permute-start.30 = (bf16[1,256,128]{2,1,0:T(8,128)(2,1)S(1)}, bf16[1,256,128]{2,1,0:T(8,128)(2,1)S(1)}, u32[]{:S(2)}, u32[]{:S(2)}) collective-permute-start(bf16[1,256,128]{2,1,0:T(8,128)(2,1)S(1)} %get-tuple-element.64.refs_0_), channel_id=1, source_target_pairs={{0,6},{1,7},{2,4},{3,5},{4,2},{5,3},{6,0},{7,1},{8,14},{9,15},{10,... | collective-permute-start | bytes 196616 | tf_op jit(solution)/shard_map/ppermute | solution.py:376
  98.9 1.8 %collective-permute-start.28 = (bf16[1,256,128]{2,1,0:T(8,128)(2,1)S(1)}, bf16[1,256,128]{2,1,0:T(8,128)(2,1)S(1)}, u32[]{:S(2)}, u32[]{:S(2)}) collective-permute-start(bf16[1,256,128]{2,1,0:T(8,128)(2,1)S(1)} %get-tuple-element.64.refs_0_), channel_id=1, source_target_pairs={{0,2},{1,3},{2,0},{3,1},{4,6},{5,7},{6,4},{7,5},{8,10},{9,11},{10,... | collective-permute-start | bytes 196616 | tf_op jit(solution)/shard_map/ppermute | solution.py:376
  100.7 1.7 %collective-permute-done.30.refs_3_ = bf16[1,256,128]{2,1,0:T(8,128)(2,1)S(1)} collective-permute-done((bf16[1,256,128]{2,1,0:T(8,128)(2,1)S(1)}, bf16[1,256,128]{2,1,0:T(8,128)(2,1)S(1)}, u32[]{:S(2)}, u32[]{:S(2)}) %collective-permute-start.30) | collective-permute-done | bytes 65568 | tf_op jit(solution)/shard_map/ppermute | solution.py:376
  106.7 1.7 %shard_map.128.refs_4_ = f32[512,256]{1,0:T(8,128)S(1)} custom-call(bf16[1,256,128]{2,1,0:T(8,128)(2,1)S(1)} %get-tuple-element.64.refs_0_, bf16[1,256,128]{2,1,0:T(8,128)(2,1)S(1)} %collective-permute-done.28.refs_1_, bf16[1,256,128]{2,1,0:T(8,128)(2,1)S(1)} %collective-permute-done.29.refs_2_, bf16[1,256,128]{2,1,0:T(8,128)(2,1)S(1)} %collective-permute-done.30.refs_3_, ...), custom_call_target="tpu_custom_call" | custom-call | flops 1207959552 | bytes 4718592 | tf_op jit(solution)/shard_map/pallas_call | solution.py:288
  108.4 2.0 %collective-permute-done.32.refs_1_ = bf16[4,1,64,128]{3,2,1,0:T(8,128)(2,1)S(1)} collective-permute-done((bf16[4,1,64,128]{3,2,1,0:T(8,128)(2,1)S(1)}, bf16[4,1,64,128]{3,2,1,0:T(8,128)(2,1)S(1)}, u32[]{:S(2)}, u32[]{:S(2)}) %collective-permute-start.32) | collective-permute-done | bytes 65568 | tf_op jit(solution)/shard_map/ppermute | solution.py:392
  113.2 1.7 %collective-permute-start.34 = (bf16[128,128]{1,0:T(8,128)(2,1)S(1)}, bf16[128,128]{1,0:T(8,128)(2,1)S(1)}, u32[]{:S(2)}, u32[]{:S(2)}) collective-permute-start(bf16[128,128]{1,0:T(8,128)(2,1)S(1)} %bitcast.165), channel_id=1, source_target_pairs={{0,4},{1,5},{2,6},{3,7},{4,0},{5,1},{6,2},{7,3},{8,12},{9,13},{10,... | collective-permute-start | bytes 98312 | tf_op jit(solution)/shard_map/ppermute | solution.py:463
  116.3 4.3 %collective-permute-done.35.refs_3_ = bf16[128,128]{1,0:T(8,128)(2,1)S(1)} collective-permute-done((bf16[128,128]{1,0:T(8,128)(2,1)S(1)}, bf16[128,128]{1,0:T(8,128)(2,1)S(1)}, u32[]{:S(2)}, u32[]{:S(2)}) %collective-permute-start.35) | collective-permute-done | bytes 32800 | tf_op jit(solution)/shard_map/ppermute | solution.py:463
  121.5 1.9 %collective-permute-start.37 = (bf16[4,1,64,128]{3,2,1,0:T(8,128)(2,1)S(1)}, bf16[4,1,64,128]{3,2,1,0:T(8,128)(2,1)S(1)}, u32[]{:S(2)}, u32[]{:S(2)}) collective-permute-start(bf16[4,1,64,128]{3,2,1,0:T(8,128)(2,1)S(1)} %get-tuple-element.100), channel_id=1, source_target_pairs={{0,24},{8,16},{16,8},{24,0},{1,25},{9,17},{17,9},{25,1},{2,26},{10... | collective-permute-start | bytes 196616 | tf_op jit(solution)/shard_map/ppermute | solution.py:392
  123.5 2.4 %shard_map.130.refs_6_ = bf16[3,3,1,512,512]{4,3,2,1,0:T(8,128)(2,1)S(1)} custom-call(bf16[3,3,512,512]{3,2,1,0:T(8,128)(2,1)} %refs_0_), custom_call_target="tpu_custom_call" | custom-call | flops 471859200 | bytes 4718592 | tf_op jit(solution)/shard_map/pallas_call | solution.py:242
  125.9 2.4 %shard_map.131.refs_8_ = bf16[3,3,1,512,512]{4,3,2,1,0:T(8,128)(2,1)S(1)} custom-call(bf16[3,3,512,512]{3,2,1,0:T(8,128)(2,1)} %refs_0_.1), custom_call_target="tpu_custom_call" | custom-call | flops 471859200 | bytes 4718592 | tf_op jit(solution)/shard_map/pallas_call | solution.py:242
  128.4 2.1 %shard_map.132 = bf16[128,512]{1,0:T(8,128)(2,1)S(1)} custom-call(bf16[128,128]{1,0:T(8,128)(2,1)S(1)} %bitcast.150, bf16[128,128]{1,0:T(8,128)(2,1)S(1)} %collective-permute-done.33.refs_1_, bf16[128,128]{1,0:T(8,128)(2,1)S(1)} %collective-permute-done.34.refs_2_, bf16[128,128]{1,0:T(8,128)(2,1)S(1)} %collective-permute-done.35.refs_3_, ...), custom_call_target="tpu_custom_call" | custom-call | flops 1509949440 | bytes 9437184 | tf_op jit(solution)/shard_map/pallas_call | solution.py:330
  (113 shorter events, 43.8 us)
Async XLA Ops:
  3.7 5.5 %collective-permute-start.15 = (bf16[3,4,64,64]{3,2,1,0:T(8,128)(2,1)S(1)}, bf16[3,4,64,64]{3,2,1,0:T(8,128)(2,1)S(1)}, u32[]{:S(2)}, u32[]{:S(2)}) collective-permute-start(bf16[3,4,64,64]{3,2,1,0:T(8,128)(2,1)S(1)} %get-tuple-element.58), channel_id=1, source_target_pairs={{0,1},{1,0},{2,3},{3,2},{4,5},{5,4},{6,7},{7,6},{8,9},{9,8},{10,11... | collective-permute-start | bytes 294920 | tf_op jit(solution)/shard_map/ppermute | solution.py:372
  4.1 44.2 %collective-permute-start.8 = (bf16[3,3,256,512]{3,2,1,0:T(8,128)(2,1)}, bf16[3,3,256,512]{3,2,1,0:T(8,128)(2,1)}, u32[]{:S(2)}, u32[]{:S(2)}) collective-permute-start(bf16[3,3,256,512]{3,2,1,0:T(8,128)(2,1)} %bitcast.157), channel_id=1, source_target_pairs={{0,1},{1,0},{2,3},{3,2},{4,5},{5,4},{6,7},{7,6},{8,9},{9,8},{10,11... | collective-permute-start | bytes 7077896 | tf_op jit(solution)/shard_map/ppermute | solution.py:372
  4.3 49.8 %collective-permute-start.9 = (bf16[3,3,256,512]{3,2,1,0:T(8,128)(2,1)}, bf16[3,3,256,512]{3,2,1,0:T(8,128)(2,1)S(1)}, u32[]{:S(2)}, u32[]{:S(2)}) collective-permute-start(bf16[3,3,256,512]{3,2,1,0:T(8,128)(2,1)} %bitcast.155), channel_id=1, source_target_pairs={{0,1},{1,0},{2,3},{3,2},{4,5},{5,4},{6,7},{7,6},{8,9},{9,8},{10,11... | collective-permute-start | bytes 7077896 | tf_op jit(solution)/shard_map/ppermute | solution.py:372
  6.3 11.2 %collective-permute-start.1 = (bf16[2,256,128]{2,1,0:T(8,128)(2,1)S(1)}, bf16[2,256,128]{2,1,0:T(8,128)(2,1)S(1)}, u32[]{:S(2)}, u32[]{:S(2)}) collective-permute-start(bf16[2,256,128]{2,1,0:T(8,128)(2,1)S(1)} %maximum_select_fusion.2.refs_0_), channel_id=1, source_target_pairs={{0,2},{1,3},{2,0},{3,1},{4,6},{5,7},{6,4},{7,5},{8,10},{9,11},{10,... | collective-permute-start | bytes 393224 | tf_op jit(solution)/shard_map/ppermute | solution.py:376
  9.1 7.1 %collective-permute-start.4 = (f32[4,64,64]{2,1,0:T(8,128)S(1)}, f32[4,64,64]{2,1,0:T(8,128)S(1)}, u32[]{:S(2)}, u32[]{:S(2)}) collective-permute-start(f32[4,64,64]{2,1,0:T(8,128)S(1)} %get-tuple-element.46), channel_id=1, source_target_pairs={{0,1},{1,0},{2,3},{3,2},{4,5},{5,4},{6,7},{7,6},{8,9},{9,8},{10,11... | collective-permute-start | bytes 196616 | tf_op jit(solution)/shard_map/ppermute | solution.py:372
  12.4 17.9 %collective-permute-start.2 = (bf16[2,256,128]{2,1,0:T(8,128)(2,1)S(1)}, bf16[2,256,128]{2,1,0:T(8,128)(2,1)S(1)}, u32[]{:S(2)}, u32[]{:S(2)}) collective-permute-start(bf16[2,256,128]{2,1,0:T(8,128)(2,1)S(1)} %maximum_select_fusion.2.refs_0_), channel_id=1, source_target_pairs={{0,4},{1,5},{2,6},{3,7},{4,0},{5,1},{6,2},{7,3},{8,12},{9,13},{10,... | collective-permute-start | bytes 393224 | tf_op jit(solution)/shard_map/ppermute | solution.py:376
  16.2 14.6 %collective-permute-start.3 = (bf16[2,256,128]{2,1,0:T(8,128)(2,1)S(1)}, bf16[2,256,128]{2,1,0:T(8,128)(2,1)S(1)}, u32[]{:S(2)}, u32[]{:S(2)}) collective-permute-start(bf16[2,256,128]{2,1,0:T(8,128)(2,1)S(1)} %maximum_select_fusion.2.refs_0_), channel_id=1, source_target_pairs={{0,6},{1,7},{2,4},{3,5},{4,2},{5,3},{6,0},{7,1},{8,14},{9,15},{10,... | collective-permute-start | bytes 393224 | tf_op jit(solution)/shard_map/ppermute | solution.py:376
  17.5 19.6 %collective-permute-start.17 = (bf16[3,256,128]{2,1,0:T(8,128)(2,1)S(1)}, bf16[3,256,128]{2,1,0:T(8,128)(2,1)S(1)}, u32[]{:S(2)}, u32[]{:S(2)}) collective-permute-start(bf16[3,256,128]{2,1,0:T(8,128)(2,1)S(1)} %maximum_select_fusion.1.refs_0_), channel_id=1, source_target_pairs={{0,4},{1,5},{2,6},{3,7},{4,0},{5,1},{6,2},{7,3},{8,12},{9,13},{10,... | collective-permute-start | bytes 589832 | tf_op jit(solution)/shard_map/ppermute | solution.py:380
  30.3 10.5 %collective-permute-start.16 = (bf16[3,256,128]{2,1,0:T(8,128)(2,1)S(1)}, bf16[3,256,128]{2,1,0:T(8,128)(2,1)S(1)}, u32[]{:S(2)}, u32[]{:S(2)}) collective-permute-start(bf16[3,256,128]{2,1,0:T(8,128)(2,1)S(1)} %maximum_select_fusion.1.refs_0_), channel_id=1, source_target_pairs={{0,2},{1,3},{2,0},{3,1},{4,6},{5,7},{6,4},{7,5},{8,10},{9,11},{10,... | collective-permute-start | bytes 589832 | tf_op jit(solution)/shard_map/ppermute | solution.py:380
  30.9 26.4 %collective-permute-start.6 = (bf16[4,2,64,128]{3,2,1,0:T(8,128)(2,1)S(1)}, bf16[4,2,64,128]{3,2,1,0:T(8,128)(2,1)S(1)}, u32[]{:S(2)}, u32[]{:S(2)}) collective-permute-start(bf16[4,2,64,128]{3,2,1,0:T(8,128)(2,1)S(1)} %get-tuple-element.81), channel_id=1, source_target_pairs={{0,8},{8,0},{16,24},{24,16},{1,9},{9,1},{17,25},{25,17},{2,10},{10... | collective-permute-start | bytes 393224 | tf_op jit(solution)/shard_map/ppermute | solution.py:391
  37.1 21.2 %collective-permute-start.7 = (bf16[4,2,64,128]{3,2,1,0:T(8,128)(2,1)S(1)}, bf16[4,2,64,128]{3,2,1,0:T(8,128)(2,1)S(1)}, u32[]{:S(2)}, u32[]{:S(2)}) collective-permute-start(bf16[4,2,64,128]{3,2,1,0:T(8,128)(2,1)S(1)} %get-tuple-element.80), channel_id=1, source_target_pairs={{0,24},{8,16},{16,8},{24,0},{1,25},{9,17},{17,9},{25,1},{2,26},{10... | collective-permute-start | bytes 393224 | tf_op jit(solution)/shard_map/ppermute | solution.py:392
  40.8 6.4 %collective-permute-start.18 = (bf16[3,256,128]{2,1,0:T(8,128)(2,1)S(1)}, bf16[3,256,128]{2,1,0:T(8,128)(2,1)S(1)}, u32[]{:S(2)}, u32[]{:S(2)}) collective-permute-start(bf16[3,256,128]{2,1,0:T(8,128)(2,1)S(1)} %collective-permute-done.17.refs_2_), channel_id=1, source_target_pairs={{0,2},{1,3},{2,0},{3,1},{4,6},{5,7},{6,4},{7,5},{8,10},{9,11},{10,... | collective-permute-start | bytes 589832 | tf_op jit(solution)/shard_map/ppermute | solution.py:380
  47.2 30.8 %collective-permute-start.19 = (bf16[4,1,64,128]{3,2,1,0:T(8,128)(2,1)S(1)}, bf16[4,1,64,128]{3,2,1,0:T(8,128)(2,1)S(1)}, u32[]{:S(2)}, u32[]{:S(2)}) collective-permute-start(bf16[4,1,64,128]{3,2,1,0:T(8,128)(2,1)S(1)} %get-tuple-element.107), channel_id=1, source_target_pairs={{0,8},{8,0},{16,24},{24,16},{1,9},{9,1},{17,25},{25,17},{2,10},{10... | collective-permute-start | bytes 196616 | tf_op jit(solution)/shard_map/ppermute | solution.py:391
  48.4 29.7 %collective-permute-start.20 = (bf16[4,1,64,128]{3,2,1,0:T(8,128)(2,1)S(1)}, bf16[4,1,64,128]{3,2,1,0:T(8,128)(2,1)S(1)}, u32[]{:S(2)}, u32[]{:S(2)}) collective-permute-start(bf16[4,1,64,128]{3,2,1,0:T(8,128)(2,1)S(1)} %get-tuple-element.106), channel_id=1, source_target_pairs={{0,24},{8,16},{16,8},{24,0},{1,25},{9,17},{17,9},{25,1},{2,26},{10... | collective-permute-start | bytes 196616 | tf_op jit(solution)/shard_map/ppermute | solution.py:392
  54.1 13.9 %collective-permute-start.26 = (bf16[4,2,64,128]{3,2,1,0:T(8,128)(2,1)S(1)}, bf16[4,2,64,128]{3,2,1,0:T(8,128)(2,1)S(1)}, u32[]{:S(2)}, u32[]{:S(2)}) collective-permute-start(bf16[4,2,64,128]{3,2,1,0:T(8,128)(2,1)S(1)} %get-tuple-element.79), channel_id=1, source_target_pairs={{0,8},{8,0},{16,24},{24,16},{1,9},{9,1},{17,25},{25,17},{2,10},{10... | collective-permute-start | bytes 393224 | tf_op jit(solution)/shard_map/ppermute | solution.py:391
  57.3 10.8 %collective-permute-start.27 = (bf16[4,2,64,128]{3,2,1,0:T(8,128)(2,1)S(1)}, bf16[4,2,64,128]{3,2,1,0:T(8,128)(2,1)S(1)}, u32[]{:S(2)}, u32[]{:S(2)}) collective-permute-start(bf16[4,2,64,128]{3,2,1,0:T(8,128)(2,1)S(1)} %get-tuple-element.78), channel_id=1, source_target_pairs={{0,24},{8,16},{16,8},{24,0},{1,25},{9,17},{17,9},{25,1},{2,26},{10... | collective-permute-start | bytes 393224 | tf_op jit(solution)/shard_map/ppermute | solution.py:392
  60.5 10.0 %collective-permute-start.12 = (bf16[1,256,128]{2,1,0:T(8,128)(2,1)S(1)}, bf16[1,256,128]{2,1,0:T(8,128)(2,1)S(1)}, u32[]{:S(2)}, u32[]{:S(2)}) collective-permute-start(bf16[1,256,128]{2,1,0:T(8,128)(2,1)S(1)} %get-tuple-element.56.refs_0_), channel_id=1, source_target_pairs={{0,6},{1,7},{2,4},{3,5},{4,2},{5,3},{6,0},{7,1},{8,14},{9,15},{10,... | collective-permute-start | bytes 196616 | tf_op jit(solution)/shard_map/ppermute | solution.py:376
  68.0 5.2 %collective-permute-start.11 = (bf16[1,256,128]{2,1,0:T(8,128)(2,1)S(1)}, bf16[1,256,128]{2,1,0:T(8,128)(2,1)S(1)}, u32[]{:S(2)}, u32[]{:S(2)}) collective-permute-start(bf16[1,256,128]{2,1,0:T(8,128)(2,1)S(1)} %get-tuple-element.56.refs_0_), channel_id=1, source_target_pairs={{0,4},{1,5},{2,6},{3,7},{4,0},{5,1},{6,2},{7,3},{8,12},{9,13},{10,... | collective-permute-start | bytes 196616 | tf_op jit(solution)/shard_map/ppermute | solution.py:376
  73.3 5.8 %collective-permute-start.13 = (bf16[4,1,64,128]{3,2,1,0:T(8,128)(2,1)S(1)}, bf16[4,1,64,128]{3,2,1,0:T(8,128)(2,1)S(1)}, u32[]{:S(2)}, u32[]{:S(2)}) collective-permute-start(bf16[4,1,64,128]{3,2,1,0:T(8,128)(2,1)S(1)} %get-tuple-element.109), channel_id=1, source_target_pairs={{0,8},{8,0},{16,24},{24,16},{1,9},{9,1},{17,25},{25,17},{2,10},{10... | collective-permute-start | bytes 196616 | tf_op jit(solution)/shard_map/ppermute | solution.py:391
  81.4 6.2 %collective-permute-start.23 = (bf16[1,256,128]{2,1,0:T(8,128)(2,1)S(1)}, bf16[1,256,128]{2,1,0:T(8,128)(2,1)S(1)}, u32[]{:S(2)}, u32[]{:S(2)}) collective-permute-start(bf16[1,256,128]{2,1,0:T(8,128)(2,1)S(1)} %get-tuple-element.61.refs_0_), channel_id=1, source_target_pairs={{0,6},{1,7},{2,4},{3,5},{4,2},{5,3},{6,0},{7,1},{8,14},{9,15},{10,... | collective-permute-start | bytes 196616 | tf_op jit(solution)/shard_map/ppermute | solution.py:376
  82.9 6.0 %collective-permute-start.22 = (bf16[1,256,128]{2,1,0:T(8,128)(2,1)S(1)}, bf16[1,256,128]{2,1,0:T(8,128)(2,1)S(1)}, u32[]{:S(2)}, u32[]{:S(2)}) collective-permute-start(bf16[1,256,128]{2,1,0:T(8,128)(2,1)S(1)} %get-tuple-element.61.refs_0_), channel_id=1, source_target_pairs={{0,4},{1,5},{2,6},{3,7},{4,0},{5,1},{6,2},{7,3},{8,12},{9,13},{10,... | collective-permute-start | bytes 196616 | tf_op jit(solution)/shard_map/ppermute | solution.py:376
  83.6 5.4 %collective-permute-start.21 = (bf16[1,256,128]{2,1,0:T(8,128)(2,1)S(1)}, bf16[1,256,128]{2,1,0:T(8,128)(2,1)S(1)}, u32[]{:S(2)}, u32[]{:S(2)}) collective-permute-start(bf16[1,256,128]{2,1,0:T(8,128)(2,1)S(1)} %get-tuple-element.61.refs_0_), channel_id=1, source_target_pairs={{0,2},{1,3},{2,0},{3,1},{4,6},{5,7},{6,4},{7,5},{8,10},{9,11},{10,... | collective-permute-start | bytes 196616 | tf_op jit(solution)/shard_map/ppermute | solution.py:376
  89.0 5.8 %collective-permute-start.24 = (bf16[4,1,64,128]{3,2,1,0:T(8,128)(2,1)S(1)}, bf16[4,1,64,128]{3,2,1,0:T(8,128)(2,1)S(1)}, u32[]{:S(2)}, u32[]{:S(2)}) collective-permute-start(bf16[4,1,64,128]{3,2,1,0:T(8,128)(2,1)S(1)} %get-tuple-element.105), channel_id=1, source_target_pairs={{0,8},{8,0},{16,24},{24,16},{1,9},{9,1},{17,25},{25,17},{2,10},{10... | collective-permute-start | bytes 196616 | tf_op jit(solution)/shard_map/ppermute | solution.py:391
  89.8 5.2 %collective-permute-start.25 = (bf16[4,1,64,128]{3,2,1,0:T(8,128)(2,1)S(1)}, bf16[4,1,64,128]{3,2,1,0:T(8,128)(2,1)S(1)}, u32[]{:S(2)}, u32[]{:S(2)}) collective-permute-start(bf16[4,1,64,128]{3,2,1,0:T(8,128)(2,1)S(1)} %get-tuple-element.104), channel_id=1, source_target_pairs={{0,24},{8,16},{16,8},{24,0},{1,25},{9,17},{17,9},{25,1},{2,26},{10... | collective-permute-start | bytes 196616 | tf_op jit(solution)/shard_map/ppermute | solution.py:392
  96.2 6.1 %collective-permute-start.30 = (bf16[1,256,128]{2,1,0:T(8,128)(2,1)S(1)}, bf16[1,256,128]{2,1,0:T(8,128)(2,1)S(1)}, u32[]{:S(2)}, u32[]{:S(2)}) collective-permute-start(bf16[1,256,128]{2,1,0:T(8,128)(2,1)S(1)} %get-tuple-element.64.refs_0_), channel_id=1, source_target_pairs={{0,6},{1,7},{2,4},{3,5},{4,2},{5,3},{6,0},{7,1},{8,14},{9,15},{10,... | collective-permute-start | bytes 196616 | tf_op jit(solution)/shard_map/ppermute | solution.py:376
  98.7 5.2 %collective-permute-start.29 = (bf16[1,256,128]{2,1,0:T(8,128)(2,1)S(1)}, bf16[1,256,128]{2,1,0:T(8,128)(2,1)S(1)}, u32[]{:S(2)}, u32[]{:S(2)}) collective-permute-start(bf16[1,256,128]{2,1,0:T(8,128)(2,1)S(1)} %get-tuple-element.64.refs_0_), channel_id=1, source_target_pairs={{0,4},{1,5},{2,6},{3,7},{4,0},{5,1},{6,2},{7,3},{8,12},{9,13},{10,... | collective-permute-start | bytes 196616 | tf_op jit(solution)/shard_map/ppermute | solution.py:376
  105.2 5.2 %collective-permute-start.32 = (bf16[4,1,64,128]{3,2,1,0:T(8,128)(2,1)S(1)}, bf16[4,1,64,128]{3,2,1,0:T(8,128)(2,1)S(1)}, u32[]{:S(2)}, u32[]{:S(2)}) collective-permute-start(bf16[4,1,64,128]{3,2,1,0:T(8,128)(2,1)S(1)} %get-tuple-element.102), channel_id=1, source_target_pairs={{0,24},{8,16},{16,8},{24,0},{1,25},{9,17},{17,9},{25,1},{2,26},{10... | collective-permute-start | bytes 196616 | tf_op jit(solution)/shard_map/ppermute | solution.py:392
  111.7 8.9 %collective-permute-start.33 = (bf16[128,128]{1,0:T(8,128)(2,1)S(1)}, bf16[128,128]{1,0:T(8,128)(2,1)S(1)}, u32[]{:S(2)}, u32[]{:S(2)}) collective-permute-start(bf16[128,128]{1,0:T(8,128)(2,1)S(1)} %bitcast.164), channel_id=1, source_target_pairs={{0,2},{1,3},{2,0},{3,1},{4,6},{5,7},{6,4},{7,5},{8,10},{9,11},{10,... | collective-permute-start | bytes 98312 | tf_op jit(solution)/shard_map/ppermute | solution.py:463
  113.2 7.4 %collective-permute-start.34 = (bf16[128,128]{1,0:T(8,128)(2,1)S(1)}, bf16[128,128]{1,0:T(8,128)(2,1)S(1)}, u32[]{:S(2)}, u32[]{:S(2)}) collective-permute-start(bf16[128,128]{1,0:T(8,128)(2,1)S(1)} %bitcast.165), channel_id=1, source_target_pairs={{0,4},{1,5},{2,6},{3,7},{4,0},{5,1},{6,2},{7,3},{8,12},{9,13},{10,... | collective-permute-start | bytes 98312 | tf_op jit(solution)/shard_map/ppermute | solution.py:463
  114.9 5.7 %collective-permute-start.35 = (bf16[128,128]{1,0:T(8,128)(2,1)S(1)}, bf16[128,128]{1,0:T(8,128)(2,1)S(1)}, u32[]{:S(2)}, u32[]{:S(2)}) collective-permute-start(bf16[128,128]{1,0:T(8,128)(2,1)S(1)} %bitcast.166), channel_id=1, source_target_pairs={{0,6},{1,7},{2,4},{3,5},{4,2},{5,3},{6,0},{7,1},{8,14},{9,15},{10,... | collective-permute-start | bytes 98312 | tf_op jit(solution)/shard_map/ppermute | solution.py:463
  120.6 7.7 %collective-permute-start.36 = (bf16[4,1,64,128]{3,2,1,0:T(8,128)(2,1)S(1)}, bf16[4,1,64,128]{3,2,1,0:T(8,128)(2,1)S(1)}, u32[]{:S(2)}, u32[]{:S(2)}) collective-permute-start(bf16[4,1,64,128]{3,2,1,0:T(8,128)(2,1)S(1)} %get-tuple-element.101), channel_id=1, source_target_pairs={{0,8},{8,0},{16,24},{24,16},{1,9},{9,1},{17,25},{25,17},{2,10},{10... | collective-permute-start | bytes 196616 | tf_op jit(solution)/shard_map/ppermute | solution.py:391
  121.5 6.8 %collective-permute-start.37 = (bf16[4,1,64,128]{3,2,1,0:T(8,128)(2,1)S(1)}, bf16[4,1,64,128]{3,2,1,0:T(8,128)(2,1)S(1)}, u32[]{:S(2)}, u32[]{:S(2)}) collective-permute-start(bf16[4,1,64,128]{3,2,1,0:T(8,128)(2,1)S(1)} %get-tuple-element.100), channel_id=1, source_target_pairs={{0,24},{8,16},{16,8},{24,0},{1,25},{9,17},{17,9},{25,1},{2,26},{10... | collective-permute-start | bytes 196616 | tf_op jit(solution)/shard_map/ppermute | solution.py:392
  (11 other events, 42.5 us)
